TPU v7x, 256 devices: a 4x2x16 block of a 4x16x16 slice. The times are simulated.
256 devices in a mesh: groups: 2 (over y), tensor: 128 (over x, z, core).
Axes of the slice: x: 4, y: 2, z: 16, core: 2. Of those that a mesh axis runs over, the one named last changes fastest.
The devices are a block of a 4x16x16 slice.
Arguments:
- hidden_in: bfloat16 [32, 16384], P('groups', 'tensor'), parts along dimension 0, may hold values from -0.59765625 to 0.59765625
- norm_gain: bfloat16 [16384], P('tensor'), may hold values from 0.5 to 1.5
- w_q: bfloat16 [16384, 16384], P('tensor'), may hold values from -1 to 256
- w_kv: bfloat16 [16384, 2048], P('tensor'), may hold values from -0.046875 to 0.046875
- w_o: bfloat16 [16384, 16384], P(None, 'tensor'), may hold values from -0.046875 to 0.046875
- kv_cache: bfloat16 [8, 32, 2, 4096, 128], P(None, 'groups', None, 'tensor'), parts along dimension 1, may hold values from -8 to 8
- lengths: int32 [32], P('groups'), parts along dimension 0, may hold values from 2 to 4096, as said below
- slab_index: int32 [8, 32], P(None, 'groups'), parts along dimension 1, may hold values from 0 to 15, each once within a row
Outputs:
- hidden_out: bfloat16 [32, 16384], P('groups', 'tensor'), parts along dimension 0
There are 2 independent parts, one for each index of `groups`. A program takes and returns all parts, laid end to end along the dimension named above; an argument that names none is the same for every part. Nothing has to cross between parts.
Inputs may be any that keep to these rules, and one draw needn't show every extreme that they name: `lengths`: one request in every draw has exactly 4096 cached tokens.
All inputs are finite; a program needn't handle non-finite values.
Results may differ from a plain program's by a relative error of at most 0.0085.
The roundings to bfloat16 on the way count: a program that leaves them out, or rounds other values in their place, can miss the bound.
Values may be sent and summed in bfloat16 or wider, within the bound.
No kernel may reach another device: no remote copies, remote signals or barrier semaphores. Data moves between devices by JAX's collectives and lax.ppermute only.
A program may use at most 64 MiB of HBM per device.

v0:
```python
import functools

import jax
import jax.numpy as jnp
from jax import lax
from jax.sharding import Mesh
from jax.sharding import PartitionSpec as P

KVH = 8
HD = 128
GROUP = 16
TENSOR = ("tensor_0", "tensor_1", "tensor_2")


epsilon = 1e-05
rope_base = 500000.0


def by_axis(value, axes):
    return functools.reduce(lax.psum, axes, value)


def reduced_to_own(blocks, axes, order):
    inside = blocks.shape[1:]
    blocks = blocks.reshape(*(lax.axis_size(a) for a in axes), *inside)
    blocks = jnp.moveaxis(blocks, order, range(len(axes))).reshape(-1, *inside)
    for k in order:
        blocks = lax.psum_scatter(blocks, axes[k], scatter_dimension=0, tiled=True)
    return blocks[0]


def split_up(value, dim, length):
    before, after = (value.shape[:dim], value.shape[dim + 1 :])
    return jnp.moveaxis(value.reshape(*before, length, -1, *after), dim, 0)


def sum_by_axis(value, axes, order, dim):
    length = lax.axis_size(axes)
    return reduced_to_own(split_up(value, dim, length), axes, order)


def laid_out(blocks, dim):
    shape = list(blocks.shape[1:])
    shape[dim] *= blocks.shape[0]
    return jnp.moveaxis(blocks, 0, dim).reshape(shape)


def gather_in_order(value, axes, order):
    blocks = value
    for k in order:
        blocks = lax.all_gather(blocks, axes[k])
    done = order[::-1]
    back = [done.index(k) for k in range(len(axes))]
    blocks = blocks.transpose(*back, *range(len(axes), blocks.ndim))
    return blocks.reshape(-1, *value.shape)


def whole_of(value, axes, order, dim):
    return laid_out(gather_in_order(value, axes, order), dim)


def rotate(values, position):
    head_dim = values.shape[-1]
    half_dim = head_dim // 2
    frequency = rope_base ** (-2.0 * jnp.arange(half_dim, dtype=jnp.float32) / head_dim)
    angles = position[..., None] * frequency
    cosine = jnp.cos(angles)
    sines = jnp.sin(angles)
    lower_half = values[..., :half_dim]
    upper_half = values[..., half_dim:]
    return jnp.concatenate(
        [lower_half * cosine - upper_half * sines, upper_half * cosine + lower_half * sines],
        axis=-1,
    )


def body(hidden_in, norm_gain, w_q, w_kv, w_o, kv_cache, lengths, slab_index):
    my_index = lax.axis_index(TENSOR)
    requests = hidden_in.shape[0]
    model_width = KVH * GROUP * HD
    query_width = GROUP * HD
    stream = hidden_in.astype(jnp.float32)
    squares = by_axis(jnp.sum(stream * stream, axis=1), TENSOR)
    normed = (
        stream * lax.rsqrt(squares[:, None] / model_width + epsilon) * norm_gain.astype(jnp.float32)
    ).astype(jnp.bfloat16)
    part_q = jnp.dot(normed, w_q, preferred_element_type=jnp.float32)
    part_kv = jnp.dot(normed, w_kv, preferred_element_type=jnp.float32)
    counter = jnp.arange(requests, dtype=jnp.int32)
    slab_match = (slab_index[:, None, :] == counter[None, :, None]).astype(jnp.int32)
    inverse = jnp.sum(slab_match * counter[None, None, :], axis=2)
    kv_rows = jnp.transpose(part_kv.reshape(requests, 2, KVH, HD), (0, 2, 1, 3)).reshape(
        requests, KVH, 2 * HD
    )
    proj_rows = jnp.concatenate([part_q.reshape(requests, KVH, query_width), kv_rows], axis=2)
    proj_rows = jnp.take_along_axis(
        jnp.transpose(proj_rows, (1, 0, 2)), inverse[:, :, None], axis=1
    )
    proj_rows = proj_rows.reshape(KVH * requests, query_width + 2 * HD)
    my_row = sum_by_axis(proj_rows, TENSOR, (2, 1, 0), 0)[0]
    slab_pos = my_index % requests
    head_pos = my_index // requests
    request = inverse[head_pos, slab_pos]
    length = lengths[request]
    position = length.astype(jnp.float32)
    q_row = rotate(my_row[:query_width].reshape(GROUP, HD), position).astype(jnp.bfloat16)
    k_row = rotate(my_row[query_width : query_width + HD], position).astype(jnp.bfloat16)
    v_row = my_row[query_width + HD :].astype(jnp.bfloat16)
    score_scale = 1.0 / HD**0.5
    local_cache = kv_cache.reshape(KVH * kv_cache.shape[1], 2, kv_cache.shape[3], HD)
    slab_data = lax.all_to_all(local_cache, TENSOR, split_axis=0, concat_axis=2, tiled=True)[0]
    full_len = slab_data.shape[1]
    scores = (
        jnp.einsum("gd,pd->gp", q_row, slab_data[0], preferred_element_type=jnp.float32)
        * score_scale
    )
    new_score = jnp.dot(q_row, k_row, preferred_element_type=jnp.float32) * score_scale
    visible = jnp.arange(full_len, dtype=jnp.int32)[None, :] < length
    row_max = jnp.maximum(jnp.max(jnp.where(visible, scores, -1e30), axis=1), new_score)
    weights = jnp.where(visible, jnp.exp(scores - row_max[:, None]), 0.0)
    new_weight = jnp.exp(new_score - row_max)
    denominator = jnp.sum(weights, axis=1) + new_weight
    weighted = jnp.dot(
        weights.astype(jnp.bfloat16), slab_data[1], preferred_element_type=jnp.float32
    )
    weighted = (
        weighted
        + new_weight.astype(jnp.bfloat16).astype(jnp.float32)[:, None]
        * v_row.astype(jnp.float32)[None, :]
    )
    out_row = (weighted / denominator[:, None]).astype(jnp.bfloat16).reshape(1, query_width)
    gathered = whole_of(out_row, TENSOR, (0, 1, 2), 0)
    ordered = jnp.take_along_axis(
        gathered.reshape(KVH, requests, query_width), slab_index[:, :, None], axis=1
    )
    attention = jnp.transpose(ordered, (1, 0, 2)).reshape(requests, model_width)
    result = stream + jnp.dot(attention, w_o, preferred_element_type=jnp.float32)
    return result.astype(jnp.bfloat16)


def solution(mesh):
    torus = Mesh(
        mesh.devices.reshape(mesh.shape["groups"], 4, 16, 2),
        ("groups", "tensor_0", "tensor_1", "tensor_2"),
    )
    placed = (
        P("groups", TENSOR),
        P(TENSOR),
        P(TENSOR, None),
        P(TENSOR, None),
        P(None, TENSOR),
        P(None, "groups", None, TENSOR, None),
        P("groups"),
        P(None, "groups"),
    )
    return jax.shard_map(
        body, mesh=torus, in_specs=placed, out_specs=P("groups", TENSOR), check_vma=False
    )
```

profile of v0, /device:TPU:33, one launch (start us, length us, event | category | flops | bytes accessed | tf_op | source)
XLA Modules:
  0.0 424.8 jit_solution(6418112302490340078)
XLA Ops:
  6.6 31.5 %all-to-all-start = ((bf16[128,2,32,128]{3,2,1,0:T(8,128)(2,1)}), bf16[128,2,32,128]{3,2,1,0:T(8,128)(2,1)}, u32[]{:S(2)}, u32[]{:S(2)}) async-start(bf16[128,2,32,128]{3,2,1,0:T(8,128)(2,1)} %bitcast.89), calls=%async_computation | async-start | bytes 4194304 | tf_op jit(solution)/shard_map/all_to_all | solution.py:111
  38.1 0.1 fusion.10
  38.3 10.8 %psum.21 = f32[16]{0:T(128)S(1)} all-reduce(f32[16]{0:T(128)S(1)} %fusion.10), channel_id=1, replica_groups=mesh['groups'=2,'tensor_0'=4,'tensor_1'=16,'tensor_2'=2] {'tensor_0'}, use_global_device_ids=true, to_apply=%region_2.0 | all-reduce | flops 16 | bytes 128 | tf_op jit(solution)/shard_map/psum | solution.py:20
  49.1 97.3 %psum.22 = f32[16]{0:T(128)S(1)} all-reduce(f32[16]{0:T(128)S(1)} %psum.21), channel_id=1, replica_groups=mesh['groups'=2,'tensor_0'=4,'tensor_1'=16,'tensor_2'=2] {'tensor_1'}, use_global_device_ids=true, to_apply=%region_3.0 | all-reduce | flops 16 | bytes 128 | tf_op jit(solution)/shard_map/psum | solution.py:20
  146.4 7.8 %psum.23 = f32[16]{0:T(128)S(1)} all-reduce(f32[16]{0:T(128)S(1)} %psum.22), channel_id=1, replica_groups=mesh['groups'=2,'tensor_0'=4,'tensor_1'=16,'tensor_2'=2] {'tensor_2'}, use_global_device_ids=true, to_apply=%region_4.0 | all-reduce | flops 16 | bytes 128 | tf_op jit(solution)/shard_map/psum | solution.py:20
  154.2 2.9 fusion.17
  157.1 0.1 copy.42
  157.2 0.2 convolution_bitcast_fusion
  157.5 0.1 reshape.109
  157.7 0.2 copy-done.2
  157.9 0.2 select_reduce_fusion.1
  158.3 0.1 maximum_bitcast_fusion
  158.4 2.0 gather_fusion
  160.4 0.7 gather.13
  161.1 0.6 select_bitcast_fusion
  161.7 2.3 copy.31
  164.1 0.6 dynamic_slice.6
  166.6 0.6 dynamic_slice.7
  167.9 0.6 dynamic-slice
  168.5 0.7 dynamic-slice.2
  169.2 0.6 dynamic-slice.4
  170.4 33.4 %all-reduce.6.cloned.1.call-done = f32[128,1,2304]{2,1,0:T(1,128)} async-done(((f32[128,1,2304]{2,1,0:T(1,128)}), f32[128,1,2304]{2,1,0:T(1,128)}) %all-reduce.6.cloned.1.call-update) | async-done | bytes 1179664
  203.8 2.0 constant_dynamic-slice_fusion.5
  205.9 0.1 copy.28
  206.8 0.7 iota_compare_fusion.1
  207.4 123.5 %all-reduce.8.cloned.1.call-done = f32[64,1,2304]{2,1,0:T(1,128)} async-done(((f32[64,1,2304]{2,1,0:T(1,128)}), f32[64,1,2304]{2,1,0:T(1,128)}) %all-reduce.8.cloned.1.call-update) | async-done | bytes 589840
  330.9 0.8 constant_dynamic-slice_fusion.4
  331.7 13.6 %all-reduce.2 = f32[4,1,2304]{2,1,0:T(1,128)S(1)} all-reduce(f32[4,1,2304]{2,1,0:T(1,128)S(1)} %constant_dynamic-slice_fusion.4), channel_id=6, replica_groups=mesh['groups'=2,'tensor_0'=4,'tensor_1'=16,'tensor_2'=2] {'tensor_0'}, use_global_device_ids=true, to_apply=%region_7.8.clone | all-reduce | flops 9216 | bytes 73728
  345.3 0.6 fusion.21
  346.0 0.6 subtract_convert_fusion.1
  346.6 0.6 constant_dynamic-slice_fusion.2
  347.3 1.9 fusion.32
  349.2 0.5 select_reduce_fusion
  349.7 0.2 convert_convert_fusion
  349.9 0.3 fusion.4
  350.2 0.3 fusion.1
  350.5 9.3 %all_gather.15 = bf16[4,1,2048]{2,1,0:T(2,128)(2,1)S(1)} all-gather(bf16[1,1,2048]{2,1,0:T(2,128)(2,1)S(1)} %all_gather_reshape.3), channel_id=1, replica_groups=mesh['groups'=2,'tensor_0'=4,'tensor_1'=16,'tensor_2'=2] {'tensor_0'}, dimensions={0}, use_global_device_ids=true | all-gather | bytes 20480 | tf_op jit(solution)/shard_map/all_gather | solution.py:51
  359.8 23.1 %all-gather = bf16[64,1,2048]{2,1,0:T(2,128)(2,1)S(1)} all-gather(bf16[4,1,2048]{2,1,0:T(2,128)(2,1)S(1)} %all_gather.15), channel_id=2, replica_groups=mesh['groups'=2,'tensor_0'=4,'tensor_1'=16,'tensor_2'=2] {'tensor_1'}, dimensions={0}, use_global_device_ids=true | all-gather | bytes 278528 | tf_op jit(solution)/shard_map/all_gather | solution.py:51
  382.9 1.5 reduce
  384.4 0.1 reshape.127
  384.5 25.9 %all-gather.1 = bf16[32,4,1,2048]{3,1,2,0:T(4,128)(2,1)S(1)} all-gather(bf16[16,4,1,2048]{3,1,2,0:T(4,128)(2,1)S(1)} %bitcast.92), channel_id=3, replica_groups=mesh['groups'=2,'tensor_0'=4,'tensor_1'=16,'tensor_2'=2] {'tensor_2'}, dimensions={0}, use_global_device_ids=true | all-gather | bytes 786432 | tf_op jit(solution)/shard_map/all_gather | solution.py:51
  410.4 0.3 copy.33
  410.7 0.5 copy.34
  411.2 0.2 reshape_reshape_reshape.4
  411.4 2.4 gather_fusion.1
  413.8 0.3 bitcast_select_fusion
  414.2 0.3 copy.39
  414.5 3.5 fusion.2
  (35 shorter events, 0.8 us)
Async XLA Ops:
  6.5 150.6 %copy-start = (bf16[128,2048]{1,0:T(8,128)(2,1)S(1)}, bf16[128,2048]{1,0:T(8,128)(2,1)}, u32[]{:S(2)}) copy-start(bf16[128,2048]{1,0:T(8,128)(2,1)} %param.11) | copy-start | bytes 1572868
  6.6 31.6 %copy-start.3 = (bf16[128]{0:T(256)(128)(2,1)S(1)}, bf16[128]{0:T(256)(128)(2,1)}, u32[]{:S(2)}) copy-start(bf16[128]{0:T(256)(128)(2,1)} %param.9) | copy-start | bytes 772
  6.6 31.6 %copy-start.1 = (bf16[16,128]{1,0:T(8,128)(2,1)S(1)}, bf16[16,128]{1,0:T(8,128)(2,1)}, u32[]{:S(2)}) copy-start(bf16[16,128]{1,0:T(8,128)(2,1)} %param.8) | copy-start | bytes 12292
  6.6 340.7 %all-to-all-start = ((bf16[128,2,32,128]{3,2,1,0:T(8,128)(2,1)}), bf16[128,2,32,128]{3,2,1,0:T(8,128)(2,1)}, u32[]{:S(2)}, u32[]{:S(2)}) async-start(bf16[128,2,32,128]{3,2,1,0:T(8,128)(2,1)} %bitcast.89), calls=%async_computation | async-start | bytes 4194304 | tf_op jit(solution)/shard_map/all_to_all | solution.py:111
  38.0 165.8 %all-reduce.6.cloned.1.call-start = ((), (), s32[]{:S(2)}) async-start(), calls=%async_computation.1 | async-start | bytes 2359296
  157.2 0.7 copy-start.2
  163.9 2.7 copy-start.4
  163.9 4.0 copy-start.7
  163.9 4.6 %copy-start.6 = (u32[256]{0:T(256)S(1)}, u32[256]{0:T(256)}, u32[]{:S(2)}) copy-start(u32[256]{0:T(256)} %constant.126) | copy-start | bytes 3076
  163.9 5.3 %copy-start.5 = (u32[256]{0:T(256)S(1)}, u32[256]{0:T(256)}, u32[]{:S(2)}) copy-start(u32[256]{0:T(256)} %constant.130) | copy-start | bytes 3076
  164.0 166.9 %all-reduce.8.cloned.1.call-start = ((), (), s32[]{:S(2)}) async-start(), calls=%async_computation.2 | async-start | bytes 1179648
Sparse Core Ops, SparseCore 0:
  164.1 39.6 all-reduce.5
  206.2 124.6 all-reduce.7
where the time goes:
time: 425 us
  blocking collectives  188 us (44%)
  waiting for transfers between devices  157 us (37%)
  starting transfers between devices  31.6 us (7%)
  local copies, waits for them, and re-layouts  18 us (4%)
  between operations  17.7 us (4%)
  matrix products  7.66 us (2%)
  other arithmetic  5.23 us (1%)
    unnamed x4, waiting for transfers between devices  157 us
    psum x3, blocking collectives, by_axis(): return functools.reduce(lax.psum, axes, value)  116 us
    all_gather x3, blocking collectives, gather_in_order(): blocks = lax.all_gather(blocks, axes[k])  58.2 us
    all_to_all x1, starting transfers between devices, body(): lax.all_to_all(local_cache, TENSOR, split_axis=0, concat_axis=2, tiled=True)  31.5 us
    unnamed x1, blocking collectives  13.6 us
  transfers between devices with their start and end apart: 3, of which 2 were waited for; matrix products, arithmetic and copies ran while one was open for 4% of the time, Pallas kernels for 0%

commit v1 on v0

v1 whole, which is shorter than its diff:
```python
import functools

import jax
import jax.numpy as jnp
from jax import lax
from jax.experimental import pallas as pl
from jax.experimental.pallas import tpu as pltpu
from jax.sharding import Mesh
from jax.sharding import PartitionSpec as P

NX, NZ, NC = 4, 16, 2
KVH = NX * NC
HD = 128
GROUP = 16
ROWS = GROUP + 2
QW = GROUP * HD
PW = ROWS * HD
MODEL = KVH * QW
TENSOR = ("x", "z", "c")
MOVES = ((0, 0), (1, 0), (3, 0), (2, 0), (0, 1), (1, 1), (3, 1), (2, 1))

EPS = 1e-05
ROPE_BASE = 500000.0
SCALE = 1.0 / HD**0.5
NEG = -1e30


F32, BF16 = jnp.float32, jnp.bfloat16
VMEM = pl.BlockSpec(memory_space=pltpu.VMEM)
SMEM = pl.BlockSpec(memory_space=pltpu.SMEM)
HBM = pl.BlockSpec(memory_space=pltpu.HBM)
LIMIT = pltpu.CompilerParams(vmem_limit_bytes=16 * 2**20)


def struct(shape, dtype):
    return jax.ShapeDtypeStruct(shape, dtype)


def call(kernel, out, specs, *args, scratch=()):
    outs = jax.tree.map(lambda _: VMEM, out)
    return pl.pallas_call(
        kernel,
        in_specs=specs,
        out_specs=outs,
        out_shape=out,
        scratch_shapes=scratch,
        compiler_params=LIMIT,
    )(*args)


def diagonal(rows):
    lane = lax.broadcasted_iota(jnp.int32, (rows, HD), 1)
    return lane == lax.broadcasted_iota(jnp.int32, (rows, HD), 0)


def column(row, mask):
    return jnp.sum(jnp.where(mask, row, 0.0), axis=1, keepdims=True)


def as_row(col, mask):
    return jnp.sum(jnp.where(mask, col, 0.0), axis=0, keepdims=True)


def squares_kernel(x, out):
    stream = x[...].astype(F32)
    total = jnp.sum(stream * stream, axis=1, keepdims=True)
    out[...] = jnp.broadcast_to(as_row(total, diagonal(x.shape[0])), out.shape)


def fetch_in_kernel(place, wq, wkv, theirs, mine, sems):
    copies = []
    for k in range(2 * NX):
        out = theirs if k < NX else mine
        core = 1 - place[2] if k < NX else place[2]
        head = lax.rem(place[0] + k % NX, NX) * NC + core
        for part, (source, start, width, at) in enumerate(
            (
                (wq, head * QW, QW, 0),
                (wkv, head * HD, HD, QW),
                (wkv, (KVH + head) * HD, HD, QW + HD),
            )
        ):
            copy = pltpu.make_async_copy(
                source.at[:, pl.ds(pl.multiple_of(start, HD), width)],
                out.at[k % NX, :, pl.ds(at, width)],
                sems.at[k, part],
            )
            copy.start()
            copies.append(copy)
    for copy in copies:
        copy.wait()


def fetch_out_kernel(other, place, wo, out, sems):
    copies = []
    for k in range(NX):
        core = 1 - place[2] if other else place[2]
        head = lax.rem(place[0] + k, NX) * NC + core
        copy = pltpu.make_async_copy(
            wo.at[pl.ds(pl.multiple_of(head * QW, HD), QW)], out.at[k], sems.at[k]
        )
        copy.start()
        copies.append(copy)
    for copy in copies:
        copy.wait()


def fetch_cache_kernel(place, cache, *refs):
    outs, sems = refs[:-1], refs[-1]
    copies = []
    for k, (j, d) in enumerate(MOVES):
        core = 1 - place[2] if d else place[2]
        head = lax.rem(place[0] + j, NX) * NC + core
        copy = pltpu.make_async_copy(cache.at[head], outs[k], sems.at[k])
        copy.start()
        copies.append(copy)
    for copy in copies:
        copy.wait()


def project_first_kernel(sums, x, gain, w, normed_out, out):
    squares = column(jnp.sum(sums[...], axis=0, keepdims=True), diagonal(x.shape[0]))
    stream = x[...].astype(F32)
    normed = (stream * lax.rsqrt(squares / MODEL + EPS) * gain[...].astype(F32)).astype(BF16)
    normed_out[...] = normed
    for k in range(NX):
        out[k] = jnp.dot(normed, w[k], preferred_element_type=F32)


def project_kernel(normed, w, out):
    for k in range(NX):
        out[k] = jnp.dot(normed[...], w[k], preferred_element_type=F32)


def pair_sum_kernel(a, b, *outs):
    for k, out in enumerate(outs):
        out[...] = a[k] + b[k]


def x_sum_kernel(a, b, c, d, out):
    n = a.shape[0]
    for k in range(ROWS):
        cut = slice(k * HD, (k + 1) * HD)
        total = (a[:, cut] + b[:, cut]) + (c[:, cut] + d[:, cut])
        out[pl.ds(k, n, stride=ROWS), :] = total


def queries_kernel(parts, cosine, sine, q_out, new_score, new_value):
    n = parts.shape[0] // ROWS
    total = parts[:ROWS]
    for k in range(1, n):
        total = total + parts[k * ROWS : (k + 1) * ROWS]
    lead = total[: GROUP + 1]
    turned = lead * cosine[...] + pltpu.roll(lead, HD // 2, 1) * sine[...]
    turned = turned.astype(BF16)
    q = turned[:GROUP]
    q_out[...] = jnp.broadcast_to(q[None], q_out.shape)
    key = turned[GROUP : GROUP + 1].astype(F32)
    score = jnp.sum(q.astype(F32) * key, axis=1, keepdims=True) * SCALE
    new_score[...] = as_row(score, diagonal(GROUP))
    new_value[...] = total[GROUP + 1 :].astype(BF16).astype(F32)


def attend_kernel(lengths, place, slabs, q, *refs):
    caches, out = refs[:-1], refs[-1]
    local = caches[0].shape[2]
    count = len(caches) * local
    head = place[0] * NC + place[2]
    index = lax.broadcasted_iota(jnp.int32, (1, count), 1)
    start = jnp.zeros_like(index)
    for k, (j, d) in enumerate(MOVES):
        core = 1 - place[2] if d else place[2]
        block = (lax.rem(place[0] + (NX - j), NX) * NZ + place[1]) * NC + core
        start = jnp.where(index // local == k, block * local, start)
    position = start + index % local
    mask = diagonal(GROUP)
    for b in range(q.shape[0]):
        slab = slabs[head, b]
        keys = jnp.concatenate([cache[slab, 0] for cache in caches], axis=0)
        values = jnp.concatenate([cache[slab, 1] for cache in caches], axis=0)
        scores = SCALE * lax.dot_general(
            q[b], keys, (((1,), (1,)), ((), ())), preferred_element_type=F32
        )
        visible = position < lengths[b]
        top = jnp.max(jnp.where(visible, scores, NEG), axis=1, keepdims=True)
        weights = jnp.where(visible, jnp.exp(scores - top), 0.0)
        total = jnp.sum(weights, axis=1, keepdims=True)
        at = b * ROWS
        out[at : at + GROUP] = jnp.dot(
            weights.astype(BF16), values, preferred_element_type=F32
        )
        out[at + GROUP : at + GROUP + 1] = as_row(top, mask)
        out[at + GROUP + 1 : at + ROWS] = as_row(total, mask)


def combine_kernel(parts, new_score, new_value, out):
    n = parts.shape[0] // ROWS
    mask = diagonal(GROUP)
    lanes = lax.broadcasted_iota(jnp.int32, (1, HD), 1) < GROUP
    tops = parts[pl.ds(GROUP, n, stride=ROWS), :]
    totals = parts[pl.ds(GROUP + 1, n, stride=ROWS), :]
    fresh = new_score[...]
    top = jnp.maximum(jnp.max(tops, axis=0, keepdims=True), fresh)
    share = jnp.where(lanes, jnp.exp(tops - top), 0.0)
    fresh_weight = jnp.where(lanes, jnp.exp(fresh - top), 0.0)
    total = jnp.sum(share * totals, axis=0, keepdims=True) + fresh_weight
    weighted = column(fresh_weight, mask).astype(BF16).astype(F32) * new_value[...]
    for k in range(n):
        at = k * ROWS
        weighted = weighted + column(share[k : k + 1], mask) * parts[at : at + GROUP]
    done = (weighted / column(total, mask)).astype(BF16)
    out[...] = jnp.broadcast_to(done[None], out.shape)


def rows_kernel(heads, out, wide):
    wide[...] = heads[...].astype(F32)
    for k in range(GROUP):
        out[:, k * HD : (k + 1) * HD] = wide[:, k, :].astype(BF16)


def output_kernel(a, b, c, d, e, f, g, h, w_mine, w_theirs, x, out):
    total = x[...].astype(F32)
    for k, rows in enumerate((a, b, c, d)):
        total = total + jnp.dot(rows[...], w_mine[k], preferred_element_type=F32)
    for k, rows in enumerate((e, f, g, h)):
        total = total + jnp.dot(rows[...], w_theirs[k], preferred_element_type=F32)
    out[...] = total.astype(BF16)


def shift_x(value, by):
    return lax.ppermute(value, "x", [(i, (i + by) % NX) for i in range(NX)])


def swap_c(value):
    return lax.ppermute(value, "c", [(0, 1), (1, 0)])


def across_z(value):
    return lax.all_to_all(value, "z", 0, 0, tiled=True)


def step(hidden_in, norm_gain, w_q, w_kv, w_o, kv_cache, lengths, slab_index):
    n, depth = hidden_in.shape
    members = NX * NZ * NC
    w_q, w_kv, w_o, kv_cache = (
        pltpu.with_memory_space_constraint(v, pltpu.HBM) for v in (w_q, w_kv, w_o, kv_cache)
    )
    place = jnp.stack([lax.axis_index(a) for a in TENSOR]).astype(jnp.int32)

    position = lengths[lax.axis_index("z")].astype(F32)
    frequency = ROPE_BASE ** (-2.0 * jnp.arange(HD // 2, dtype=F32) / HD)
    angles = position * frequency
    cosine, sine = jnp.cos(angles), jnp.sin(angles)
    cosine = jnp.concatenate([cosine, cosine])[None]
    sine = jnp.concatenate([-sine, sine])[None]

    sums = call(squares_kernel, struct((members, HD), F32), [VMEM], hidden_in)
    sums = lax.all_to_all(
        sums.reshape(members, 1, HD), TENSOR, 0, 0, tiled=True
    ).reshape(members, HD)

    half = struct((NX, depth, PW), BF16)
    w_theirs, w_mine = call(
        fetch_in_kernel,
        [half, half],
        [SMEM, HBM, HBM],
        place,
        w_q,
        w_kv,
        scratch=[pltpu.SemaphoreType.DMA((2 * NX, 3))],
    )

    cache = list(call(
        fetch_cache_kernel,
        [struct(kv_cache.shape[1:], BF16)] * len(MOVES),
        [SMEM, HBM],
        place,
        kv_cache,
        scratch=[pltpu.SemaphoreType.DMA((len(MOVES),))],
    ))

    product = struct((NX, n, PW), F32)
    normed, sent = call(
        project_first_kernel,
        [struct((n, depth), BF16), product],
        [VMEM] * 4,
        sums,
        hidden_in,
        norm_gain[None],
        w_theirs,
    )
    got = swap_c(sent)
    kept = call(project_kernel, product, [VMEM] * 2, normed, w_mine)
    blocks = call(pair_sum_kernel, [struct((n, PW), F32)] * NX, [VMEM] * 2, kept, got)
    parts = [blocks[0]]
    for k in (1, 3, 2):
        parts.append(shift_x(blocks[k], k))
    rows = call(x_sum_kernel, struct((n * ROWS, HD), F32), [VMEM] * NX, *parts)
    for k, (j, d) in enumerate(MOVES[1:], 1):
        pairs = [
            (x * NC + c, (x + j) % NX * NC + (c + d) % NC)
            for x in range(NX)
            for c in range(NC)
        ]
        cache[k] = lax.ppermute(cache[k], ("x", "c"), pairs)
    rows = across_z(rows.reshape(n, 1, PW)).reshape(n * ROWS, HD)
    w_rows = []
    for other in (0, 1):
        w_rows.append(
            call(
                functools.partial(fetch_out_kernel, other),
                struct((NX, QW, w_o.shape[1]), BF16),
                [SMEM, HBM],
                place,
                w_o,
                scratch=[pltpu.SemaphoreType.DMA((NX,))],
            )
        )
    q, new_score, new_value = call(
        queries_kernel,
        [struct((n, GROUP, HD), BF16), struct((1, HD), F32), struct((1, HD), F32)],
        [VMEM] * 3,
        rows,
        cosine,
        sine,
    )
    q = across_z(q)

    partial = call(
        attend_kernel,
        struct((n * ROWS, HD), F32),
        [SMEM, SMEM, SMEM] + [VMEM] * (1 + len(MOVES)),
        lengths,
        place,
        slab_index,
        q,
        *cache,
    )
    partial = across_z(partial.reshape(n, 1, PW)).reshape(n * ROWS, HD)
    done = call(
        combine_kernel, struct((n, GROUP, HD), BF16), [VMEM] * 3, partial, new_score, new_value
    )
    done = across_z(done)
    done = call(
        rows_kernel,
        struct((n, QW), BF16),
        [VMEM],
        done,
        scratch=[pltpu.VMEM((n, GROUP, HD), F32)],
    )
    beside = {0: done}
    for k in (1, 3, 2):
        beside[k] = shift_x(done, -k)
    mine = [beside[k] for k in range(NX)]
    theirs = [swap_c(block) for block in mine]
    return call(
        output_kernel, struct((n, depth), BF16), [VMEM] * 11, *mine, *theirs, *w_rows, hidden_in
    )


def solution(mesh):
    torus = Mesh(
        mesh.devices.reshape(mesh.shape["groups"], NX, NZ, NC),
        ("groups",) + TENSOR,
    )
    placed = (
        P("groups", TENSOR),
        P(TENSOR),
        P(TENSOR, None),
        P(TENSOR, None),
        P(None, TENSOR),
        P(None, "groups", None, TENSOR, None),
        P("groups"),
        P(None, "groups"),
    )
    return jax.shard_map(
        step, mesh=torus, in_specs=placed, out_specs=P("groups", TENSOR), check_vma=False
    )
```

time: 425 us -> 167 us (0.39)
  blocking collectives: 188 us -> 32.1 us
  waiting for transfers between devices: 157 us -> 34.4 us
  starting transfers between devices: 31.6 us -> 75.3 us
  Pallas kernels: 0 us -> 19.3 us
  between operations: 17.7 us -> 0.85 us
  local copies, waits for them, and re-layouts: 18 us -> 4.36 us
  matrix products: 7.66 us -> 0 us
  other arithmetic: 5.23 us -> 0.33 us
    unnamed x4 -> x0, waiting for transfers between devices: 157 us -> none
    psum x3 -> x0, blocking collectives: 116 us -> none  [by_axis(): return functools.reduce(lax.psum, axes, value)]
    all_gather x3 -> x0, blocking collectives: 58.2 us -> none  [gather_in_order(): blocks = lax.all_gather(blocks, axes[k])]
    all_to_all x0 -> x2, blocking collectives: none -> 32.1 us  [across_z(): return lax.all_to_all(value, 'z', 0, 0, tiled=True)]
    ppermute x0 -> x18, starting transfers between devices: none -> 28.8 us  [the longest x7 10.2 us: step(): cache[k] = lax.ppermute(cache[k], ('x', 'c'), pairs)]
    all_to_all x1 -> x3, waiting for transfers between devices: 0.01 us -> 21.7 us  [the longest x2 11.3 us: across_z(): return lax.all_to_all(value, 'z', 0, 0, tiled=True)]
    pallas_call x0 -> x14, Pallas kernels: none -> 19.3 us  [call(): pl.pallas_call(kernel, in_specs=specs, out_specs=outs, out_shape=out, scr...]
    all_to_all x1 -> x3, starting transfers between devices: 31.5 us -> 46.5 us  [the longest x1 31 us: step(): lax.all_to_all(sums.reshape(members, 1, HD), TENSOR, 0, 0, tiled=True)]
  transfers between devices with their start and end apart: 3 -> 21, of which waited for: 2 -> 7; matrix products, arithmetic and copies ran while one was open for 4% -> 1% of each run, Pallas kernels for 0% -> 7%
where the time goes in v1:
time: 167 us
  starting transfers between devices  75.3 us (45%)
  waiting for transfers between devices  34.4 us (21%)
  blocking collectives  32.1 us (19%)
  Pallas kernels  19.3 us (12%)
  local copies, waits for them, and re-layouts  4.36 us (3%)
    all_to_all x2, blocking collectives, across_z(): return lax.all_to_all(value, 'z', 0, 0, tiled=True)  32.1 us
    all_to_all x1, starting transfers between devices, step(): lax.all_to_all(sums.reshape(members, 1, HD), TENSOR, 0, 0, tiled=True)  31 us
    pallas_call x14, Pallas kernels, call(): pl.pallas_call(kernel, in_specs=specs, out_specs=outs, out_shape=out, scr...  19.3 us
    all_to_all x2, starting transfers between devices, across_z(): return lax.all_to_all(value, 'z', 0, 0, tiled=True)  15.5 us
    all_to_all x2, waiting for transfers between devices, across_z(): return lax.all_to_all(value, 'z', 0, 0, tiled=True)  11.3 us
    all_to_all x1, waiting for transfers between devices, step(): lax.all_to_all(sums.reshape(members, 1, HD), TENSOR, 0, 0, tiled=True)  10.3 us
    ppermute x7, starting transfers between devices, step(): cache[k] = lax.ppermute(cache[k], ('x', 'c'), pairs)  10.2 us
    ppermute x5, starting transfers between devices, swap_c(): return lax.ppermute(value, 'c', [(0, 1), (1, 0)])  9.72 us
  transfers between devices with their start and end apart: 21, of which 7 were waited for; matrix products, arithmetic and copies ran while one was open for 1% of the time, Pallas kernels for 7%

profile of v1, /device:TPU:33, one launch (start us, length us, event | category | flops | bytes accessed | tf_op | source)
XLA Modules:
  0.0 166.7 jit_solution(5003103814990617115)
XLA Ops:
  0.0 0.7 copy-done.2
  0.7 0.7 shard_map.82
  1.4 31.0 %all-to-all-start = ((f32[128,1,128]{2,1,0:T(1,128)}), f32[128,1,128]{2,1,0:T(1,128)S(1)}, u32[]{:S(2)}, u32[]{:S(2)}) async-start(f32[128,1,128]{2,1,0:T(1,128)} %bitcast.4), calls=%async_computation | async-start | bytes 131072 | tf_op jit(solution)/shard_map/all_to_all | solution.py:258
  32.4 0.1 pad_add_fusion.place
  32.5 3.1 %shard_map.83 = (bf16[4,128,2304]{2,1,0:T(8,128)(2,1)S(1)}, bf16[4,128,2304]{2,1,0:T(8,128)(2,1)S(1)}) custom-call(s32[3]{0:T(128)S(1)} %pad_add_fusion.place, bf16[128,16384]{1,0:T(8,128)(2,1)} %wq.1, bf16[128,2048]{1,0:T(8,128)(2,1)} %wkv.1), custom_call_target="tpu_custom_call" | custom-call | tf_op jit(solution)/shard_map/pallas_call | solution.py:41
  35.6 1.4 copy-done
  37.0 10.3 %all-to-all-done = f32[128,1,128]{2,1,0:T(1,128)S(1)} async-done(((f32[128,1,128]{2,1,0:T(1,128)}), f32[128,1,128]{2,1,0:T(1,128)S(1)}, u32[]{:S(2)}, u32[]{:S(2)}) %all-to-all-start) | async-done | bytes 65568 | tf_op jit(solution)/shard_map/all_to_all | solution.py:258
  47.4 1.7 copy-done.1
  49.0 0.5 shard_map.84
  49.5 1.4 collective-permute-start
  50.9 0.4 shard_map.85.a
  51.4 1.2 collective-permute-done.b
  52.6 0.1 shard_map.86
  52.6 0.1 collective-permute-start.1
  52.8 2.6 %collective-permute-start.2 = (f32[16,2304]{1,0:T(8,128)S(1)}, f32[16,2304]{1,0:T(8,128)S(1)}, u32[]{:S(2)}, u32[]{:S(2)}) collective-permute-start(f32[16,2304]{1,0:T(8,128)S(1)} %get-tuple-element.30), channel_id=1, source_target_pairs={{0,96},{32,0},{64,32},{96,64},{1,97},{33,1},{65,33},{97,65},{2,98}... | collective-permute-start | bytes 442376 | tf_op jit(solution)/shard_map/ppermute | solution.py:231
  55.4 0.1 collective-permute-start.3
  55.5 3.5 %collective-permute-done.1.b = f32[16,2304]{1,0:T(8,128)S(1)} collective-permute-done((f32[16,2304]{1,0:T(8,128)S(1)}, f32[16,2304]{1,0:T(8,128)S(1)}, u32[]{:S(2)}, u32[]{:S(2)}) %collective-permute-start.1) | collective-permute-done | bytes 147488 | tf_op jit(solution)/shard_map/ppermute | solution.py:231
  59.0 2.5 %collective-permute-done.3.d = f32[16,2304]{1,0:T(8,128)S(1)} collective-permute-done((f32[16,2304]{1,0:T(8,128)S(1)}, f32[16,2304]{1,0:T(8,128)S(1)}, u32[]{:S(2)}, u32[]{:S(2)}) %collective-permute-start.3) | collective-permute-done | bytes 147488 | tf_op jit(solution)/shard_map/ppermute | solution.py:231
  61.5 0.7 shard_map.87
  62.2 4.0 %all-to-all-start.1 = ((f32[16,1,2304]{2,1,0:T(1,128)}), f32[16,1,2304]{2,1,0:T(1,128)S(1)}, u32[]{:S(2)}, u32[]{:S(2)}) async-start(f32[16,1,2304]{2,1,0:T(1,128)} %bitcast.7), calls=%async_computation.1 | async-start | bytes 294912 | tf_op jit(solution)/shard_map/all_to_all | solution.py:239
  66.2 2.8 %shard_map.89 = (bf16[16,2,32,128]{3,2,1,0:T(8,128)(2,1)S(1)}, bf16[16,2,32,128]{3,2,1,0:T(8,128)(2,1)S(1)}, bf16[16,2,32,128]{3,2,1,0:T(8,128)(2,1)}, bf16[16,2...) custom-call(s32[3]{0:T(128)S(1)} %pad_add_fusion.place, ...), custom_call_target="tpu_custom_call" | custom-call | tf_op jit(solution)/shard_map/pallas_call | solution.py:41
  69.0 2.2 %collective-permute-start.10 = (bf16[16,2,32,128]{3,2,1,0:T(8,128)(2,1)S(1)}, bf16[16,2,32,128]{3,2,1,0:T(8,128)(2,1)S(1)}, u32[]{:S(2)}, u32[]{:S(2)}) collective-permute-start(bf16[16,2,32,128]{3,2,1,0:T(8,128)(2,1)S(1)} %get-tuple-element.40), channel_id=1, source_target_pairs={{0,65},{1,64},{32,97},{33,96},{64,1},{65,0},{96,33},{97,32},{2,67}... | collective-permute-start | bytes 786440 | tf_op jit(solution)/shard_map/ppermute | solution.py:305
  71.2 2.9 %collective-permute-start.4 = (bf16[16,2,32,128]{3,2,1,0:T(8,128)(2,1)S(1)}, bf16[16,2,32,128]{3,2,1,0:T(8,128)(2,1)S(1)}, u32[]{:S(2)}, u32[]{:S(2)}) collective-permute-start(bf16[16,2,32,128]{3,2,1,0:T(8,128)(2,1)S(1)} %get-tuple-element.34), channel_id=1, source_target_pairs={{0,32},{1,33},{32,64},{33,65},{64,96},{65,97},{96,0},{97,1},{2,34}... | collective-permute-start | bytes 786440 | tf_op jit(solution)/shard_map/ppermute | solution.py:305
  74.1 1.8 %collective-permute-start.6 = (bf16[16,2,32,128]{3,2,1,0:T(8,128)(2,1)S(1)}, bf16[16,2,32,128]{3,2,1,0:T(8,128)(2,1)S(1)}, u32[]{:S(2)}, u32[]{:S(2)}) collective-permute-start(bf16[16,2,32,128]{3,2,1,0:T(8,128)(2,1)S(1)} %get-tuple-element.36), channel_id=1, source_target_pairs={{0,64},{1,65},{32,96},{33,97},{64,0},{65,1},{96,32},{97,33},{2,66}... | collective-permute-start | bytes 786440 | tf_op jit(solution)/shard_map/ppermute | solution.py:305
  75.9 0.6 dynamic_slice.3
  77.2 0.1 fusion
  77.3 0.1 maximum_bitcast_fusion.cosine
  77.4 1.0 collective-permute-done.10.refs_7_
  78.3 3.3 %collective-permute-start.8 = (bf16[16,2,32,128]{3,2,1,0:T(8,128)(2,1)S(1)}, bf16[16,2,32,128]{3,2,1,0:T(8,128)(2,1)S(1)}, u32[]{:S(2)}, u32[]{:S(2)}) collective-permute-start(bf16[16,2,32,128]{3,2,1,0:T(8,128)(2,1)S(1)} %get-tuple-element.38), channel_id=1, source_target_pairs={{0,33},{1,32},{32,65},{33,64},{64,97},{65,96},{96,1},{97,0},{2,35}... | collective-permute-start | bytes 786440 | tf_op jit(solution)/shard_map/ppermute | solution.py:305
  81.6 4.6 %collective-permute-done.4.refs_1_ = bf16[16,2,32,128]{3,2,1,0:T(8,128)(2,1)S(1)} collective-permute-done((bf16[16,2,32,128]{3,2,1,0:T(8,128)(2,1)S(1)}, bf16[16,2,32,128]{3,2,1,0:T(8,128)(2,1)S(1)}, u32[]{:S(2)}, u32[]{:S(2)}) %collective-permute-start.4) | collective-permute-done | bytes 262176 | tf_op jit(solution)/shard_map/ppermute | solution.py:305
  86.2 0.1 maximum_bitcast_fusion.1.sine
  86.3 0.7 shard_map.88
  87.0 11.5 %all-to-all-start.2 = ((bf16[16,16,128]{2,1,0:T(8,128)(2,1)}), bf16[16,16,128]{2,1,0:T(8,128)(2,1)S(1)}, u32[]{:S(2)}, u32[]{:S(2)}) async-start(bf16[16,16,128]{2,1,0:T(8,128)(2,1)} %get-tuple-element.32), calls=%async_computation.2 | async-start | bytes 131072 | tf_op jit(solution)/shard_map/all_to_all | solution.py:239
  98.6 11.3 %all-to-all-done.2.q = bf16[16,16,128]{2,1,0:T(8,128)(2,1)S(1)} async-done(((bf16[16,16,128]{2,1,0:T(8,128)(2,1)}), bf16[16,16,128]{2,1,0:T(8,128)(2,1)S(1)}, u32[]{:S(2)}, u32[]{:S(2)}) %all-to-all-start.2) | async-done | bytes 65568 | tf_op jit(solution)/shard_map/all_to_all | solution.py:239
  110.0 4.5 %shard_map.90 = f32[288,128]{1,0:T(8,128)S(1)} custom-call(s32[16]{0:T(128)S(1)} %copy-done.6, s32[3]{0:T(128)S(1)} %pad_add_fusion.place, s32[8,16]{1,0:T(8,128)S(1)} %copy-done.4, bf16[16,16,128]{2,1,0:T(8,128)(2,1)S(1)} %all-to-all-done.2.q, bf16[16,2,32,128]{3,2,1,0:T(8,128)(2,1)S(1)} %get-tuple-element.33.refs_0_, ...), custom_call_target="tpu_custom_call" | custom-call | tf_op jit(solution)/shard_map/pallas_call | solution.py:41
  114.5 14.9 %all_to_all.25 = f32[16,1,2304]{2,1,0:T(1,128)S(1)} all-to-all(f32[16,1,2304]{2,1,0:T(1,128)S(1)} %bitcast.17), channel_id=1, replica_groups=mesh['groups'=2,'x'=4,'z'=16,'c'=2] {'z'}, dimensions={0} | all-to-all | bytes 294912 | tf_op jit(solution)/shard_map/all_to_all | solution.py:239
  129.3 0.1 shard_map.91
  129.5 17.2 %all_to_all.26.heads = bf16[16,16,128]{2,1,0:T(8,128)(2,1)S(1)} all-to-all(bf16[16,16,128]{2,1,0:T(8,128)(2,1)S(1)} %shard_map.91), channel_id=1, replica_groups=mesh['groups'=2,'x'=4,'z'=16,'c'=2] {'z'}, dimensions={0} | all-to-all | bytes 131072 | tf_op jit(solution)/shard_map/all_to_all | solution.py:239
  146.7 0.1 shard_map.92.a
  146.9 3.0 %collective-permute-start.11 = (bf16[16,2048]{1,0:T(8,128)(2,1)S(1)}, bf16[16,2048]{1,0:T(8,128)(2,1)S(1)}, u32[]{:S(2)}, u32[]{:S(2)}) collective-permute-start(bf16[16,2048]{1,0:T(8,128)(2,1)S(1)} %shard_map.92.a), channel_id=1, source_target_pairs={{0,96},{32,0},{64,32},{96,64},{1,97},{33,1},{65,33},{97,65},{2,98}... | collective-permute-start | bytes 196616 | tf_op jit(solution)/shard_map/ppermute | solution.py:231
  149.8 3.0 %collective-permute-start.12 = (bf16[16,2048]{1,0:T(8,128)(2,1)S(1)}, bf16[16,2048]{1,0:T(8,128)(2,1)S(1)}, u32[]{:S(2)}, u32[]{:S(2)}) collective-permute-start(bf16[16,2048]{1,0:T(8,128)(2,1)S(1)} %shard_map.92.a), channel_id=1, source_target_pairs={{0,64},{32,96},{64,0},{96,32},{1,65},{33,97},{65,1},{97,33},{2,66}... | collective-permute-start | bytes 196616 | tf_op jit(solution)/shard_map/ppermute | solution.py:231
  152.8 2.9 %collective-permute-start.14 = (bf16[16,2048]{1,0:T(8,128)(2,1)S(1)}, bf16[16,2048]{1,0:T(8,128)(2,1)S(1)}, u32[]{:S(2)}, u32[]{:S(2)}) collective-permute-start(bf16[16,2048]{1,0:T(8,128)(2,1)S(1)} %shard_map.92.a), channel_id=1, source_target_pairs={{0,1},{1,0},{2,3},{3,2},{4,5},{5,4},{6,7},{7,6},{8,9},{9,8},{10,11... | collective-permute-start | bytes 196616 | tf_op jit(solution)/shard_map/ppermute | solution.py:235
  155.7 0.2 collective-permute-start.15
  155.8 2.6 %collective-permute-start.16 = (bf16[16,2048]{1,0:T(8,128)(2,1)S(1)}, bf16[16,2048]{1,0:T(8,128)(2,1)S(1)}, u32[]{:S(2)}, u32[]{:S(2)}) collective-permute-start(bf16[16,2048]{1,0:T(8,128)(2,1)S(1)} %collective-permute-done.12.c), channel_id=1, source_target_pairs={{0,1},{1,0},{2,3},{3,2},{4,5},{5,4},{6,7},{7,6},{8,9},{9,8},{10,11... | collective-permute-start | bytes 196616 | tf_op jit(solution)/shard_map/ppermute | solution.py:235
  158.4 2.7 %collective-permute-start.17 = (bf16[16,2048]{1,0:T(8,128)(2,1)S(1)}, bf16[16,2048]{1,0:T(8,128)(2,1)S(1)}, u32[]{:S(2)}, u32[]{:S(2)}) collective-permute-start(bf16[16,2048]{1,0:T(8,128)(2,1)S(1)} %collective-permute-done.13.d), channel_id=1, source_target_pairs={{0,1},{1,0},{2,3},{3,2},{4,5},{5,4},{6,7},{7,6},{8,9},{9,8},{10,11... | collective-permute-start | bytes 196616 | tf_op jit(solution)/shard_map/ppermute | solution.py:235
  161.1 2.1 %shard_map.93.w_mine = bf16[4,2048,128]{2,1,0:T(8,128)(2,1)S(1)} custom-call(s32[3]{0:T(128)S(1)} %pad_add_fusion.place, bf16[16384,128]{1,0:T(8,128)(2,1)} %wo.3), custom_call_target="tpu_custom_call" | custom-call | tf_op jit(solution)/shard_map/pallas_call | solution.py:41
  163.2 2.1 %shard_map.94.w_theirs = bf16[4,2048,128]{2,1,0:T(8,128)(2,1)S(1)} custom-call(s32[3]{0:T(128)S(1)} %pad_add_fusion.place, bf16[16384,128]{1,0:T(8,128)(2,1)} %wo.3), custom_call_target="tpu_custom_call" | custom-call | tf_op jit(solution)/shard_map/pallas_call | solution.py:41
  165.4 1.3 shard_map.95
  (30 shorter events, 0.1 us)
Async XLA Ops:
  0.0 0.7 copy-start.2
  1.4 46.0 %all-to-all-start = ((f32[128,1,128]{2,1,0:T(1,128)}), f32[128,1,128]{2,1,0:T(1,128)S(1)}, u32[]{:S(2)}, u32[]{:S(2)}) async-start(f32[128,1,128]{2,1,0:T(1,128)} %bitcast.4), calls=%async_computation | async-start | bytes 131072 | tf_op jit(solution)/shard_map/all_to_all | solution.py:258
  32.5 14.9 %copy-start.3 = (bf16[16,128]{1,0:T(8,128)(2,1)S(1)}, bf16[16,128]{1,0:T(8,128)(2,1)}, u32[]{:S(2)}) copy-start(bf16[16,128]{1,0:T(8,128)(2,1)} %x.5) | copy-start | bytes 12292
  32.5 14.9 %copy-start.5 = (bf16[128]{0:T(256)(128)(2,1)S(1)}, bf16[128]{0:T(256)(128)(2,1)}, u32[]{:S(2)}) copy-start(bf16[128]{0:T(256)(128)(2,1)} %param.9) | copy-start | bytes 772
  35.6 1.4 copy-start
  47.4 1.7 %copy-start.1 = (bf16[4,128,2304]{2,1,0:T(8,128)(2,1)S(1)}, bf16[4,128,2304]{2,1,0:T(8,128)(2,1)}, u32[]{:S(2)}) copy-start(bf16[4,128,2304]{2,1,0:T(8,128)(2,1)} %copy-done) | copy-start | bytes 7077892
  49.5 3.0 %collective-permute-start = (f32[4,16,2304]{2,1,0:T(8,128)S(1)}, f32[4,16,2304]{2,1,0:T(8,128)S(1)}, u32[]{:S(2)}, u32[]{:S(2)}) collective-permute-start(f32[4,16,2304]{2,1,0:T(8,128)S(1)} %get-tuple-element.27), channel_id=1, source_target_pairs={{0,1},{1,0},{2,3},{3,2},{4,5},{5,4},{6,7},{7,6},{8,9},{9,8},{10,11... | collective-permute-start | bytes 1769480 | tf_op jit(solution)/shard_map/ppermute | solution.py:235
  51.4 24.6 %copy-start.6 = (s32[16]{0:T(128)S(1)}, s32[16]{0:T(128)}, u32[]{:S(2)}) copy-start(s32[16]{0:T(128)} %lengths.1) | copy-start | bytes 196
  51.4 58.6 %copy-start.4 = (s32[8,16]{1,0:T(8,128)S(1)}, s32[8,16]{1,0:T(8,128)}, u32[]{:S(2)}) copy-start(s32[8,16]{1,0:T(8,128)} %slabs.1) | copy-start | bytes 1540
  52.6 6.4 %collective-permute-start.1 = (f32[16,2304]{1,0:T(8,128)S(1)}, f32[16,2304]{1,0:T(8,128)S(1)}, u32[]{:S(2)}, u32[]{:S(2)}) collective-permute-start(f32[16,2304]{1,0:T(8,128)S(1)} %get-tuple-element.29), channel_id=1, source_target_pairs={{0,32},{32,64},{64,96},{96,0},{1,33},{33,65},{65,97},{97,1},{2,34}... | collective-permute-start | bytes 442376 | tf_op jit(solution)/shard_map/ppermute | solution.py:231
  52.8 6.2 %collective-permute-start.2 = (f32[16,2304]{1,0:T(8,128)S(1)}, f32[16,2304]{1,0:T(8,128)S(1)}, u32[]{:S(2)}, u32[]{:S(2)}) collective-permute-start(f32[16,2304]{1,0:T(8,128)S(1)} %get-tuple-element.30), channel_id=1, source_target_pairs={{0,96},{32,0},{64,32},{96,64},{1,97},{33,1},{65,33},{97,65},{2,98}... | collective-permute-start | bytes 442376 | tf_op jit(solution)/shard_map/ppermute | solution.py:231
  55.4 6.1 %collective-permute-start.3 = (f32[16,2304]{1,0:T(8,128)S(1)}, f32[16,2304]{1,0:T(8,128)S(1)}, u32[]{:S(2)}, u32[]{:S(2)}) collective-permute-start(f32[16,2304]{1,0:T(8,128)S(1)} %get-tuple-element.31), channel_id=1, source_target_pairs={{0,64},{32,96},{64,0},{96,32},{1,65},{33,97},{65,1},{97,33},{2,66}... | collective-permute-start | bytes 442376 | tf_op jit(solution)/shard_map/ppermute | solution.py:231
  62.2 24.1 %all-to-all-start.1 = ((f32[16,1,2304]{2,1,0:T(1,128)}), f32[16,1,2304]{2,1,0:T(1,128)S(1)}, u32[]{:S(2)}, u32[]{:S(2)}) async-start(f32[16,1,2304]{2,1,0:T(1,128)} %bitcast.7), calls=%async_computation.1 | async-start | bytes 294912 | tf_op jit(solution)/shard_map/all_to_all | solution.py:239
  69.0 9.4 %collective-permute-start.10 = (bf16[16,2,32,128]{3,2,1,0:T(8,128)(2,1)S(1)}, bf16[16,2,32,128]{3,2,1,0:T(8,128)(2,1)S(1)}, u32[]{:S(2)}, u32[]{:S(2)}) collective-permute-start(bf16[16,2,32,128]{3,2,1,0:T(8,128)(2,1)S(1)} %get-tuple-element.40), channel_id=1, source_target_pairs={{0,65},{1,64},{32,97},{33,96},{64,1},{65,0},{96,33},{97,32},{2,67}... | collective-permute-start | bytes 786440 | tf_op jit(solution)/shard_map/ppermute | solution.py:305
  71.2 15.0 %collective-permute-start.4 = (bf16[16,2,32,128]{3,2,1,0:T(8,128)(2,1)S(1)}, bf16[16,2,32,128]{3,2,1,0:T(8,128)(2,1)S(1)}, u32[]{:S(2)}, u32[]{:S(2)}) collective-permute-start(bf16[16,2,32,128]{3,2,1,0:T(8,128)(2,1)S(1)} %get-tuple-element.34), channel_id=1, source_target_pairs={{0,32},{1,33},{32,64},{33,65},{64,96},{65,97},{96,0},{97,1},{2,34}... | collective-permute-start | bytes 786440 | tf_op jit(solution)/shard_map/ppermute | solution.py:305
  74.1 24.4 %collective-permute-start.5 = (bf16[16,2,32,128]{3,2,1,0:T(8,128)(2,1)}, bf16[16,2,32,128]{3,2,1,0:T(8,128)(2,1)S(1)}, u32[]{:S(2)}, u32[]{:S(2)}) collective-permute-start(bf16[16,2,32,128]{3,2,1,0:T(8,128)(2,1)} %get-tuple-element.35), channel_id=1, source_target_pairs={{0,96},{1,97},{32,0},{33,1},{64,32},{65,33},{96,64},{97,65},{2,98}... | collective-permute-start | bytes 786440 | tf_op jit(solution)/shard_map/ppermute | solution.py:305
  74.1 24.4 %collective-permute-start.6 = (bf16[16,2,32,128]{3,2,1,0:T(8,128)(2,1)S(1)}, bf16[16,2,32,128]{3,2,1,0:T(8,128)(2,1)S(1)}, u32[]{:S(2)}, u32[]{:S(2)}) collective-permute-start(bf16[16,2,32,128]{3,2,1,0:T(8,128)(2,1)S(1)} %get-tuple-element.36), channel_id=1, source_target_pairs={{0,64},{1,65},{32,96},{33,97},{64,0},{65,1},{96,32},{97,33},{2,66}... | collective-permute-start | bytes 786440 | tf_op jit(solution)/shard_map/ppermute | solution.py:305
  75.9 22.7 %collective-permute-start.7 = (bf16[16,2,32,128]{3,2,1,0:T(8,128)(2,1)S(1)}, bf16[16,2,32,128]{3,2,1,0:T(8,128)(2,1)S(1)}, u32[]{:S(2)}, u32[]{:S(2)}) collective-permute-start(bf16[16,2,32,128]{3,2,1,0:T(8,128)(2,1)S(1)} %get-tuple-element.37), channel_id=1, source_target_pairs={{0,1},{1,0},{32,33},{33,32},{64,65},{65,64},{96,97},{97,96},{2,3},... | collective-permute-start | bytes 786440 | tf_op jit(solution)/shard_map/ppermute | solution.py:305
  78.3 20.3 %collective-permute-start.8 = (bf16[16,2,32,128]{3,2,1,0:T(8,128)(2,1)S(1)}, bf16[16,2,32,128]{3,2,1,0:T(8,128)(2,1)S(1)}, u32[]{:S(2)}, u32[]{:S(2)}) collective-permute-start(bf16[16,2,32,128]{3,2,1,0:T(8,128)(2,1)S(1)} %get-tuple-element.38), channel_id=1, source_target_pairs={{0,33},{1,32},{32,65},{33,64},{64,97},{65,96},{96,1},{97,0},{2,35}... | collective-permute-start | bytes 786440 | tf_op jit(solution)/shard_map/ppermute | solution.py:305
  86.2 12.4 %collective-permute-start.9 = (bf16[16,2,32,128]{3,2,1,0:T(8,128)(2,1)S(1)}, bf16[16,2,32,128]{3,2,1,0:T(8,128)(2,1)S(1)}, u32[]{:S(2)}, u32[]{:S(2)}) collective-permute-start(bf16[16,2,32,128]{3,2,1,0:T(8,128)(2,1)S(1)} %get-tuple-element.39), channel_id=1, source_target_pairs={{0,97},{1,96},{32,1},{33,0},{64,33},{65,32},{96,65},{97,64},{2,99}... | collective-permute-start | bytes 786440 | tf_op jit(solution)/shard_map/ppermute | solution.py:305
  87.0 22.9 %all-to-all-start.2 = ((bf16[16,16,128]{2,1,0:T(8,128)(2,1)}), bf16[16,16,128]{2,1,0:T(8,128)(2,1)S(1)}, u32[]{:S(2)}, u32[]{:S(2)}) async-start(bf16[16,16,128]{2,1,0:T(8,128)(2,1)} %get-tuple-element.32), calls=%async_computation.2 | async-start | bytes 131072 | tf_op jit(solution)/shard_map/all_to_all | solution.py:239
  146.9 8.8 %collective-permute-start.11 = (bf16[16,2048]{1,0:T(8,128)(2,1)S(1)}, bf16[16,2048]{1,0:T(8,128)(2,1)S(1)}, u32[]{:S(2)}, u32[]{:S(2)}) collective-permute-start(bf16[16,2048]{1,0:T(8,128)(2,1)S(1)} %shard_map.92.a), channel_id=1, source_target_pairs={{0,96},{32,0},{64,32},{96,64},{1,97},{33,1},{65,33},{97,65},{2,98}... | collective-permute-start | bytes 196616 | tf_op jit(solution)/shard_map/ppermute | solution.py:231
  149.8 6.0 %collective-permute-start.12 = (bf16[16,2048]{1,0:T(8,128)(2,1)S(1)}, bf16[16,2048]{1,0:T(8,128)(2,1)S(1)}, u32[]{:S(2)}, u32[]{:S(2)}) collective-permute-start(bf16[16,2048]{1,0:T(8,128)(2,1)S(1)} %shard_map.92.a), channel_id=1, source_target_pairs={{0,64},{32,96},{64,0},{96,32},{1,65},{33,97},{65,1},{97,33},{2,66}... | collective-permute-start | bytes 196616 | tf_op jit(solution)/shard_map/ppermute | solution.py:231
  152.8 5.6 %collective-permute-start.13 = (bf16[16,2048]{1,0:T(8,128)(2,1)S(1)}, bf16[16,2048]{1,0:T(8,128)(2,1)S(1)}, u32[]{:S(2)}, u32[]{:S(2)}) collective-permute-start(bf16[16,2048]{1,0:T(8,128)(2,1)S(1)} %shard_map.92.a), channel_id=1, source_target_pairs={{0,32},{32,64},{64,96},{96,0},{1,33},{33,65},{65,97},{97,1},{2,34}... | collective-permute-start | bytes 196616 | tf_op jit(solution)/shard_map/ppermute | solution.py:231
  152.8 12.6 %collective-permute-start.14 = (bf16[16,2048]{1,0:T(8,128)(2,1)S(1)}, bf16[16,2048]{1,0:T(8,128)(2,1)S(1)}, u32[]{:S(2)}, u32[]{:S(2)}) collective-permute-start(bf16[16,2048]{1,0:T(8,128)(2,1)S(1)} %shard_map.92.a), channel_id=1, source_target_pairs={{0,1},{1,0},{2,3},{3,2},{4,5},{5,4},{6,7},{7,6},{8,9},{9,8},{10,11... | collective-permute-start | bytes 196616 | tf_op jit(solution)/shard_map/ppermute | solution.py:235
  155.7 9.7 %collective-permute-start.15 = (bf16[16,2048]{1,0:T(8,128)(2,1)S(1)}, bf16[16,2048]{1,0:T(8,128)(2,1)S(1)}, u32[]{:S(2)}, u32[]{:S(2)}) collective-permute-start(bf16[16,2048]{1,0:T(8,128)(2,1)S(1)} %collective-permute-done.11.b), channel_id=1, source_target_pairs={{0,1},{1,0},{2,3},{3,2},{4,5},{5,4},{6,7},{7,6},{8,9},{9,8},{10,11... | collective-permute-start | bytes 196616 | tf_op jit(solution)/shard_map/ppermute | solution.py:235
  155.8 9.5 %collective-permute-start.16 = (bf16[16,2048]{1,0:T(8,128)(2,1)S(1)}, bf16[16,2048]{1,0:T(8,128)(2,1)S(1)}, u32[]{:S(2)}, u32[]{:S(2)}) collective-permute-start(bf16[16,2048]{1,0:T(8,128)(2,1)S(1)} %collective-permute-done.12.c), channel_id=1, source_target_pairs={{0,1},{1,0},{2,3},{3,2},{4,5},{5,4},{6,7},{7,6},{8,9},{9,8},{10,11... | collective-permute-start | bytes 196616 | tf_op jit(solution)/shard_map/ppermute | solution.py:235
  158.4 7.0 %collective-permute-start.17 = (bf16[16,2048]{1,0:T(8,128)(2,1)S(1)}, bf16[16,2048]{1,0:T(8,128)(2,1)S(1)}, u32[]{:S(2)}, u32[]{:S(2)}) collective-permute-start(bf16[16,2048]{1,0:T(8,128)(2,1)S(1)} %collective-permute-done.13.d), channel_id=1, source_target_pairs={{0,1},{1,0},{2,3},{3,2},{4,5},{5,4},{6,7},{7,6},{8,9},{9,8},{10,11... | collective-permute-start | bytes 196616 | tf_op jit(solution)/shard_map/ppermute | solution.py:235

commit v2 on v1

--- a/solution.py
+++ b/solution.py
@@ -17,6 +17,8 @@
 PW = ROWS * HD
 MODEL = KVH * QW
 TENSOR = ("x", "z", "c")
+NEAR = ((0, 0), (0, 1))
+FAR = ((1, 0), (3, 0), (2, 0), (1, 1), (3, 1), (2, 1))
 MOVES = ((0, 0), (1, 0), (3, 0), (2, 0), (0, 1), (1, 1), (3, 1), (2, 1))
 
 EPS = 1e-05
@@ -67,12 +69,15 @@
     out[...] = jnp.broadcast_to(as_row(total, diagonal(x.shape[0])), out.shape)
 
 
-def fetch_in_kernel(place, wq, wkv, theirs, mine, sems):
+def head_of(place, j, d):
+    core = 1 - place[2] if d else place[2]
+    return lax.rem(place[0] + j, NX) * NC + core
+
+
+def in_copies(place, d, wq, wkv, out, sems):
     copies = []
-    for k in range(2 * NX):
-        out = theirs if k < NX else mine
-        core = 1 - place[2] if k < NX else place[2]
-        head = lax.rem(place[0] + k % NX, NX) * NC + core
+    for k in range(NX):
+        head = head_of(place, k, d)
         for part, (source, start, width, at) in enumerate(
             (
                 (wq, head * QW, QW, 0),
@@ -80,42 +85,50 @@
                 (wkv, (KVH + head) * HD, HD, QW + HD),
             )
         ):
-            copy = pltpu.make_async_copy(
-                source.at[:, pl.ds(pl.multiple_of(start, HD), width)],
-                out.at[k % NX, :, pl.ds(at, width)],
-                sems.at[k, part],
+            copies.append(
+                pltpu.make_async_copy(
+                    source.at[:, pl.ds(pl.multiple_of(start, HD), width)],
+                    out.at[k, :, pl.ds(at, width)],
+                    sems.at[k, part],
+                )
             )
-            copy.start()
-            copies.append(copy)
+    return copies
+
+
+def out_copies(place, moves, wo, out, sems):
+    return [
+        pltpu.make_async_copy(
+            wo.at[pl.ds(pl.multiple_of(head_of(place, j, d) * QW, HD), QW)],
+            out.at[k],
+            sems.at[k],
+        )
+        for k, (j, d) in enumerate(moves)
+    ]
+
+
+def run_all(copies):
+    for copy in copies:
+        copy.start()
     for copy in copies:
         copy.wait()
 
 
-def fetch_out_kernel(other, place, wo, out, sems):
-    copies = []
-    for k in range(NX):
-        core = 1 - place[2] if other else place[2]
-        head = lax.rem(place[0] + k, NX) * NC + core
-        copy = pltpu.make_async_copy(
-            wo.at[pl.ds(pl.multiple_of(head * QW, HD), QW)], out.at[k], sems.at[k]
-        )
-        copy.start()
-        copies.append(copy)
-    for copy in copies:
-        copy.wait()
+def fetch_in_kernel(place, wq, wkv, out, sems):
+    run_all(in_copies(place, 1, wq, wkv, out, sems))
+
+
+def fetch_out_kernel(place, wo, out, sems):
+    run_all(out_copies(place, FAR, wo, out, sems))
 
 
 def fetch_cache_kernel(place, cache, *refs):
     outs, sems = refs[:-1], refs[-1]
-    copies = []
-    for k, (j, d) in enumerate(MOVES):
-        core = 1 - place[2] if d else place[2]
-        head = lax.rem(place[0] + j, NX) * NC + core
-        copy = pltpu.make_async_copy(cache.at[head], outs[k], sems.at[k])
-        copy.start()
-        copies.append(copy)
-    for copy in copies:
-        copy.wait()
+    run_all(
+        [
+            pltpu.make_async_copy(cache.at[head_of(place, j, d)], outs[k], sems.at[k])
+            for k, (j, d) in enumerate(MOVES)
+        ]
+    )
 
 
 def project_first_kernel(sums, x, gain, w, normed_out, out):
@@ -127,8 +140,13 @@
         out[k] = jnp.dot(normed, w[k], preferred_element_type=F32)
 
 
-def project_kernel(normed, w, out):
+def project_kernel(place, normed, wq, wkv, out, w, sems):
+    copies = in_copies(place, 0, wq, wkv, w, sems)
+    for copy in copies:
+        copy.start()
     for k in range(NX):
+        for copy in copies[3 * k : 3 * k + 3]:
+            copy.wait()
         out[k] = jnp.dot(normed[...], w[k], preferred_element_type=F32)
 
 
@@ -161,36 +179,44 @@
     new_value[...] = total[GROUP + 1 :].astype(BF16).astype(F32)
 
 
-def attend_kernel(lengths, place, slabs, q, *refs):
-    caches, out = refs[:-1], refs[-1]
-    local = caches[0].shape[2]
-    count = len(caches) * local
-    head = place[0] * NC + place[2]
-    index = lax.broadcasted_iota(jnp.int32, (1, count), 1)
+def positions_kernel(local, place, out):
+    index = lax.broadcasted_iota(jnp.int32, out.shape, 1)
     start = jnp.zeros_like(index)
     for k, (j, d) in enumerate(MOVES):
         core = 1 - place[2] if d else place[2]
         block = (lax.rem(place[0] + (NX - j), NX) * NZ + place[1]) * NC + core
         start = jnp.where(index // local == k, block * local, start)
-    position = start + index % local
+    out[...] = start + index % local
+
+
+def attend_kernel(lengths, place, slabs, positions, q, *refs):
+    caches, out, scores, weights = refs[: len(MOVES)], *refs[len(MOVES) :]
+    n = q.shape[0]
+    head = place[0] * NC + place[2]
     mask = diagonal(GROUP)
-    for b in range(q.shape[0]):
+    for b in range(n):
         slab = slabs[head, b]
         keys = jnp.concatenate([cache[slab, 0] for cache in caches], axis=0)
-        values = jnp.concatenate([cache[slab, 1] for cache in caches], axis=0)
-        scores = SCALE * lax.dot_general(
+        scores[b * GROUP : (b + 1) * GROUP] = SCALE * lax.dot_general(
             q[b], keys, (((1,), (1,)), ((), ())), preferred_element_type=F32
         )
-        visible = position < lengths[b]
-        top = jnp.max(jnp.where(visible, scores, NEG), axis=1, keepdims=True)
-        weights = jnp.where(visible, jnp.exp(scores - top), 0.0)
-        total = jnp.sum(weights, axis=1, keepdims=True)
-        at = b * ROWS
-        out[at : at + GROUP] = jnp.dot(
-            weights.astype(BF16), values, preferred_element_type=F32
+    for b in range(n):
+        rows = slice(b * GROUP, (b + 1) * GROUP)
+        visible = positions[...] < lengths[b]
+        score = jnp.where(visible, scores[rows], NEG)
+        top = jnp.max(score, axis=1, keepdims=True)
+        weight = jnp.where(visible, jnp.exp(score - top), 0.0)
+        total = jnp.sum(weight, axis=1, keepdims=True)
+        weights[rows] = weight.astype(BF16)
+        at = b * ROWS + GROUP
+        out[at : at + 1] = as_row(top, mask)
+        out[at + 1 : at + 2] = as_row(total, mask)
+    for b in range(n):
+        slab = slabs[head, b]
+        values = jnp.concatenate([cache[slab, 1] for cache in caches], axis=0)
+        out[b * ROWS : b * ROWS + GROUP] = jnp.dot(
+            weights[b * GROUP : (b + 1) * GROUP], values, preferred_element_type=F32
         )
-        out[at + GROUP : at + GROUP + 1] = as_row(top, mask)
-        out[at + GROUP + 1 : at + ROWS] = as_row(total, mask)
 
 
 def combine_kernel(parts, new_score, new_value, out):
@@ -218,12 +244,19 @@
         out[:, k * HD : (k + 1) * HD] = wide[:, k, :].astype(BF16)
 
 
-def output_kernel(a, b, c, d, e, f, g, h, w_mine, w_theirs, x, out):
+def output_near_kernel(place, a, b, wo, x, out, w, sems):
+    run_all(out_copies(place, NEAR, wo, w, sems))
     total = x[...].astype(F32)
-    for k, rows in enumerate((a, b, c, d)):
-        total = total + jnp.dot(rows[...], w_mine[k], preferred_element_type=F32)
-    for k, rows in enumerate((e, f, g, h)):
-        total = total + jnp.dot(rows[...], w_theirs[k], preferred_element_type=F32)
+    for k, rows in enumerate((a, b)):
+        total = total + jnp.dot(rows[...], w[k], preferred_element_type=F32)
+    out[...] = total
+
+
+def output_far_kernel(*refs):
+    near, *rows, w, out = refs
+    total = near[...]
+    for k, block in enumerate(rows):
+        total = total + jnp.dot(block[...], w[k], preferred_element_type=F32)
     out[...] = total.astype(BF16)
 
 
@@ -247,12 +280,13 @@
     )
     place = jnp.stack([lax.axis_index(a) for a in TENSOR]).astype(jnp.int32)
 
-    position = lengths[lax.axis_index("z")].astype(F32)
-    frequency = ROPE_BASE ** (-2.0 * jnp.arange(HD // 2, dtype=F32) / HD)
+    mine = jnp.arange(n, dtype=jnp.int32) == lax.axis_index("z")
+    position = jnp.sum(jnp.where(mine, lengths, 0)).astype(F32)
+    lane = jnp.arange(HD, dtype=jnp.int32)[None]
+    frequency = ROPE_BASE ** (-2.0 * (lane % (HD // 2)).astype(F32) / HD)
     angles = position * frequency
-    cosine, sine = jnp.cos(angles), jnp.sin(angles)
-    cosine = jnp.concatenate([cosine, cosine])[None]
-    sine = jnp.concatenate([-sine, sine])[None]
+    cosine = jnp.cos(angles)
+    sine = jnp.sin(angles) * jnp.where(lane < HD // 2, -1.0, 1.0)
 
     sums = call(squares_kernel, struct((members, HD), F32), [VMEM], hidden_in)
     sums = lax.all_to_all(
@@ -260,15 +294,8 @@
     ).reshape(members, HD)
 
     half = struct((NX, depth, PW), BF16)
-    w_theirs, w_mine = call(
-        fetch_in_kernel,
-        [half, half],
-        [SMEM, HBM, HBM],
-        place,
-        w_q,
-        w_kv,
-        scratch=[pltpu.SemaphoreType.DMA((2 * NX, 3))],
-    )
+    dmas = pltpu.SemaphoreType.DMA((NX, 3))
+    w_theirs = call(fetch_in_kernel, half, [SMEM, HBM, HBM], place, w_q, w_kv, scratch=[dmas])
 
     cache = list(call(
         fetch_cache_kernel,
@@ -290,7 +317,16 @@
         w_theirs,
     )
     got = swap_c(sent)
-    kept = call(project_kernel, product, [VMEM] * 2, normed, w_mine)
+    kept = call(
+        project_kernel,
+        product,
+        [SMEM, VMEM, HBM, HBM],
+        place,
+        normed,
+        w_q,
+        w_kv,
+        scratch=[pltpu.VMEM(half.shape, BF16), dmas],
+    )
     blocks = call(pair_sum_kernel, [struct((n, PW), F32)] * NX, [VMEM] * 2, kept, got)
     parts = [blocks[0]]
     for k in (1, 3, 2):
@@ -302,20 +338,25 @@
             for x in range(NX)
             for c in range(NC)
         ]
+        cache[k] = pltpu.with_memory_space_constraint(cache[k], pltpu.HBM)
         cache[k] = lax.ppermute(cache[k], ("x", "c"), pairs)
+    local = kv_cache.shape[3]
+    seen = len(MOVES) * local
+    positions = call(
+        functools.partial(positions_kernel, local),
+        struct((1, seen), jnp.int32),
+        [SMEM],
+        place,
+    )
     rows = across_z(rows.reshape(n, 1, PW)).reshape(n * ROWS, HD)
-    w_rows = []
-    for other in (0, 1):
-        w_rows.append(
-            call(
-                functools.partial(fetch_out_kernel, other),
-                struct((NX, QW, w_o.shape[1]), BF16),
-                [SMEM, HBM],
-                place,
-                w_o,
-                scratch=[pltpu.SemaphoreType.DMA((NX,))],
-            )
-        )
+    w_far = call(
+        fetch_out_kernel,
+        struct((len(FAR), QW, w_o.shape[1]), BF16),
+        [SMEM, HBM],
+        place,
+        w_o,
+        scratch=[pltpu.SemaphoreType.DMA((len(FAR),))],
+    )
     q, new_score, new_value = call(
         queries_kernel,
         [struct((n, GROUP, HD), BF16), struct((1, HD), F32), struct((1, HD), F32)],
@@ -329,12 +370,14 @@
     partial = call(
         attend_kernel,
         struct((n * ROWS, HD), F32),
-        [SMEM, SMEM, SMEM] + [VMEM] * (1 + len(MOVES)),
+        [SMEM, SMEM, SMEM] + [VMEM] * (2 + len(MOVES)),
         lengths,
         place,
         slab_index,
+        positions,
         q,
         *cache,
+        scratch=[pltpu.VMEM((n * GROUP, seen), F32), pltpu.VMEM((n * GROUP, seen), BF16)],
     )
     partial = across_z(partial.reshape(n, 1, PW)).reshape(n * ROWS, HD)
     done = call(
@@ -348,13 +391,31 @@
         done,
         scratch=[pltpu.VMEM((n, GROUP, HD), F32)],
     )
-    beside = {0: done}
+    rows = {(0, 0): done}
     for k in (1, 3, 2):
-        beside[k] = shift_x(done, -k)
-    mine = [beside[k] for k in range(NX)]
-    theirs = [swap_c(block) for block in mine]
+        rows[k, 0] = shift_x(done, -k)
+    for k in (0, 1, 3, 2):
+        rows[k, 1] = swap_c(rows[k, 0])
+    total = call(
+        output_near_kernel,
+        struct((n, depth), F32),
+        [SMEM, VMEM, VMEM, HBM, VMEM],
+        place,
+        *(rows[move] for move in NEAR),
+        w_o,
+        hidden_in,
+        scratch=[
+            pltpu.VMEM((len(NEAR), QW, w_o.shape[1]), BF16),
+            pltpu.SemaphoreType.DMA((len(NEAR),)),
+        ],
+    )
     return call(
-        output_kernel, struct((n, depth), BF16), [VMEM] * 11, *mine, *theirs, *w_rows, hidden_in
+        output_far_kernel,
+        struct((n, depth), BF16),
+        [VMEM] * (2 + len(FAR)),
+        total,
+        *(rows[move] for move in FAR),
+        w_far,
     )
 
 

time: 167 us -> 162 us (0.970)
  local copies, waits for them, and re-layouts: 4.36 us -> 0.73 us
  starting transfers between devices: 75.3 us -> 72.6 us
    unnamed x14 -> x22, local copies, waits for them, and re-layouts: 3.77 us -> 0.73 us
    all_to_all x1, waiting for transfers between devices: 10.3 us -> 12.6 us  [step(): lax.all_to_all(sums.reshape(members, 1, HD), TENSOR, 0, 0, tiled=True)]
    ppermute x5, starting transfers between devices: 9.72 us -> 8.03 us  [swap_c(): return lax.ppermute(value, 'c', [(0, 1), (1, 0)])]
    pallas_call x14 -> x15, Pallas kernels: 19.3 us -> 18.1 us  [call(): pl.pallas_call(kernel, in_specs=specs, out_specs=outs, out_shape=out, scr...]
  transfers between devices with their start and end apart: 21 -> 21, of which waited for: 7 -> 7; matrix products, arithmetic and copies ran while one was open for 1% -> 0% of each run, Pallas kernels for 7% -> 8%
where the time goes in v2:
time: 162 us; the launch traced here: 161 us
  starting transfers between devices  72.6 us (45%)
  waiting for transfers between devices  36 us (22%)
  blocking collectives  32.1 us (20%)
  Pallas kernels  18.1 us (11%)
    all_to_all x2, blocking collectives, across_z(): return lax.all_to_all(value, 'z', 0, 0, tiled=True)  32.1 us
    all_to_all x1, starting transfers between devices, step(): lax.all_to_all(sums.reshape(members, 1, HD), TENSOR, 0, 0, tiled=True)  31 us
    pallas_call x15, Pallas kernels, call(): pl.pallas_call(kernel, in_specs=specs, out_specs=outs, out_shape=out, scr...  18.1 us
    all_to_all x2, starting transfers between devices, across_z(): return lax.all_to_all(value, 'z', 0, 0, tiled=True)  15.5 us
    all_to_all x1, waiting for transfers between devices, step(): lax.all_to_all(sums.reshape(members, 1, HD), TENSOR, 0, 0, tiled=True)  12.6 us
    all_to_all x2, waiting for transfers between devices, across_z(): return lax.all_to_all(value, 'z', 0, 0, tiled=True)  10.7 us
    ppermute x7, starting transfers between devices, step(): cache[k] = lax.ppermute(cache[k], ('x', 'c'), pairs)  9.21 us
    ppermute x6, starting transfers between devices, shift_x(): return lax.ppermute(value, 'x', [(i, (i + by) % NX) for i in range(NX)])  8.87 us
  transfers between devices with their start and end apart: 21, of which 7 were waited for; matrix products, arithmetic and copies ran while one was open for 0% of the time, Pallas kernels for 8%

profile of v2, /device:TPU:33, one launch (start us, length us, event | category | flops | bytes accessed | tf_op | source)
XLA Modules:
  0.0 161.2 jit_solution(7517544503991888657)
XLA Ops:
  0.0 0.7 copy-done
  0.7 0.7 shard_map.83
  1.4 31.0 %all-to-all-start = ((f32[128,1,128]{2,1,0:T(1,128)}), f32[128,1,128]{2,1,0:T(1,128)S(1)}, u32[]{:S(2)}, u32[]{:S(2)}) async-start(f32[128,1,128]{2,1,0:T(1,128)} %bitcast.4), calls=%async_computation | async-start | bytes 131072 | tf_op jit(solution)/shard_map/all_to_all | solution.py:292
  32.4 0.1 pad_add_fusion.place
  32.5 2.3 %shard_map.84.w = bf16[4,128,2304]{2,1,0:T(8,128)(2,1)S(1)} custom-call(s32[3]{0:T(128)S(1)} %pad_add_fusion.place, bf16[128,16384]{1,0:T(8,128)(2,1)} %wq.3, bf16[128,2048]{1,0:T(8,128)(2,1)} %wkv.3), custom_call_target="tpu_custom_call" | custom-call | tf_op jit(solution)/shard_map/pallas_call | solution.py:43
  34.8 12.6 %all-to-all-done = f32[128,1,128]{2,1,0:T(1,128)S(1)} async-done(((f32[128,1,128]{2,1,0:T(1,128)}), f32[128,1,128]{2,1,0:T(1,128)S(1)}, u32[]{:S(2)}, u32[]{:S(2)}) %all-to-all-start) | async-done | bytes 65568 | tf_op jit(solution)/shard_map/all_to_all | solution.py:292
  47.4 0.5 shard_map.85
  47.9 1.3 collective-permute-start
  49.2 2.5 %shard_map.86.a = f32[4,16,2304]{2,1,0:T(8,128)S(1)} custom-call(s32[3]{0:T(128)S(1)} %pad_add_fusion.place, bf16[16,128]{1,0:T(8,128)(2,1)S(1)} %get-tuple-element.22.normed, bf16[128,16384]{1,0:T(8,128)(2,1)} %wq.3, bf16[128,2048]{1,0:T(8,128)(2,1)} %wkv.3), custom_call_target="tpu_custom_call" | custom-call | tf_op jit(solution)/shard_map/pallas_call | solution.py:43
  51.7 0.0 copy-start.4
  51.7 0.0 copy-start.2
  51.8 0.0 collective-permute-done.b
  51.8 0.1 shard_map.87
  51.8 0.1 collective-permute-start.1
  52.0 2.6 %collective-permute-start.2 = (f32[16,2304]{1,0:T(8,128)S(1)}, f32[16,2304]{1,0:T(8,128)S(1)}, u32[]{:S(2)}, u32[]{:S(2)}) collective-permute-start(f32[16,2304]{1,0:T(8,128)S(1)} %get-tuple-element.26), channel_id=1, source_target_pairs={{0,96},{32,0},{64,32},{96,64},{1,97},{33,1},{65,33},{97,65},{2,98}... | collective-permute-start | bytes 442376 | tf_op jit(solution)/shard_map/ppermute | solution.py:264
  54.6 0.2 collective-permute-start.3
  54.8 3.8 %collective-permute-done.1.b = f32[16,2304]{1,0:T(8,128)S(1)} collective-permute-done((f32[16,2304]{1,0:T(8,128)S(1)}, f32[16,2304]{1,0:T(8,128)S(1)}, u32[]{:S(2)}, u32[]{:S(2)}) %collective-permute-start.1) | collective-permute-done | bytes 147488 | tf_op jit(solution)/shard_map/ppermute | solution.py:264
  58.5 2.0 %collective-permute-done.2.c = f32[16,2304]{1,0:T(8,128)S(1)} collective-permute-done((f32[16,2304]{1,0:T(8,128)S(1)}, f32[16,2304]{1,0:T(8,128)S(1)}, u32[]{:S(2)}, u32[]{:S(2)}) %collective-permute-start.2) | collective-permute-done | bytes 147488 | tf_op jit(solution)/shard_map/ppermute | solution.py:264
  60.5 0.5 collective-permute-done.3.d
  61.0 0.7 shard_map.88
  61.7 4.0 %all-to-all-start.1 = ((f32[16,1,2304]{2,1,0:T(1,128)}), f32[16,1,2304]{2,1,0:T(1,128)S(1)}, u32[]{:S(2)}, u32[]{:S(2)}) async-start(f32[16,1,2304]{2,1,0:T(1,128)} %bitcast.7), calls=%async_computation.1 | async-start | bytes 294912 | tf_op jit(solution)/shard_map/all_to_all | solution.py:272
  65.7 2.1 %shard_map.90 = (bf16[16,2,32,128]{3,2,1,0:T(8,128)(2,1)S(1)}, bf16[16,2,32,128]{3,2,1,0:T(8,128)(2,1)S(1)}, bf16[16,2,32,128]{3,2,1,0:T(8,128)(2,1)S(1)}, bf16[...) custom-call(s32[3]{0:T(128)S(1)} %pad_add_fusion.place, ...), custom_call_target="tpu_custom_call" | custom-call | tf_op jit(solution)/shard_map/pallas_call | solution.py:43
  67.8 1.9 %collective-permute-start.10 = (bf16[16,2,32,128]{3,2,1,0:T(8,128)(2,1)S(1)}, bf16[16,2,32,128]{3,2,1,0:T(8,128)(2,1)S(1)}, u32[]{:S(2)}, u32[]{:S(2)}) collective-permute-start(bf16[16,2,32,128]{3,2,1,0:T(8,128)(2,1)S(1)} %get-tuple-element.36), channel_id=1, source_target_pairs={{0,65},{1,64},{32,97},{33,96},{64,1},{65,0},{96,33},{97,32},{2,67}... | collective-permute-start | bytes 786440 | tf_op jit(solution)/shard_map/ppermute | solution.py:342
  69.7 2.9 %collective-permute-start.4 = (bf16[16,2,32,128]{3,2,1,0:T(8,128)(2,1)S(1)}, bf16[16,2,32,128]{3,2,1,0:T(8,128)(2,1)S(1)}, u32[]{:S(2)}, u32[]{:S(2)}) collective-permute-start(bf16[16,2,32,128]{3,2,1,0:T(8,128)(2,1)S(1)} %get-tuple-element.30), channel_id=1, source_target_pairs={{0,32},{1,33},{32,64},{33,65},{64,96},{65,97},{96,0},{97,1},{2,34}... | collective-permute-start | bytes 786440 | tf_op jit(solution)/shard_map/ppermute | solution.py:342
  72.6 1.8 %collective-permute-start.6 = (bf16[16,2,32,128]{3,2,1,0:T(8,128)(2,1)S(1)}, bf16[16,2,32,128]{3,2,1,0:T(8,128)(2,1)S(1)}, u32[]{:S(2)}, u32[]{:S(2)}) collective-permute-start(bf16[16,2,32,128]{3,2,1,0:T(8,128)(2,1)S(1)} %get-tuple-element.32), channel_id=1, source_target_pairs={{0,64},{1,65},{32,96},{33,97},{64,0},{65,1},{96,32},{97,33},{2,66}... | collective-permute-start | bytes 786440 | tf_op jit(solution)/shard_map/ppermute | solution.py:342
  74.4 0.6 fusion
  75.7 1.8 %collective-permute-done.10.refs_7_ = bf16[16,2,32,128]{3,2,1,0:T(8,128)(2,1)S(1)} collective-permute-done((bf16[16,2,32,128]{3,2,1,0:T(8,128)(2,1)S(1)}, bf16[16,2,32,128]{3,2,1,0:T(8,128)(2,1)S(1)}, u32[]{:S(2)}, u32[]{:S(2)}) %collective-permute-start.10) | collective-permute-done | bytes 262176 | tf_op jit(solution)/shard_map/ppermute | solution.py:342
  77.5 2.6 %collective-permute-start.8 = (bf16[16,2,32,128]{3,2,1,0:T(8,128)(2,1)S(1)}, bf16[16,2,32,128]{3,2,1,0:T(8,128)(2,1)S(1)}, u32[]{:S(2)}, u32[]{:S(2)}) collective-permute-start(bf16[16,2,32,128]{3,2,1,0:T(8,128)(2,1)S(1)} %get-tuple-element.34), channel_id=1, source_target_pairs={{0,33},{1,32},{32,65},{33,64},{64,97},{65,96},{96,1},{97,0},{2,35}... | collective-permute-start | bytes 786440 | tf_op jit(solution)/shard_map/ppermute | solution.py:342
  80.2 4.6 %collective-permute-done.4.refs_1_ = bf16[16,2,32,128]{3,2,1,0:T(8,128)(2,1)S(1)} collective-permute-done((bf16[16,2,32,128]{3,2,1,0:T(8,128)(2,1)S(1)}, bf16[16,2,32,128]{3,2,1,0:T(8,128)(2,1)S(1)}, u32[]{:S(2)}, u32[]{:S(2)}) %collective-permute-start.4) | collective-permute-done | bytes 262176 | tf_op jit(solution)/shard_map/ppermute | solution.py:342
  84.8 0.7 shard_map.89
  85.5 11.5 %all-to-all-start.2 = ((bf16[16,16,128]{2,1,0:T(8,128)(2,1)}), bf16[16,16,128]{2,1,0:T(8,128)(2,1)S(1)}, u32[]{:S(2)}, u32[]{:S(2)}) async-start(bf16[16,16,128]{2,1,0:T(8,128)(2,1)} %get-tuple-element.28), calls=%async_computation.2 | async-start | bytes 131072 | tf_op jit(solution)/shard_map/all_to_all | solution.py:272
  97.0 0.6 shard_map.82.positions
  97.7 10.7 %all-to-all-done.2.q = bf16[16,16,128]{2,1,0:T(8,128)(2,1)S(1)} async-done(((bf16[16,16,128]{2,1,0:T(8,128)(2,1)}), bf16[16,16,128]{2,1,0:T(8,128)(2,1)S(1)}, u32[]{:S(2)}, u32[]{:S(2)}) %all-to-all-start.2) | async-done | bytes 65568 | tf_op jit(solution)/shard_map/all_to_all | solution.py:272
  108.5 2.0 %shard_map.91 = f32[288,128]{1,0:T(8,128)S(1)} custom-call(s32[16]{0:T(128)S(1)} %copy-done.4, s32[3]{0:T(128)S(1)} %pad_add_fusion.place, s32[8,16]{1,0:T(8,128)S(1)} %copy-done.2, s32[1,256]{1,0:T(1,128)S(1)} %shard_map.82.positions, bf16[16,16,128]{2,1,0:T(8,128)(2,1)S(1)} %all-to-all-done.2.q, bf16[16,2,32,128]{3,2,1,0:T(8,128)(2,1)S(1)} %get-tuple-element.29.refs_0_, ...), custom_call_target="tpu_custom_call" | custom-call | tf_op jit(solution)/shard_map/pallas_call | solution.py:43
  110.5 14.9 %all_to_all.25 = f32[16,1,2304]{2,1,0:T(1,128)S(1)} all-to-all(f32[16,1,2304]{2,1,0:T(1,128)S(1)} %bitcast.14), channel_id=1, replica_groups=mesh['groups'=2,'x'=4,'z'=16,'c'=2] {'z'}, dimensions={0} | all-to-all | bytes 294912 | tf_op jit(solution)/shard_map/all_to_all | solution.py:272
  125.4 0.1 shard_map.92
  125.5 17.2 %all_to_all.26.heads = bf16[16,16,128]{2,1,0:T(8,128)(2,1)S(1)} all-to-all(bf16[16,16,128]{2,1,0:T(8,128)(2,1)S(1)} %shard_map.92), channel_id=1, replica_groups=mesh['groups'=2,'x'=4,'z'=16,'c'=2] {'z'}, dimensions={0} | all-to-all | bytes 131072 | tf_op jit(solution)/shard_map/all_to_all | solution.py:272
  142.8 0.1 shard_map.93.a
  142.9 3.0 %collective-permute-start.12 = (bf16[16,2048]{1,0:T(8,128)(2,1)S(1)}, bf16[16,2048]{1,0:T(8,128)(2,1)S(1)}, u32[]{:S(2)}, u32[]{:S(2)}) collective-permute-start(bf16[16,2048]{1,0:T(8,128)(2,1)S(1)} %shard_map.93.a), channel_id=1, source_target_pairs={{0,96},{32,0},{64,32},{96,64},{1,97},{33,1},{65,33},{97,65},{2,98}... | collective-permute-start | bytes 196616 | tf_op jit(solution)/shard_map/ppermute | solution.py:264
  145.9 1.3 collective-permute-start.13
  147.2 1.7 %collective-permute-start.14 = (bf16[16,2048]{1,0:T(8,128)(2,1)S(1)}, bf16[16,2048]{1,0:T(8,128)(2,1)S(1)}, u32[]{:S(2)}, u32[]{:S(2)}) collective-permute-start(bf16[16,2048]{1,0:T(8,128)(2,1)S(1)} %shard_map.93.a), channel_id=1, source_target_pairs={{0,64},{32,96},{64,0},{96,32},{1,65},{33,97},{65,1},{97,33},{2,66}... | collective-permute-start | bytes 196616 | tf_op jit(solution)/shard_map/ppermute | solution.py:264
  148.9 2.9 %collective-permute-start.11 = (bf16[16,2048]{1,0:T(8,128)(2,1)S(1)}, bf16[16,2048]{1,0:T(8,128)(2,1)S(1)}, u32[]{:S(2)}, u32[]{:S(2)}) collective-permute-start(bf16[16,2048]{1,0:T(8,128)(2,1)S(1)} %shard_map.93.a), channel_id=1, source_target_pairs={{0,1},{1,0},{2,3},{3,2},{4,5},{5,4},{6,7},{7,6},{8,9},{9,8},{10,11... | collective-permute-start | bytes 196616 | tf_op jit(solution)/shard_map/ppermute | solution.py:268
  151.7 0.5 collective-permute-start.15
  152.2 1.9 %collective-permute-start.16 = (bf16[16,2048]{1,0:T(8,128)(2,1)S(1)}, bf16[16,2048]{1,0:T(8,128)(2,1)S(1)}, u32[]{:S(2)}, u32[]{:S(2)}) collective-permute-start(bf16[16,2048]{1,0:T(8,128)(2,1)S(1)} %collective-permute-done.13.refs_2_), channel_id=1, source_target_pairs={{0,1},{1,0},{2,3},{3,2},{4,5},{5,4},{6,7},{7,6},{8,9},{9,8},{10,11... | collective-permute-start | bytes 196616 | tf_op jit(solution)/shard_map/ppermute | solution.py:268
  154.1 1.4 collective-permute-start.17
  155.6 2.4 %shard_map.95.refs_7_ = bf16[6,2048,128]{2,1,0:T(8,128)(2,1)S(1)} custom-call(s32[3]{0:T(128)S(1)} %pad_add_fusion.place, bf16[16384,128]{1,0:T(8,128)(2,1)} %wo.3), custom_call_target="tpu_custom_call" | custom-call | tf_op jit(solution)/shard_map/pallas_call | solution.py:43
  158.0 2.0 %shard_map.94.refs_0_ = f32[16,128]{1,0:T(8,128)S(1)} custom-call(s32[3]{0:T(128)S(1)} %pad_add_fusion.place, bf16[16,2048]{1,0:T(8,128)(2,1)S(1)} %shard_map.93.a, bf16[16,2048]{1,0:T(8,128)(2,1)S(1)} %collective-permute-done.11.b, bf16[16384,128]{1,0:T(8,128)(2,1)} %wo.3, bf16[16,128]{1,0:T(8,128)(2,1)S(1)} %copy-done.1), custom_call_target="tpu_custom_call" | custom-call | tf_op jit(solution)/shard_map/pallas_call | solution.py:43
  160.1 1.1 shard_map.96
  (36 shorter events, 0.1 us)
Async XLA Ops:
  0.0 0.7 copy-start
  1.4 46.0 %all-to-all-start = ((f32[128,1,128]{2,1,0:T(1,128)}), f32[128,1,128]{2,1,0:T(1,128)S(1)}, u32[]{:S(2)}, u32[]{:S(2)}) async-start(f32[128,1,128]{2,1,0:T(1,128)} %bitcast.4), calls=%async_computation | async-start | bytes 131072 | tf_op jit(solution)/shard_map/all_to_all | solution.py:292
  32.5 14.9 %copy-start.1 = (bf16[16,128]{1,0:T(8,128)(2,1)S(1)}, bf16[16,128]{1,0:T(8,128)(2,1)}, u32[]{:S(2)}) copy-start(bf16[16,128]{1,0:T(8,128)(2,1)} %x.5) | copy-start | bytes 12292
  32.5 14.9 %copy-start.3 = (bf16[128]{0:T(256)(128)(2,1)S(1)}, bf16[128]{0:T(256)(128)(2,1)}, u32[]{:S(2)}) copy-start(bf16[128]{0:T(256)(128)(2,1)} %param.9) | copy-start | bytes 772
  47.9 3.9 %collective-permute-start = (f32[4,16,2304]{2,1,0:T(8,128)S(1)}, f32[4,16,2304]{2,1,0:T(8,128)S(1)}, u32[]{:S(2)}, u32[]{:S(2)}) collective-permute-start(f32[4,16,2304]{2,1,0:T(8,128)S(1)} %get-tuple-element.23), channel_id=1, source_target_pairs={{0,1},{1,0},{2,3},{3,2},{4,5},{5,4},{6,7},{7,6},{8,9},{9,8},{10,11... | collective-permute-start | bytes 1769480 | tf_op jit(solution)/shard_map/ppermute | solution.py:268
  51.7 22.7 %copy-start.4 = (s32[16]{0:T(128)S(1)}, s32[16]{0:T(128)}, u32[]{:S(2)}) copy-start(s32[16]{0:T(128)} %lengths.1) | copy-start | bytes 196
  51.7 56.7 %copy-start.2 = (s32[8,16]{1,0:T(8,128)S(1)}, s32[8,16]{1,0:T(8,128)}, u32[]{:S(2)}) copy-start(s32[8,16]{1,0:T(8,128)} %slabs.1) | copy-start | bytes 1540
  51.8 6.7 %collective-permute-start.1 = (f32[16,2304]{1,0:T(8,128)S(1)}, f32[16,2304]{1,0:T(8,128)S(1)}, u32[]{:S(2)}, u32[]{:S(2)}) collective-permute-start(f32[16,2304]{1,0:T(8,128)S(1)} %get-tuple-element.25), channel_id=1, source_target_pairs={{0,32},{32,64},{64,96},{96,0},{1,33},{33,65},{65,97},{97,1},{2,34}... | collective-permute-start | bytes 442376 | tf_op jit(solution)/shard_map/ppermute | solution.py:264
  52.0 8.6 %collective-permute-start.2 = (f32[16,2304]{1,0:T(8,128)S(1)}, f32[16,2304]{1,0:T(8,128)S(1)}, u32[]{:S(2)}, u32[]{:S(2)}) collective-permute-start(f32[16,2304]{1,0:T(8,128)S(1)} %get-tuple-element.26), channel_id=1, source_target_pairs={{0,96},{32,0},{64,32},{96,64},{1,97},{33,1},{65,33},{97,65},{2,98}... | collective-permute-start | bytes 442376 | tf_op jit(solution)/shard_map/ppermute | solution.py:264
  54.6 6.4 %collective-permute-start.3 = (f32[16,2304]{1,0:T(8,128)S(1)}, f32[16,2304]{1,0:T(8,128)S(1)}, u32[]{:S(2)}, u32[]{:S(2)}) collective-permute-start(f32[16,2304]{1,0:T(8,128)S(1)} %get-tuple-element.27), channel_id=1, source_target_pairs={{0,64},{32,96},{64,0},{96,32},{1,65},{33,97},{65,1},{97,33},{2,66}... | collective-permute-start | bytes 442376 | tf_op jit(solution)/shard_map/ppermute | solution.py:264
  61.7 23.0 %all-to-all-start.1 = ((f32[16,1,2304]{2,1,0:T(1,128)}), f32[16,1,2304]{2,1,0:T(1,128)S(1)}, u32[]{:S(2)}, u32[]{:S(2)}) async-start(f32[16,1,2304]{2,1,0:T(1,128)} %bitcast.7), calls=%async_computation.1 | async-start | bytes 294912 | tf_op jit(solution)/shard_map/all_to_all | solution.py:272
  67.8 9.7 %collective-permute-start.10 = (bf16[16,2,32,128]{3,2,1,0:T(8,128)(2,1)S(1)}, bf16[16,2,32,128]{3,2,1,0:T(8,128)(2,1)S(1)}, u32[]{:S(2)}, u32[]{:S(2)}) collective-permute-start(bf16[16,2,32,128]{3,2,1,0:T(8,128)(2,1)S(1)} %get-tuple-element.36), channel_id=1, source_target_pairs={{0,65},{1,64},{32,97},{33,96},{64,1},{65,0},{96,33},{97,32},{2,67}... | collective-permute-start | bytes 786440 | tf_op jit(solution)/shard_map/ppermute | solution.py:342
  69.7 15.0 %collective-permute-start.4 = (bf16[16,2,32,128]{3,2,1,0:T(8,128)(2,1)S(1)}, bf16[16,2,32,128]{3,2,1,0:T(8,128)(2,1)S(1)}, u32[]{:S(2)}, u32[]{:S(2)}) collective-permute-start(bf16[16,2,32,128]{3,2,1,0:T(8,128)(2,1)S(1)} %get-tuple-element.30), channel_id=1, source_target_pairs={{0,32},{1,33},{32,64},{33,65},{64,96},{65,97},{96,0},{97,1},{2,34}... | collective-permute-start | bytes 786440 | tf_op jit(solution)/shard_map/ppermute | solution.py:342
  72.6 25.0 %collective-permute-start.5 = (bf16[16,2,32,128]{3,2,1,0:T(8,128)(2,1)S(1)}, bf16[16,2,32,128]{3,2,1,0:T(8,128)(2,1)S(1)}, u32[]{:S(2)}, u32[]{:S(2)}) collective-permute-start(bf16[16,2,32,128]{3,2,1,0:T(8,128)(2,1)S(1)} %get-tuple-element.31), channel_id=1, source_target_pairs={{0,96},{1,97},{32,0},{33,1},{64,32},{65,33},{96,64},{97,65},{2,98}... | collective-permute-start | bytes 786440 | tf_op jit(solution)/shard_map/ppermute | solution.py:342
  72.6 25.0 %collective-permute-start.6 = (bf16[16,2,32,128]{3,2,1,0:T(8,128)(2,1)S(1)}, bf16[16,2,32,128]{3,2,1,0:T(8,128)(2,1)S(1)}, u32[]{:S(2)}, u32[]{:S(2)}) collective-permute-start(bf16[16,2,32,128]{3,2,1,0:T(8,128)(2,1)S(1)} %get-tuple-element.32), channel_id=1, source_target_pairs={{0,64},{1,65},{32,96},{33,97},{64,0},{65,1},{96,32},{97,33},{2,66}... | collective-permute-start | bytes 786440 | tf_op jit(solution)/shard_map/ppermute | solution.py:342
  74.4 23.2 %collective-permute-start.7 = (bf16[16,2,32,128]{3,2,1,0:T(8,128)(2,1)S(1)}, bf16[16,2,32,128]{3,2,1,0:T(8,128)(2,1)}, u32[]{:S(2)}, u32[]{:S(2)}) collective-permute-start(bf16[16,2,32,128]{3,2,1,0:T(8,128)(2,1)S(1)} %get-tuple-element.33), channel_id=1, source_target_pairs={{0,1},{1,0},{32,33},{33,32},{64,65},{65,64},{96,97},{97,96},{2,3},... | collective-permute-start | bytes 786440 | tf_op jit(solution)/shard_map/ppermute | solution.py:342
  77.5 30.9 %copy-start.5 = (bf16[16,2,32,128]{3,2,1,0:T(8,128)(2,1)}, bf16[16,2,32,128]{3,2,1,0:T(8,128)(2,1)S(1)}, u32[]{:S(2)}) copy-start(bf16[16,2,32,128]{3,2,1,0:T(8,128)(2,1)S(1)} %collective-permute-done.10.refs_7_) | copy-start | bytes 786436
  77.5 20.1 %collective-permute-start.8 = (bf16[16,2,32,128]{3,2,1,0:T(8,128)(2,1)S(1)}, bf16[16,2,32,128]{3,2,1,0:T(8,128)(2,1)S(1)}, u32[]{:S(2)}, u32[]{:S(2)}) collective-permute-start(bf16[16,2,32,128]{3,2,1,0:T(8,128)(2,1)S(1)} %get-tuple-element.34), channel_id=1, source_target_pairs={{0,33},{1,32},{32,65},{33,64},{64,97},{65,96},{96,1},{97,0},{2,35}... | collective-permute-start | bytes 786440 | tf_op jit(solution)/shard_map/ppermute | solution.py:342
  84.7 23.7 %copy-start.6 = (bf16[16,2,32,128]{3,2,1,0:T(8,128)(2,1)}, bf16[16,2,32,128]{3,2,1,0:T(8,128)(2,1)S(1)}, u32[]{:S(2)}) copy-start(bf16[16,2,32,128]{3,2,1,0:T(8,128)(2,1)S(1)} %collective-permute-done.4.refs_1_) | copy-start | bytes 786436
  84.7 13.0 %collective-permute-start.9 = (bf16[16,2,32,128]{3,2,1,0:T(8,128)(2,1)S(1)}, bf16[16,2,32,128]{3,2,1,0:T(8,128)(2,1)S(1)}, u32[]{:S(2)}, u32[]{:S(2)}) collective-permute-start(bf16[16,2,32,128]{3,2,1,0:T(8,128)(2,1)S(1)} %get-tuple-element.35), channel_id=1, source_target_pairs={{0,97},{1,96},{32,1},{33,0},{64,33},{65,32},{96,65},{97,64},{2,99}... | collective-permute-start | bytes 786440 | tf_op jit(solution)/shard_map/ppermute | solution.py:342
  85.5 22.9 %all-to-all-start.2 = ((bf16[16,16,128]{2,1,0:T(8,128)(2,1)}), bf16[16,16,128]{2,1,0:T(8,128)(2,1)S(1)}, u32[]{:S(2)}, u32[]{:S(2)}) async-start(bf16[16,16,128]{2,1,0:T(8,128)(2,1)} %get-tuple-element.28), calls=%async_computation.2 | async-start | bytes 131072 | tf_op jit(solution)/shard_map/all_to_all | solution.py:272
  97.6 10.8 %copy-start.7 = (bf16[16,2,32,128]{3,2,1,0:T(8,128)(2,1)}, bf16[16,2,32,128]{3,2,1,0:T(8,128)(2,1)S(1)}, u32[]{:S(2)}) copy-start(bf16[16,2,32,128]{3,2,1,0:T(8,128)(2,1)S(1)} %collective-permute-done.5.refs_2_) | copy-start | bytes 786436
  97.7 10.8 %copy-start.8 = (bf16[16,2,32,128]{3,2,1,0:T(8,128)(2,1)}, bf16[16,2,32,128]{3,2,1,0:T(8,128)(2,1)S(1)}, u32[]{:S(2)}) copy-start(bf16[16,2,32,128]{3,2,1,0:T(8,128)(2,1)S(1)} %collective-permute-done.6.refs_3_) | copy-start | bytes 786436
  97.7 10.8 %copy-start.9 = (bf16[16,2,32,128]{3,2,1,0:T(8,128)(2,1)}, bf16[16,2,32,128]{3,2,1,0:T(8,128)(2,1)S(1)}, u32[]{:S(2)}) copy-start(bf16[16,2,32,128]{3,2,1,0:T(8,128)(2,1)S(1)} %collective-permute-done.8.refs_5_) | copy-start | bytes 786436
  97.7 10.8 %copy-start.10 = (bf16[16,2,32,128]{3,2,1,0:T(8,128)(2,1)}, bf16[16,2,32,128]{3,2,1,0:T(8,128)(2,1)S(1)}, u32[]{:S(2)}) copy-start(bf16[16,2,32,128]{3,2,1,0:T(8,128)(2,1)S(1)} %collective-permute-done.9.refs_6_) | copy-start | bytes 786436
  142.9 8.8 %collective-permute-start.12 = (bf16[16,2048]{1,0:T(8,128)(2,1)S(1)}, bf16[16,2048]{1,0:T(8,128)(2,1)S(1)}, u32[]{:S(2)}, u32[]{:S(2)}) collective-permute-start(bf16[16,2048]{1,0:T(8,128)(2,1)S(1)} %shard_map.93.a), channel_id=1, source_target_pairs={{0,96},{32,0},{64,32},{96,64},{1,97},{33,1},{65,33},{97,65},{2,98}... | collective-permute-start | bytes 196616 | tf_op jit(solution)/shard_map/ppermute | solution.py:264
  145.9 6.3 %collective-permute-start.13 = (bf16[16,2048]{1,0:T(8,128)(2,1)S(1)}, bf16[16,2048]{1,0:T(8,128)(2,1)S(1)}, u32[]{:S(2)}, u32[]{:S(2)}) collective-permute-start(bf16[16,2048]{1,0:T(8,128)(2,1)S(1)} %shard_map.93.a), channel_id=1, source_target_pairs={{0,32},{32,64},{64,96},{96,0},{1,33},{33,65},{65,97},{97,1},{2,34}... | collective-permute-start | bytes 196616 | tf_op jit(solution)/shard_map/ppermute | solution.py:264
  147.2 6.9 %collective-permute-start.14 = (bf16[16,2048]{1,0:T(8,128)(2,1)S(1)}, bf16[16,2048]{1,0:T(8,128)(2,1)S(1)}, u32[]{:S(2)}, u32[]{:S(2)}) collective-permute-start(bf16[16,2048]{1,0:T(8,128)(2,1)S(1)} %shard_map.93.a), channel_id=1, source_target_pairs={{0,64},{32,96},{64,0},{96,32},{1,65},{33,97},{65,1},{97,33},{2,66}... | collective-permute-start | bytes 196616 | tf_op jit(solution)/shard_map/ppermute | solution.py:264
  148.9 9.1 %collective-permute-start.11 = (bf16[16,2048]{1,0:T(8,128)(2,1)S(1)}, bf16[16,2048]{1,0:T(8,128)(2,1)S(1)}, u32[]{:S(2)}, u32[]{:S(2)}) collective-permute-start(bf16[16,2048]{1,0:T(8,128)(2,1)S(1)} %shard_map.93.a), channel_id=1, source_target_pairs={{0,1},{1,0},{2,3},{3,2},{4,5},{5,4},{6,7},{7,6},{8,9},{9,8},{10,11... | collective-permute-start | bytes 196616 | tf_op jit(solution)/shard_map/ppermute | solution.py:268
  151.7 8.3 %collective-permute-start.15 = (bf16[16,2048]{1,0:T(8,128)(2,1)S(1)}, bf16[16,2048]{1,0:T(8,128)(2,1)S(1)}, u32[]{:S(2)}, u32[]{:S(2)}) collective-permute-start(bf16[16,2048]{1,0:T(8,128)(2,1)S(1)} %collective-permute-done.12.refs_1_), channel_id=1, source_target_pairs={{0,1},{1,0},{2,3},{3,2},{4,5},{5,4},{6,7},{7,6},{8,9},{9,8},{10,11... | collective-permute-start | bytes 196616 | tf_op jit(solution)/shard_map/ppermute | solution.py:268
  152.2 7.8 %collective-permute-start.16 = (bf16[16,2048]{1,0:T(8,128)(2,1)S(1)}, bf16[16,2048]{1,0:T(8,128)(2,1)S(1)}, u32[]{:S(2)}, u32[]{:S(2)}) collective-permute-start(bf16[16,2048]{1,0:T(8,128)(2,1)S(1)} %collective-permute-done.13.refs_2_), channel_id=1, source_target_pairs={{0,1},{1,0},{2,3},{3,2},{4,5},{5,4},{6,7},{7,6},{8,9},{9,8},{10,11... | collective-permute-start | bytes 196616 | tf_op jit(solution)/shard_map/ppermute | solution.py:268
  154.1 6.0 %collective-permute-start.17 = (bf16[16,2048]{1,0:T(8,128)(2,1)S(1)}, bf16[16,2048]{1,0:T(8,128)(2,1)S(1)}, u32[]{:S(2)}, u32[]{:S(2)}) collective-permute-start(bf16[16,2048]{1,0:T(8,128)(2,1)S(1)} %collective-permute-done.14.refs_3_), channel_id=1, source_target_pairs={{0,1},{1,0},{2,3},{3,2},{4,5},{5,4},{6,7},{7,6},{8,9},{9,8},{10,11... | collective-permute-start | bytes 196616 | tf_op jit(solution)/shard_map/ppermute | solution.py:268

commit v3 on v2

--- a/solution.py
+++ b/solution.py
@@ -39,7 +39,8 @@
 
 
 def call(kernel, out, specs, *args, scratch=()):
-    outs = jax.tree.map(lambda _: VMEM, out)
+    is_out = lambda v: not isinstance(v, (list, tuple))
+    outs = jax.tree.map(lambda v: VMEM if isinstance(v, jax.ShapeDtypeStruct) else HBM, out, is_leaf=is_out)
     return pl.pallas_call(
         kernel,
         in_specs=specs,
@@ -115,10 +116,6 @@
 
 def fetch_in_kernel(place, wq, wkv, out, sems):
     run_all(in_copies(place, 1, wq, wkv, out, sems))
-
-
-def fetch_out_kernel(place, wo, out, sems):
-    run_all(out_copies(place, FAR, wo, out, sems))
 
 
 def fetch_cache_kernel(place, cache, *refs):
@@ -244,12 +241,19 @@
         out[:, k * HD : (k + 1) * HD] = wide[:, k, :].astype(BF16)
 
 
-def output_near_kernel(place, a, b, wo, x, out, w, sems):
-    run_all(out_copies(place, NEAR, wo, w, sems))
+def output_near_kernel(place, a, b, wo, x, out, w_far, w, sems, far_sems):
+    near = out_copies(place, NEAR, wo, w, sems)
+    far = out_copies(place, FAR, wo, w_far, far_sems)
+    for copy in near + far:
+        copy.start()
+    for copy in near:
+        copy.wait()
     total = x[...].astype(F32)
     for k, rows in enumerate((a, b)):
         total = total + jnp.dot(rows[...], w[k], preferred_element_type=F32)
     out[...] = total
+    for copy in far:
+        copy.wait()
 
 
 def output_far_kernel(*refs):
@@ -299,7 +303,7 @@
 
     cache = list(call(
         fetch_cache_kernel,
-        [struct(kv_cache.shape[1:], BF16)] * len(MOVES),
+        [pltpu.HBM(kv_cache.shape[1:], BF16)] * len(MOVES),
         [SMEM, HBM],
         place,
         kv_cache,
@@ -329,7 +333,7 @@
     )
     blocks = call(pair_sum_kernel, [struct((n, PW), F32)] * NX, [VMEM] * 2, kept, got)
     parts = [blocks[0]]
-    for k in (1, 3, 2):
+    for k in (2, 1, 3):
         parts.append(shift_x(blocks[k], k))
     rows = call(x_sum_kernel, struct((n * ROWS, HD), F32), [VMEM] * NX, *parts)
     for k, (j, d) in enumerate(MOVES[1:], 1):
@@ -338,7 +342,6 @@
             for x in range(NX)
             for c in range(NC)
         ]
-        cache[k] = pltpu.with_memory_space_constraint(cache[k], pltpu.HBM)
         cache[k] = lax.ppermute(cache[k], ("x", "c"), pairs)
     local = kv_cache.shape[3]
     seen = len(MOVES) * local
@@ -349,14 +352,6 @@
         place,
     )
     rows = across_z(rows.reshape(n, 1, PW)).reshape(n * ROWS, HD)
-    w_far = call(
-        fetch_out_kernel,
-        struct((len(FAR), QW, w_o.shape[1]), BF16),
-        [SMEM, HBM],
-        place,
-        w_o,
-        scratch=[pltpu.SemaphoreType.DMA((len(FAR),))],
-    )
     q, new_score, new_value = call(
         queries_kernel,
         [struct((n, GROUP, HD), BF16), struct((1, HD), F32), struct((1, HD), F32)],
@@ -396,9 +391,9 @@
         rows[k, 0] = shift_x(done, -k)
     for k in (0, 1, 3, 2):
         rows[k, 1] = swap_c(rows[k, 0])
-    total = call(
+    total, w_far = call(
         output_near_kernel,
-        struct((n, depth), F32),
+        [struct((n, depth), F32), struct((len(FAR), QW, w_o.shape[1]), BF16)],
         [SMEM, VMEM, VMEM, HBM, VMEM],
         place,
         *(rows[move] for move in NEAR),
@@ -407,6 +402,7 @@
         scratch=[
             pltpu.VMEM((len(NEAR), QW, w_o.shape[1]), BF16),
             pltpu.SemaphoreType.DMA((len(NEAR),)),
+            pltpu.SemaphoreType.DMA((len(FAR),)),
         ],
     )
     return call(

time: 162 us -> 224 us (1.38)
  Pallas kernels: 18.1 us -> 78.8 us
  starting transfers between devices: 72.6 us -> 68.9 us
  waiting for transfers between devices: 36 us -> 38.7 us
    pallas_call x15 -> x14, Pallas kernels: 18.1 us -> 78.8 us  [call(): pl.pallas_call(kernel, in_specs=specs, out_specs=outs, out_shape=out, scr...]
    ppermute x7, waiting for transfers between devices: 6.39 us -> 8.87 us  [step(): cache[k] = lax.ppermute(cache[k], ('x', 'c'), pairs)]
    ppermute x7, starting transfers between devices: 9.21 us -> 6.81 us  [step(): cache[k] = lax.ppermute(cache[k], ('x', 'c'), pairs)]
  transfers between devices with their start and end apart: 21 -> 21, of which waited for: 7 -> 6; matrix products, arithmetic and copies ran while one was open for 0% -> 0% of each run, Pallas kernels for 8% -> 33%
where the time goes in v3:
time: 224 us
  Pallas kernels  78.8 us (35%)
  starting transfers between devices  68.9 us (31%)
  waiting for transfers between devices  38.7 us (17%)
  blocking collectives  34.1 us (15%)
    pallas_call x14, Pallas kernels, call(): pl.pallas_call(kernel, in_specs=specs, out_specs=outs, out_shape=out, scr...  78.8 us
    all_to_all x2, blocking collectives, across_z(): return lax.all_to_all(value, 'z', 0, 0, tiled=True)  34.1 us
    all_to_all x1, starting transfers between devices, step(): lax.all_to_all(sums.reshape(members, 1, HD), TENSOR, 0, 0, tiled=True)  31 us
    all_to_all x2, starting transfers between devices, across_z(): return lax.all_to_all(value, 'z', 0, 0, tiled=True)  15.2 us
    all_to_all x1, waiting for transfers between devices, step(): lax.all_to_all(sums.reshape(members, 1, HD), TENSOR, 0, 0, tiled=True)  12.6 us
    all_to_all x2, waiting for transfers between devices, across_z(): return lax.all_to_all(value, 'z', 0, 0, tiled=True)  10.8 us
    ppermute x7, waiting for transfers between devices, step(): cache[k] = lax.ppermute(cache[k], ('x', 'c'), pairs)  8.87 us
    ppermute x5, starting transfers between devices, swap_c(): return lax.ppermute(value, 'c', [(0, 1), (1, 0)])  8.39 us
  transfers between devices with their start and end apart: 21, of which 6 were waited for; matrix products, arithmetic and copies ran while one was open for 0% of the time, Pallas kernels for 33%

profile of v3, /device:TPU:33, one launch (start us, length us, event | category | flops | bytes accessed | tf_op | source)
XLA Modules:
  0.0 223.8 jit_solution(18253685152479242887)
XLA Ops:
  0.0 0.7 copy-done.1
  0.7 0.7 shard_map.83
  1.4 31.0 %all-to-all-start = ((f32[128,1,128]{2,1,0:T(1,128)}), f32[128,1,128]{2,1,0:T(1,128)S(1)}, u32[]{:S(2)}, u32[]{:S(2)}) async-start(f32[128,1,128]{2,1,0:T(1,128)} %bitcast.4), calls=%async_computation | async-start | bytes 131072 | tf_op jit(solution)/shard_map/all_to_all | solution.py:296
  32.4 0.1 pad_add_fusion.place
  32.5 2.3 %shard_map.84.w = bf16[4,128,2304]{2,1,0:T(8,128)(2,1)S(1)} custom-call(s32[3]{0:T(128)S(1)} %pad_add_fusion.place, bf16[128,16384]{1,0:T(8,128)(2,1)} %wq.3, bf16[128,2048]{1,0:T(8,128)(2,1)} %wkv.3), custom_call_target="tpu_custom_call" | custom-call | tf_op jit(solution)/shard_map/pallas_call | solution.py:44
  34.8 12.6 %all-to-all-done = f32[128,1,128]{2,1,0:T(1,128)S(1)} async-done(((f32[128,1,128]{2,1,0:T(1,128)}), f32[128,1,128]{2,1,0:T(1,128)S(1)}, u32[]{:S(2)}, u32[]{:S(2)}) %all-to-all-start) | async-done | bytes 65568 | tf_op jit(solution)/shard_map/all_to_all | solution.py:296
  47.4 0.5 shard_map.85
  47.9 1.3 collective-permute-start
  49.2 2.5 %shard_map.86.a = f32[4,16,2304]{2,1,0:T(8,128)S(1)} custom-call(s32[3]{0:T(128)S(1)} %pad_add_fusion.place, bf16[16,128]{1,0:T(8,128)(2,1)S(1)} %get-tuple-element.24.normed, bf16[128,16384]{1,0:T(8,128)(2,1)} %wq.3, bf16[128,2048]{1,0:T(8,128)(2,1)} %wkv.3), custom_call_target="tpu_custom_call" | custom-call | tf_op jit(solution)/shard_map/pallas_call | solution.py:44
  51.7 0.0 copy-start.5
  51.7 0.0 copy-start.3
  51.8 0.0 collective-permute-done.b
  51.8 0.1 shard_map.87
  51.8 1.5 collective-permute-start.1
  53.3 2.7 %collective-permute-start.3 = (f32[16,2304]{1,0:T(8,128)S(1)}, f32[16,2304]{1,0:T(8,128)S(1)}, u32[]{:S(2)}, u32[]{:S(2)}) collective-permute-start(f32[16,2304]{1,0:T(8,128)S(1)} %get-tuple-element.29), channel_id=1, source_target_pairs={{0,96},{32,0},{64,32},{96,64},{1,97},{33,1},{65,33},{97,65},{2,98}... | collective-permute-start | bytes 442376 | tf_op jit(solution)/shard_map/ppermute | solution.py:268
  56.0 2.8 %collective-permute-done.1.b = f32[16,2304]{1,0:T(8,128)S(1)} collective-permute-done((f32[16,2304]{1,0:T(8,128)S(1)}, f32[16,2304]{1,0:T(8,128)S(1)}, u32[]{:S(2)}, u32[]{:S(2)}) %collective-permute-start.1) | collective-permute-done | bytes 147488 | tf_op jit(solution)/shard_map/ppermute | solution.py:268
  58.9 3.6 %collective-permute-done.2.c = f32[16,2304]{1,0:T(8,128)S(1)} collective-permute-done((f32[16,2304]{1,0:T(8,128)S(1)}, f32[16,2304]{1,0:T(8,128)S(1)}, u32[]{:S(2)}, u32[]{:S(2)}) %collective-permute-start.2) | collective-permute-done | bytes 147488 | tf_op jit(solution)/shard_map/ppermute | solution.py:268
  62.4 0.7 shard_map.88
  63.1 4.0 %all-to-all-start.1 = ((f32[16,1,2304]{2,1,0:T(1,128)}), f32[16,1,2304]{2,1,0:T(1,128)S(1)}, u32[]{:S(2)}, u32[]{:S(2)}) async-start(f32[16,1,2304]{2,1,0:T(1,128)} %bitcast.7), calls=%async_computation.1 | async-start | bytes 294912 | tf_op jit(solution)/shard_map/all_to_all | solution.py:276
  67.1 65.3 %shard_map.90 = (bf16[16,2,32,128]{3,2,1,0:T(8,128)(2,1)}, bf16[16,2,32,128]{3,2,1,0:T(8,128)(2,1)}, bf16[16,2,32,128]{3,2,1,0:T(8,128)(2,1)}, bf16[16,2,32,128]...) custom-call(s32[3]{0:T(128)S(1)} %pad_add_fusion.place, ...), custom_call_target="tpu_custom_call" | custom-call | tf_op jit(solution)/shard_map/pallas_call | solution.py:44
  132.3 1.8 collective-permute-start.10
  134.2 2.7 %collective-permute-start.5 = (bf16[16,2,32,128]{3,2,1,0:T(8,128)(2,1)}, bf16[16,2,32,128]{3,2,1,0:T(8,128)(2,1)S(1)}, u32[]{:S(2)}, u32[]{:S(2)}) collective-permute-start(bf16[16,2,32,128]{3,2,1,0:T(8,128)(2,1)} %get-tuple-element.33), channel_id=1, source_target_pairs={{0,96},{1,97},{32,0},{33,1},{64,32},{65,33},{96,64},{97,65},{2,98}... | collective-permute-start | bytes 786440 | tf_op jit(solution)/shard_map/ppermute | solution.py:345
  136.9 0.4 collective-permute-start.6
  137.3 0.9 collective-permute-start.7
  138.1 0.6 fusion
  139.4 3.4 %collective-permute-done.10.refs_7_ = bf16[16,2,32,128]{3,2,1,0:T(8,128)(2,1)S(1)} collective-permute-done((bf16[16,2,32,128]{3,2,1,0:T(8,128)(2,1)}, bf16[16,2,32,128]{3,2,1,0:T(8,128)(2,1)S(1)}, u32[]{:S(2)}, u32[]{:S(2)}) %collective-permute-start.10) | collective-permute-done | bytes 262176 | tf_op jit(solution)/shard_map/ppermute | solution.py:345
  142.8 0.3 collective-permute-start.8
  143.1 5.5 %collective-permute-done.4.refs_1_ = bf16[16,2,32,128]{3,2,1,0:T(8,128)(2,1)S(1)} collective-permute-done((bf16[16,2,32,128]{3,2,1,0:T(8,128)(2,1)}, bf16[16,2,32,128]{3,2,1,0:T(8,128)(2,1)S(1)}, u32[]{:S(2)}, u32[]{:S(2)}) %collective-permute-start.4) | collective-permute-done | bytes 262176 | tf_op jit(solution)/shard_map/ppermute | solution.py:345
  148.5 0.7 collective-permute-start.9
  149.4 0.7 shard_map.89
  150.1 11.2 %all-to-all-start.2 = ((bf16[16,16,128]{2,1,0:T(8,128)(2,1)}), bf16[16,16,128]{2,1,0:T(8,128)(2,1)S(1)}, u32[]{:S(2)}, u32[]{:S(2)}) async-start(bf16[16,16,128]{2,1,0:T(8,128)(2,1)} %get-tuple-element.30), calls=%async_computation.2 | async-start | bytes 131072 | tf_op jit(solution)/shard_map/all_to_all | solution.py:276
  161.3 0.6 shard_map.82.positions
  161.9 0.0 collective-permute-done.5.refs_2_
  161.9 10.8 %all-to-all-done.2.q = bf16[16,16,128]{2,1,0:T(8,128)(2,1)S(1)} async-done(((bf16[16,16,128]{2,1,0:T(8,128)(2,1)}), bf16[16,16,128]{2,1,0:T(8,128)(2,1)S(1)}, u32[]{:S(2)}, u32[]{:S(2)}) %all-to-all-start.2) | async-done | bytes 65568 | tf_op jit(solution)/shard_map/all_to_all | solution.py:276
  172.7 0.9 copy-done
  173.6 1.2 shard_map.91
  174.8 15.8 %all_to_all.25 = f32[16,1,2304]{2,1,0:T(1,128)S(1)} all-to-all(f32[16,1,2304]{2,1,0:T(1,128)S(1)} %bitcast.14), channel_id=1, replica_groups=mesh['groups'=2,'x'=4,'z'=16,'c'=2] {'z'}, dimensions={0} | all-to-all | bytes 294912 | tf_op jit(solution)/shard_map/all_to_all | solution.py:276
  190.6 0.1 shard_map.92
  190.8 18.3 %all_to_all.26.heads = bf16[16,16,128]{2,1,0:T(8,128)(2,1)S(1)} all-to-all(bf16[16,16,128]{2,1,0:T(8,128)(2,1)S(1)} %shard_map.92), channel_id=1, replica_groups=mesh['groups'=2,'x'=4,'z'=16,'c'=2] {'z'}, dimensions={0} | all-to-all | bytes 131072 | tf_op jit(solution)/shard_map/all_to_all | solution.py:276
  209.1 0.1 shard_map.93.a
  209.2 1.8 collective-permute-start.12
  211.0 1.6 collective-permute-start.14
  212.6 2.8 %collective-permute-start.11 = (bf16[16,2048]{1,0:T(8,128)(2,1)S(1)}, bf16[16,2048]{1,0:T(8,128)(2,1)S(1)}, u32[]{:S(2)}, u32[]{:S(2)}) collective-permute-start(bf16[16,2048]{1,0:T(8,128)(2,1)S(1)} %shard_map.93.a), channel_id=1, source_target_pairs={{0,1},{1,0},{2,3},{3,2},{4,5},{5,4},{6,7},{7,6},{8,9},{9,8},{10,11... | collective-permute-start | bytes 196616 | tf_op jit(solution)/shard_map/ppermute | solution.py:272
  215.4 0.7 collective-permute-start.15
  216.1 3.6 %collective-permute-start.16 = (bf16[16,2048]{1,0:T(8,128)(2,1)S(1)}, bf16[16,2048]{1,0:T(8,128)(2,1)S(1)}, u32[]{:S(2)}, u32[]{:S(2)}) collective-permute-start(bf16[16,2048]{1,0:T(8,128)(2,1)S(1)} %collective-permute-done.13.refs_2_), channel_id=1, source_target_pairs={{0,1},{1,0},{2,3},{3,2},{4,5},{5,4},{6,7},{7,6},{8,9},{9,8},{10,11... | collective-permute-start | bytes 196616 | tf_op jit(solution)/shard_map/ppermute | solution.py:272
  219.7 0.0 collective-permute-start.17
  219.7 2.9 %shard_map.94 = (f32[16,128]{1,0:T(8,128)S(1)}, bf16[6,2048,128]{2,1,0:T(8,128)(2,1)S(1)}) custom-call(s32[3]{0:T(128)S(1)} %pad_add_fusion.place, bf16[16,2048]{1,0:T(8,128)(2,1)S(1)} %shard_map.93.a, bf16[16,2048]{1,0:T(8,128)(2,1)S(1)} %collective-permute-done.11.b, bf16[16384,128]{1,0:T(8,128)(2,1)} %wo.1, bf16[16,128]{1,0:T(8,128)(2,1)S(1)} %copy-done.2), custom_call_target="tpu_custom_call" | custom-call | tf_op jit(solution)/shard_map/pallas_call | solution.py:44
  222.7 1.1 shard_map.95
  (25 shorter events, 0.1 us)
Async XLA Ops:
  0.0 0.7 copy-start.1
  1.4 46.0 %all-to-all-start = ((f32[128,1,128]{2,1,0:T(1,128)}), f32[128,1,128]{2,1,0:T(1,128)S(1)}, u32[]{:S(2)}, u32[]{:S(2)}) async-start(f32[128,1,128]{2,1,0:T(1,128)} %bitcast.4), calls=%async_computation | async-start | bytes 131072 | tf_op jit(solution)/shard_map/all_to_all | solution.py:296
  32.5 14.9 %copy-start.2 = (bf16[16,128]{1,0:T(8,128)(2,1)S(1)}, bf16[16,128]{1,0:T(8,128)(2,1)}, u32[]{:S(2)}) copy-start(bf16[16,128]{1,0:T(8,128)(2,1)} %x.5) | copy-start | bytes 12292
  32.5 14.9 %copy-start.4 = (bf16[128]{0:T(256)(128)(2,1)S(1)}, bf16[128]{0:T(256)(128)(2,1)}, u32[]{:S(2)}) copy-start(bf16[128]{0:T(256)(128)(2,1)} %param.9) | copy-start | bytes 772
  47.9 3.8 %collective-permute-start = (f32[4,16,2304]{2,1,0:T(8,128)S(1)}, f32[4,16,2304]{2,1,0:T(8,128)S(1)}, u32[]{:S(2)}, u32[]{:S(2)}) collective-permute-start(f32[4,16,2304]{2,1,0:T(8,128)S(1)} %get-tuple-element.25), channel_id=1, source_target_pairs={{0,1},{1,0},{2,3},{3,2},{4,5},{5,4},{6,7},{7,6},{8,9},{9,8},{10,11... | collective-permute-start | bytes 1769480 | tf_op jit(solution)/shard_map/ppermute | solution.py:272
  51.7 86.4 %copy-start.5 = (s32[16]{0:T(128)S(1)}, s32[16]{0:T(128)}, u32[]{:S(2)}) copy-start(s32[16]{0:T(128)} %lengths.1) | copy-start | bytes 196
  51.7 120.9 %copy-start.3 = (s32[8,16]{1,0:T(8,128)S(1)}, s32[8,16]{1,0:T(8,128)}, u32[]{:S(2)}) copy-start(s32[8,16]{1,0:T(8,128)} %slabs.1) | copy-start | bytes 1540
  51.8 7.0 %collective-permute-start.1 = (f32[16,2304]{1,0:T(8,128)S(1)}, f32[16,2304]{1,0:T(8,128)S(1)}, u32[]{:S(2)}, u32[]{:S(2)}) collective-permute-start(f32[16,2304]{1,0:T(8,128)S(1)} %get-tuple-element.27), channel_id=1, source_target_pairs={{0,64},{32,96},{64,0},{96,32},{1,65},{33,97},{65,1},{97,33},{2,66}... | collective-permute-start | bytes 442376 | tf_op jit(solution)/shard_map/ppermute | solution.py:268
  53.3 9.1 %collective-permute-start.2 = (f32[16,2304]{1,0:T(8,128)S(1)}, f32[16,2304]{1,0:T(8,128)S(1)}, u32[]{:S(2)}, u32[]{:S(2)}) collective-permute-start(f32[16,2304]{1,0:T(8,128)S(1)} %get-tuple-element.28), channel_id=1, source_target_pairs={{0,32},{32,64},{64,96},{96,0},{1,33},{33,65},{65,97},{97,1},{2,34}... | collective-permute-start | bytes 442376 | tf_op jit(solution)/shard_map/ppermute | solution.py:268
  53.3 9.1 %collective-permute-start.3 = (f32[16,2304]{1,0:T(8,128)S(1)}, f32[16,2304]{1,0:T(8,128)S(1)}, u32[]{:S(2)}, u32[]{:S(2)}) collective-permute-start(f32[16,2304]{1,0:T(8,128)S(1)} %get-tuple-element.29), channel_id=1, source_target_pairs={{0,96},{32,0},{64,32},{96,64},{1,97},{33,1},{65,33},{97,65},{2,98}... | collective-permute-start | bytes 442376 | tf_op jit(solution)/shard_map/ppermute | solution.py:268
  63.1 86.2 %all-to-all-start.1 = ((f32[16,1,2304]{2,1,0:T(1,128)}), f32[16,1,2304]{2,1,0:T(1,128)S(1)}, u32[]{:S(2)}, u32[]{:S(2)}) async-start(f32[16,1,2304]{2,1,0:T(1,128)} %bitcast.7), calls=%async_computation.1 | async-start | bytes 294912 | tf_op jit(solution)/shard_map/all_to_all | solution.py:276
  132.3 10.5 %collective-permute-start.10 = (bf16[16,2,32,128]{3,2,1,0:T(8,128)(2,1)}, bf16[16,2,32,128]{3,2,1,0:T(8,128)(2,1)S(1)}, u32[]{:S(2)}, u32[]{:S(2)}) collective-permute-start(bf16[16,2,32,128]{3,2,1,0:T(8,128)(2,1)} %get-tuple-element.38), channel_id=1, source_target_pairs={{0,65},{1,64},{32,97},{33,96},{64,1},{65,0},{96,33},{97,32},{2,67}... | collective-permute-start | bytes 786440 | tf_op jit(solution)/shard_map/ppermute | solution.py:345
  134.2 14.4 %collective-permute-start.4 = (bf16[16,2,32,128]{3,2,1,0:T(8,128)(2,1)}, bf16[16,2,32,128]{3,2,1,0:T(8,128)(2,1)S(1)}, u32[]{:S(2)}, u32[]{:S(2)}) collective-permute-start(bf16[16,2,32,128]{3,2,1,0:T(8,128)(2,1)} %get-tuple-element.32), channel_id=1, source_target_pairs={{0,32},{1,33},{32,64},{33,65},{64,96},{65,97},{96,0},{97,1},{2,34}... | collective-permute-start | bytes 786440 | tf_op jit(solution)/shard_map/ppermute | solution.py:345
  134.2 27.7 %collective-permute-start.5 = (bf16[16,2,32,128]{3,2,1,0:T(8,128)(2,1)}, bf16[16,2,32,128]{3,2,1,0:T(8,128)(2,1)S(1)}, u32[]{:S(2)}, u32[]{:S(2)}) collective-permute-start(bf16[16,2,32,128]{3,2,1,0:T(8,128)(2,1)} %get-tuple-element.33), channel_id=1, source_target_pairs={{0,96},{1,97},{32,0},{33,1},{64,32},{65,33},{96,64},{97,65},{2,98}... | collective-permute-start | bytes 786440 | tf_op jit(solution)/shard_map/ppermute | solution.py:345
  136.9 25.0 %collective-permute-start.6 = (bf16[16,2,32,128]{3,2,1,0:T(8,128)(2,1)}, bf16[16,2,32,128]{3,2,1,0:T(8,128)(2,1)S(1)}, u32[]{:S(2)}, u32[]{:S(2)}) collective-permute-start(bf16[16,2,32,128]{3,2,1,0:T(8,128)(2,1)} %get-tuple-element.34), channel_id=1, source_target_pairs={{0,64},{1,65},{32,96},{33,97},{64,0},{65,1},{96,32},{97,33},{2,66}... | collective-permute-start | bytes 786440 | tf_op jit(solution)/shard_map/ppermute | solution.py:345
  137.3 24.6 %collective-permute-start.7 = (bf16[16,2,32,128]{3,2,1,0:T(8,128)(2,1)}, bf16[16,2,32,128]{3,2,1,0:T(8,128)(2,1)S(1)}, u32[]{:S(2)}, u32[]{:S(2)}) collective-permute-start(bf16[16,2,32,128]{3,2,1,0:T(8,128)(2,1)} %get-tuple-element.35), channel_id=1, source_target_pairs={{0,1},{1,0},{32,33},{33,32},{64,65},{65,64},{96,97},{97,96},{2,3},... | collective-permute-start | bytes 786440 | tf_op jit(solution)/shard_map/ppermute | solution.py:345
  142.8 19.1 %collective-permute-start.8 = (bf16[16,2,32,128]{3,2,1,0:T(8,128)(2,1)}, bf16[16,2,32,128]{3,2,1,0:T(8,128)(2,1)S(1)}, u32[]{:S(2)}, u32[]{:S(2)}) collective-permute-start(bf16[16,2,32,128]{3,2,1,0:T(8,128)(2,1)} %get-tuple-element.36), channel_id=1, source_target_pairs={{0,33},{1,32},{32,65},{33,64},{64,97},{65,96},{96,1},{97,0},{2,35}... | collective-permute-start | bytes 786440 | tf_op jit(solution)/shard_map/ppermute | solution.py:345
  148.5 13.4 %collective-permute-start.9 = (bf16[16,2,32,128]{3,2,1,0:T(8,128)(2,1)}, bf16[16,2,32,128]{3,2,1,0:T(8,128)(2,1)S(1)}, u32[]{:S(2)}, u32[]{:S(2)}) collective-permute-start(bf16[16,2,32,128]{3,2,1,0:T(8,128)(2,1)} %get-tuple-element.37), channel_id=1, source_target_pairs={{0,97},{1,96},{32,1},{33,0},{64,33},{65,32},{96,65},{97,64},{2,99}... | collective-permute-start | bytes 786440 | tf_op jit(solution)/shard_map/ppermute | solution.py:345
  150.1 22.6 %all-to-all-start.2 = ((bf16[16,16,128]{2,1,0:T(8,128)(2,1)}), bf16[16,16,128]{2,1,0:T(8,128)(2,1)S(1)}, u32[]{:S(2)}, u32[]{:S(2)}) async-start(bf16[16,16,128]{2,1,0:T(8,128)(2,1)} %get-tuple-element.30), calls=%async_computation.2 | async-start | bytes 131072 | tf_op jit(solution)/shard_map/all_to_all | solution.py:276
  172.7 1.0 copy-start
  209.2 6.2 %collective-permute-start.12 = (bf16[16,2048]{1,0:T(8,128)(2,1)S(1)}, bf16[16,2048]{1,0:T(8,128)(2,1)S(1)}, u32[]{:S(2)}, u32[]{:S(2)}) collective-permute-start(bf16[16,2048]{1,0:T(8,128)(2,1)S(1)} %shard_map.93.a), channel_id=1, source_target_pairs={{0,96},{32,0},{64,32},{96,64},{1,97},{33,1},{65,33},{97,65},{2,98}... | collective-permute-start | bytes 196616 | tf_op jit(solution)/shard_map/ppermute | solution.py:268
  211.0 5.1 %collective-permute-start.13 = (bf16[16,2048]{1,0:T(8,128)(2,1)S(1)}, bf16[16,2048]{1,0:T(8,128)(2,1)S(1)}, u32[]{:S(2)}, u32[]{:S(2)}) collective-permute-start(bf16[16,2048]{1,0:T(8,128)(2,1)S(1)} %shard_map.93.a), channel_id=1, source_target_pairs={{0,32},{32,64},{64,96},{96,0},{1,33},{33,65},{65,97},{97,1},{2,34}... | collective-permute-start | bytes 196616 | tf_op jit(solution)/shard_map/ppermute | solution.py:268
  211.0 8.7 %collective-permute-start.14 = (bf16[16,2048]{1,0:T(8,128)(2,1)S(1)}, bf16[16,2048]{1,0:T(8,128)(2,1)S(1)}, u32[]{:S(2)}, u32[]{:S(2)}) collective-permute-start(bf16[16,2048]{1,0:T(8,128)(2,1)S(1)} %shard_map.93.a), channel_id=1, source_target_pairs={{0,64},{32,96},{64,0},{96,32},{1,65},{33,97},{65,1},{97,33},{2,66}... | collective-permute-start | bytes 196616 | tf_op jit(solution)/shard_map/ppermute | solution.py:268
  212.6 7.1 %collective-permute-start.11 = (bf16[16,2048]{1,0:T(8,128)(2,1)S(1)}, bf16[16,2048]{1,0:T(8,128)(2,1)S(1)}, u32[]{:S(2)}, u32[]{:S(2)}) collective-permute-start(bf16[16,2048]{1,0:T(8,128)(2,1)S(1)} %shard_map.93.a), channel_id=1, source_target_pairs={{0,1},{1,0},{2,3},{3,2},{4,5},{5,4},{6,7},{7,6},{8,9},{9,8},{10,11... | collective-permute-start | bytes 196616 | tf_op jit(solution)/shard_map/ppermute | solution.py:272
  215.4 7.2 %collective-permute-start.15 = (bf16[16,2048]{1,0:T(8,128)(2,1)S(1)}, bf16[16,2048]{1,0:T(8,128)(2,1)S(1)}, u32[]{:S(2)}, u32[]{:S(2)}) collective-permute-start(bf16[16,2048]{1,0:T(8,128)(2,1)S(1)} %collective-permute-done.12.refs_1_), channel_id=1, source_target_pairs={{0,1},{1,0},{2,3},{3,2},{4,5},{5,4},{6,7},{7,6},{8,9},{9,8},{10,11... | collective-permute-start | bytes 196616 | tf_op jit(solution)/shard_map/ppermute | solution.py:272
  216.1 6.5 %collective-permute-start.16 = (bf16[16,2048]{1,0:T(8,128)(2,1)S(1)}, bf16[16,2048]{1,0:T(8,128)(2,1)S(1)}, u32[]{:S(2)}, u32[]{:S(2)}) collective-permute-start(bf16[16,2048]{1,0:T(8,128)(2,1)S(1)} %collective-permute-done.13.refs_2_), channel_id=1, source_target_pairs={{0,1},{1,0},{2,3},{3,2},{4,5},{5,4},{6,7},{7,6},{8,9},{9,8},{10,11... | collective-permute-start | bytes 196616 | tf_op jit(solution)/shard_map/ppermute | solution.py:272
  219.7 2.9 %collective-permute-start.17 = (bf16[16,2048]{1,0:T(8,128)(2,1)S(1)}, bf16[16,2048]{1,0:T(8,128)(2,1)S(1)}, u32[]{:S(2)}, u32[]{:S(2)}) collective-permute-start(bf16[16,2048]{1,0:T(8,128)(2,1)S(1)} %collective-permute-done.14.refs_3_), channel_id=1, source_target_pairs={{0,1},{1,0},{2,3},{3,2},{4,5},{5,4},{6,7},{7,6},{8,9},{9,8},{10,11... | collective-permute-start | bytes 196616 | tf_op jit(solution)/shard_map/ppermute | solution.py:272

commit v4 on v3

--- a/solution.py
+++ b/solution.py
@@ -119,13 +119,19 @@
 
 
 def fetch_cache_kernel(place, cache, *refs):
-    outs, sems = refs[:-1], refs[-1]
-    run_all(
-        [
-            pltpu.make_async_copy(cache.at[head_of(place, j, d)], outs[k], sems.at[k])
-            for k, (j, d) in enumerate(MOVES)
-        ]
-    )
+    outs, held, sems, out_sems = refs[:-3], *refs[-3:]
+    first, second = [], []
+    for k, (j, d) in enumerate(MOVES):
+        to = outs[k] if k == 0 else held.at[k]
+        first.append(pltpu.make_async_copy(cache.at[head_of(place, j, d)], to, sems.at[k]))
+        first[k].start()
+    for k in range(1, len(MOVES)):
+        first[k].wait()
+        second.append(pltpu.make_async_copy(held.at[k], outs[k], out_sems.at[k]))
+        second[-1].start()
+    first[0].wait()
+    for copy in second:
+        copy.wait()
 
 
 def project_first_kernel(sums, x, gain, w, normed_out, out):
@@ -303,11 +309,16 @@
 
     cache = list(call(
         fetch_cache_kernel,
-        [pltpu.HBM(kv_cache.shape[1:], BF16)] * len(MOVES),
+        [struct(kv_cache.shape[1:], BF16)]
+        + [pltpu.HBM(kv_cache.shape[1:], BF16)] * (len(MOVES) - 1),
         [SMEM, HBM],
         place,
         kv_cache,
-        scratch=[pltpu.SemaphoreType.DMA((len(MOVES),))],
+        scratch=[
+            pltpu.VMEM(kv_cache.shape, BF16),
+            pltpu.SemaphoreType.DMA((len(MOVES),)),
+            pltpu.SemaphoreType.DMA((len(MOVES),)),
+        ],
     ))
 
     product = struct((NX, n, PW), F32)
@@ -333,7 +344,7 @@
     )
     blocks = call(pair_sum_kernel, [struct((n, PW), F32)] * NX, [VMEM] * 2, kept, got)
     parts = [blocks[0]]
-    for k in (2, 1, 3):
+    for k in (1, 3, 2):
         parts.append(shift_x(blocks[k], k))
     rows = call(x_sum_kernel, struct((n * ROWS, HD), F32), [VMEM] * NX, *parts)
     for k, (j, d) in enumerate(MOVES[1:], 1):

time: 224 us -> 160 us (0.71)
  Pallas kernels: 78.8 us -> 16.5 us
  starting transfers between devices: 68.9 us -> 72.4 us
    pallas_call x14, Pallas kernels: 78.8 us -> 16.5 us  [call(): pl.pallas_call(kernel, in_specs=specs, out_specs=outs, out_shape=out, scr...]
    ppermute x7, starting transfers between devices: 6.81 us -> 9.21 us  [step(): cache[k] = lax.ppermute(cache[k], ('x', 'c'), pairs)]
    ppermute x7, waiting for transfers between devices: 8.87 us -> 6.6 us  [step(): cache[k] = lax.ppermute(cache[k], ('x', 'c'), pairs)]
  transfers between devices with their start and end apart: 21 -> 21, of which waited for: 6 -> 7; matrix products, arithmetic and copies ran while one was open for 0% -> 0% of each run, Pallas kernels for 33% -> 7%
where the time goes in v4:
time: 160 us
  starting transfers between devices  72.4 us (45%)
  waiting for transfers between devices  36.5 us (23%)
  blocking collectives  32.1 us (20%)
  Pallas kernels  16.5 us (10%)
    all_to_all x2, blocking collectives, across_z(): return lax.all_to_all(value, 'z', 0, 0, tiled=True)  32.1 us
    all_to_all x1, starting transfers between devices, step(): lax.all_to_all(sums.reshape(members, 1, HD), TENSOR, 0, 0, tiled=True)  31 us
    pallas_call x14, Pallas kernels, call(): pl.pallas_call(kernel, in_specs=specs, out_specs=outs, out_shape=out, scr...  16.5 us
    all_to_all x2, starting transfers between devices, across_z(): return lax.all_to_all(value, 'z', 0, 0, tiled=True)  15.5 us
    all_to_all x1, waiting for transfers between devices, step(): lax.all_to_all(sums.reshape(members, 1, HD), TENSOR, 0, 0, tiled=True)  12.7 us
    all_to_all x2, waiting for transfers between devices, across_z(): return lax.all_to_all(value, 'z', 0, 0, tiled=True)  10.8 us
    ppermute x7, starting transfers between devices, step(): cache[k] = lax.ppermute(cache[k], ('x', 'c'), pairs)  9.21 us
    ppermute x6, starting transfers between devices, shift_x(): return lax.ppermute(value, 'x', [(i, (i + by) % NX) for i in range(NX)])  8.74 us
  transfers between devices with their start and end apart: 21, of which 7 were waited for; matrix products, arithmetic and copies ran while one was open for 0% of the time, Pallas kernels for 7%

profile of v4, /device:TPU:33, one launch (start us, length us, event | category | flops | bytes accessed | tf_op | source)
XLA Modules:
  0.0 159.9 jit_solution(14069878557739128414)
XLA Ops:
  0.0 0.7 copy-done
  0.7 0.7 shard_map.83
  1.4 31.0 %all-to-all-start = ((f32[128,1,128]{2,1,0:T(1,128)}), f32[128,1,128]{2,1,0:T(1,128)S(1)}, u32[]{:S(2)}, u32[]{:S(2)}) async-start(f32[128,1,128]{2,1,0:T(1,128)} %bitcast.4), calls=%async_computation | async-start | bytes 131072 | tf_op jit(solution)/shard_map/all_to_all | solution.py:302
  32.4 0.1 pad_add_fusion.place
  32.5 2.3 %shard_map.84.w = bf16[4,128,2304]{2,1,0:T(8,128)(2,1)S(1)} custom-call(s32[3]{0:T(128)S(1)} %pad_add_fusion.place, bf16[128,16384]{1,0:T(8,128)(2,1)} %wq.3, bf16[128,2048]{1,0:T(8,128)(2,1)} %wkv.3), custom_call_target="tpu_custom_call" | custom-call | tf_op jit(solution)/shard_map/pallas_call | solution.py:44
  34.8 12.7 %all-to-all-done = f32[128,1,128]{2,1,0:T(1,128)S(1)} async-done(((f32[128,1,128]{2,1,0:T(1,128)}), f32[128,1,128]{2,1,0:T(1,128)S(1)}, u32[]{:S(2)}, u32[]{:S(2)}) %all-to-all-start) | async-done | bytes 65568 | tf_op jit(solution)/shard_map/all_to_all | solution.py:302
  47.5 0.5 shard_map.85
  48.0 1.3 collective-permute-start
  49.3 2.5 %shard_map.86.a = f32[4,16,2304]{2,1,0:T(8,128)S(1)} custom-call(s32[3]{0:T(128)S(1)} %pad_add_fusion.place, bf16[16,128]{1,0:T(8,128)(2,1)S(1)} %get-tuple-element.24.normed, bf16[128,16384]{1,0:T(8,128)(2,1)} %wq.3, bf16[128,2048]{1,0:T(8,128)(2,1)} %wkv.3), custom_call_target="tpu_custom_call" | custom-call | tf_op jit(solution)/shard_map/pallas_call | solution.py:44
  51.8 0.0 copy-start.4
  51.8 0.0 copy-start.2
  51.8 0.0 collective-permute-done.b
  51.8 0.1 shard_map.87
  51.9 0.1 collective-permute-start.1
  52.1 2.6 %collective-permute-start.2 = (f32[16,2304]{1,0:T(8,128)S(1)}, f32[16,2304]{1,0:T(8,128)S(1)}, u32[]{:S(2)}, u32[]{:S(2)}) collective-permute-start(f32[16,2304]{1,0:T(8,128)S(1)} %get-tuple-element.28), channel_id=1, source_target_pairs={{0,96},{32,0},{64,32},{96,64},{1,97},{33,1},{65,33},{97,65},{2,98}... | collective-permute-start | bytes 442376 | tf_op jit(solution)/shard_map/ppermute | solution.py:274
  54.7 0.0 collective-permute-start.3
  54.7 3.9 %collective-permute-done.1.b = f32[16,2304]{1,0:T(8,128)S(1)} collective-permute-done((f32[16,2304]{1,0:T(8,128)S(1)}, f32[16,2304]{1,0:T(8,128)S(1)}, u32[]{:S(2)}, u32[]{:S(2)}) %collective-permute-start.1) | collective-permute-done | bytes 147488 | tf_op jit(solution)/shard_map/ppermute | solution.py:274
  58.6 2.0 %collective-permute-done.2.c = f32[16,2304]{1,0:T(8,128)S(1)} collective-permute-done((f32[16,2304]{1,0:T(8,128)S(1)}, f32[16,2304]{1,0:T(8,128)S(1)}, u32[]{:S(2)}, u32[]{:S(2)}) %collective-permute-start.2) | collective-permute-done | bytes 147488 | tf_op jit(solution)/shard_map/ppermute | solution.py:274
  60.6 0.5 collective-permute-done.3.d
  61.1 0.7 shard_map.88
  61.8 4.0 %all-to-all-start.1 = ((f32[16,1,2304]{2,1,0:T(1,128)}), f32[16,1,2304]{2,1,0:T(1,128)S(1)}, u32[]{:S(2)}, u32[]{:S(2)}) async-start(f32[16,1,2304]{2,1,0:T(1,128)} %bitcast.7), calls=%async_computation.1 | async-start | bytes 294912 | tf_op jit(solution)/shard_map/all_to_all | solution.py:282
  65.8 3.0 %shard_map.90 = (bf16[16,2,32,128]{3,2,1,0:T(8,128)(2,1)S(1)}, bf16[16,2,32,128]{3,2,1,0:T(8,128)(2,1)}, bf16[16,2,32,128]{3,2,1,0:T(8,128)(2,1)}, bf16[16,2,32,...) custom-call(s32[3]{0:T(128)S(1)} %pad_add_fusion.place, ...), custom_call_target="tpu_custom_call" | custom-call | tf_op jit(solution)/shard_map/pallas_call | solution.py:44
  68.8 1.9 %collective-permute-start.10 = (bf16[16,2,32,128]{3,2,1,0:T(8,128)(2,1)}, bf16[16,2,32,128]{3,2,1,0:T(8,128)(2,1)S(1)}, u32[]{:S(2)}, u32[]{:S(2)}) collective-permute-start(bf16[16,2,32,128]{3,2,1,0:T(8,128)(2,1)} %get-tuple-element.38), channel_id=1, source_target_pairs={{0,65},{1,64},{32,97},{33,96},{64,1},{65,0},{96,33},{97,32},{2,67}... | collective-permute-start | bytes 786440 | tf_op jit(solution)/shard_map/ppermute | solution.py:356
  70.6 2.9 %collective-permute-start.4 = (bf16[16,2,32,128]{3,2,1,0:T(8,128)(2,1)}, bf16[16,2,32,128]{3,2,1,0:T(8,128)(2,1)S(1)}, u32[]{:S(2)}, u32[]{:S(2)}) collective-permute-start(bf16[16,2,32,128]{3,2,1,0:T(8,128)(2,1)} %get-tuple-element.32), channel_id=1, source_target_pairs={{0,32},{1,33},{32,64},{33,65},{64,96},{65,97},{96,0},{97,1},{2,34}... | collective-permute-start | bytes 786440 | tf_op jit(solution)/shard_map/ppermute | solution.py:356
  73.6 1.8 %collective-permute-start.6 = (bf16[16,2,32,128]{3,2,1,0:T(8,128)(2,1)}, bf16[16,2,32,128]{3,2,1,0:T(8,128)(2,1)S(1)}, u32[]{:S(2)}, u32[]{:S(2)}) collective-permute-start(bf16[16,2,32,128]{3,2,1,0:T(8,128)(2,1)} %get-tuple-element.34), channel_id=1, source_target_pairs={{0,64},{1,65},{32,96},{33,97},{64,0},{65,1},{96,32},{97,33},{2,66}... | collective-permute-start | bytes 786440 | tf_op jit(solution)/shard_map/ppermute | solution.py:356
  75.4 0.0 collective-permute-start.7
  75.4 0.6 fusion
  76.7 2.0 %collective-permute-done.10.refs_7_ = bf16[16,2,32,128]{3,2,1,0:T(8,128)(2,1)S(1)} collective-permute-done((bf16[16,2,32,128]{3,2,1,0:T(8,128)(2,1)}, bf16[16,2,32,128]{3,2,1,0:T(8,128)(2,1)S(1)}, u32[]{:S(2)}, u32[]{:S(2)}) %collective-permute-start.10) | collective-permute-done | bytes 262176 | tf_op jit(solution)/shard_map/ppermute | solution.py:356
  78.7 2.6 %collective-permute-start.8 = (bf16[16,2,32,128]{3,2,1,0:T(8,128)(2,1)}, bf16[16,2,32,128]{3,2,1,0:T(8,128)(2,1)S(1)}, u32[]{:S(2)}, u32[]{:S(2)}) collective-permute-start(bf16[16,2,32,128]{3,2,1,0:T(8,128)(2,1)} %get-tuple-element.36), channel_id=1, source_target_pairs={{0,33},{1,32},{32,65},{33,64},{64,97},{65,96},{96,1},{97,0},{2,35}... | collective-permute-start | bytes 786440 | tf_op jit(solution)/shard_map/ppermute | solution.py:356
  81.3 4.6 %collective-permute-done.4.refs_1_ = bf16[16,2,32,128]{3,2,1,0:T(8,128)(2,1)S(1)} collective-permute-done((bf16[16,2,32,128]{3,2,1,0:T(8,128)(2,1)}, bf16[16,2,32,128]{3,2,1,0:T(8,128)(2,1)S(1)}, u32[]{:S(2)}, u32[]{:S(2)}) %collective-permute-start.4) | collective-permute-done | bytes 262176 | tf_op jit(solution)/shard_map/ppermute | solution.py:356
  85.9 0.7 shard_map.89
  86.6 11.5 %all-to-all-start.2 = ((bf16[16,16,128]{2,1,0:T(8,128)(2,1)}), bf16[16,16,128]{2,1,0:T(8,128)(2,1)S(1)}, u32[]{:S(2)}, u32[]{:S(2)}) async-start(bf16[16,16,128]{2,1,0:T(8,128)(2,1)} %get-tuple-element.30), calls=%async_computation.2 | async-start | bytes 131072 | tf_op jit(solution)/shard_map/all_to_all | solution.py:282
  98.2 0.6 shard_map.82.positions
  98.8 10.8 %all-to-all-done.2.q = bf16[16,16,128]{2,1,0:T(8,128)(2,1)S(1)} async-done(((bf16[16,16,128]{2,1,0:T(8,128)(2,1)}), bf16[16,16,128]{2,1,0:T(8,128)(2,1)S(1)}, u32[]{:S(2)}, u32[]{:S(2)}) %all-to-all-start.2) | async-done | bytes 65568 | tf_op jit(solution)/shard_map/all_to_all | solution.py:282
  109.6 1.2 shard_map.91
  110.8 14.9 %all_to_all.25 = f32[16,1,2304]{2,1,0:T(1,128)S(1)} all-to-all(f32[16,1,2304]{2,1,0:T(1,128)S(1)} %bitcast.14), channel_id=1, replica_groups=mesh['groups'=2,'x'=4,'z'=16,'c'=2] {'z'}, dimensions={0} | all-to-all | bytes 294912 | tf_op jit(solution)/shard_map/all_to_all | solution.py:282
  125.7 0.1 shard_map.92
  125.8 17.2 %all_to_all.26.heads = bf16[16,16,128]{2,1,0:T(8,128)(2,1)S(1)} all-to-all(bf16[16,16,128]{2,1,0:T(8,128)(2,1)S(1)} %shard_map.92), channel_id=1, replica_groups=mesh['groups'=2,'x'=4,'z'=16,'c'=2] {'z'}, dimensions={0} | all-to-all | bytes 131072 | tf_op jit(solution)/shard_map/all_to_all | solution.py:282
  143.0 0.1 shard_map.93.a
  143.2 3.0 %collective-permute-start.12 = (bf16[16,2048]{1,0:T(8,128)(2,1)S(1)}, bf16[16,2048]{1,0:T(8,128)(2,1)S(1)}, u32[]{:S(2)}, u32[]{:S(2)}) collective-permute-start(bf16[16,2048]{1,0:T(8,128)(2,1)S(1)} %shard_map.93.a), channel_id=1, source_target_pairs={{0,96},{32,0},{64,32},{96,64},{1,97},{33,1},{65,33},{97,65},{2,98}... | collective-permute-start | bytes 196616 | tf_op jit(solution)/shard_map/ppermute | solution.py:274
  146.2 1.3 collective-permute-start.13
  147.5 1.7 %collective-permute-start.14 = (bf16[16,2048]{1,0:T(8,128)(2,1)S(1)}, bf16[16,2048]{1,0:T(8,128)(2,1)S(1)}, u32[]{:S(2)}, u32[]{:S(2)}) collective-permute-start(bf16[16,2048]{1,0:T(8,128)(2,1)S(1)} %shard_map.93.a), channel_id=1, source_target_pairs={{0,64},{32,96},{64,0},{96,32},{1,65},{33,97},{65,1},{97,33},{2,66}... | collective-permute-start | bytes 196616 | tf_op jit(solution)/shard_map/ppermute | solution.py:274
  149.1 2.9 %collective-permute-start.11 = (bf16[16,2048]{1,0:T(8,128)(2,1)S(1)}, bf16[16,2048]{1,0:T(8,128)(2,1)S(1)}, u32[]{:S(2)}, u32[]{:S(2)}) collective-permute-start(bf16[16,2048]{1,0:T(8,128)(2,1)S(1)} %shard_map.93.a), channel_id=1, source_target_pairs={{0,1},{1,0},{2,3},{3,2},{4,5},{5,4},{6,7},{7,6},{8,9},{9,8},{10,11... | collective-permute-start | bytes 196616 | tf_op jit(solution)/shard_map/ppermute | solution.py:278
  152.0 0.5 collective-permute-start.15
  152.5 1.9 %collective-permute-start.16 = (bf16[16,2048]{1,0:T(8,128)(2,1)S(1)}, bf16[16,2048]{1,0:T(8,128)(2,1)S(1)}, u32[]{:S(2)}, u32[]{:S(2)}) collective-permute-start(bf16[16,2048]{1,0:T(8,128)(2,1)S(1)} %collective-permute-done.13.refs_2_), channel_id=1, source_target_pairs={{0,1},{1,0},{2,3},{3,2},{4,5},{5,4},{6,7},{7,6},{8,9},{9,8},{10,11... | collective-permute-start | bytes 196616 | tf_op jit(solution)/shard_map/ppermute | solution.py:278
  154.4 1.4 collective-permute-start.17
  155.8 2.9 %shard_map.94 = (f32[16,128]{1,0:T(8,128)S(1)}, bf16[6,2048,128]{2,1,0:T(8,128)(2,1)S(1)}) custom-call(s32[3]{0:T(128)S(1)} %pad_add_fusion.place, bf16[16,2048]{1,0:T(8,128)(2,1)S(1)} %shard_map.93.a, bf16[16,2048]{1,0:T(8,128)(2,1)S(1)} %collective-permute-done.11.b, bf16[16384,128]{1,0:T(8,128)(2,1)} %wo.1, bf16[16,128]{1,0:T(8,128)(2,1)S(1)} %copy-done.1), custom_call_target="tpu_custom_call" | custom-call | tf_op jit(solution)/shard_map/pallas_call | solution.py:44
  158.7 1.1 shard_map.95
  (23 shorter events, 0.1 us)
Async XLA Ops:
  0.0 0.7 copy-start
  1.4 46.1 %all-to-all-start = ((f32[128,1,128]{2,1,0:T(1,128)}), f32[128,1,128]{2,1,0:T(1,128)S(1)}, u32[]{:S(2)}, u32[]{:S(2)}) async-start(f32[128,1,128]{2,1,0:T(1,128)} %bitcast.4), calls=%async_computation | async-start | bytes 131072 | tf_op jit(solution)/shard_map/all_to_all | solution.py:302
  32.5 15.0 %copy-start.1 = (bf16[16,128]{1,0:T(8,128)(2,1)S(1)}, bf16[16,128]{1,0:T(8,128)(2,1)}, u32[]{:S(2)}) copy-start(bf16[16,128]{1,0:T(8,128)(2,1)} %x.5) | copy-start | bytes 12292
  32.5 15.0 %copy-start.3 = (bf16[128]{0:T(256)(128)(2,1)S(1)}, bf16[128]{0:T(256)(128)(2,1)}, u32[]{:S(2)}) copy-start(bf16[128]{0:T(256)(128)(2,1)} %param.9) | copy-start | bytes 772
  48.0 3.8 %collective-permute-start = (f32[4,16,2304]{2,1,0:T(8,128)S(1)}, f32[4,16,2304]{2,1,0:T(8,128)S(1)}, u32[]{:S(2)}, u32[]{:S(2)}) collective-permute-start(f32[4,16,2304]{2,1,0:T(8,128)S(1)} %get-tuple-element.25), channel_id=1, source_target_pairs={{0,1},{1,0},{2,3},{3,2},{4,5},{5,4},{6,7},{7,6},{8,9},{9,8},{10,11... | collective-permute-start | bytes 1769480 | tf_op jit(solution)/shard_map/ppermute | solution.py:278
  51.8 23.6 %copy-start.4 = (s32[16]{0:T(128)S(1)}, s32[16]{0:T(128)}, u32[]{:S(2)}) copy-start(s32[16]{0:T(128)} %lengths.1) | copy-start | bytes 196
  51.8 57.8 %copy-start.2 = (s32[8,16]{1,0:T(8,128)S(1)}, s32[8,16]{1,0:T(8,128)}, u32[]{:S(2)}) copy-start(s32[8,16]{1,0:T(8,128)} %slabs.1) | copy-start | bytes 1540
  51.9 6.7 %collective-permute-start.1 = (f32[16,2304]{1,0:T(8,128)S(1)}, f32[16,2304]{1,0:T(8,128)S(1)}, u32[]{:S(2)}, u32[]{:S(2)}) collective-permute-start(f32[16,2304]{1,0:T(8,128)S(1)} %get-tuple-element.27), channel_id=1, source_target_pairs={{0,32},{32,64},{64,96},{96,0},{1,33},{33,65},{65,97},{97,1},{2,34}... | collective-permute-start | bytes 442376 | tf_op jit(solution)/shard_map/ppermute | solution.py:274
  52.1 8.6 %collective-permute-start.2 = (f32[16,2304]{1,0:T(8,128)S(1)}, f32[16,2304]{1,0:T(8,128)S(1)}, u32[]{:S(2)}, u32[]{:S(2)}) collective-permute-start(f32[16,2304]{1,0:T(8,128)S(1)} %get-tuple-element.28), channel_id=1, source_target_pairs={{0,96},{32,0},{64,32},{96,64},{1,97},{33,1},{65,33},{97,65},{2,98}... | collective-permute-start | bytes 442376 | tf_op jit(solution)/shard_map/ppermute | solution.py:274
  54.7 6.4 %collective-permute-start.3 = (f32[16,2304]{1,0:T(8,128)S(1)}, f32[16,2304]{1,0:T(8,128)S(1)}, u32[]{:S(2)}, u32[]{:S(2)}) collective-permute-start(f32[16,2304]{1,0:T(8,128)S(1)} %get-tuple-element.29), channel_id=1, source_target_pairs={{0,64},{32,96},{64,0},{96,32},{1,65},{33,97},{65,1},{97,33},{2,66}... | collective-permute-start | bytes 442376 | tf_op jit(solution)/shard_map/ppermute | solution.py:274
  61.8 24.1 %all-to-all-start.1 = ((f32[16,1,2304]{2,1,0:T(1,128)}), f32[16,1,2304]{2,1,0:T(1,128)S(1)}, u32[]{:S(2)}, u32[]{:S(2)}) async-start(f32[16,1,2304]{2,1,0:T(1,128)} %bitcast.7), calls=%async_computation.1 | async-start | bytes 294912 | tf_op jit(solution)/shard_map/all_to_all | solution.py:282
  68.8 9.9 %collective-permute-start.10 = (bf16[16,2,32,128]{3,2,1,0:T(8,128)(2,1)}, bf16[16,2,32,128]{3,2,1,0:T(8,128)(2,1)S(1)}, u32[]{:S(2)}, u32[]{:S(2)}) collective-permute-start(bf16[16,2,32,128]{3,2,1,0:T(8,128)(2,1)} %get-tuple-element.38), channel_id=1, source_target_pairs={{0,65},{1,64},{32,97},{33,96},{64,1},{65,0},{96,33},{97,32},{2,67}... | collective-permute-start | bytes 786440 | tf_op jit(solution)/shard_map/ppermute | solution.py:356
  70.6 15.2 %collective-permute-start.4 = (bf16[16,2,32,128]{3,2,1,0:T(8,128)(2,1)}, bf16[16,2,32,128]{3,2,1,0:T(8,128)(2,1)S(1)}, u32[]{:S(2)}, u32[]{:S(2)}) collective-permute-start(bf16[16,2,32,128]{3,2,1,0:T(8,128)(2,1)} %get-tuple-element.32), channel_id=1, source_target_pairs={{0,32},{1,33},{32,64},{33,65},{64,96},{65,97},{96,0},{97,1},{2,34}... | collective-permute-start | bytes 786440 | tf_op jit(solution)/shard_map/ppermute | solution.py:356
  73.6 25.2 %collective-permute-start.5 = (bf16[16,2,32,128]{3,2,1,0:T(8,128)(2,1)}, bf16[16,2,32,128]{3,2,1,0:T(8,128)(2,1)S(1)}, u32[]{:S(2)}, u32[]{:S(2)}) collective-permute-start(bf16[16,2,32,128]{3,2,1,0:T(8,128)(2,1)} %get-tuple-element.33), channel_id=1, source_target_pairs={{0,96},{1,97},{32,0},{33,1},{64,32},{65,33},{96,64},{97,65},{2,98}... | collective-permute-start | bytes 786440 | tf_op jit(solution)/shard_map/ppermute | solution.py:356
  73.6 25.2 %collective-permute-start.6 = (bf16[16,2,32,128]{3,2,1,0:T(8,128)(2,1)}, bf16[16,2,32,128]{3,2,1,0:T(8,128)(2,1)S(1)}, u32[]{:S(2)}, u32[]{:S(2)}) collective-permute-start(bf16[16,2,32,128]{3,2,1,0:T(8,128)(2,1)} %get-tuple-element.34), channel_id=1, source_target_pairs={{0,64},{1,65},{32,96},{33,97},{64,0},{65,1},{96,32},{97,33},{2,66}... | collective-permute-start | bytes 786440 | tf_op jit(solution)/shard_map/ppermute | solution.py:356
  75.4 23.4 %collective-permute-start.7 = (bf16[16,2,32,128]{3,2,1,0:T(8,128)(2,1)}, bf16[16,2,32,128]{3,2,1,0:T(8,128)(2,1)S(1)}, u32[]{:S(2)}, u32[]{:S(2)}) collective-permute-start(bf16[16,2,32,128]{3,2,1,0:T(8,128)(2,1)} %get-tuple-element.35), channel_id=1, source_target_pairs={{0,1},{1,0},{32,33},{33,32},{64,65},{65,64},{96,97},{97,96},{2,3},... | collective-permute-start | bytes 786440 | tf_op jit(solution)/shard_map/ppermute | solution.py:356
  78.7 20.1 %collective-permute-start.8 = (bf16[16,2,32,128]{3,2,1,0:T(8,128)(2,1)}, bf16[16,2,32,128]{3,2,1,0:T(8,128)(2,1)S(1)}, u32[]{:S(2)}, u32[]{:S(2)}) collective-permute-start(bf16[16,2,32,128]{3,2,1,0:T(8,128)(2,1)} %get-tuple-element.36), channel_id=1, source_target_pairs={{0,33},{1,32},{32,65},{33,64},{64,97},{65,96},{96,1},{97,0},{2,35}... | collective-permute-start | bytes 786440 | tf_op jit(solution)/shard_map/ppermute | solution.py:356
  85.9 13.0 %collective-permute-start.9 = (bf16[16,2,32,128]{3,2,1,0:T(8,128)(2,1)}, bf16[16,2,32,128]{3,2,1,0:T(8,128)(2,1)S(1)}, u32[]{:S(2)}, u32[]{:S(2)}) collective-permute-start(bf16[16,2,32,128]{3,2,1,0:T(8,128)(2,1)} %get-tuple-element.37), channel_id=1, source_target_pairs={{0,97},{1,96},{32,1},{33,0},{64,33},{65,32},{96,65},{97,64},{2,99}... | collective-permute-start | bytes 786440 | tf_op jit(solution)/shard_map/ppermute | solution.py:356
  86.6 22.9 %all-to-all-start.2 = ((bf16[16,16,128]{2,1,0:T(8,128)(2,1)}), bf16[16,16,128]{2,1,0:T(8,128)(2,1)S(1)}, u32[]{:S(2)}, u32[]{:S(2)}) async-start(bf16[16,16,128]{2,1,0:T(8,128)(2,1)} %get-tuple-element.30), calls=%async_computation.2 | async-start | bytes 131072 | tf_op jit(solution)/shard_map/all_to_all | solution.py:282
  143.2 8.8 %collective-permute-start.12 = (bf16[16,2048]{1,0:T(8,128)(2,1)S(1)}, bf16[16,2048]{1,0:T(8,128)(2,1)S(1)}, u32[]{:S(2)}, u32[]{:S(2)}) collective-permute-start(bf16[16,2048]{1,0:T(8,128)(2,1)S(1)} %shard_map.93.a), channel_id=1, source_target_pairs={{0,96},{32,0},{64,32},{96,64},{1,97},{33,1},{65,33},{97,65},{2,98}... | collective-permute-start | bytes 196616 | tf_op jit(solution)/shard_map/ppermute | solution.py:274
  146.2 6.3 %collective-permute-start.13 = (bf16[16,2048]{1,0:T(8,128)(2,1)S(1)}, bf16[16,2048]{1,0:T(8,128)(2,1)S(1)}, u32[]{:S(2)}, u32[]{:S(2)}) collective-permute-start(bf16[16,2048]{1,0:T(8,128)(2,1)S(1)} %shard_map.93.a), channel_id=1, source_target_pairs={{0,32},{32,64},{64,96},{96,0},{1,33},{33,65},{65,97},{97,1},{2,34}... | collective-permute-start | bytes 196616 | tf_op jit(solution)/shard_map/ppermute | solution.py:274
  147.5 6.9 %collective-permute-start.14 = (bf16[16,2048]{1,0:T(8,128)(2,1)S(1)}, bf16[16,2048]{1,0:T(8,128)(2,1)S(1)}, u32[]{:S(2)}, u32[]{:S(2)}) collective-permute-start(bf16[16,2048]{1,0:T(8,128)(2,1)S(1)} %shard_map.93.a), channel_id=1, source_target_pairs={{0,64},{32,96},{64,0},{96,32},{1,65},{33,97},{65,1},{97,33},{2,66}... | collective-permute-start | bytes 196616 | tf_op jit(solution)/shard_map/ppermute | solution.py:274
  149.1 6.7 %collective-permute-start.11 = (bf16[16,2048]{1,0:T(8,128)(2,1)S(1)}, bf16[16,2048]{1,0:T(8,128)(2,1)S(1)}, u32[]{:S(2)}, u32[]{:S(2)}) collective-permute-start(bf16[16,2048]{1,0:T(8,128)(2,1)S(1)} %shard_map.93.a), channel_id=1, source_target_pairs={{0,1},{1,0},{2,3},{3,2},{4,5},{5,4},{6,7},{7,6},{8,9},{9,8},{10,11... | collective-permute-start | bytes 196616 | tf_op jit(solution)/shard_map/ppermute | solution.py:278
  152.0 6.7 %collective-permute-start.15 = (bf16[16,2048]{1,0:T(8,128)(2,1)S(1)}, bf16[16,2048]{1,0:T(8,128)(2,1)S(1)}, u32[]{:S(2)}, u32[]{:S(2)}) collective-permute-start(bf16[16,2048]{1,0:T(8,128)(2,1)S(1)} %collective-permute-done.12.refs_1_), channel_id=1, source_target_pairs={{0,1},{1,0},{2,3},{3,2},{4,5},{5,4},{6,7},{7,6},{8,9},{9,8},{10,11... | collective-permute-start | bytes 196616 | tf_op jit(solution)/shard_map/ppermute | solution.py:278
  152.5 6.2 %collective-permute-start.16 = (bf16[16,2048]{1,0:T(8,128)(2,1)S(1)}, bf16[16,2048]{1,0:T(8,128)(2,1)S(1)}, u32[]{:S(2)}, u32[]{:S(2)}) collective-permute-start(bf16[16,2048]{1,0:T(8,128)(2,1)S(1)} %collective-permute-done.13.refs_2_), channel_id=1, source_target_pairs={{0,1},{1,0},{2,3},{3,2},{4,5},{5,4},{6,7},{7,6},{8,9},{9,8},{10,11... | collective-permute-start | bytes 196616 | tf_op jit(solution)/shard_map/ppermute | solution.py:278
  154.4 4.4 %collective-permute-start.17 = (bf16[16,2048]{1,0:T(8,128)(2,1)S(1)}, bf16[16,2048]{1,0:T(8,128)(2,1)S(1)}, u32[]{:S(2)}, u32[]{:S(2)}) collective-permute-start(bf16[16,2048]{1,0:T(8,128)(2,1)S(1)} %collective-permute-done.14.refs_3_), channel_id=1, source_target_pairs={{0,1},{1,0},{2,3},{3,2},{4,5},{5,4},{6,7},{7,6},{8,9},{9,8},{10,11... | collective-permute-start | bytes 196616 | tf_op jit(solution)/shard_map/ppermute | solution.py:278

commit v5 on v4

--- a/solution.py
+++ b/solution.py
@@ -19,7 +19,8 @@
 TENSOR = ("x", "z", "c")
 NEAR = ((0, 0), (0, 1))
 FAR = ((1, 0), (3, 0), (2, 0), (1, 1), (3, 1), (2, 1))
-MOVES = ((0, 0), (1, 0), (3, 0), (2, 0), (0, 1), (1, 1), (3, 1), (2, 1))
+MOVES = ((0, 0), (0, 1), (1, 0), (3, 0), (2, 0), (1, 1), (3, 1), (2, 1))
+EARLY = 4
 
 EPS = 1e-05
 ROPE_BASE = 500000.0
@@ -38,7 +39,7 @@
     return jax.ShapeDtypeStruct(shape, dtype)
 
 
-def call(kernel, out, specs, *args, scratch=()):
+def call(kernel, out, specs, *args, scratch=(), params=LIMIT):
     is_out = lambda v: not isinstance(v, (list, tuple))
     outs = jax.tree.map(lambda v: VMEM if isinstance(v, jax.ShapeDtypeStruct) else HBM, out, is_leaf=is_out)
     return pl.pallas_call(
@@ -47,7 +48,7 @@
         out_specs=outs,
         out_shape=out,
         scratch_shapes=scratch,
-        compiler_params=LIMIT,
+        compiler_params=params,
     )(*args)
 
 
@@ -118,18 +119,19 @@
     run_all(in_copies(place, 1, wq, wkv, out, sems))
 
 
-def fetch_cache_kernel(place, cache, *refs):
+def fetch_cache_kernel(moves, place, cache, *refs):
     outs, held, sems, out_sems = refs[:-3], *refs[-3:]
     first, second = [], []
-    for k, (j, d) in enumerate(MOVES):
-        to = outs[k] if k == 0 else held.at[k]
+    for k, (j, d) in enumerate(moves):
+        stays = (j, d) == (0, 0)
+        to = outs[k] if stays else held.at[k]
         first.append(pltpu.make_async_copy(cache.at[head_of(place, j, d)], to, sems.at[k]))
         first[k].start()
-    for k in range(1, len(MOVES)):
+    for k, move in enumerate(moves):
         first[k].wait()
-        second.append(pltpu.make_async_copy(held.at[k], outs[k], out_sems.at[k]))
-        second[-1].start()
-    first[0].wait()
+        if move != (0, 0):
+            second.append(pltpu.make_async_copy(held.at[k], outs[k], out_sems.at[k]))
+            second[-1].start()
     for copy in second:
         copy.wait()
 
@@ -182,17 +184,24 @@
     new_value[...] = total[GROUP + 1 :].astype(BF16).astype(F32)
 
 
-def positions_kernel(local, place, out):
+def positions_kernel(local, first, last, place, base, out):
     index = lax.broadcasted_iota(jnp.int32, out.shape, 1)
-    start = jnp.zeros_like(index)
-    for k, (j, d) in enumerate(MOVES):
+    start = base[...]
+    for k, (j, d) in list(enumerate(MOVES))[first:last]:
         core = 1 - place[2] if d else place[2]
         block = (lax.rem(place[0] + (NX - j), NX) * NZ + place[1]) * NC + core
         start = jnp.where(index // local == k, block * local, start)
-    out[...] = start + index % local
-
-
-def attend_kernel(lengths, place, slabs, positions, q, *refs):
+    out[...] = start
+
+
+def visible_kernel(local, lengths, positions, q, out):
+    del q
+    here = positions[...] + lax.broadcasted_iota(jnp.int32, positions.shape, 1) % local
+    for b in range(out.shape[0]):
+        out[b : b + 1] = (here < lengths[b]).astype(F32)
+
+
+def attend_kernel(place, slabs, seen, q, *refs):
     caches, out, scores, weights = refs[: len(MOVES)], *refs[len(MOVES) :]
     n = q.shape[0]
     head = place[0] * NC + place[2]
@@ -205,7 +214,7 @@
         )
     for b in range(n):
         rows = slice(b * GROUP, (b + 1) * GROUP)
-        visible = positions[...] < lengths[b]
+        visible = seen[b : b + 1] > 0
         score = jnp.where(visible, scores[rows], NEG)
         top = jnp.max(score, axis=1, keepdims=True)
         weight = jnp.where(visible, jnp.exp(score - top), 0.0)
@@ -298,7 +307,7 @@
     cosine = jnp.cos(angles)
     sine = jnp.sin(angles) * jnp.where(lane < HD // 2, -1.0, 1.0)
 
-    sums = call(squares_kernel, struct((members, HD), F32), [VMEM], hidden_in)
+    sums = call(squares_kernel, struct((members, HD), F32), [VMEM], hidden_in, params=None)
     sums = lax.all_to_all(
         sums.reshape(members, 1, HD), TENSOR, 0, 0, tiled=True
     ).reshape(members, HD)
@@ -307,19 +316,31 @@
     dmas = pltpu.SemaphoreType.DMA((NX, 3))
     w_theirs = call(fetch_in_kernel, half, [SMEM, HBM, HBM], place, w_q, w_kv, scratch=[dmas])
 
-    cache = list(call(
-        fetch_cache_kernel,
-        [struct(kv_cache.shape[1:], BF16)]
-        + [pltpu.HBM(kv_cache.shape[1:], BF16)] * (len(MOVES) - 1),
-        [SMEM, HBM],
+    cache = []
+    for moves in (MOVES[:EARLY], MOVES[EARLY:]):
+        block = kv_cache.shape[1:]
+        cache += call(
+            functools.partial(fetch_cache_kernel, moves),
+            [struct(block, BF16) if move == (0, 0) else pltpu.HBM(block, BF16) for move in moves],
+            [SMEM, HBM],
+            place,
+            kv_cache,
+            scratch=[
+                pltpu.VMEM((len(moves),) + block, BF16),
+                pltpu.SemaphoreType.DMA((len(moves),)),
+                pltpu.SemaphoreType.DMA((len(moves),)),
+            ],
+        )
+
+    local = kv_cache.shape[3]
+    seen = len(MOVES) * local
+    positions = call(
+        functools.partial(positions_kernel, local, 0, EARLY),
+        struct((1, seen), jnp.int32),
+        [SMEM, VMEM],
         place,
-        kv_cache,
-        scratch=[
-            pltpu.VMEM(kv_cache.shape, BF16),
-            pltpu.SemaphoreType.DMA((len(MOVES),)),
-            pltpu.SemaphoreType.DMA((len(MOVES),)),
-        ],
-    ))
+        jnp.zeros((1, seen), jnp.int32),
+    )
 
     product = struct((NX, n, PW), F32)
     normed, sent = call(
@@ -354,13 +375,12 @@
             for c in range(NC)
         ]
         cache[k] = lax.ppermute(cache[k], ("x", "c"), pairs)
-    local = kv_cache.shape[3]
-    seen = len(MOVES) * local
     positions = call(
-        functools.partial(positions_kernel, local),
+        functools.partial(positions_kernel, local, EARLY, len(MOVES)),
         struct((1, seen), jnp.int32),
-        [SMEM],
+        [SMEM, VMEM],
         place,
+        positions,
     )
     rows = across_z(rows.reshape(n, 1, PW)).reshape(n * ROWS, HD)
     q, new_score, new_value = call(
@@ -373,14 +393,21 @@
     )
     q = across_z(q)
 
+    visible = call(
+        functools.partial(visible_kernel, local),
+        struct((n, seen), F32),
+        [SMEM, VMEM, VMEM],
+        lengths,
+        positions,
+        q,
+    )
     partial = call(
         attend_kernel,
         struct((n * ROWS, HD), F32),
-        [SMEM, SMEM, SMEM] + [VMEM] * (2 + len(MOVES)),
-        lengths,
+        [SMEM, SMEM] + [VMEM] * (2 + len(MOVES)),
         place,
         slab_index,
-        positions,
+        visible,
         q,
         *cache,
         scratch=[pltpu.VMEM((n * GROUP, seen), F32), pltpu.VMEM((n * GROUP, seen), BF16)],

time: 160 us -> 158 us (0.988)
  waiting for transfers between devices: 36.5 us -> 29.3 us
  Pallas kernels: 16.5 us -> 20.5 us
    ppermute x7, waiting for transfers between devices: 6.6 us -> 0.02 us  [step(): cache[k] = lax.ppermute(cache[k], ('x', 'c'), pairs)]
    pallas_call x14 -> x17, Pallas kernels: 16.5 us -> 20.5 us  [call(): pl.pallas_call(kernel, in_specs=specs, out_specs=outs, out_shape=out, scr...]
    ppermute x6, starting transfers between devices: 8.74 us -> 6.91 us  [shift_x(): return lax.ppermute(value, 'x', [(i, (i + by) % NX) for i in range(NX)])]
  transfers between devices with their start and end apart: 21 -> 21, of which waited for: 7 -> 5; matrix products, arithmetic and copies ran while one was open for 0% -> 0% of each run, Pallas kernels for 7% -> 10%
where the time goes in v5:
time: 158 us; the launch traced here: 157 us
  starting transfers between devices  72 us (46%)
  blocking collectives  33.4 us (21%)
  waiting for transfers between devices  29.3 us (19%)
  Pallas kernels  20.5 us (13%)
    all_to_all x2, blocking collectives, across_z(): return lax.all_to_all(value, 'z', 0, 0, tiled=True)  33.4 us
    all_to_all x1, starting transfers between devices, step(): lax.all_to_all(sums.reshape(members, 1, HD), TENSOR, 0, 0, tiled=True)  31 us
    pallas_call x17, Pallas kernels, call(): pl.pallas_call(kernel, in_specs=specs, out_specs=outs, out_shape=out, scr...  20.5 us
    all_to_all x2, starting transfers between devices, across_z(): return lax.all_to_all(value, 'z', 0, 0, tiled=True)  15.5 us
    all_to_all x1, waiting for transfers between devices, step(): lax.all_to_all(sums.reshape(members, 1, HD), TENSOR, 0, 0, tiled=True)  12.7 us
    ppermute x7, starting transfers between devices, step(): cache[k] = lax.ppermute(cache[k], ('x', 'c'), pairs)  10.5 us
    all_to_all x2, waiting for transfers between devices, across_z(): return lax.all_to_all(value, 'z', 0, 0, tiled=True)  10.2 us
    ppermute x5, starting transfers between devices, swap_c(): return lax.ppermute(value, 'c', [(0, 1), (1, 0)])  8.15 us
  transfers between devices with their start and end apart: 21, of which 5 were waited for; matrix products, arithmetic and copies ran while one was open for 0% of the time, Pallas kernels for 10%

profile of v5, /device:TPU:33, one launch (start us, length us, event | category | flops | bytes accessed | tf_op | source)
XLA Modules:
  0.0 157.0 jit_solution(7493291797107101683)
XLA Ops:
  0.0 1.4 shard_map.84
  1.4 31.0 %all-to-all-start = ((f32[128,1,128]{2,1,0:T(1,128)}), f32[128,1,128]{2,1,0:T(1,128)S(1)}, u32[]{:S(2)}, u32[]{:S(2)}) async-start(f32[128,1,128]{2,1,0:T(1,128)} %bitcast.17), calls=%async_computation | async-start | bytes 131072 | tf_op jit(solution)/shard_map/all_to_all | solution.py:311
  32.4 0.1 pad_add_fusion.place
  32.5 2.3 %shard_map.85.w = bf16[4,128,2304]{2,1,0:T(8,128)(2,1)S(1)} custom-call(s32[3]{0:T(128)S(1)} %pad_add_fusion.place, bf16[128,16384]{1,0:T(8,128)(2,1)} %wq.3, bf16[128,2048]{1,0:T(8,128)(2,1)} %wkv.3), custom_call_target="tpu_custom_call" | custom-call | tf_op jit(solution)/shard_map/pallas_call | solution.py:45
  34.8 12.7 %all-to-all-done = f32[128,1,128]{2,1,0:T(1,128)S(1)} async-done(((f32[128,1,128]{2,1,0:T(1,128)}), f32[128,1,128]{2,1,0:T(1,128)S(1)}, u32[]{:S(2)}, u32[]{:S(2)}) %all-to-all-start) | async-done | bytes 65568 | tf_op jit(solution)/shard_map/all_to_all | solution.py:311
  47.5 0.5 shard_map.86
  48.0 1.3 collective-permute-start
  49.3 2.5 %shard_map.87.a = f32[4,16,2304]{2,1,0:T(8,128)S(1)} custom-call(s32[3]{0:T(128)S(1)} %pad_add_fusion.place, bf16[16,128]{1,0:T(8,128)(2,1)S(1)} %get-tuple-element.24.normed, bf16[128,16384]{1,0:T(8,128)(2,1)} %wq.3, bf16[128,2048]{1,0:T(8,128)(2,1)} %wkv.3), custom_call_target="tpu_custom_call" | custom-call | tf_op jit(solution)/shard_map/pallas_call | solution.py:45
  51.8 0.0 copy-start.2
  51.8 0.0 copy-start.1
  51.9 0.1 shard_map.88
  51.9 0.1 collective-permute-start.1
  52.1 2.6 %collective-permute-start.2 = (f32[16,2304]{1,0:T(8,128)S(1)}, f32[16,2304]{1,0:T(8,128)S(1)}, u32[]{:S(2)}, u32[]{:S(2)}) collective-permute-start(f32[16,2304]{1,0:T(8,128)S(1)} %get-tuple-element.28), channel_id=1, source_target_pairs={{0,96},{32,0},{64,32},{96,64},{1,97},{33,1},{65,33},{97,65},{2,98}... | collective-permute-start | bytes 442376 | tf_op jit(solution)/shard_map/ppermute | solution.py:283
  54.7 0.0 collective-permute-start.3
  54.7 3.9 %collective-permute-done.1.b = f32[16,2304]{1,0:T(8,128)S(1)} collective-permute-done((f32[16,2304]{1,0:T(8,128)S(1)}, f32[16,2304]{1,0:T(8,128)S(1)}, u32[]{:S(2)}, u32[]{:S(2)}) %collective-permute-start.1) | collective-permute-done | bytes 147488 | tf_op jit(solution)/shard_map/ppermute | solution.py:283
  58.6 2.0 %collective-permute-done.2.c = f32[16,2304]{1,0:T(8,128)S(1)} collective-permute-done((f32[16,2304]{1,0:T(8,128)S(1)}, f32[16,2304]{1,0:T(8,128)S(1)}, u32[]{:S(2)}, u32[]{:S(2)}) %collective-permute-start.2) | collective-permute-done | bytes 147488 | tf_op jit(solution)/shard_map/ppermute | solution.py:283
  60.6 0.5 collective-permute-done.3.d
  61.1 0.7 shard_map.89
  61.8 4.0 %all-to-all-start.1 = ((f32[16,1,2304]{2,1,0:T(1,128)}), f32[16,1,2304]{2,1,0:T(1,128)S(1)}, u32[]{:S(2)}, u32[]{:S(2)}) async-start(f32[16,1,2304]{2,1,0:T(1,128)} %bitcast.7), calls=%async_computation.1 | async-start | bytes 294912 | tf_op jit(solution)/shard_map/all_to_all | solution.py:291
  65.8 2.5 %shard_map.93 = (bf16[16,2,32,128]{3,2,1,0:T(8,128)(2,1)}, bf16[16,2,32,128]{3,2,1,0:T(8,128)(2,1)}, bf16[16,2,32,128]{3,2,1,0:T(8,128)(2,1)}, bf16[16,2,32,128]{3,2,1,0:T(8,128)(2,1)}) custom-call(s32[3]{0:T(128)S(1)} %pad_add_fusion.place, bf16[8,16,2,32,128]{4,3,2,1,0:T(8,128)(2,1)} %cache.3), custom_call_target="tpu_custom_call" | custom-call | tf_op jit(solution)/shard_map/pallas_call | solution.py:45
  68.3 1.9 %collective-permute-start.10 = (bf16[16,2,32,128]{3,2,1,0:T(8,128)(2,1)}, bf16[16,2,32,128]{3,2,1,0:T(8,128)(2,1)S(1)}, u32[]{:S(2)}, u32[]{:S(2)}) collective-permute-start(bf16[16,2,32,128]{3,2,1,0:T(8,128)(2,1)} %get-tuple-element.38), channel_id=1, source_target_pairs={{0,65},{1,64},{32,97},{33,96},{64,1},{65,0},{96,33},{97,32},{2,67}... | collective-permute-start | bytes 786440 | tf_op jit(solution)/shard_map/ppermute | solution.py:377
  70.2 2.6 %shard_map.92 = (bf16[16,2,32,128]{3,2,1,0:T(8,128)(2,1)S(1)}, bf16[16,2,32,128]{3,2,1,0:T(8,128)(2,1)}, bf16[16,2,32,128]{3,2,1,0:T(8,128)(2,1)}, bf16[16,2,32,128]{3,2,1,0:T(8,128)(2,1)}) custom-call(s32[3]{0:T(128)S(1)} %pad_add_fusion.place, bf16[8,16,2,32,128]{4,3,2,1,0:T(8,128)(2,1)} %cache.3), custom_call_target="tpu_custom_call" | custom-call | tf_op jit(solution)/shard_map/pallas_call | solution.py:45
  72.8 0.1 collective-permute-start.4
  72.9 3.1 %collective-permute-start.5 = (bf16[16,2,32,128]{3,2,1,0:T(8,128)(2,1)}, bf16[16,2,32,128]{3,2,1,0:T(8,128)(2,1)S(1)}, u32[]{:S(2)}, u32[]{:S(2)}) collective-permute-start(bf16[16,2,32,128]{3,2,1,0:T(8,128)(2,1)} %get-tuple-element.33), channel_id=1, source_target_pairs={{0,32},{1,33},{32,64},{33,65},{64,96},{65,97},{96,0},{97,1},{2,34}... | collective-permute-start | bytes 786440 | tf_op jit(solution)/shard_map/ppermute | solution.py:377
  76.0 1.9 %collective-permute-start.7 = (bf16[16,2,32,128]{3,2,1,0:T(8,128)(2,1)}, bf16[16,2,32,128]{3,2,1,0:T(8,128)(2,1)S(1)}, u32[]{:S(2)}, u32[]{:S(2)}) collective-permute-start(bf16[16,2,32,128]{3,2,1,0:T(8,128)(2,1)} %get-tuple-element.35), channel_id=1, source_target_pairs={{0,64},{1,65},{32,96},{33,97},{64,0},{65,1},{96,32},{97,33},{2,66}... | collective-permute-start | bytes 786440 | tf_op jit(solution)/shard_map/ppermute | solution.py:377
  77.9 0.6 fusion
  79.2 1.6 %collective-permute-start.8 = (bf16[16,2,32,128]{3,2,1,0:T(8,128)(2,1)}, bf16[16,2,32,128]{3,2,1,0:T(8,128)(2,1)S(1)}, u32[]{:S(2)}, u32[]{:S(2)}) collective-permute-start(bf16[16,2,32,128]{3,2,1,0:T(8,128)(2,1)} %get-tuple-element.36), channel_id=1, source_target_pairs={{0,33},{1,32},{32,65},{33,64},{64,97},{65,96},{96,1},{97,0},{2,35}... | collective-permute-start | bytes 786440 | tf_op jit(solution)/shard_map/ppermute | solution.py:377
  80.9 1.8 %collective-permute-start.9 = (bf16[16,2,32,128]{3,2,1,0:T(8,128)(2,1)}, bf16[16,2,32,128]{3,2,1,0:T(8,128)(2,1)S(1)}, u32[]{:S(2)}, u32[]{:S(2)}) collective-permute-start(bf16[16,2,32,128]{3,2,1,0:T(8,128)(2,1)} %get-tuple-element.37), channel_id=1, source_target_pairs={{0,97},{1,96},{32,1},{33,0},{64,33},{65,32},{96,65},{97,64},{2,99}... | collective-permute-start | bytes 786440 | tf_op jit(solution)/shard_map/ppermute | solution.py:377
  82.8 0.7 shard_map.90
  83.5 11.5 %all-to-all-start.2 = ((bf16[16,16,128]{2,1,0:T(8,128)(2,1)}), bf16[16,16,128]{2,1,0:T(8,128)(2,1)S(1)}, u32[]{:S(2)}, u32[]{:S(2)}) async-start(bf16[16,16,128]{2,1,0:T(8,128)(2,1)} %get-tuple-element.30), calls=%async_computation.2 | async-start | bytes 131072 | tf_op jit(solution)/shard_map/all_to_all | solution.py:291
  95.1 0.6 shard_map.82.base
  95.6 0.6 shard_map.83.positions
  96.2 10.2 %all-to-all-done.2.q = bf16[16,16,128]{2,1,0:T(8,128)(2,1)S(1)} async-done(((bf16[16,16,128]{2,1,0:T(8,128)(2,1)}), bf16[16,16,128]{2,1,0:T(8,128)(2,1)S(1)}, u32[]{:S(2)}, u32[]{:S(2)}) %all-to-all-start.2) | async-done | bytes 65568 | tf_op jit(solution)/shard_map/all_to_all | solution.py:291
  106.4 0.6 shard_map.91.seen
  107.0 1.2 shard_map.94
  108.2 15.6 %all_to_all.25 = f32[16,1,2304]{2,1,0:T(1,128)S(1)} all-to-all(f32[16,1,2304]{2,1,0:T(1,128)S(1)} %bitcast.12), channel_id=1, replica_groups=mesh['groups'=2,'x'=4,'z'=16,'c'=2] {'z'}, dimensions={0} | all-to-all | bytes 294912 | tf_op jit(solution)/shard_map/all_to_all | solution.py:291
  123.9 0.1 shard_map.95
  124.0 17.8 %all_to_all.26.heads = bf16[16,16,128]{2,1,0:T(8,128)(2,1)S(1)} all-to-all(bf16[16,16,128]{2,1,0:T(8,128)(2,1)S(1)} %shard_map.95), channel_id=1, replica_groups=mesh['groups'=2,'x'=4,'z'=16,'c'=2] {'z'}, dimensions={0} | all-to-all | bytes 131072 | tf_op jit(solution)/shard_map/all_to_all | solution.py:291
  141.8 0.1 shard_map.96.a
  142.0 0.1 collective-permute-start.12
  142.1 1.4 collective-permute-start.13
  143.5 2.5 %collective-permute-start.14 = (bf16[16,2048]{1,0:T(8,128)(2,1)S(1)}, bf16[16,2048]{1,0:T(8,128)(2,1)S(1)}, u32[]{:S(2)}, u32[]{:S(2)}) collective-permute-start(bf16[16,2048]{1,0:T(8,128)(2,1)S(1)} %shard_map.96.a), channel_id=1, source_target_pairs={{0,64},{32,96},{64,0},{96,32},{1,65},{33,97},{65,1},{97,33},{2,66}... | collective-permute-start | bytes 196616 | tf_op jit(solution)/shard_map/ppermute | solution.py:283
  146.1 3.0 %collective-permute-start.11 = (bf16[16,2048]{1,0:T(8,128)(2,1)S(1)}, bf16[16,2048]{1,0:T(8,128)(2,1)S(1)}, u32[]{:S(2)}, u32[]{:S(2)}) collective-permute-start(bf16[16,2048]{1,0:T(8,128)(2,1)S(1)} %shard_map.96.a), channel_id=1, source_target_pairs={{0,1},{1,0},{2,3},{3,2},{4,5},{5,4},{6,7},{7,6},{8,9},{9,8},{10,11... | collective-permute-start | bytes 196616 | tf_op jit(solution)/shard_map/ppermute | solution.py:287
  149.1 0.3 collective-permute-start.15
  149.4 1.3 collective-permute-start.16
  150.8 2.2 %collective-permute-start.17 = (bf16[16,2048]{1,0:T(8,128)(2,1)S(1)}, bf16[16,2048]{1,0:T(8,128)(2,1)S(1)}, u32[]{:S(2)}, u32[]{:S(2)}) collective-permute-start(bf16[16,2048]{1,0:T(8,128)(2,1)S(1)} %collective-permute-done.14.refs_3_), channel_id=1, source_target_pairs={{0,1},{1,0},{2,3},{3,2},{4,5},{5,4},{6,7},{7,6},{8,9},{9,8},{10,11... | collective-permute-start | bytes 196616 | tf_op jit(solution)/shard_map/ppermute | solution.py:287
  152.9 2.9 %shard_map.97 = (f32[16,128]{1,0:T(8,128)S(1)}, bf16[6,2048,128]{2,1,0:T(8,128)(2,1)S(1)}) custom-call(s32[3]{0:T(128)S(1)} %pad_add_fusion.place, bf16[16,2048]{1,0:T(8,128)(2,1)S(1)} %shard_map.96.a, bf16[16,2048]{1,0:T(8,128)(2,1)S(1)} %collective-permute-done.11.b, bf16[16384,128]{1,0:T(8,128)(2,1)} %wo.1, bf16[16,128]{1,0:T(8,128)(2,1)S(1)} %copy-done), custom_call_target="tpu_custom_call" | custom-call | tf_op jit(solution)/shard_map/pallas_call | solution.py:45
  155.9 1.1 shard_map.98
  (25 shorter events, 0.1 us)
Async XLA Ops:
  1.4 46.1 %all-to-all-start = ((f32[128,1,128]{2,1,0:T(1,128)}), f32[128,1,128]{2,1,0:T(1,128)S(1)}, u32[]{:S(2)}, u32[]{:S(2)}) async-start(f32[128,1,128]{2,1,0:T(1,128)} %bitcast.17), calls=%async_computation | async-start | bytes 131072 | tf_op jit(solution)/shard_map/all_to_all | solution.py:311
  32.5 15.0 %copy-start = (bf16[16,128]{1,0:T(8,128)(2,1)S(1)}, bf16[16,128]{1,0:T(8,128)(2,1)}, u32[]{:S(2)}) copy-start(bf16[16,128]{1,0:T(8,128)(2,1)} %x.5) | copy-start | bytes 12292
  32.5 15.0 %copy-start.3 = (bf16[128]{0:T(256)(128)(2,1)S(1)}, bf16[128]{0:T(256)(128)(2,1)}, u32[]{:S(2)}) copy-start(bf16[128]{0:T(256)(128)(2,1)} %param.9) | copy-start | bytes 772
  48.0 3.8 %collective-permute-start = (f32[4,16,2304]{2,1,0:T(8,128)S(1)}, f32[4,16,2304]{2,1,0:T(8,128)S(1)}, u32[]{:S(2)}, u32[]{:S(2)}) collective-permute-start(f32[4,16,2304]{2,1,0:T(8,128)S(1)} %get-tuple-element.25), channel_id=1, source_target_pairs={{0,1},{1,0},{2,3},{3,2},{4,5},{5,4},{6,7},{7,6},{8,9},{9,8},{10,11... | collective-permute-start | bytes 1769480 | tf_op jit(solution)/shard_map/ppermute | solution.py:287
  51.8 26.1 %copy-start.2 = (s32[16]{0:T(128)S(1)}, s32[16]{0:T(128)}, u32[]{:S(2)}) copy-start(s32[16]{0:T(128)} %lengths.1) | copy-start | bytes 196
  51.8 55.2 %copy-start.1 = (s32[8,16]{1,0:T(8,128)S(1)}, s32[8,16]{1,0:T(8,128)}, u32[]{:S(2)}) copy-start(s32[8,16]{1,0:T(8,128)} %slabs.1) | copy-start | bytes 1540
  51.9 6.7 %collective-permute-start.1 = (f32[16,2304]{1,0:T(8,128)S(1)}, f32[16,2304]{1,0:T(8,128)S(1)}, u32[]{:S(2)}, u32[]{:S(2)}) collective-permute-start(f32[16,2304]{1,0:T(8,128)S(1)} %get-tuple-element.27), channel_id=1, source_target_pairs={{0,32},{32,64},{64,96},{96,0},{1,33},{33,65},{65,97},{97,1},{2,34}... | collective-permute-start | bytes 442376 | tf_op jit(solution)/shard_map/ppermute | solution.py:283
  52.1 8.6 %collective-permute-start.2 = (f32[16,2304]{1,0:T(8,128)S(1)}, f32[16,2304]{1,0:T(8,128)S(1)}, u32[]{:S(2)}, u32[]{:S(2)}) collective-permute-start(f32[16,2304]{1,0:T(8,128)S(1)} %get-tuple-element.28), channel_id=1, source_target_pairs={{0,96},{32,0},{64,32},{96,64},{1,97},{33,1},{65,33},{97,65},{2,98}... | collective-permute-start | bytes 442376 | tf_op jit(solution)/shard_map/ppermute | solution.py:283
  54.7 6.4 %collective-permute-start.3 = (f32[16,2304]{1,0:T(8,128)S(1)}, f32[16,2304]{1,0:T(8,128)S(1)}, u32[]{:S(2)}, u32[]{:S(2)}) collective-permute-start(f32[16,2304]{1,0:T(8,128)S(1)} %get-tuple-element.29), channel_id=1, source_target_pairs={{0,64},{32,96},{64,0},{96,32},{1,65},{33,97},{65,1},{97,33},{2,66}... | collective-permute-start | bytes 442376 | tf_op jit(solution)/shard_map/ppermute | solution.py:283
  61.8 21.0 %all-to-all-start.1 = ((f32[16,1,2304]{2,1,0:T(1,128)}), f32[16,1,2304]{2,1,0:T(1,128)S(1)}, u32[]{:S(2)}, u32[]{:S(2)}) async-start(f32[16,1,2304]{2,1,0:T(1,128)} %bitcast.7), calls=%async_computation.1 | async-start | bytes 294912 | tf_op jit(solution)/shard_map/all_to_all | solution.py:291
  68.3 10.9 %collective-permute-start.10 = (bf16[16,2,32,128]{3,2,1,0:T(8,128)(2,1)}, bf16[16,2,32,128]{3,2,1,0:T(8,128)(2,1)S(1)}, u32[]{:S(2)}, u32[]{:S(2)}) collective-permute-start(bf16[16,2,32,128]{3,2,1,0:T(8,128)(2,1)} %get-tuple-element.38), channel_id=1, source_target_pairs={{0,65},{1,64},{32,97},{33,96},{64,1},{65,0},{96,33},{97,32},{2,67}... | collective-permute-start | bytes 786440 | tf_op jit(solution)/shard_map/ppermute | solution.py:377
  72.8 8.1 %collective-permute-start.4 = (bf16[16,2,32,128]{3,2,1,0:T(8,128)(2,1)}, bf16[16,2,32,128]{3,2,1,0:T(8,128)(2,1)S(1)}, u32[]{:S(2)}, u32[]{:S(2)}) collective-permute-start(bf16[16,2,32,128]{3,2,1,0:T(8,128)(2,1)} %get-tuple-element.32), channel_id=1, source_target_pairs={{0,1},{1,0},{32,33},{33,32},{64,65},{65,64},{96,97},{97,96},{2,3},... | collective-permute-start | bytes 786440 | tf_op jit(solution)/shard_map/ppermute | solution.py:377
  72.9 34.0 %collective-permute-start.5 = (bf16[16,2,32,128]{3,2,1,0:T(8,128)(2,1)}, bf16[16,2,32,128]{3,2,1,0:T(8,128)(2,1)S(1)}, u32[]{:S(2)}, u32[]{:S(2)}) collective-permute-start(bf16[16,2,32,128]{3,2,1,0:T(8,128)(2,1)} %get-tuple-element.33), channel_id=1, source_target_pairs={{0,32},{1,33},{32,64},{33,65},{64,96},{65,97},{96,0},{97,1},{2,34}... | collective-permute-start | bytes 786440 | tf_op jit(solution)/shard_map/ppermute | solution.py:377
  76.0 31.0 %collective-permute-start.6 = (bf16[16,2,32,128]{3,2,1,0:T(8,128)(2,1)}, bf16[16,2,32,128]{3,2,1,0:T(8,128)(2,1)S(1)}, u32[]{:S(2)}, u32[]{:S(2)}) collective-permute-start(bf16[16,2,32,128]{3,2,1,0:T(8,128)(2,1)} %get-tuple-element.34), channel_id=1, source_target_pairs={{0,96},{1,97},{32,0},{33,1},{64,32},{65,33},{96,64},{97,65},{2,98}... | collective-permute-start | bytes 786440 | tf_op jit(solution)/shard_map/ppermute | solution.py:377
  76.0 31.0 %collective-permute-start.7 = (bf16[16,2,32,128]{3,2,1,0:T(8,128)(2,1)}, bf16[16,2,32,128]{3,2,1,0:T(8,128)(2,1)S(1)}, u32[]{:S(2)}, u32[]{:S(2)}) collective-permute-start(bf16[16,2,32,128]{3,2,1,0:T(8,128)(2,1)} %get-tuple-element.35), channel_id=1, source_target_pairs={{0,64},{1,65},{32,96},{33,97},{64,0},{65,1},{96,32},{97,33},{2,66}... | collective-permute-start | bytes 786440 | tf_op jit(solution)/shard_map/ppermute | solution.py:377
  79.2 27.8 %collective-permute-start.8 = (bf16[16,2,32,128]{3,2,1,0:T(8,128)(2,1)}, bf16[16,2,32,128]{3,2,1,0:T(8,128)(2,1)S(1)}, u32[]{:S(2)}, u32[]{:S(2)}) collective-permute-start(bf16[16,2,32,128]{3,2,1,0:T(8,128)(2,1)} %get-tuple-element.36), channel_id=1, source_target_pairs={{0,33},{1,32},{32,65},{33,64},{64,97},{65,96},{96,1},{97,0},{2,35}... | collective-permute-start | bytes 786440 | tf_op jit(solution)/shard_map/ppermute | solution.py:377
  80.9 26.2 %collective-permute-start.9 = (bf16[16,2,32,128]{3,2,1,0:T(8,128)(2,1)}, bf16[16,2,32,128]{3,2,1,0:T(8,128)(2,1)S(1)}, u32[]{:S(2)}, u32[]{:S(2)}) collective-permute-start(bf16[16,2,32,128]{3,2,1,0:T(8,128)(2,1)} %get-tuple-element.37), channel_id=1, source_target_pairs={{0,97},{1,96},{32,1},{33,0},{64,33},{65,32},{96,65},{97,64},{2,99}... | collective-permute-start | bytes 786440 | tf_op jit(solution)/shard_map/ppermute | solution.py:377
  83.5 22.9 %all-to-all-start.2 = ((bf16[16,16,128]{2,1,0:T(8,128)(2,1)}), bf16[16,16,128]{2,1,0:T(8,128)(2,1)S(1)}, u32[]{:S(2)}, u32[]{:S(2)}) async-start(bf16[16,16,128]{2,1,0:T(8,128)(2,1)} %get-tuple-element.30), calls=%async_computation.2 | async-start | bytes 131072 | tf_op jit(solution)/shard_map/all_to_all | solution.py:291
  142.0 7.1 %collective-permute-start.12 = (bf16[16,2048]{1,0:T(8,128)(2,1)S(1)}, bf16[16,2048]{1,0:T(8,128)(2,1)S(1)}, u32[]{:S(2)}, u32[]{:S(2)}) collective-permute-start(bf16[16,2048]{1,0:T(8,128)(2,1)S(1)} %shard_map.96.a), channel_id=1, source_target_pairs={{0,96},{32,0},{64,32},{96,64},{1,97},{33,1},{65,33},{97,65},{2,98}... | collective-permute-start | bytes 196616 | tf_op jit(solution)/shard_map/ppermute | solution.py:283
  142.1 7.3 %collective-permute-start.13 = (bf16[16,2048]{1,0:T(8,128)(2,1)S(1)}, bf16[16,2048]{1,0:T(8,128)(2,1)S(1)}, u32[]{:S(2)}, u32[]{:S(2)}) collective-permute-start(bf16[16,2048]{1,0:T(8,128)(2,1)S(1)} %shard_map.96.a), channel_id=1, source_target_pairs={{0,32},{32,64},{64,96},{96,0},{1,33},{33,65},{65,97},{97,1},{2,34}... | collective-permute-start | bytes 196616 | tf_op jit(solution)/shard_map/ppermute | solution.py:283
  143.5 7.2 %collective-permute-start.14 = (bf16[16,2048]{1,0:T(8,128)(2,1)S(1)}, bf16[16,2048]{1,0:T(8,128)(2,1)S(1)}, u32[]{:S(2)}, u32[]{:S(2)}) collective-permute-start(bf16[16,2048]{1,0:T(8,128)(2,1)S(1)} %shard_map.96.a), channel_id=1, source_target_pairs={{0,64},{32,96},{64,0},{96,32},{1,65},{33,97},{65,1},{97,33},{2,66}... | collective-permute-start | bytes 196616 | tf_op jit(solution)/shard_map/ppermute | solution.py:283
  146.1 6.9 %collective-permute-start.11 = (bf16[16,2048]{1,0:T(8,128)(2,1)S(1)}, bf16[16,2048]{1,0:T(8,128)(2,1)S(1)}, u32[]{:S(2)}, u32[]{:S(2)}) collective-permute-start(bf16[16,2048]{1,0:T(8,128)(2,1)S(1)} %shard_map.96.a), channel_id=1, source_target_pairs={{0,1},{1,0},{2,3},{3,2},{4,5},{5,4},{6,7},{7,6},{8,9},{9,8},{10,11... | collective-permute-start | bytes 196616 | tf_op jit(solution)/shard_map/ppermute | solution.py:287
  149.1 6.7 %collective-permute-start.15 = (bf16[16,2048]{1,0:T(8,128)(2,1)S(1)}, bf16[16,2048]{1,0:T(8,128)(2,1)S(1)}, u32[]{:S(2)}, u32[]{:S(2)}) collective-permute-start(bf16[16,2048]{1,0:T(8,128)(2,1)S(1)} %collective-permute-done.12.refs_1_), channel_id=1, source_target_pairs={{0,1},{1,0},{2,3},{3,2},{4,5},{5,4},{6,7},{7,6},{8,9},{9,8},{10,11... | collective-permute-start | bytes 196616 | tf_op jit(solution)/shard_map/ppermute | solution.py:287
  149.4 6.4 %collective-permute-start.16 = (bf16[16,2048]{1,0:T(8,128)(2,1)S(1)}, bf16[16,2048]{1,0:T(8,128)(2,1)S(1)}, u32[]{:S(2)}, u32[]{:S(2)}) collective-permute-start(bf16[16,2048]{1,0:T(8,128)(2,1)S(1)} %collective-permute-done.13.refs_2_), channel_id=1, source_target_pairs={{0,1},{1,0},{2,3},{3,2},{4,5},{5,4},{6,7},{7,6},{8,9},{9,8},{10,11... | collective-permute-start | bytes 196616 | tf_op jit(solution)/shard_map/ppermute | solution.py:287
  150.8 5.1 %collective-permute-start.17 = (bf16[16,2048]{1,0:T(8,128)(2,1)S(1)}, bf16[16,2048]{1,0:T(8,128)(2,1)S(1)}, u32[]{:S(2)}, u32[]{:S(2)}) collective-permute-start(bf16[16,2048]{1,0:T(8,128)(2,1)S(1)} %collective-permute-done.14.refs_3_), channel_id=1, source_target_pairs={{0,1},{1,0},{2,3},{3,2},{4,5},{5,4},{6,7},{7,6},{8,9},{9,8},{10,11... | collective-permute-start | bytes 196616 | tf_op jit(solution)/shard_map/ppermute | solution.py:287

commit v6 on v5

--- a/solution.py
+++ b/solution.py
@@ -17,6 +17,8 @@
 PW = ROWS * HD
 MODEL = KVH * QW
 TENSOR = ("x", "z", "c")
+FIRST = ((0, 1), (1, 1), (2, 1), (3, 1))
+REST = ((0, 0), (1, 0), (2, 0), (3, 0))
 NEAR = ((0, 0), (0, 1))
 FAR = ((1, 0), (3, 0), (2, 0), (1, 1), (3, 1), (2, 1))
 MOVES = ((0, 0), (0, 1), (1, 0), (3, 0), (2, 0), (1, 1), (3, 1), (2, 1))
@@ -68,7 +70,11 @@
 def squares_kernel(x, out):
     stream = x[...].astype(F32)
     total = jnp.sum(stream * stream, axis=1, keepdims=True)
-    out[...] = jnp.broadcast_to(as_row(total, diagonal(x.shape[0])), out.shape)
+    out[...] = as_row(total, diagonal(x.shape[0]))
+
+
+def spread_kernel(a, b, c, d, out):
+    out[...] = jnp.broadcast_to((a[...] + b[...]) + (c[...] + d[...]), out.shape)
 
 
 def head_of(place, j, d):
@@ -76,10 +82,10 @@
     return lax.rem(place[0] + j, NX) * NC + core
 
 
-def in_copies(place, d, wq, wkv, out, sems):
+def in_copies(place, moves, wq, wkv, out, sems):
     copies = []
-    for k in range(NX):
-        head = head_of(place, k, d)
+    for k, (j, d) in enumerate(moves):
+        head = head_of(place, j, d)
         for part, (source, start, width, at) in enumerate(
             (
                 (wq, head * QW, QW, 0),
@@ -116,7 +122,7 @@
 
 
 def fetch_in_kernel(place, wq, wkv, out, sems):
-    run_all(in_copies(place, 1, wq, wkv, out, sems))
+    run_all(in_copies(place, FIRST, wq, wkv, out, sems))
 
 
 def fetch_cache_kernel(moves, place, cache, *refs):
@@ -146,7 +152,7 @@
 
 
 def project_kernel(place, normed, wq, wkv, out, w, sems):
-    copies = in_copies(place, 0, wq, wkv, w, sems)
+    copies = in_copies(place, REST, wq, wkv, w, sems)
     for copy in copies:
         copy.start()
     for k in range(NX):
@@ -293,7 +299,6 @@
 
 def step(hidden_in, norm_gain, w_q, w_kv, w_o, kv_cache, lengths, slab_index):
     n, depth = hidden_in.shape
-    members = NX * NZ * NC
     w_q, w_kv, w_o, kv_cache = (
         pltpu.with_memory_space_constraint(v, pltpu.HBM) for v in (w_q, w_kv, w_o, kv_cache)
     )
@@ -307,14 +312,26 @@
     cosine = jnp.cos(angles)
     sine = jnp.sin(angles) * jnp.where(lane < HD // 2, -1.0, 1.0)
 
-    sums = call(squares_kernel, struct((members, HD), F32), [VMEM], hidden_in, params=None)
+    line = struct((1, HD), F32)
+    own = call(squares_kernel, line, [VMEM], hidden_in, params=None)
+    lines = [own]
+    for k in (1, 3, 2):
+        lines.append(shift_x(own, k))
+    sums = call(spread_kernel, struct((NZ * NC, HD), F32), [VMEM] * NX, *lines)
     sums = lax.all_to_all(
-        sums.reshape(members, 1, HD), TENSOR, 0, 0, tiled=True
-    ).reshape(members, HD)
-
-    half = struct((NX, depth, PW), BF16)
-    dmas = pltpu.SemaphoreType.DMA((NX, 3))
-    w_theirs = call(fetch_in_kernel, half, [SMEM, HBM, HBM], place, w_q, w_kv, scratch=[dmas])
+        sums.reshape(NZ * NC, 1, HD), ("z", "c"), 0, 0, tiled=True
+    ).reshape(NZ * NC, HD)
+
+    dmas = lambda moves: pltpu.SemaphoreType.DMA((len(moves), 3))
+    held = call(
+        fetch_in_kernel,
+        struct((len(FIRST), depth, PW), BF16),
+        [SMEM, HBM, HBM],
+        place,
+        w_q,
+        w_kv,
+        scratch=[dmas(FIRST)],
+    )
 
     cache = []
     for moves in (MOVES[:EARLY], MOVES[EARLY:]):
@@ -350,7 +367,7 @@
         sums,
         hidden_in,
         norm_gain[None],
-        w_theirs,
+        held,
     )
     got = swap_c(sent)
     kept = call(
@@ -361,7 +378,7 @@
         normed,
         w_q,
         w_kv,
-        scratch=[pltpu.VMEM(half.shape, BF16), dmas],
+        scratch=[pltpu.VMEM((len(REST), depth, PW), BF16), dmas(REST)],
     )
     blocks = call(pair_sum_kernel, [struct((n, PW), F32)] * NX, [VMEM] * 2, kept, got)
     parts = [blocks[0]]

time: 158 us -> 162 us (1.025)
  waiting for transfers between devices: 29.3 us -> 34.8 us
  starting transfers between devices: 72 us -> 68.9 us
    ppermute x7, waiting for transfers between devices: 0.02 us -> 6.31 us  [step(): cache[k] = lax.ppermute(cache[k], ('x', 'c'), pairs)]
    all_to_all x1, starting transfers between devices: 31 us -> 26 us  [step(): lax.all_to_all(sums.reshape(NZ * NC, 1, HD), ('z', 'c'), 0, 0, tiled=True)]
    ppermute x6 -> x9, starting transfers between devices: 6.91 us -> 11.5 us  [shift_x(): return lax.ppermute(value, 'x', [(i, (i + by) % NX) for i in range(NX)])]
    all_to_all x1, waiting for transfers between devices: 12.7 us -> 9.18 us  [step(): lax.all_to_all(sums.reshape(NZ * NC, 1, HD), ('z', 'c'), 0, 0, tiled=True)]
    ppermute x7, starting transfers between devices: 10.5 us -> 7.5 us  [step(): cache[k] = lax.ppermute(cache[k], ('x', 'c'), pairs)]
    ppermute x6 -> x9, waiting for transfers between devices: 6.39 us -> 9.02 us  [shift_x(): return lax.ppermute(value, 'x', [(i, (i + by) % NX) for i in range(NX)])]
    pallas_call x17 -> x18, Pallas kernels: 20.5 us -> 21 us  [call(): pl.pallas_call(kernel, in_specs=specs, out_specs=outs, out_shape=out, scr...]
  transfers between devices with their start and end apart: 21 -> 24, of which waited for: 5 -> 7; matrix products, arithmetic and copies ran while one was open for 0% -> 0% of each run, Pallas kernels for 10% -> 9%
where the time goes in v6:
time: 162 us; the launch traced here: 161 us
  starting transfers between devices  68.9 us (43%)
  waiting for transfers between devices  34.8 us (21%)
  blocking collectives  34.2 us (21%)
  Pallas kernels  21 us (13%)
    all_to_all x2, blocking collectives, across_z(): return lax.all_to_all(value, 'z', 0, 0, tiled=True)  34.2 us
    all_to_all x1, starting transfers between devices, step(): lax.all_to_all(sums.reshape(NZ * NC, 1, HD), ('z', 'c'), 0, 0, tiled=True)  26 us
    pallas_call x18, Pallas kernels, call(): pl.pallas_call(kernel, in_specs=specs, out_specs=outs, out_shape=out, scr...  21 us
    all_to_all x2, starting transfers between devices, across_z(): return lax.all_to_all(value, 'z', 0, 0, tiled=True)  15.5 us
    ppermute x9, starting transfers between devices, shift_x(): return lax.ppermute(value, 'x', [(i, (i + by) % NX) for i in range(NX)])  11.5 us
    all_to_all x2, waiting for transfers between devices, across_z(): return lax.all_to_all(value, 'z', 0, 0, tiled=True)  10.3 us
    all_to_all x1, waiting for transfers between devices, step(): lax.all_to_all(sums.reshape(NZ * NC, 1, HD), ('z', 'c'), 0, 0, tiled=True)  9.18 us
    ppermute x9, waiting for transfers between devices, shift_x(): return lax.ppermute(value, 'x', [(i, (i + by) % NX) for i in range(NX)])  9.02 us
  transfers between devices with their start and end apart: 24, of which 7 were waited for; matrix products, arithmetic and copies ran while one was open for 0% of the time, Pallas kernels for 9%

profile of v6, /device:TPU:33, one launch (start us, length us, event | category | flops | bytes accessed | tf_op | source)
XLA Modules:
  0.0 161.3 jit_solution(17710530386949470086)
XLA Ops:
  0.0 1.3 shard_map.84.a
  1.3 2.2 %collective-permute-start = (f32[1,128]{1,0:T(1,128)}, f32[1,128]{1,0:T(1,128)S(1)}, u32[]{:S(2)}, u32[]{:S(2)}) collective-permute-start(f32[1,128]{1,0:T(1,128)} %shard_map.84.a), channel_id=1, source_target_pairs={{0,32},{32,64},{64,96},{96,0},{1,33},{33,65},{65,97},{97,1},{2,34}... | collective-permute-start | bytes 1544 | tf_op jit(solution)/shard_map/ppermute | solution.py:289
  3.5 1.5 collective-permute-start.1
  5.1 1.6 collective-permute-start.2
  6.7 2.5 %collective-permute-done.2.d = f32[1,128]{1,0:T(1,128)S(1)} collective-permute-done((f32[1,128]{1,0:T(1,128)}, f32[1,128]{1,0:T(1,128)S(1)}, u32[]{:S(2)}, u32[]{:S(2)}) %collective-permute-start.2) | collective-permute-done | bytes 544 | tf_op jit(solution)/shard_map/ppermute | solution.py:289
  9.2 0.7 copy-done.2
  9.9 0.6 shard_map.85
  10.5 26.0 %all-to-all-start = ((f32[32,1,128]{2,1,0:T(1,128)}), f32[32,1,128]{2,1,0:T(1,128)S(1)}, u32[]{:S(2)}, u32[]{:S(2)}) async-start(f32[32,1,128]{2,1,0:T(1,128)} %bitcast.4), calls=%async_computation | async-start | bytes 32768 | tf_op jit(solution)/shard_map/all_to_all | solution.py:321
  36.5 2.3 %shard_map.86.w = bf16[4,128,2304]{2,1,0:T(8,128)(2,1)S(1)} custom-call(s32[3]{0:T(128)S(1)} %pad_add_fusion.place, bf16[128,16384]{1,0:T(8,128)(2,1)} %wq.3, bf16[128,2048]{1,0:T(8,128)(2,1)} %wkv.3), custom_call_target="tpu_custom_call" | custom-call | tf_op jit(solution)/shard_map/pallas_call | solution.py:47
  38.8 9.2 %all-to-all-done = f32[32,1,128]{2,1,0:T(1,128)S(1)} async-done(((f32[32,1,128]{2,1,0:T(1,128)}), f32[32,1,128]{2,1,0:T(1,128)S(1)}, u32[]{:S(2)}, u32[]{:S(2)}) %all-to-all-start) | async-done | bytes 16416 | tf_op jit(solution)/shard_map/all_to_all | solution.py:321
  48.0 0.5 shard_map.87
  48.5 1.0 collective-permute-start.3
  49.5 2.5 %shard_map.88.a = f32[4,16,2304]{2,1,0:T(8,128)S(1)} custom-call(s32[3]{0:T(128)S(1)} %pad_add_fusion.place, bf16[16,128]{1,0:T(8,128)(2,1)S(1)} %get-tuple-element.24.normed, bf16[128,16384]{1,0:T(8,128)(2,1)} %wq.3, bf16[128,2048]{1,0:T(8,128)(2,1)} %wkv.3), custom_call_target="tpu_custom_call" | custom-call | tf_op jit(solution)/shard_map/pallas_call | solution.py:47
  52.2 0.2 collective-permute-start.4
  52.4 2.5 %collective-permute-start.5 = (f32[16,2304]{1,0:T(8,128)S(1)}, f32[16,2304]{1,0:T(8,128)S(1)}, u32[]{:S(2)}, u32[]{:S(2)}) collective-permute-start(f32[16,2304]{1,0:T(8,128)S(1)} %get-tuple-element.28), channel_id=1, source_target_pairs={{0,96},{32,0},{64,32},{96,64},{1,97},{33,1},{65,33},{97,65},{2,98}... | collective-permute-start | bytes 442376 | tf_op jit(solution)/shard_map/ppermute | solution.py:289
  55.0 0.6 collective-permute-start.6
  55.6 3.3 %collective-permute-done.4.b = f32[16,2304]{1,0:T(8,128)S(1)} collective-permute-done((f32[16,2304]{1,0:T(8,128)S(1)}, f32[16,2304]{1,0:T(8,128)S(1)}, u32[]{:S(2)}, u32[]{:S(2)}) %collective-permute-start.4) | collective-permute-done | bytes 147488 | tf_op jit(solution)/shard_map/ppermute | solution.py:289
  58.9 2.0 %collective-permute-done.5.c = f32[16,2304]{1,0:T(8,128)S(1)} collective-permute-done((f32[16,2304]{1,0:T(8,128)S(1)}, f32[16,2304]{1,0:T(8,128)S(1)}, u32[]{:S(2)}, u32[]{:S(2)}) %collective-permute-start.5) | collective-permute-done | bytes 147488 | tf_op jit(solution)/shard_map/ppermute | solution.py:289
  60.9 1.2 collective-permute-done.6.d
  62.0 0.7 shard_map.90
  62.7 4.0 %all-to-all-start.1 = ((f32[16,1,2304]{2,1,0:T(1,128)}), f32[16,1,2304]{2,1,0:T(1,128)S(1)}, u32[]{:S(2)}, u32[]{:S(2)}) async-start(f32[16,1,2304]{2,1,0:T(1,128)} %bitcast.7), calls=%async_computation.1 | async-start | bytes 294912 | tf_op jit(solution)/shard_map/all_to_all | solution.py:297
  66.7 2.6 %shard_map.94 = (bf16[16,2,32,128]{3,2,1,0:T(8,128)(2,1)}, bf16[16,2,32,128]{3,2,1,0:T(8,128)(2,1)}, bf16[16,2,32,128]{3,2,1,0:T(8,128)(2,1)}, bf16[16,2,32,128]{3,2,1,0:T(8,128)(2,1)}) custom-call(s32[3]{0:T(128)S(1)} %pad_add_fusion.place, bf16[8,16,2,32,128]{4,3,2,1,0:T(8,128)(2,1)} %cache.3), custom_call_target="tpu_custom_call" | custom-call | tf_op jit(solution)/shard_map/pallas_call | solution.py:47
  69.4 4.3 %collective-permute-start.11 = (bf16[16,2,32,128]{3,2,1,0:T(8,128)(2,1)}, bf16[16,2,32,128]{3,2,1,0:T(8,128)(2,1)S(1)}, u32[]{:S(2)}, u32[]{:S(2)}) collective-permute-start(bf16[16,2,32,128]{3,2,1,0:T(8,128)(2,1)} %get-tuple-element.36), channel_id=1, source_target_pairs={{0,33},{1,32},{32,65},{33,64},{64,97},{65,96},{96,1},{97,0},{2,35}... | collective-permute-start | bytes 786440 | tf_op jit(solution)/shard_map/ppermute | solution.py:394
  73.9 1.5 collective-permute-start.13
  75.3 2.5 %shard_map.93 = (bf16[16,2,32,128]{3,2,1,0:T(8,128)(2,1)S(1)}, bf16[16,2,32,128]{3,2,1,0:T(8,128)(2,1)}, bf16[16,2,32,128]{3,2,1,0:T(8,128)(2,1)}, bf16[16,2,32,128]{3,2,1,0:T(8,128)(2,1)}) custom-call(s32[3]{0:T(128)S(1)} %pad_add_fusion.place, bf16[8,16,2,32,128]{4,3,2,1,0:T(8,128)(2,1)} %cache.3), custom_call_target="tpu_custom_call" | custom-call | tf_op jit(solution)/shard_map/pallas_call | solution.py:47
  77.9 0.7 collective-permute-start.7
  78.6 0.6 fusion
  79.9 0.5 collective-permute-start.8
  80.3 6.3 %collective-permute-done.11.refs_5_ = bf16[16,2,32,128]{3,2,1,0:T(8,128)(2,1)S(1)} collective-permute-done((bf16[16,2,32,128]{3,2,1,0:T(8,128)(2,1)}, bf16[16,2,32,128]{3,2,1,0:T(8,128)(2,1)S(1)}, u32[]{:S(2)}, u32[]{:S(2)}) %collective-permute-start.11) | collective-permute-done | bytes 262176 | tf_op jit(solution)/shard_map/ppermute | solution.py:394
  86.6 0.3 collective-permute-start.9
  87.0 0.7 shard_map.91
  87.7 11.5 %all-to-all-start.2 = ((bf16[16,16,128]{2,1,0:T(8,128)(2,1)}), bf16[16,16,128]{2,1,0:T(8,128)(2,1)S(1)}, u32[]{:S(2)}, u32[]{:S(2)}) async-start(bf16[16,16,128]{2,1,0:T(8,128)(2,1)} %get-tuple-element.30), calls=%async_computation.2 | async-start | bytes 131072 | tf_op jit(solution)/shard_map/all_to_all | solution.py:297
  99.3 0.6 shard_map.82.base
  99.8 0.6 shard_map.83.positions
  100.4 10.3 %all-to-all-done.2.q = bf16[16,16,128]{2,1,0:T(8,128)(2,1)S(1)} async-done(((bf16[16,16,128]{2,1,0:T(8,128)(2,1)}), bf16[16,16,128]{2,1,0:T(8,128)(2,1)S(1)}, u32[]{:S(2)}, u32[]{:S(2)}) %all-to-all-start.2) | async-done | bytes 65568 | tf_op jit(solution)/shard_map/all_to_all | solution.py:297
  110.7 0.6 shard_map.92.seen
  111.3 1.2 shard_map.95
  112.5 15.8 %all_to_all.25 = f32[16,1,2304]{2,1,0:T(1,128)S(1)} all-to-all(f32[16,1,2304]{2,1,0:T(1,128)S(1)} %bitcast.12), channel_id=1, replica_groups=mesh['groups'=2,'x'=4,'z'=16,'c'=2] {'z'}, dimensions={0} | all-to-all | bytes 294912 | tf_op jit(solution)/shard_map/all_to_all | solution.py:297
  128.5 18.4 %all_to_all.26.heads = bf16[16,16,128]{2,1,0:T(8,128)(2,1)S(1)} all-to-all(bf16[16,16,128]{2,1,0:T(8,128)(2,1)S(1)} %shard_map.96), channel_id=1, replica_groups=mesh['groups'=2,'x'=4,'z'=16,'c'=2] {'z'}, dimensions={0} | all-to-all | bytes 131072 | tf_op jit(solution)/shard_map/all_to_all | solution.py:297
  147.0 0.2 collective-permute-start.15
  147.2 1.4 collective-permute-start.16
  148.6 1.2 collective-permute-start.17
  149.8 3.1 %collective-permute-start.14 = (bf16[16,2048]{1,0:T(8,128)(2,1)S(1)}, bf16[16,2048]{1,0:T(8,128)(2,1)S(1)}, u32[]{:S(2)}, u32[]{:S(2)}) collective-permute-start(bf16[16,2048]{1,0:T(8,128)(2,1)S(1)} %shard_map.97.a), channel_id=1, source_target_pairs={{0,1},{1,0},{2,3},{3,2},{4,5},{5,4},{6,7},{7,6},{8,9},{9,8},{10,11... | collective-permute-start | bytes 196616 | tf_op jit(solution)/shard_map/ppermute | solution.py:293
  153.0 0.7 collective-permute-start.18
  153.7 1.5 collective-permute-start.19
  155.2 2.0 %collective-permute-start.20 = (bf16[16,2048]{1,0:T(8,128)(2,1)S(1)}, bf16[16,2048]{1,0:T(8,128)(2,1)S(1)}, u32[]{:S(2)}, u32[]{:S(2)}) collective-permute-start(bf16[16,2048]{1,0:T(8,128)(2,1)S(1)} %collective-permute-done.17.refs_3_), channel_id=1, source_target_pairs={{0,1},{1,0},{2,3},{3,2},{4,5},{5,4},{6,7},{7,6},{8,9},{9,8},{10,11... | collective-permute-start | bytes 196616 | tf_op jit(solution)/shard_map/ppermute | solution.py:293
  157.2 2.9 %shard_map.98 = (f32[16,128]{1,0:T(8,128)S(1)}, bf16[6,2048,128]{2,1,0:T(8,128)(2,1)S(1)}) custom-call(s32[3]{0:T(128)S(1)} %pad_add_fusion.place, bf16[16,2048]{1,0:T(8,128)(2,1)S(1)} %shard_map.97.a, bf16[16,2048]{1,0:T(8,128)(2,1)S(1)} %collective-permute-done.14.b, bf16[16384,128]{1,0:T(8,128)(2,1)} %wo.1, bf16[16,128]{1,0:T(8,128)(2,1)S(1)} %copy-done), custom_call_target="tpu_custom_call" | custom-call | tf_op jit(solution)/shard_map/pallas_call | solution.py:47
  160.1 1.1 shard_map.99
  (34 shorter events, 0.9 us)
Async XLA Ops:
  1.3 5.3 %collective-permute-start = (f32[1,128]{1,0:T(1,128)}, f32[1,128]{1,0:T(1,128)S(1)}, u32[]{:S(2)}, u32[]{:S(2)}) collective-permute-start(f32[1,128]{1,0:T(1,128)} %shard_map.84.a), channel_id=1, source_target_pairs={{0,32},{32,64},{64,96},{96,0},{1,33},{33,65},{65,97},{97,1},{2,34}... | collective-permute-start | bytes 1544 | tf_op jit(solution)/shard_map/ppermute | solution.py:289
  3.5 3.1 %collective-permute-start.1 = (f32[1,128]{1,0:T(1,128)}, f32[1,128]{1,0:T(1,128)S(1)}, u32[]{:S(2)}, u32[]{:S(2)}) collective-permute-start(f32[1,128]{1,0:T(1,128)} %shard_map.84.a), channel_id=1, source_target_pairs={{0,96},{32,0},{64,32},{96,64},{1,97},{33,1},{65,33},{97,65},{2,98}... | collective-permute-start | bytes 1544 | tf_op jit(solution)/shard_map/ppermute | solution.py:289
  5.1 4.1 %collective-permute-start.2 = (f32[1,128]{1,0:T(1,128)}, f32[1,128]{1,0:T(1,128)S(1)}, u32[]{:S(2)}, u32[]{:S(2)}) collective-permute-start(f32[1,128]{1,0:T(1,128)} %shard_map.84.a), channel_id=1, source_target_pairs={{0,64},{32,96},{64,0},{96,32},{1,65},{33,97},{65,1},{97,33},{2,66}... | collective-permute-start | bytes 1544 | tf_op jit(solution)/shard_map/ppermute | solution.py:289
  9.2 0.7 copy-start.2
  10.5 37.5 %all-to-all-start = ((f32[32,1,128]{2,1,0:T(1,128)}), f32[32,1,128]{2,1,0:T(1,128)S(1)}, u32[]{:S(2)}, u32[]{:S(2)}) async-start(f32[32,1,128]{2,1,0:T(1,128)} %bitcast.4), calls=%async_computation | async-start | bytes 32768 | tf_op jit(solution)/shard_map/all_to_all | solution.py:321
  36.5 11.5 %copy-start = (bf16[16,128]{1,0:T(8,128)(2,1)S(1)}, bf16[16,128]{1,0:T(8,128)(2,1)}, u32[]{:S(2)}) copy-start(bf16[16,128]{1,0:T(8,128)(2,1)} %x.5) | copy-start | bytes 12292
  36.5 11.5 %copy-start.4 = (bf16[128]{0:T(256)(128)(2,1)S(1)}, bf16[128]{0:T(256)(128)(2,1)}, u32[]{:S(2)}) copy-start(bf16[128]{0:T(256)(128)(2,1)} %param.9) | copy-start | bytes 772
  48.5 3.6 %collective-permute-start.3 = (f32[4,16,2304]{2,1,0:T(8,128)S(1)}, f32[4,16,2304]{2,1,0:T(8,128)S(1)}, u32[]{:S(2)}, u32[]{:S(2)}) collective-permute-start(f32[4,16,2304]{2,1,0:T(8,128)S(1)} %get-tuple-element.25), channel_id=1, source_target_pairs={{0,1},{1,0},{2,3},{3,2},{4,5},{5,4},{6,7},{7,6},{8,9},{9,8},{10,11... | collective-permute-start | bytes 1769480 | tf_op jit(solution)/shard_map/ppermute | solution.py:293
  52.1 26.5 %copy-start.3 = (s32[16]{0:T(128)S(1)}, s32[16]{0:T(128)}, u32[]{:S(2)}) copy-start(s32[16]{0:T(128)} %lengths.1) | copy-start | bytes 196
  52.1 59.3 %copy-start.1 = (s32[8,16]{1,0:T(8,128)S(1)}, s32[8,16]{1,0:T(8,128)}, u32[]{:S(2)}) copy-start(s32[8,16]{1,0:T(8,128)} %slabs.1) | copy-start | bytes 1540
  52.2 6.7 %collective-permute-start.4 = (f32[16,2304]{1,0:T(8,128)S(1)}, f32[16,2304]{1,0:T(8,128)S(1)}, u32[]{:S(2)}, u32[]{:S(2)}) collective-permute-start(f32[16,2304]{1,0:T(8,128)S(1)} %get-tuple-element.27), channel_id=1, source_target_pairs={{0,32},{32,64},{64,96},{96,0},{1,33},{33,65},{65,97},{97,1},{2,34}... | collective-permute-start | bytes 442376 | tf_op jit(solution)/shard_map/ppermute | solution.py:289
  52.4 8.5 %collective-permute-start.5 = (f32[16,2304]{1,0:T(8,128)S(1)}, f32[16,2304]{1,0:T(8,128)S(1)}, u32[]{:S(2)}, u32[]{:S(2)}) collective-permute-start(f32[16,2304]{1,0:T(8,128)S(1)} %get-tuple-element.28), channel_id=1, source_target_pairs={{0,96},{32,0},{64,32},{96,64},{1,97},{33,1},{65,33},{97,65},{2,98}... | collective-permute-start | bytes 442376 | tf_op jit(solution)/shard_map/ppermute | solution.py:289
  55.0 7.1 %collective-permute-start.6 = (f32[16,2304]{1,0:T(8,128)S(1)}, f32[16,2304]{1,0:T(8,128)S(1)}, u32[]{:S(2)}, u32[]{:S(2)}) collective-permute-start(f32[16,2304]{1,0:T(8,128)S(1)} %get-tuple-element.29), channel_id=1, source_target_pairs={{0,64},{32,96},{64,0},{96,32},{1,65},{33,97},{65,1},{97,33},{2,66}... | collective-permute-start | bytes 442376 | tf_op jit(solution)/shard_map/ppermute | solution.py:289
  62.7 24.3 %all-to-all-start.1 = ((f32[16,1,2304]{2,1,0:T(1,128)}), f32[16,1,2304]{2,1,0:T(1,128)S(1)}, u32[]{:S(2)}, u32[]{:S(2)}) async-start(f32[16,1,2304]{2,1,0:T(1,128)} %bitcast.7), calls=%async_computation.1 | async-start | bytes 294912 | tf_op jit(solution)/shard_map/all_to_all | solution.py:297
  69.3 10.6 %collective-permute-start.10 = (bf16[16,2,32,128]{3,2,1,0:T(8,128)(2,1)}, bf16[16,2,32,128]{3,2,1,0:T(8,128)(2,1)S(1)}, u32[]{:S(2)}, u32[]{:S(2)}) collective-permute-start(bf16[16,2,32,128]{3,2,1,0:T(8,128)(2,1)} %get-tuple-element.35), channel_id=1, source_target_pairs={{0,64},{1,65},{32,96},{33,97},{64,0},{65,1},{96,32},{97,33},{2,66}... | collective-permute-start | bytes 786440 | tf_op jit(solution)/shard_map/ppermute | solution.py:394
  69.4 17.2 %collective-permute-start.11 = (bf16[16,2,32,128]{3,2,1,0:T(8,128)(2,1)}, bf16[16,2,32,128]{3,2,1,0:T(8,128)(2,1)S(1)}, u32[]{:S(2)}, u32[]{:S(2)}) collective-permute-start(bf16[16,2,32,128]{3,2,1,0:T(8,128)(2,1)} %get-tuple-element.36), channel_id=1, source_target_pairs={{0,33},{1,32},{32,65},{33,64},{64,97},{65,96},{96,1},{97,0},{2,35}... | collective-permute-start | bytes 786440 | tf_op jit(solution)/shard_map/ppermute | solution.py:394
  73.7 37.6 %collective-permute-start.12 = (bf16[16,2,32,128]{3,2,1,0:T(8,128)(2,1)}, bf16[16,2,32,128]{3,2,1,0:T(8,128)(2,1)S(1)}, u32[]{:S(2)}, u32[]{:S(2)}) collective-permute-start(bf16[16,2,32,128]{3,2,1,0:T(8,128)(2,1)} %get-tuple-element.37), channel_id=1, source_target_pairs={{0,97},{1,96},{32,1},{33,0},{64,33},{65,32},{96,65},{97,64},{2,99}... | collective-permute-start | bytes 786440 | tf_op jit(solution)/shard_map/ppermute | solution.py:394
  73.9 37.4 %collective-permute-start.13 = (bf16[16,2,32,128]{3,2,1,0:T(8,128)(2,1)}, bf16[16,2,32,128]{3,2,1,0:T(8,128)(2,1)S(1)}, u32[]{:S(2)}, u32[]{:S(2)}) collective-permute-start(bf16[16,2,32,128]{3,2,1,0:T(8,128)(2,1)} %get-tuple-element.38), channel_id=1, source_target_pairs={{0,65},{1,64},{32,97},{33,96},{64,1},{65,0},{96,33},{97,32},{2,67}... | collective-permute-start | bytes 786440 | tf_op jit(solution)/shard_map/ppermute | solution.py:394
  77.9 33.4 %collective-permute-start.7 = (bf16[16,2,32,128]{3,2,1,0:T(8,128)(2,1)}, bf16[16,2,32,128]{3,2,1,0:T(8,128)(2,1)S(1)}, u32[]{:S(2)}, u32[]{:S(2)}) collective-permute-start(bf16[16,2,32,128]{3,2,1,0:T(8,128)(2,1)} %get-tuple-element.32), channel_id=1, source_target_pairs={{0,1},{1,0},{32,33},{33,32},{64,65},{65,64},{96,97},{97,96},{2,3},... | collective-permute-start | bytes 786440 | tf_op jit(solution)/shard_map/ppermute | solution.py:394
  79.9 31.5 %collective-permute-start.8 = (bf16[16,2,32,128]{3,2,1,0:T(8,128)(2,1)}, bf16[16,2,32,128]{3,2,1,0:T(8,128)(2,1)S(1)}, u32[]{:S(2)}, u32[]{:S(2)}) collective-permute-start(bf16[16,2,32,128]{3,2,1,0:T(8,128)(2,1)} %get-tuple-element.33), channel_id=1, source_target_pairs={{0,32},{1,33},{32,64},{33,65},{64,96},{65,97},{96,0},{97,1},{2,34}... | collective-permute-start | bytes 786440 | tf_op jit(solution)/shard_map/ppermute | solution.py:394
  86.6 24.7 %collective-permute-start.9 = (bf16[16,2,32,128]{3,2,1,0:T(8,128)(2,1)}, bf16[16,2,32,128]{3,2,1,0:T(8,128)(2,1)S(1)}, u32[]{:S(2)}, u32[]{:S(2)}) collective-permute-start(bf16[16,2,32,128]{3,2,1,0:T(8,128)(2,1)} %get-tuple-element.34), channel_id=1, source_target_pairs={{0,96},{1,97},{32,0},{33,1},{64,32},{65,33},{96,64},{97,65},{2,98}... | collective-permute-start | bytes 786440 | tf_op jit(solution)/shard_map/ppermute | solution.py:394
  87.7 23.0 %all-to-all-start.2 = ((bf16[16,16,128]{2,1,0:T(8,128)(2,1)}), bf16[16,16,128]{2,1,0:T(8,128)(2,1)S(1)}, u32[]{:S(2)}, u32[]{:S(2)}) async-start(bf16[16,16,128]{2,1,0:T(8,128)(2,1)} %get-tuple-element.30), calls=%async_computation.2 | async-start | bytes 131072 | tf_op jit(solution)/shard_map/all_to_all | solution.py:297
  147.0 5.9 %collective-permute-start.15 = (bf16[16,2048]{1,0:T(8,128)(2,1)S(1)}, bf16[16,2048]{1,0:T(8,128)(2,1)S(1)}, u32[]{:S(2)}, u32[]{:S(2)}) collective-permute-start(bf16[16,2048]{1,0:T(8,128)(2,1)S(1)} %shard_map.97.a), channel_id=1, source_target_pairs={{0,96},{32,0},{64,32},{96,64},{1,97},{33,1},{65,33},{97,65},{2,98}... | collective-permute-start | bytes 196616 | tf_op jit(solution)/shard_map/ppermute | solution.py:289
  147.2 6.5 %collective-permute-start.16 = (bf16[16,2048]{1,0:T(8,128)(2,1)S(1)}, bf16[16,2048]{1,0:T(8,128)(2,1)S(1)}, u32[]{:S(2)}, u32[]{:S(2)}) collective-permute-start(bf16[16,2048]{1,0:T(8,128)(2,1)S(1)} %shard_map.97.a), channel_id=1, source_target_pairs={{0,32},{32,64},{64,96},{96,0},{1,33},{33,65},{65,97},{97,1},{2,34}... | collective-permute-start | bytes 196616 | tf_op jit(solution)/shard_map/ppermute | solution.py:289
  148.6 6.6 %collective-permute-start.17 = (bf16[16,2048]{1,0:T(8,128)(2,1)S(1)}, bf16[16,2048]{1,0:T(8,128)(2,1)S(1)}, u32[]{:S(2)}, u32[]{:S(2)}) collective-permute-start(bf16[16,2048]{1,0:T(8,128)(2,1)S(1)} %shard_map.97.a), channel_id=1, source_target_pairs={{0,64},{32,96},{64,0},{96,32},{1,65},{33,97},{65,1},{97,33},{2,66}... | collective-permute-start | bytes 196616 | tf_op jit(solution)/shard_map/ppermute | solution.py:289
  149.8 7.4 %collective-permute-start.14 = (bf16[16,2048]{1,0:T(8,128)(2,1)S(1)}, bf16[16,2048]{1,0:T(8,128)(2,1)S(1)}, u32[]{:S(2)}, u32[]{:S(2)}) collective-permute-start(bf16[16,2048]{1,0:T(8,128)(2,1)S(1)} %shard_map.97.a), channel_id=1, source_target_pairs={{0,1},{1,0},{2,3},{3,2},{4,5},{5,4},{6,7},{7,6},{8,9},{9,8},{10,11... | collective-permute-start | bytes 196616 | tf_op jit(solution)/shard_map/ppermute | solution.py:293
  153.0 7.2 %collective-permute-start.18 = (bf16[16,2048]{1,0:T(8,128)(2,1)S(1)}, bf16[16,2048]{1,0:T(8,128)(2,1)S(1)}, u32[]{:S(2)}, u32[]{:S(2)}) collective-permute-start(bf16[16,2048]{1,0:T(8,128)(2,1)S(1)} %collective-permute-done.15.refs_1_), channel_id=1, source_target_pairs={{0,1},{1,0},{2,3},{3,2},{4,5},{5,4},{6,7},{7,6},{8,9},{9,8},{10,11... | collective-permute-start | bytes 196616 | tf_op jit(solution)/shard_map/ppermute | solution.py:293
  153.7 6.4 %collective-permute-start.19 = (bf16[16,2048]{1,0:T(8,128)(2,1)S(1)}, bf16[16,2048]{1,0:T(8,128)(2,1)S(1)}, u32[]{:S(2)}, u32[]{:S(2)}) collective-permute-start(bf16[16,2048]{1,0:T(8,128)(2,1)S(1)} %collective-permute-done.16.refs_2_), channel_id=1, source_target_pairs={{0,1},{1,0},{2,3},{3,2},{4,5},{5,4},{6,7},{7,6},{8,9},{9,8},{10,11... | collective-permute-start | bytes 196616 | tf_op jit(solution)/shard_map/ppermute | solution.py:293
  155.2 4.9 %collective-permute-start.20 = (bf16[16,2048]{1,0:T(8,128)(2,1)S(1)}, bf16[16,2048]{1,0:T(8,128)(2,1)S(1)}, u32[]{:S(2)}, u32[]{:S(2)}) collective-permute-start(bf16[16,2048]{1,0:T(8,128)(2,1)S(1)} %collective-permute-done.17.refs_3_), channel_id=1, source_target_pairs={{0,1},{1,0},{2,3},{3,2},{4,5},{5,4},{6,7},{7,6},{8,9},{9,8},{10,11... | collective-permute-start | bytes 196616 | tf_op jit(solution)/shard_map/ppermute | solution.py:293

commit v7 on v6

--- a/solution.py
+++ b/solution.py
@@ -20,7 +20,8 @@
 FIRST = ((0, 1), (1, 1), (2, 1), (3, 1))
 REST = ((0, 0), (1, 0), (2, 0), (3, 0))
 NEAR = ((0, 0), (0, 1))
-FAR = ((1, 0), (3, 0), (2, 0), (1, 1), (3, 1), (2, 1))
+SIDE = ((1, 0), (3, 0), (2, 0))
+ACROSS = ((1, 1), (3, 1), (2, 1))
 MOVES = ((0, 0), (0, 1), (1, 0), (3, 0), (2, 0), (1, 1), (3, 1), (2, 1))
 EARLY = 4
 
@@ -125,17 +126,16 @@
     run_all(in_copies(place, FIRST, wq, wkv, out, sems))
 
 
-def fetch_cache_kernel(moves, place, cache, *refs):
+def fetch_cache_kernel(moves, staged, place, cache, *refs):
     outs, held, sems, out_sems = refs[:-3], *refs[-3:]
     first, second = [], []
     for k, (j, d) in enumerate(moves):
-        stays = (j, d) == (0, 0)
-        to = outs[k] if stays else held.at[k]
+        to = held.at[k] if k in staged else outs[k]
         first.append(pltpu.make_async_copy(cache.at[head_of(place, j, d)], to, sems.at[k]))
         first[k].start()
-    for k, move in enumerate(moves):
+    for k in range(len(moves)):
         first[k].wait()
-        if move != (0, 0):
+        if k in staged:
             second.append(pltpu.make_async_copy(held.at[k], outs[k], out_sems.at[k]))
             second[-1].start()
     for copy in second:
@@ -174,13 +174,14 @@
         out[pl.ds(k, n, stride=ROWS), :] = total
 
 
-def queries_kernel(parts, cosine, sine, q_out, new_score, new_value):
+def queries_kernel(place, parts, cosine, sine, q_out, new_score, new_value):
     n = parts.shape[0] // ROWS
     total = parts[:ROWS]
     for k in range(1, n):
         total = total + parts[k * ROWS : (k + 1) * ROWS]
     lead = total[: GROUP + 1]
-    turned = lead * cosine[...] + pltpu.roll(lead, HD // 2, 1) * sine[...]
+    mine = pl.ds(place[1], 1)
+    turned = lead * cosine[mine] + pltpu.roll(lead, HD // 2, 1) * sine[mine]
     turned = turned.astype(BF16)
     q = turned[:GROUP]
     q_out[...] = jnp.broadcast_to(q[None], q_out.shape)
@@ -190,21 +191,16 @@
     new_value[...] = total[GROUP + 1 :].astype(BF16).astype(F32)
 
 
-def positions_kernel(local, first, last, place, base, out):
-    index = lax.broadcasted_iota(jnp.int32, out.shape, 1)
-    start = base[...]
-    for k, (j, d) in list(enumerate(MOVES))[first:last]:
+def visible_kernel(local, place, lengths, q, out):
+    del q
+    index = lax.broadcasted_iota(jnp.int32, (1, out.shape[1]), 1)
+    position = index % local
+    for k, (j, d) in enumerate(MOVES):
         core = 1 - place[2] if d else place[2]
         block = (lax.rem(place[0] + (NX - j), NX) * NZ + place[1]) * NC + core
-        start = jnp.where(index // local == k, block * local, start)
-    out[...] = start
-
-
-def visible_kernel(local, lengths, positions, q, out):
-    del q
-    here = positions[...] + lax.broadcasted_iota(jnp.int32, positions.shape, 1) % local
+        position = jnp.where(index // local == k, position + block * local, position)
     for b in range(out.shape[0]):
-        out[b : b + 1] = (here < lengths[b]).astype(F32)
+        out[b : b + 1] = (position < lengths[b]).astype(F32)
 
 
 def attend_kernel(place, slabs, seen, q, *refs):
@@ -262,27 +258,35 @@
         out[:, k * HD : (k + 1) * HD] = wide[:, k, :].astype(BF16)
 
 
-def output_near_kernel(place, a, b, wo, x, out, w_far, w, sems, far_sems):
+def add_products(total, rows, w):
+    for k, block in enumerate(rows):
+        total = total + jnp.dot(block[...], w[k], preferred_element_type=F32)
+    return total
+
+
+def output_near_kernel(place, a, b, wo, x, out, w_next, w, sems, next_sems):
     near = out_copies(place, NEAR, wo, w, sems)
-    far = out_copies(place, FAR, wo, w_far, far_sems)
-    for copy in near + far:
+    after = out_copies(place, SIDE, wo, w_next, next_sems)
+    for copy in near + after:
         copy.start()
     for copy in near:
         copy.wait()
-    total = x[...].astype(F32)
-    for k, rows in enumerate((a, b)):
-        total = total + jnp.dot(rows[...], w[k], preferred_element_type=F32)
-    out[...] = total
-    for copy in far:
+    out[...] = add_products(x[...].astype(F32), (a, b), w)
+    for copy in after:
         copy.wait()
 
 
-def output_far_kernel(*refs):
-    near, *rows, w, out = refs
-    total = near[...]
-    for k, block in enumerate(rows):
-        total = total + jnp.dot(block[...], w[k], preferred_element_type=F32)
-    out[...] = total.astype(BF16)
+def output_side_kernel(place, total, a, b, c, w, wo, out, w_next, sems):
+    after = out_copies(place, ACROSS, wo, w_next, sems)
+    for copy in after:
+        copy.start()
+    out[...] = add_products(total[...], (a, b, c), w)
+    for copy in after:
+        copy.wait()
+
+
+def output_across_kernel(total, a, b, c, w, out):
+    out[...] = add_products(total[...], (a, b, c), w).astype(BF16)
 
 
 def shift_x(value, by):
@@ -304,11 +308,9 @@
     )
     place = jnp.stack([lax.axis_index(a) for a in TENSOR]).astype(jnp.int32)
 
-    mine = jnp.arange(n, dtype=jnp.int32) == lax.axis_index("z")
-    position = jnp.sum(jnp.where(mine, lengths, 0)).astype(F32)
     lane = jnp.arange(HD, dtype=jnp.int32)[None]
     frequency = ROPE_BASE ** (-2.0 * (lane % (HD // 2)).astype(F32) / HD)
-    angles = position * frequency
+    angles = lengths.astype(F32)[:, None] * frequency
     cosine = jnp.cos(angles)
     sine = jnp.sin(angles) * jnp.where(lane < HD // 2, -1.0, 1.0)
 
@@ -334,11 +336,14 @@
     )
 
     cache = []
-    for moves in (MOVES[:EARLY], MOVES[EARLY:]):
+    for moves, staged in ((MOVES[:EARLY], range(1, EARLY)), (MOVES[EARLY:], ())):
         block = kv_cache.shape[1:]
         cache += call(
-            functools.partial(fetch_cache_kernel, moves),
-            [struct(block, BF16) if move == (0, 0) else pltpu.HBM(block, BF16) for move in moves],
+            functools.partial(fetch_cache_kernel, moves, staged),
+            [
+                pltpu.HBM(block, BF16) if k in staged else struct(block, BF16)
+                for k in range(len(moves))
+            ],
             [SMEM, HBM],
             place,
             kv_cache,
@@ -351,14 +356,6 @@
 
     local = kv_cache.shape[3]
     seen = len(MOVES) * local
-    positions = call(
-        functools.partial(positions_kernel, local, 0, EARLY),
-        struct((1, seen), jnp.int32),
-        [SMEM, VMEM],
-        place,
-        jnp.zeros((1, seen), jnp.int32),
-    )
-
     product = struct((NX, n, PW), F32)
     normed, sent = call(
         project_first_kernel,
@@ -392,18 +389,12 @@
             for c in range(NC)
         ]
         cache[k] = lax.ppermute(cache[k], ("x", "c"), pairs)
-    positions = call(
-        functools.partial(positions_kernel, local, EARLY, len(MOVES)),
-        struct((1, seen), jnp.int32),
-        [SMEM, VMEM],
-        place,
-        positions,
-    )
     rows = across_z(rows.reshape(n, 1, PW)).reshape(n * ROWS, HD)
     q, new_score, new_value = call(
         queries_kernel,
         [struct((n, GROUP, HD), BF16), struct((1, HD), F32), struct((1, HD), F32)],
-        [VMEM] * 3,
+        [SMEM] + [VMEM] * 3,
+        place,
         rows,
         cosine,
         sine,
@@ -413,9 +404,9 @@
     visible = call(
         functools.partial(visible_kernel, local),
         struct((n, seen), F32),
-        [SMEM, VMEM, VMEM],
+        [SMEM, SMEM, VMEM],
+        place,
         lengths,
-        positions,
         q,
     )
     partial = call(
@@ -446,27 +437,40 @@
         rows[k, 0] = shift_x(done, -k)
     for k in (0, 1, 3, 2):
         rows[k, 1] = swap_c(rows[k, 0])
-    total, w_far = call(
+    block = (QW, w_o.shape[1])
+    part = struct((n, depth), F32)
+    total, w_side = call(
         output_near_kernel,
-        [struct((n, depth), F32), struct((len(FAR), QW, w_o.shape[1]), BF16)],
+        [part, struct((len(SIDE),) + block, BF16)],
         [SMEM, VMEM, VMEM, HBM, VMEM],
         place,
         *(rows[move] for move in NEAR),
         w_o,
         hidden_in,
         scratch=[
-            pltpu.VMEM((len(NEAR), QW, w_o.shape[1]), BF16),
+            pltpu.VMEM((len(NEAR),) + block, BF16),
             pltpu.SemaphoreType.DMA((len(NEAR),)),
-            pltpu.SemaphoreType.DMA((len(FAR),)),
+            pltpu.SemaphoreType.DMA((len(SIDE),)),
         ],
     )
+    total, w_across = call(
+        output_side_kernel,
+        [part, struct((len(ACROSS),) + block, BF16)],
+        [SMEM] + [VMEM] * 5 + [HBM],
+        place,
+        total,
+        *(rows[move] for move in SIDE),
+        w_side,
+        w_o,
+        scratch=[pltpu.SemaphoreType.DMA((len(ACROSS),))],
+    )
     return call(
-        output_far_kernel,
+        output_across_kernel,
         struct((n, depth), BF16),
-        [VMEM] * (2 + len(FAR)),
+        [VMEM] * 5,
         total,
-        *(rows[move] for move in FAR),
-        w_far,
+        *(rows[move] for move in ACROSS),
+        w_across,
     )
 
 

time: 162 us -> 162 us (level)
  blocking collectives: 34.2 us -> 57 us
  starting transfers between devices: 68.9 us -> 57.8 us
  waiting for transfers between devices: 34.8 us -> 25.4 us
    all_to_all x2 -> x3, blocking collectives: 34.2 us -> 57 us  [across_z(): return lax.all_to_all(value, 'z', 0, 0, tiled=True)]
    all_to_all x2 -> x1, starting transfers between devices: 15.5 us -> 4.09 us  [across_z(): return lax.all_to_all(value, 'z', 0, 0, tiled=True)]
    all_to_all x2 -> x1, waiting for transfers between devices: 10.3 us -> 0.01 us  [across_z(): return lax.all_to_all(value, 'z', 0, 0, tiled=True)]
    pallas_call x18 -> x17, Pallas kernels: 21 us -> 20.5 us  [call(): pl.pallas_call(kernel, in_specs=specs, out_specs=outs, out_shape=out, scr...]
  transfers between devices with their start and end apart: 24 -> 23, of which waited for: 7 -> 6; matrix products, arithmetic and copies ran while one was open for 0% -> 0% of each run, Pallas kernels for 9% -> 9%
where the time goes in v7:
time: 162 us
  starting transfers between devices  57.8 us (36%)
  blocking collectives  57 us (35%)
  waiting for transfers between devices  25.4 us (16%)
  Pallas kernels  20.5 us (13%)
    all_to_all x3, blocking collectives, across_z(): return lax.all_to_all(value, 'z', 0, 0, tiled=True)  57 us
    all_to_all x1, starting transfers between devices, step(): lax.all_to_all(sums.reshape(NZ * NC, 1, HD), ('z', 'c'), 0, 0, tiled=True)  26.3 us
    pallas_call x17, Pallas kernels, call(): pl.pallas_call(kernel, in_specs=specs, out_specs=outs, out_shape=out, scr...  20.5 us
    ppermute x9, starting transfers between devices, shift_x(): return lax.ppermute(value, 'x', [(i, (i + by) % NX) for i in range(NX)])  11.5 us
    all_to_all x1, waiting for transfers between devices, step(): lax.all_to_all(sums.reshape(NZ * NC, 1, HD), ('z', 'c'), 0, 0, tiled=True)  9.19 us
    ppermute x9, waiting for transfers between devices, shift_x(): return lax.ppermute(value, 'x', [(i, (i + by) % NX) for i in range(NX)])  8.86 us
    ppermute x5, starting transfers between devices, swap_c(): return lax.ppermute(value, 'c', [(0, 1), (1, 0)])  8.44 us
    ppermute x7, starting transfers between devices, step(): cache[k] = lax.ppermute(cache[k], ('x', 'c'), pairs)  7.51 us
  transfers between devices with their start and end apart: 23, of which 6 were waited for; matrix products, arithmetic and copies ran while one was open for 0% of the time, Pallas kernels for 9%

profile of v7, /device:TPU:33, one launch (start us, length us, event | category | flops | bytes accessed | tf_op | source)
XLA Modules:
  0.0 161.7 jit_solution(6244705568872741375)
XLA Ops:
  0.0 1.3 shard_map.82.a
  1.3 2.2 %collective-permute-start = (f32[1,128]{1,0:T(1,128)}, f32[1,128]{1,0:T(1,128)S(1)}, u32[]{:S(2)}, u32[]{:S(2)}) collective-permute-start(f32[1,128]{1,0:T(1,128)} %shard_map.82.a), channel_id=1, source_target_pairs={{0,32},{32,64},{64,96},{96,0},{1,33},{33,65},{65,97},{97,1},{2,34}... | collective-permute-start | bytes 1544 | tf_op jit(solution)/shard_map/ppermute | solution.py:293
  3.4 1.5 collective-permute-start.1
  5.0 1.6 collective-permute-start.2
  6.6 2.4 %collective-permute-done.2.d = f32[1,128]{1,0:T(1,128)S(1)} collective-permute-done((f32[1,128]{1,0:T(1,128)}, f32[1,128]{1,0:T(1,128)S(1)}, u32[]{:S(2)}, u32[]{:S(2)}) %collective-permute-start.2) | collective-permute-done | bytes 544 | tf_op jit(solution)/shard_map/ppermute | solution.py:293
  9.0 0.6 copy-done.2
  9.6 0.6 shard_map.83
  10.2 26.3 %all-to-all-start = ((f32[32,1,128]{2,1,0:T(1,128)}), f32[32,1,128]{2,1,0:T(1,128)S(1)}, u32[]{:S(2)}, u32[]{:S(2)}) async-start(f32[32,1,128]{2,1,0:T(1,128)} %bitcast.4), calls=%async_computation | async-start | bytes 32768 | tf_op jit(solution)/shard_map/all_to_all | solution.py:323
  36.6 2.3 %shard_map.84.w = bf16[4,128,2304]{2,1,0:T(8,128)(2,1)S(1)} custom-call(s32[3]{0:T(128)S(1)} %pad_add_fusion.place, bf16[128,16384]{1,0:T(8,128)(2,1)} %wq.3, bf16[128,2048]{1,0:T(8,128)(2,1)} %wkv.3), custom_call_target="tpu_custom_call" | custom-call | tf_op jit(solution)/shard_map/pallas_call | solution.py:48
  38.8 9.2 %all-to-all-done = f32[32,1,128]{2,1,0:T(1,128)S(1)} async-done(((f32[32,1,128]{2,1,0:T(1,128)}), f32[32,1,128]{2,1,0:T(1,128)S(1)}, u32[]{:S(2)}, u32[]{:S(2)}) %all-to-all-start) | async-done | bytes 16416 | tf_op jit(solution)/shard_map/all_to_all | solution.py:323
  48.0 0.5 shard_map.85
  48.5 1.0 collective-permute-start.3
  49.6 2.5 %shard_map.86.a = f32[4,16,2304]{2,1,0:T(8,128)S(1)} custom-call(s32[3]{0:T(128)S(1)} %pad_add_fusion.place, bf16[16,128]{1,0:T(8,128)(2,1)S(1)} %get-tuple-element.26.normed, bf16[128,16384]{1,0:T(8,128)(2,1)} %wq.3, bf16[128,2048]{1,0:T(8,128)(2,1)} %wkv.3), custom_call_target="tpu_custom_call" | custom-call | tf_op jit(solution)/shard_map/pallas_call | solution.py:48
  52.2 0.2 collective-permute-start.4
  52.4 2.5 %collective-permute-start.5 = (f32[16,2304]{1,0:T(8,128)S(1)}, f32[16,2304]{1,0:T(8,128)S(1)}, u32[]{:S(2)}, u32[]{:S(2)}) collective-permute-start(f32[16,2304]{1,0:T(8,128)S(1)} %get-tuple-element.30), channel_id=1, source_target_pairs={{0,96},{32,0},{64,32},{96,64},{1,97},{33,1},{65,33},{97,65},{2,98}... | collective-permute-start | bytes 442376 | tf_op jit(solution)/shard_map/ppermute | solution.py:293
  55.0 0.6 collective-permute-start.6
  55.5 3.3 %collective-permute-done.4.b = f32[16,2304]{1,0:T(8,128)S(1)} collective-permute-done((f32[16,2304]{1,0:T(8,128)S(1)}, f32[16,2304]{1,0:T(8,128)S(1)}, u32[]{:S(2)}, u32[]{:S(2)}) %collective-permute-start.4) | collective-permute-done | bytes 147488 | tf_op jit(solution)/shard_map/ppermute | solution.py:293
  58.9 2.0 %collective-permute-done.5.c = f32[16,2304]{1,0:T(8,128)S(1)} collective-permute-done((f32[16,2304]{1,0:T(8,128)S(1)}, f32[16,2304]{1,0:T(8,128)S(1)}, u32[]{:S(2)}, u32[]{:S(2)}) %collective-permute-start.5) | collective-permute-done | bytes 147488 | tf_op jit(solution)/shard_map/ppermute | solution.py:293
  60.9 1.2 collective-permute-done.6.d
  62.0 0.7 shard_map.88
  62.7 4.1 %all-to-all-start.1 = ((f32[16,1,2304]{2,1,0:T(1,128)}), f32[16,1,2304]{2,1,0:T(1,128)S(1)}, u32[]{:S(2)}, u32[]{:S(2)}) async-start(f32[16,1,2304]{2,1,0:T(1,128)} %bitcast.7), calls=%async_computation.1 | async-start | bytes 294912 | tf_op jit(solution)/shard_map/all_to_all | solution.py:301
  66.8 1.8 %shard_map.92 = (bf16[16,2,32,128]{3,2,1,0:T(8,128)(2,1)S(1)}, bf16[16,2,32,128]{3,2,1,0:T(8,128)(2,1)S(1)}, bf16[16,2,32,128]{3,2,1,0:T(8,128)(2,1)S(1)}, bf16[16,2,32,128]{3,2,1,0:T(8,128)(2,1)S(1)}) custom-call(s32[3]{0:T(128)S(1)} %pad_add_fusion.place, bf16[8,16,2,32,128]{4,3,2,1,0:T(8,128)(2,1)} %cache.3), custom_call_target="tpu_custom_call" | custom-call | tf_op jit(solution)/shard_map/pallas_call | solution.py:48
  68.6 0.1 collective-permute-start.10
  68.8 4.3 %collective-permute-start.11 = (bf16[16,2,32,128]{3,2,1,0:T(8,128)(2,1)S(1)}, bf16[16,2,32,128]{3,2,1,0:T(8,128)(2,1)S(1)}, u32[]{:S(2)}, u32[]{:S(2)}) collective-permute-start(bf16[16,2,32,128]{3,2,1,0:T(8,128)(2,1)S(1)} %get-tuple-element.38), channel_id=1, source_target_pairs={{0,33},{1,32},{32,65},{33,64},{64,97},{65,96},{96,1},{97,0},{2,35}... | collective-permute-start | bytes 786440 | tf_op jit(solution)/shard_map/ppermute | solution.py:391
  73.1 0.2 collective-permute-start.12
  73.3 1.5 collective-permute-start.13
  74.7 2.5 %shard_map.91 = (bf16[16,2,32,128]{3,2,1,0:T(8,128)(2,1)S(1)}, bf16[16,2,32,128]{3,2,1,0:T(8,128)(2,1)}, bf16[16,2,32,128]{3,2,1,0:T(8,128)(2,1)}, bf16[16,2,32,128]{3,2,1,0:T(8,128)(2,1)}) custom-call(s32[3]{0:T(128)S(1)} %pad_add_fusion.place, bf16[8,16,2,32,128]{4,3,2,1,0:T(8,128)(2,1)} %cache.3), custom_call_target="tpu_custom_call" | custom-call | tf_op jit(solution)/shard_map/pallas_call | solution.py:48
  77.3 0.7 collective-permute-start.7
  77.9 0.5 collective-permute-start.8
  78.4 7.3 %collective-permute-done.11.refs_5_ = bf16[16,2,32,128]{3,2,1,0:T(8,128)(2,1)S(1)} collective-permute-done((bf16[16,2,32,128]{3,2,1,0:T(8,128)(2,1)S(1)}, bf16[16,2,32,128]{3,2,1,0:T(8,128)(2,1)S(1)}, u32[]{:S(2)}, u32[]{:S(2)}) %collective-permute-start.11) | collective-permute-done | bytes 262176 | tf_op jit(solution)/shard_map/ppermute | solution.py:391
  85.8 0.3 collective-permute-start.9
  86.2 0.7 shard_map.89
  86.9 22.8 %all_to_all.25.q = bf16[16,16,128]{2,1,0:T(8,128)(2,1)S(1)} all-to-all(bf16[16,16,128]{2,1,0:T(8,128)(2,1)S(1)} %get-tuple-element.32), channel_id=1, replica_groups=mesh['groups'=2,'x'=4,'z'=16,'c'=2] {'z'}, dimensions={0} | all-to-all | bytes 131072 | tf_op jit(solution)/shard_map/all_to_all | solution.py:301
  109.7 0.6 shard_map.90.seen
  110.4 1.2 shard_map.93
  111.6 15.8 %all_to_all.26 = f32[16,1,2304]{2,1,0:T(1,128)S(1)} all-to-all(f32[16,1,2304]{2,1,0:T(1,128)S(1)} %bitcast.12), channel_id=1, replica_groups=mesh['groups'=2,'x'=4,'z'=16,'c'=2] {'z'}, dimensions={0} | all-to-all | bytes 294912 | tf_op jit(solution)/shard_map/all_to_all | solution.py:301
  127.3 0.1 shard_map.94
  127.5 18.4 %all_to_all.27.heads = bf16[16,16,128]{2,1,0:T(8,128)(2,1)S(1)} all-to-all(bf16[16,16,128]{2,1,0:T(8,128)(2,1)S(1)} %shard_map.94), channel_id=1, replica_groups=mesh['groups'=2,'x'=4,'z'=16,'c'=2] {'z'}, dimensions={0} | all-to-all | bytes 131072 | tf_op jit(solution)/shard_map/all_to_all | solution.py:301
  145.9 0.1 shard_map.95.a
  146.2 1.4 collective-permute-start.16
  147.6 1.2 collective-permute-start.17
  148.8 3.1 %collective-permute-start.14 = (bf16[16,2048]{1,0:T(8,128)(2,1)S(1)}, bf16[16,2048]{1,0:T(8,128)(2,1)S(1)}, u32[]{:S(2)}, u32[]{:S(2)}) collective-permute-start(bf16[16,2048]{1,0:T(8,128)(2,1)S(1)} %shard_map.95.a), channel_id=1, source_target_pairs={{0,1},{1,0},{2,3},{3,2},{4,5},{5,4},{6,7},{7,6},{8,9},{9,8},{10,11... | collective-permute-start | bytes 196616 | tf_op jit(solution)/shard_map/ppermute | solution.py:297
  152.0 0.7 collective-permute-start.18
  152.7 1.5 collective-permute-start.19
  154.2 2.0 %collective-permute-start.20 = (bf16[16,2048]{1,0:T(8,128)(2,1)S(1)}, bf16[16,2048]{1,0:T(8,128)(2,1)S(1)}, u32[]{:S(2)}, u32[]{:S(2)}) collective-permute-start(bf16[16,2048]{1,0:T(8,128)(2,1)S(1)} %collective-permute-done.17.c), channel_id=1, source_target_pairs={{0,1},{1,0},{2,3},{3,2},{4,5},{5,4},{6,7},{7,6},{8,9},{9,8},{10,11... | collective-permute-start | bytes 196616 | tf_op jit(solution)/shard_map/ppermute | solution.py:297
  156.3 2.4 %shard_map.96 = (f32[16,128]{1,0:T(8,128)S(1)}, bf16[3,2048,128]{2,1,0:T(8,128)(2,1)S(1)}) custom-call(s32[3]{0:T(128)S(1)} %pad_add_fusion.place, bf16[16,2048]{1,0:T(8,128)(2,1)S(1)} %shard_map.95.a, bf16[16,2048]{1,0:T(8,128)(2,1)S(1)} %collective-permute-done.14.b, bf16[16384,128]{1,0:T(8,128)(2,1)} %wo.3, bf16[16,128]{1,0:T(8,128)(2,1)S(1)} %copy-done), custom_call_target="tpu_custom_call" | custom-call | tf_op jit(solution)/shard_map/pallas_call | solution.py:48
  158.6 2.1 %shard_map.97 = (f32[16,128]{1,0:T(8,128)S(1)}, bf16[3,2048,128]{2,1,0:T(8,128)(2,1)S(1)}) custom-call(s32[3]{0:T(128)S(1)} %pad_add_fusion.place, f32[16,128]{1,0:T(8,128)S(1)} %get-tuple-element.43.total, bf16[16,2048]{1,0:T(8,128)(2,1)S(1)} %collective-permute-done.15.a, bf16[16,2048]{1,0:T(8,128)(2,1)S(1)} %collective-permute-done.16.b, ...), custom_call_target="tpu_custom_call" | custom-call | tf_op jit(solution)/shard_map/pallas_call | solution.py:48
  160.8 0.9 shard_map.98
  (32 shorter events, 0.5 us)
Async XLA Ops:
  1.3 5.3 %collective-permute-start = (f32[1,128]{1,0:T(1,128)}, f32[1,128]{1,0:T(1,128)S(1)}, u32[]{:S(2)}, u32[]{:S(2)}) collective-permute-start(f32[1,128]{1,0:T(1,128)} %shard_map.82.a), channel_id=1, source_target_pairs={{0,32},{32,64},{64,96},{96,0},{1,33},{33,65},{65,97},{97,1},{2,34}... | collective-permute-start | bytes 1544 | tf_op jit(solution)/shard_map/ppermute | solution.py:293
  3.4 3.1 %collective-permute-start.1 = (f32[1,128]{1,0:T(1,128)}, f32[1,128]{1,0:T(1,128)S(1)}, u32[]{:S(2)}, u32[]{:S(2)}) collective-permute-start(f32[1,128]{1,0:T(1,128)} %shard_map.82.a), channel_id=1, source_target_pairs={{0,96},{32,0},{64,32},{96,64},{1,97},{33,1},{65,33},{97,65},{2,98}... | collective-permute-start | bytes 1544 | tf_op jit(solution)/shard_map/ppermute | solution.py:293
  5.0 4.0 %collective-permute-start.2 = (f32[1,128]{1,0:T(1,128)}, f32[1,128]{1,0:T(1,128)S(1)}, u32[]{:S(2)}, u32[]{:S(2)}) collective-permute-start(f32[1,128]{1,0:T(1,128)} %shard_map.82.a), channel_id=1, source_target_pairs={{0,64},{32,96},{64,0},{96,32},{1,65},{33,97},{65,1},{97,33},{2,66}... | collective-permute-start | bytes 1544 | tf_op jit(solution)/shard_map/ppermute | solution.py:293
  9.0 0.6 copy-start.2
  10.2 37.9 %all-to-all-start = ((f32[32,1,128]{2,1,0:T(1,128)}), f32[32,1,128]{2,1,0:T(1,128)S(1)}, u32[]{:S(2)}, u32[]{:S(2)}) async-start(f32[32,1,128]{2,1,0:T(1,128)} %bitcast.4), calls=%async_computation | async-start | bytes 32768 | tf_op jit(solution)/shard_map/all_to_all | solution.py:323
  36.5 11.5 %copy-start = (bf16[16,128]{1,0:T(8,128)(2,1)S(1)}, bf16[16,128]{1,0:T(8,128)(2,1)}, u32[]{:S(2)}) copy-start(bf16[16,128]{1,0:T(8,128)(2,1)} %x.5) | copy-start | bytes 12292
  36.6 11.5 %copy-start.4 = (bf16[128]{0:T(256)(128)(2,1)S(1)}, bf16[128]{0:T(256)(128)(2,1)}, u32[]{:S(2)}) copy-start(bf16[128]{0:T(256)(128)(2,1)} %param.9) | copy-start | bytes 772
  48.5 3.6 %collective-permute-start.3 = (f32[4,16,2304]{2,1,0:T(8,128)S(1)}, f32[4,16,2304]{2,1,0:T(8,128)S(1)}, u32[]{:S(2)}, u32[]{:S(2)}) collective-permute-start(f32[4,16,2304]{2,1,0:T(8,128)S(1)} %get-tuple-element.27), channel_id=1, source_target_pairs={{0,1},{1,0},{2,3},{3,2},{4,5},{5,4},{6,7},{7,6},{8,9},{9,8},{10,11... | collective-permute-start | bytes 1769480 | tf_op jit(solution)/shard_map/ppermute | solution.py:297
  52.2 6.7 %collective-permute-start.4 = (f32[16,2304]{1,0:T(8,128)S(1)}, f32[16,2304]{1,0:T(8,128)S(1)}, u32[]{:S(2)}, u32[]{:S(2)}) collective-permute-start(f32[16,2304]{1,0:T(8,128)S(1)} %get-tuple-element.29), channel_id=1, source_target_pairs={{0,32},{32,64},{64,96},{96,0},{1,33},{33,65},{65,97},{97,1},{2,34}... | collective-permute-start | bytes 442376 | tf_op jit(solution)/shard_map/ppermute | solution.py:293
  52.4 8.5 %collective-permute-start.5 = (f32[16,2304]{1,0:T(8,128)S(1)}, f32[16,2304]{1,0:T(8,128)S(1)}, u32[]{:S(2)}, u32[]{:S(2)}) collective-permute-start(f32[16,2304]{1,0:T(8,128)S(1)} %get-tuple-element.30), channel_id=1, source_target_pairs={{0,96},{32,0},{64,32},{96,64},{1,97},{33,1},{65,33},{97,65},{2,98}... | collective-permute-start | bytes 442376 | tf_op jit(solution)/shard_map/ppermute | solution.py:293
  55.0 7.1 %collective-permute-start.6 = (f32[16,2304]{1,0:T(8,128)S(1)}, f32[16,2304]{1,0:T(8,128)S(1)}, u32[]{:S(2)}, u32[]{:S(2)}) collective-permute-start(f32[16,2304]{1,0:T(8,128)S(1)} %get-tuple-element.31), channel_id=1, source_target_pairs={{0,64},{32,96},{64,0},{96,32},{1,65},{33,97},{65,1},{97,33},{2,66}... | collective-permute-start | bytes 442376 | tf_op jit(solution)/shard_map/ppermute | solution.py:293
  62.7 15.2 %copy-start.3 = (s32[16]{0:T(128)S(1)}, s32[16]{0:T(128)}, u32[]{:S(2)}) copy-start(s32[16]{0:T(128)} %lengths.1) | copy-start | bytes 196
  62.7 23.5 %all-to-all-start.1 = ((f32[16,1,2304]{2,1,0:T(1,128)}), f32[16,1,2304]{2,1,0:T(1,128)S(1)}, u32[]{:S(2)}, u32[]{:S(2)}) async-start(f32[16,1,2304]{2,1,0:T(1,128)} %bitcast.7), calls=%async_computation.1 | async-start | bytes 294912 | tf_op jit(solution)/shard_map/all_to_all | solution.py:301
  66.8 43.5 %copy-start.1 = (s32[8,16]{1,0:T(8,128)S(1)}, s32[8,16]{1,0:T(8,128)}, u32[]{:S(2)}) copy-start(s32[8,16]{1,0:T(8,128)} %slabs.1) | copy-start | bytes 1540
  68.6 9.3 %collective-permute-start.10 = (bf16[16,2,32,128]{3,2,1,0:T(8,128)(2,1)S(1)}, bf16[16,2,32,128]{3,2,1,0:T(8,128)(2,1)S(1)}, u32[]{:S(2)}, u32[]{:S(2)}) collective-permute-start(bf16[16,2,32,128]{3,2,1,0:T(8,128)(2,1)S(1)} %get-tuple-element.37), channel_id=1, source_target_pairs={{0,64},{1,65},{32,96},{33,97},{64,0},{65,1},{96,32},{97,33},{2,66}... | collective-permute-start | bytes 786440 | tf_op jit(solution)/shard_map/ppermute | solution.py:391
  68.8 17.0 %collective-permute-start.11 = (bf16[16,2,32,128]{3,2,1,0:T(8,128)(2,1)S(1)}, bf16[16,2,32,128]{3,2,1,0:T(8,128)(2,1)S(1)}, u32[]{:S(2)}, u32[]{:S(2)}) collective-permute-start(bf16[16,2,32,128]{3,2,1,0:T(8,128)(2,1)S(1)} %get-tuple-element.38), channel_id=1, source_target_pairs={{0,33},{1,32},{32,65},{33,64},{64,97},{65,96},{96,1},{97,0},{2,35}... | collective-permute-start | bytes 786440 | tf_op jit(solution)/shard_map/ppermute | solution.py:391
  73.1 37.2 %collective-permute-start.12 = (bf16[16,2,32,128]{3,2,1,0:T(8,128)(2,1)S(1)}, bf16[16,2,32,128]{3,2,1,0:T(8,128)(2,1)S(1)}, u32[]{:S(2)}, u32[]{:S(2)}) collective-permute-start(bf16[16,2,32,128]{3,2,1,0:T(8,128)(2,1)S(1)} %get-tuple-element.39), channel_id=1, source_target_pairs={{0,97},{1,96},{32,1},{33,0},{64,33},{65,32},{96,65},{97,64},{2,99}... | collective-permute-start | bytes 786440 | tf_op jit(solution)/shard_map/ppermute | solution.py:391
  73.3 37.1 %collective-permute-start.13 = (bf16[16,2,32,128]{3,2,1,0:T(8,128)(2,1)S(1)}, bf16[16,2,32,128]{3,2,1,0:T(8,128)(2,1)S(1)}, u32[]{:S(2)}, u32[]{:S(2)}) collective-permute-start(bf16[16,2,32,128]{3,2,1,0:T(8,128)(2,1)S(1)} %get-tuple-element.40), channel_id=1, source_target_pairs={{0,65},{1,64},{32,97},{33,96},{64,1},{65,0},{96,33},{97,32},{2,67}... | collective-permute-start | bytes 786440 | tf_op jit(solution)/shard_map/ppermute | solution.py:391
  77.3 33.1 %collective-permute-start.7 = (bf16[16,2,32,128]{3,2,1,0:T(8,128)(2,1)}, bf16[16,2,32,128]{3,2,1,0:T(8,128)(2,1)S(1)}, u32[]{:S(2)}, u32[]{:S(2)}) collective-permute-start(bf16[16,2,32,128]{3,2,1,0:T(8,128)(2,1)} %get-tuple-element.34), channel_id=1, source_target_pairs={{0,1},{1,0},{32,33},{33,32},{64,65},{65,64},{96,97},{97,96},{2,3},... | collective-permute-start | bytes 786440 | tf_op jit(solution)/shard_map/ppermute | solution.py:391
  77.9 32.4 %collective-permute-start.8 = (bf16[16,2,32,128]{3,2,1,0:T(8,128)(2,1)}, bf16[16,2,32,128]{3,2,1,0:T(8,128)(2,1)S(1)}, u32[]{:S(2)}, u32[]{:S(2)}) collective-permute-start(bf16[16,2,32,128]{3,2,1,0:T(8,128)(2,1)} %get-tuple-element.35), channel_id=1, source_target_pairs={{0,32},{1,33},{32,64},{33,65},{64,96},{65,97},{96,0},{97,1},{2,34}... | collective-permute-start | bytes 786440 | tf_op jit(solution)/shard_map/ppermute | solution.py:391
  85.8 24.6 %collective-permute-start.9 = (bf16[16,2,32,128]{3,2,1,0:T(8,128)(2,1)}, bf16[16,2,32,128]{3,2,1,0:T(8,128)(2,1)S(1)}, u32[]{:S(2)}, u32[]{:S(2)}) collective-permute-start(bf16[16,2,32,128]{3,2,1,0:T(8,128)(2,1)} %get-tuple-element.36), channel_id=1, source_target_pairs={{0,96},{1,97},{32,0},{33,1},{64,32},{65,33},{96,64},{97,65},{2,98}... | collective-permute-start | bytes 786440 | tf_op jit(solution)/shard_map/ppermute | solution.py:391
  146.0 5.9 %collective-permute-start.15 = (bf16[16,2048]{1,0:T(8,128)(2,1)S(1)}, bf16[16,2048]{1,0:T(8,128)(2,1)S(1)}, u32[]{:S(2)}, u32[]{:S(2)}) collective-permute-start(bf16[16,2048]{1,0:T(8,128)(2,1)S(1)} %shard_map.95.a), channel_id=1, source_target_pairs={{0,96},{32,0},{64,32},{96,64},{1,97},{33,1},{65,33},{97,65},{2,98}... | collective-permute-start | bytes 196616 | tf_op jit(solution)/shard_map/ppermute | solution.py:293
  146.2 6.5 %collective-permute-start.16 = (bf16[16,2048]{1,0:T(8,128)(2,1)S(1)}, bf16[16,2048]{1,0:T(8,128)(2,1)S(1)}, u32[]{:S(2)}, u32[]{:S(2)}) collective-permute-start(bf16[16,2048]{1,0:T(8,128)(2,1)S(1)} %shard_map.95.a), channel_id=1, source_target_pairs={{0,32},{32,64},{64,96},{96,0},{1,33},{33,65},{65,97},{97,1},{2,34}... | collective-permute-start | bytes 196616 | tf_op jit(solution)/shard_map/ppermute | solution.py:293
  147.6 6.6 %collective-permute-start.17 = (bf16[16,2048]{1,0:T(8,128)(2,1)S(1)}, bf16[16,2048]{1,0:T(8,128)(2,1)S(1)}, u32[]{:S(2)}, u32[]{:S(2)}) collective-permute-start(bf16[16,2048]{1,0:T(8,128)(2,1)S(1)} %shard_map.95.a), channel_id=1, source_target_pairs={{0,64},{32,96},{64,0},{96,32},{1,65},{33,97},{65,1},{97,33},{2,66}... | collective-permute-start | bytes 196616 | tf_op jit(solution)/shard_map/ppermute | solution.py:293
  148.8 7.4 %collective-permute-start.14 = (bf16[16,2048]{1,0:T(8,128)(2,1)S(1)}, bf16[16,2048]{1,0:T(8,128)(2,1)S(1)}, u32[]{:S(2)}, u32[]{:S(2)}) collective-permute-start(bf16[16,2048]{1,0:T(8,128)(2,1)S(1)} %shard_map.95.a), channel_id=1, source_target_pairs={{0,1},{1,0},{2,3},{3,2},{4,5},{5,4},{6,7},{7,6},{8,9},{9,8},{10,11... | collective-permute-start | bytes 196616 | tf_op jit(solution)/shard_map/ppermute | solution.py:297
  152.0 8.8 %collective-permute-start.18 = (bf16[16,2048]{1,0:T(8,128)(2,1)S(1)}, bf16[16,2048]{1,0:T(8,128)(2,1)S(1)}, u32[]{:S(2)}, u32[]{:S(2)}) collective-permute-start(bf16[16,2048]{1,0:T(8,128)(2,1)S(1)} %collective-permute-done.15.a), channel_id=1, source_target_pairs={{0,1},{1,0},{2,3},{3,2},{4,5},{5,4},{6,7},{7,6},{8,9},{9,8},{10,11... | collective-permute-start | bytes 196616 | tf_op jit(solution)/shard_map/ppermute | solution.py:297
  152.7 8.1 %collective-permute-start.19 = (bf16[16,2048]{1,0:T(8,128)(2,1)S(1)}, bf16[16,2048]{1,0:T(8,128)(2,1)S(1)}, u32[]{:S(2)}, u32[]{:S(2)}) collective-permute-start(bf16[16,2048]{1,0:T(8,128)(2,1)S(1)} %collective-permute-done.16.b), channel_id=1, source_target_pairs={{0,1},{1,0},{2,3},{3,2},{4,5},{5,4},{6,7},{7,6},{8,9},{9,8},{10,11... | collective-permute-start | bytes 196616 | tf_op jit(solution)/shard_map/ppermute | solution.py:297
  154.2 6.6 %collective-permute-start.20 = (bf16[16,2048]{1,0:T(8,128)(2,1)S(1)}, bf16[16,2048]{1,0:T(8,128)(2,1)S(1)}, u32[]{:S(2)}, u32[]{:S(2)}) collective-permute-start(bf16[16,2048]{1,0:T(8,128)(2,1)S(1)} %collective-permute-done.17.c), channel_id=1, source_target_pairs={{0,1},{1,0},{2,3},{3,2},{4,5},{5,4},{6,7},{7,6},{8,9},{9,8},{10,11... | collective-permute-start | bytes 196616 | tf_op jit(solution)/shard_map/ppermute | solution.py:297

commit v8 on v6

--- a/solution.py
+++ b/solution.py
@@ -125,17 +125,16 @@
     run_all(in_copies(place, FIRST, wq, wkv, out, sems))
 
 
-def fetch_cache_kernel(moves, place, cache, *refs):
+def fetch_cache_kernel(moves, staged, place, cache, *refs):
     outs, held, sems, out_sems = refs[:-3], *refs[-3:]
     first, second = [], []
     for k, (j, d) in enumerate(moves):
-        stays = (j, d) == (0, 0)
-        to = outs[k] if stays else held.at[k]
+        to = held.at[k] if k in staged else outs[k]
         first.append(pltpu.make_async_copy(cache.at[head_of(place, j, d)], to, sems.at[k]))
         first[k].start()
-    for k, move in enumerate(moves):
+    for k in range(len(moves)):
         first[k].wait()
-        if move != (0, 0):
+        if k in staged:
             second.append(pltpu.make_async_copy(held.at[k], outs[k], out_sems.at[k]))
             second[-1].start()
     for copy in second:
@@ -174,13 +173,14 @@
         out[pl.ds(k, n, stride=ROWS), :] = total
 
 
-def queries_kernel(parts, cosine, sine, q_out, new_score, new_value):
+def queries_kernel(place, parts, cosine, sine, q_out, new_score, new_value):
     n = parts.shape[0] // ROWS
     total = parts[:ROWS]
     for k in range(1, n):
         total = total + parts[k * ROWS : (k + 1) * ROWS]
     lead = total[: GROUP + 1]
-    turned = lead * cosine[...] + pltpu.roll(lead, HD // 2, 1) * sine[...]
+    mine = pl.ds(place[1], 1)
+    turned = lead * cosine[mine] + pltpu.roll(lead, HD // 2, 1) * sine[mine]
     turned = turned.astype(BF16)
     q = turned[:GROUP]
     q_out[...] = jnp.broadcast_to(q[None], q_out.shape)
@@ -190,21 +190,16 @@
     new_value[...] = total[GROUP + 1 :].astype(BF16).astype(F32)
 
 
-def positions_kernel(local, first, last, place, base, out):
-    index = lax.broadcasted_iota(jnp.int32, out.shape, 1)
-    start = base[...]
-    for k, (j, d) in list(enumerate(MOVES))[first:last]:
+def visible_kernel(local, place, lengths, q, out):
+    del q
+    index = lax.broadcasted_iota(jnp.int32, (1, out.shape[1]), 1)
+    position = index % local
+    for k, (j, d) in enumerate(MOVES):
         core = 1 - place[2] if d else place[2]
         block = (lax.rem(place[0] + (NX - j), NX) * NZ + place[1]) * NC + core
-        start = jnp.where(index // local == k, block * local, start)
-    out[...] = start
-
-
-def visible_kernel(local, lengths, positions, q, out):
-    del q
-    here = positions[...] + lax.broadcasted_iota(jnp.int32, positions.shape, 1) % local
+        position = jnp.where(index // local == k, position + block * local, position)
     for b in range(out.shape[0]):
-        out[b : b + 1] = (here < lengths[b]).astype(F32)
+        out[b : b + 1] = (position < lengths[b]).astype(F32)
 
 
 def attend_kernel(place, slabs, seen, q, *refs):
@@ -304,11 +299,9 @@
     )
     place = jnp.stack([lax.axis_index(a) for a in TENSOR]).astype(jnp.int32)
 
-    mine = jnp.arange(n, dtype=jnp.int32) == lax.axis_index("z")
-    position = jnp.sum(jnp.where(mine, lengths, 0)).astype(F32)
     lane = jnp.arange(HD, dtype=jnp.int32)[None]
     frequency = ROPE_BASE ** (-2.0 * (lane % (HD // 2)).astype(F32) / HD)
-    angles = position * frequency
+    angles = lengths.astype(F32)[:, None] * frequency
     cosine = jnp.cos(angles)
     sine = jnp.sin(angles) * jnp.where(lane < HD // 2, -1.0, 1.0)
 
@@ -334,11 +327,14 @@
     )
 
     cache = []
-    for moves in (MOVES[:EARLY], MOVES[EARLY:]):
+    for moves, staged in ((MOVES[:EARLY], range(1, EARLY)), (MOVES[EARLY:], ())):
         block = kv_cache.shape[1:]
         cache += call(
-            functools.partial(fetch_cache_kernel, moves),
-            [struct(block, BF16) if move == (0, 0) else pltpu.HBM(block, BF16) for move in moves],
+            functools.partial(fetch_cache_kernel, moves, staged),
+            [
+                pltpu.HBM(block, BF16) if k in staged else struct(block, BF16)
+                for k in range(len(moves))
+            ],
             [SMEM, HBM],
             place,
             kv_cache,
@@ -351,14 +347,6 @@
 
     local = kv_cache.shape[3]
     seen = len(MOVES) * local
-    positions = call(
-        functools.partial(positions_kernel, local, 0, EARLY),
-        struct((1, seen), jnp.int32),
-        [SMEM, VMEM],
-        place,
-        jnp.zeros((1, seen), jnp.int32),
-    )
-
     product = struct((NX, n, PW), F32)
     normed, sent = call(
         project_first_kernel,
@@ -392,18 +380,12 @@
             for c in range(NC)
         ]
         cache[k] = lax.ppermute(cache[k], ("x", "c"), pairs)
-    positions = call(
-        functools.partial(positions_kernel, local, EARLY, len(MOVES)),
-        struct((1, seen), jnp.int32),
-        [SMEM, VMEM],
-        place,
-        positions,
-    )
     rows = across_z(rows.reshape(n, 1, PW)).reshape(n * ROWS, HD)
     q, new_score, new_value = call(
         queries_kernel,
         [struct((n, GROUP, HD), BF16), struct((1, HD), F32), struct((1, HD), F32)],
-        [VMEM] * 3,
+        [SMEM] + [VMEM] * 3,
+        place,
         rows,
         cosine,
         sine,
@@ -413,9 +395,9 @@
     visible = call(
         functools.partial(visible_kernel, local),
         struct((n, seen), F32),
-        [SMEM, VMEM, VMEM],
+        [SMEM, SMEM, VMEM],
+        place,
         lengths,
-        positions,
         q,
     )
     partial = call(

time: 162 us -> 161 us (level)
  blocking collectives: 34.2 us -> 57 us
  starting transfers between devices: 68.9 us -> 57.4 us
  waiting for transfers between devices: 34.8 us -> 25.6 us
  Pallas kernels: 21 us -> 19.1 us
    all_to_all x2 -> x3, blocking collectives: 34.2 us -> 57 us  [across_z(): return lax.all_to_all(value, 'z', 0, 0, tiled=True)]
    all_to_all x2 -> x1, starting transfers between devices: 15.5 us -> 3.95 us  [across_z(): return lax.all_to_all(value, 'z', 0, 0, tiled=True)]
    all_to_all x2 -> x1, waiting for transfers between devices: 10.3 us -> 0.01 us  [across_z(): return lax.all_to_all(value, 'z', 0, 0, tiled=True)]
    pallas_call x18 -> x16, Pallas kernels: 21 us -> 19.1 us  [call(): pl.pallas_call(kernel, in_specs=specs, out_specs=outs, out_shape=out, scr...]
  transfers between devices with their start and end apart: 24 -> 23, of which waited for: 7 -> 6; matrix products, arithmetic and copies ran while one was open for 0% -> 0% of each run, Pallas kernels for 9% -> 8%
where the time goes in v8:
time: 161 us; the launch traced here: 160 us
  starting transfers between devices  57.4 us (36%)
  blocking collectives  57 us (35%)
  waiting for transfers between devices  25.6 us (16%)
  Pallas kernels  19.1 us (12%)
    all_to_all x3, blocking collectives, across_z(): return lax.all_to_all(value, 'z', 0, 0, tiled=True)  57 us
    all_to_all x1, starting transfers between devices, step(): lax.all_to_all(sums.reshape(NZ * NC, 1, HD), ('z', 'c'), 0, 0, tiled=True)  26 us
    pallas_call x16, Pallas kernels, call(): pl.pallas_call(kernel, in_specs=specs, out_specs=outs, out_shape=out, scr...  19.1 us
    ppermute x9, starting transfers between devices, shift_x(): return lax.ppermute(value, 'x', [(i, (i + by) % NX) for i in range(NX)])  11.5 us
    all_to_all x1, waiting for transfers between devices, step(): lax.all_to_all(sums.reshape(NZ * NC, 1, HD), ('z', 'c'), 0, 0, tiled=True)  9.15 us
    ppermute x9, waiting for transfers between devices, shift_x(): return lax.ppermute(value, 'x', [(i, (i + by) % NX) for i in range(NX)])  9.02 us
    ppermute x5, starting transfers between devices, swap_c(): return lax.ppermute(value, 'c', [(0, 1), (1, 0)])  8.46 us
    ppermute x7, starting transfers between devices, step(): cache[k] = lax.ppermute(cache[k], ('x', 'c'), pairs)  7.51 us
  transfers between devices with their start and end apart: 23, of which 6 were waited for; matrix products, arithmetic and copies ran while one was open for 0% of the time, Pallas kernels for 8%

profile of v8, /device:TPU:33, one launch (start us, length us, event | category | flops | bytes accessed | tf_op | source)
XLA Modules:
  0.0 160.2 jit_solution(13148723431610071674)
XLA Ops:
  0.0 1.3 shard_map.82.a
  1.4 2.2 %collective-permute-start = (f32[1,128]{1,0:T(1,128)}, f32[1,128]{1,0:T(1,128)S(1)}, u32[]{:S(2)}, u32[]{:S(2)}) collective-permute-start(f32[1,128]{1,0:T(1,128)} %shard_map.82.a), channel_id=1, source_target_pairs={{0,32},{32,64},{64,96},{96,0},{1,33},{33,65},{65,97},{97,1},{2,34}... | collective-permute-start | bytes 1544 | tf_op jit(solution)/shard_map/ppermute | solution.py:284
  3.5 1.5 collective-permute-start.1
  5.1 1.6 collective-permute-start.2
  6.7 2.5 %collective-permute-done.2.d = f32[1,128]{1,0:T(1,128)S(1)} collective-permute-done((f32[1,128]{1,0:T(1,128)}, f32[1,128]{1,0:T(1,128)S(1)}, u32[]{:S(2)}, u32[]{:S(2)}) %collective-permute-start.2) | collective-permute-done | bytes 544 | tf_op jit(solution)/shard_map/ppermute | solution.py:284
  9.2 0.7 copy-done.2
  9.9 0.6 shard_map.83
  10.5 26.0 %all-to-all-start = ((f32[32,1,128]{2,1,0:T(1,128)}), f32[32,1,128]{2,1,0:T(1,128)S(1)}, u32[]{:S(2)}, u32[]{:S(2)}) async-start(f32[32,1,128]{2,1,0:T(1,128)} %bitcast.4), calls=%async_computation | async-start | bytes 32768 | tf_op jit(solution)/shard_map/all_to_all | solution.py:314
  36.5 2.3 %shard_map.84.w = bf16[4,128,2304]{2,1,0:T(8,128)(2,1)S(1)} custom-call(s32[3]{0:T(128)S(1)} %pad_add_fusion.place, bf16[128,16384]{1,0:T(8,128)(2,1)} %wq.3, bf16[128,2048]{1,0:T(8,128)(2,1)} %wkv.3), custom_call_target="tpu_custom_call" | custom-call | tf_op jit(solution)/shard_map/pallas_call | solution.py:47
  38.8 9.2 %all-to-all-done = f32[32,1,128]{2,1,0:T(1,128)S(1)} async-done(((f32[32,1,128]{2,1,0:T(1,128)}), f32[32,1,128]{2,1,0:T(1,128)S(1)}, u32[]{:S(2)}, u32[]{:S(2)}) %all-to-all-start) | async-done | bytes 16416 | tf_op jit(solution)/shard_map/all_to_all | solution.py:314
  48.0 0.5 shard_map.85
  48.5 1.1 collective-permute-start.3
  49.5 2.5 %shard_map.86.a = f32[4,16,2304]{2,1,0:T(8,128)S(1)} custom-call(s32[3]{0:T(128)S(1)} %pad_add_fusion.place, bf16[16,128]{1,0:T(8,128)(2,1)S(1)} %get-tuple-element.24.normed, bf16[128,16384]{1,0:T(8,128)(2,1)} %wq.3, bf16[128,2048]{1,0:T(8,128)(2,1)} %wkv.3), custom_call_target="tpu_custom_call" | custom-call | tf_op jit(solution)/shard_map/pallas_call | solution.py:47
  52.2 0.2 collective-permute-start.4
  52.4 2.5 %collective-permute-start.5 = (f32[16,2304]{1,0:T(8,128)S(1)}, f32[16,2304]{1,0:T(8,128)S(1)}, u32[]{:S(2)}, u32[]{:S(2)}) collective-permute-start(f32[16,2304]{1,0:T(8,128)S(1)} %get-tuple-element.28), channel_id=1, source_target_pairs={{0,96},{32,0},{64,32},{96,64},{1,97},{33,1},{65,33},{97,65},{2,98}... | collective-permute-start | bytes 442376 | tf_op jit(solution)/shard_map/ppermute | solution.py:284
  55.0 0.6 collective-permute-start.6
  55.6 3.3 %collective-permute-done.4.b = f32[16,2304]{1,0:T(8,128)S(1)} collective-permute-done((f32[16,2304]{1,0:T(8,128)S(1)}, f32[16,2304]{1,0:T(8,128)S(1)}, u32[]{:S(2)}, u32[]{:S(2)}) %collective-permute-start.4) | collective-permute-done | bytes 147488 | tf_op jit(solution)/shard_map/ppermute | solution.py:284
  58.9 2.0 %collective-permute-done.5.c = f32[16,2304]{1,0:T(8,128)S(1)} collective-permute-done((f32[16,2304]{1,0:T(8,128)S(1)}, f32[16,2304]{1,0:T(8,128)S(1)}, u32[]{:S(2)}, u32[]{:S(2)}) %collective-permute-start.5) | collective-permute-done | bytes 147488 | tf_op jit(solution)/shard_map/ppermute | solution.py:284
  60.9 1.2 collective-permute-done.6.d
  62.0 0.7 shard_map.88
  62.7 4.0 %all-to-all-start.1 = ((f32[16,1,2304]{2,1,0:T(1,128)}), f32[16,1,2304]{2,1,0:T(1,128)S(1)}, u32[]{:S(2)}, u32[]{:S(2)}) async-start(f32[16,1,2304]{2,1,0:T(1,128)} %bitcast.7), calls=%async_computation.1 | async-start | bytes 294912 | tf_op jit(solution)/shard_map/all_to_all | solution.py:292
  66.7 1.8 %shard_map.92 = (bf16[16,2,32,128]{3,2,1,0:T(8,128)(2,1)S(1)}, bf16[16,2,32,128]{3,2,1,0:T(8,128)(2,1)S(1)}, bf16[16,2,32,128]{3,2,1,0:T(8,128)(2,1)S(1)}, bf16[16,2,32,128]{3,2,1,0:T(8,128)(2,1)S(1)}) custom-call(s32[3]{0:T(128)S(1)} %pad_add_fusion.place, bf16[8,16,2,32,128]{4,3,2,1,0:T(8,128)(2,1)} %cache.3), custom_call_target="tpu_custom_call" | custom-call | tf_op jit(solution)/shard_map/pallas_call | solution.py:47
  68.5 0.1 collective-permute-start.10
  68.6 4.3 %collective-permute-start.11 = (bf16[16,2,32,128]{3,2,1,0:T(8,128)(2,1)S(1)}, bf16[16,2,32,128]{3,2,1,0:T(8,128)(2,1)S(1)}, u32[]{:S(2)}, u32[]{:S(2)}) collective-permute-start(bf16[16,2,32,128]{3,2,1,0:T(8,128)(2,1)S(1)} %get-tuple-element.36), channel_id=1, source_target_pairs={{0,33},{1,32},{32,65},{33,64},{64,97},{65,96},{96,1},{97,0},{2,35}... | collective-permute-start | bytes 786440 | tf_op jit(solution)/shard_map/ppermute | solution.py:382
  72.9 0.2 collective-permute-start.12
  73.1 1.5 collective-permute-start.13
  74.6 2.5 %shard_map.91 = (bf16[16,2,32,128]{3,2,1,0:T(8,128)(2,1)S(1)}, bf16[16,2,32,128]{3,2,1,0:T(8,128)(2,1)}, bf16[16,2,32,128]{3,2,1,0:T(8,128)(2,1)}, bf16[16,2,32,128]{3,2,1,0:T(8,128)(2,1)}) custom-call(s32[3]{0:T(128)S(1)} %pad_add_fusion.place, bf16[8,16,2,32,128]{4,3,2,1,0:T(8,128)(2,1)} %cache.3), custom_call_target="tpu_custom_call" | custom-call | tf_op jit(solution)/shard_map/pallas_call | solution.py:47
  77.1 0.7 collective-permute-start.7
  77.8 0.5 collective-permute-start.8
  78.3 7.3 %collective-permute-done.11.refs_5_ = bf16[16,2,32,128]{3,2,1,0:T(8,128)(2,1)S(1)} collective-permute-done((bf16[16,2,32,128]{3,2,1,0:T(8,128)(2,1)S(1)}, bf16[16,2,32,128]{3,2,1,0:T(8,128)(2,1)S(1)}, u32[]{:S(2)}, u32[]{:S(2)}) %collective-permute-start.11) | collective-permute-done | bytes 262176 | tf_op jit(solution)/shard_map/ppermute | solution.py:382
  85.6 0.3 collective-permute-start.9
  86.1 0.7 shard_map.89
  86.8 22.8 %all_to_all.25.q = bf16[16,16,128]{2,1,0:T(8,128)(2,1)S(1)} all-to-all(bf16[16,16,128]{2,1,0:T(8,128)(2,1)S(1)} %get-tuple-element.30), channel_id=1, replica_groups=mesh['groups'=2,'x'=4,'z'=16,'c'=2] {'z'}, dimensions={0} | all-to-all | bytes 131072 | tf_op jit(solution)/shard_map/all_to_all | solution.py:292
  109.6 0.6 shard_map.90.seen
  110.2 1.2 shard_map.93
  111.4 15.8 %all_to_all.26 = f32[16,1,2304]{2,1,0:T(1,128)S(1)} all-to-all(f32[16,1,2304]{2,1,0:T(1,128)S(1)} %bitcast.12), channel_id=1, replica_groups=mesh['groups'=2,'x'=4,'z'=16,'c'=2] {'z'}, dimensions={0} | all-to-all | bytes 294912 | tf_op jit(solution)/shard_map/all_to_all | solution.py:292
  127.2 0.1 shard_map.94
  127.4 18.4 %all_to_all.27.heads = bf16[16,16,128]{2,1,0:T(8,128)(2,1)S(1)} all-to-all(bf16[16,16,128]{2,1,0:T(8,128)(2,1)S(1)} %shard_map.94), channel_id=1, replica_groups=mesh['groups'=2,'x'=4,'z'=16,'c'=2] {'z'}, dimensions={0} | all-to-all | bytes 131072 | tf_op jit(solution)/shard_map/all_to_all | solution.py:292
  145.8 0.1 shard_map.95.a
  145.9 0.1 collective-permute-start.15
  146.0 1.4 collective-permute-start.16
  147.5 1.2 collective-permute-start.17
  148.7 3.1 %collective-permute-start.14 = (bf16[16,2048]{1,0:T(8,128)(2,1)S(1)}, bf16[16,2048]{1,0:T(8,128)(2,1)S(1)}, u32[]{:S(2)}, u32[]{:S(2)}) collective-permute-start(bf16[16,2048]{1,0:T(8,128)(2,1)S(1)} %shard_map.95.a), channel_id=1, source_target_pairs={{0,1},{1,0},{2,3},{3,2},{4,5},{5,4},{6,7},{7,6},{8,9},{9,8},{10,11... | collective-permute-start | bytes 196616 | tf_op jit(solution)/shard_map/ppermute | solution.py:288
  151.8 0.7 collective-permute-start.18
  152.6 1.5 collective-permute-start.19
  154.1 2.0 %collective-permute-start.20 = (bf16[16,2048]{1,0:T(8,128)(2,1)S(1)}, bf16[16,2048]{1,0:T(8,128)(2,1)S(1)}, u32[]{:S(2)}, u32[]{:S(2)}) collective-permute-start(bf16[16,2048]{1,0:T(8,128)(2,1)S(1)} %collective-permute-done.17.refs_3_), channel_id=1, source_target_pairs={{0,1},{1,0},{2,3},{3,2},{4,5},{5,4},{6,7},{7,6},{8,9},{9,8},{10,11... | collective-permute-start | bytes 196616 | tf_op jit(solution)/shard_map/ppermute | solution.py:288
  156.1 2.9 %shard_map.96 = (f32[16,128]{1,0:T(8,128)S(1)}, bf16[6,2048,128]{2,1,0:T(8,128)(2,1)S(1)}) custom-call(s32[3]{0:T(128)S(1)} %pad_add_fusion.place, bf16[16,2048]{1,0:T(8,128)(2,1)S(1)} %shard_map.95.a, bf16[16,2048]{1,0:T(8,128)(2,1)S(1)} %collective-permute-done.14.b, bf16[16384,128]{1,0:T(8,128)(2,1)} %wo.1, bf16[16,128]{1,0:T(8,128)(2,1)S(1)} %copy-done), custom_call_target="tpu_custom_call" | custom-call | tf_op jit(solution)/shard_map/pallas_call | solution.py:47
  159.0 1.1 shard_map.97
  (31 shorter events, 0.3 us)
Async XLA Ops:
  1.4 5.3 %collective-permute-start = (f32[1,128]{1,0:T(1,128)}, f32[1,128]{1,0:T(1,128)S(1)}, u32[]{:S(2)}, u32[]{:S(2)}) collective-permute-start(f32[1,128]{1,0:T(1,128)} %shard_map.82.a), channel_id=1, source_target_pairs={{0,32},{32,64},{64,96},{96,0},{1,33},{33,65},{65,97},{97,1},{2,34}... | collective-permute-start | bytes 1544 | tf_op jit(solution)/shard_map/ppermute | solution.py:284
  3.5 3.1 %collective-permute-start.1 = (f32[1,128]{1,0:T(1,128)}, f32[1,128]{1,0:T(1,128)S(1)}, u32[]{:S(2)}, u32[]{:S(2)}) collective-permute-start(f32[1,128]{1,0:T(1,128)} %shard_map.82.a), channel_id=1, source_target_pairs={{0,96},{32,0},{64,32},{96,64},{1,97},{33,1},{65,33},{97,65},{2,98}... | collective-permute-start | bytes 1544 | tf_op jit(solution)/shard_map/ppermute | solution.py:284
  5.1 4.1 %collective-permute-start.2 = (f32[1,128]{1,0:T(1,128)}, f32[1,128]{1,0:T(1,128)S(1)}, u32[]{:S(2)}, u32[]{:S(2)}) collective-permute-start(f32[1,128]{1,0:T(1,128)} %shard_map.82.a), channel_id=1, source_target_pairs={{0,64},{32,96},{64,0},{96,32},{1,65},{33,97},{65,1},{97,33},{2,66}... | collective-permute-start | bytes 1544 | tf_op jit(solution)/shard_map/ppermute | solution.py:284
  9.2 0.7 copy-start.2
  10.5 37.5 %all-to-all-start = ((f32[32,1,128]{2,1,0:T(1,128)}), f32[32,1,128]{2,1,0:T(1,128)S(1)}, u32[]{:S(2)}, u32[]{:S(2)}) async-start(f32[32,1,128]{2,1,0:T(1,128)} %bitcast.4), calls=%async_computation | async-start | bytes 32768 | tf_op jit(solution)/shard_map/all_to_all | solution.py:314
  36.5 11.4 %copy-start = (bf16[16,128]{1,0:T(8,128)(2,1)S(1)}, bf16[16,128]{1,0:T(8,128)(2,1)}, u32[]{:S(2)}) copy-start(bf16[16,128]{1,0:T(8,128)(2,1)} %x.5) | copy-start | bytes 12292
  36.5 11.4 %copy-start.4 = (bf16[128]{0:T(256)(128)(2,1)S(1)}, bf16[128]{0:T(256)(128)(2,1)}, u32[]{:S(2)}) copy-start(bf16[128]{0:T(256)(128)(2,1)} %param.9) | copy-start | bytes 772
  48.5 3.6 %collective-permute-start.3 = (f32[4,16,2304]{2,1,0:T(8,128)S(1)}, f32[4,16,2304]{2,1,0:T(8,128)S(1)}, u32[]{:S(2)}, u32[]{:S(2)}) collective-permute-start(f32[4,16,2304]{2,1,0:T(8,128)S(1)} %get-tuple-element.25), channel_id=1, source_target_pairs={{0,1},{1,0},{2,3},{3,2},{4,5},{5,4},{6,7},{7,6},{8,9},{9,8},{10,11... | collective-permute-start | bytes 1769480 | tf_op jit(solution)/shard_map/ppermute | solution.py:288
  52.1 25.7 %copy-start.3 = (s32[16]{0:T(128)S(1)}, s32[16]{0:T(128)}, u32[]{:S(2)}) copy-start(s32[16]{0:T(128)} %lengths.1) | copy-start | bytes 196
  52.1 58.1 %copy-start.1 = (s32[8,16]{1,0:T(8,128)S(1)}, s32[8,16]{1,0:T(8,128)}, u32[]{:S(2)}) copy-start(s32[8,16]{1,0:T(8,128)} %slabs.1) | copy-start | bytes 1540
  52.2 6.7 %collective-permute-start.4 = (f32[16,2304]{1,0:T(8,128)S(1)}, f32[16,2304]{1,0:T(8,128)S(1)}, u32[]{:S(2)}, u32[]{:S(2)}) collective-permute-start(f32[16,2304]{1,0:T(8,128)S(1)} %get-tuple-element.27), channel_id=1, source_target_pairs={{0,32},{32,64},{64,96},{96,0},{1,33},{33,65},{65,97},{97,1},{2,34}... | collective-permute-start | bytes 442376 | tf_op jit(solution)/shard_map/ppermute | solution.py:284
  52.4 8.5 %collective-permute-start.5 = (f32[16,2304]{1,0:T(8,128)S(1)}, f32[16,2304]{1,0:T(8,128)S(1)}, u32[]{:S(2)}, u32[]{:S(2)}) collective-permute-start(f32[16,2304]{1,0:T(8,128)S(1)} %get-tuple-element.28), channel_id=1, source_target_pairs={{0,96},{32,0},{64,32},{96,64},{1,97},{33,1},{65,33},{97,65},{2,98}... | collective-permute-start | bytes 442376 | tf_op jit(solution)/shard_map/ppermute | solution.py:284
  55.0 7.1 %collective-permute-start.6 = (f32[16,2304]{1,0:T(8,128)S(1)}, f32[16,2304]{1,0:T(8,128)S(1)}, u32[]{:S(2)}, u32[]{:S(2)}) collective-permute-start(f32[16,2304]{1,0:T(8,128)S(1)} %get-tuple-element.29), channel_id=1, source_target_pairs={{0,64},{32,96},{64,0},{96,32},{1,65},{33,97},{65,1},{97,33},{2,66}... | collective-permute-start | bytes 442376 | tf_op jit(solution)/shard_map/ppermute | solution.py:284
  62.7 23.3 %all-to-all-start.1 = ((f32[16,1,2304]{2,1,0:T(1,128)}), f32[16,1,2304]{2,1,0:T(1,128)S(1)}, u32[]{:S(2)}, u32[]{:S(2)}) async-start(f32[16,1,2304]{2,1,0:T(1,128)} %bitcast.7), calls=%async_computation.1 | async-start | bytes 294912 | tf_op jit(solution)/shard_map/all_to_all | solution.py:292
  68.5 9.3 %collective-permute-start.10 = (bf16[16,2,32,128]{3,2,1,0:T(8,128)(2,1)S(1)}, bf16[16,2,32,128]{3,2,1,0:T(8,128)(2,1)S(1)}, u32[]{:S(2)}, u32[]{:S(2)}) collective-permute-start(bf16[16,2,32,128]{3,2,1,0:T(8,128)(2,1)S(1)} %get-tuple-element.35), channel_id=1, source_target_pairs={{0,64},{1,65},{32,96},{33,97},{64,0},{65,1},{96,32},{97,33},{2,66}... | collective-permute-start | bytes 786440 | tf_op jit(solution)/shard_map/ppermute | solution.py:382
  68.6 17.0 %collective-permute-start.11 = (bf16[16,2,32,128]{3,2,1,0:T(8,128)(2,1)S(1)}, bf16[16,2,32,128]{3,2,1,0:T(8,128)(2,1)S(1)}, u32[]{:S(2)}, u32[]{:S(2)}) collective-permute-start(bf16[16,2,32,128]{3,2,1,0:T(8,128)(2,1)S(1)} %get-tuple-element.36), channel_id=1, source_target_pairs={{0,33},{1,32},{32,65},{33,64},{64,97},{65,96},{96,1},{97,0},{2,35}... | collective-permute-start | bytes 786440 | tf_op jit(solution)/shard_map/ppermute | solution.py:382
  72.9 37.2 %collective-permute-start.12 = (bf16[16,2,32,128]{3,2,1,0:T(8,128)(2,1)S(1)}, bf16[16,2,32,128]{3,2,1,0:T(8,128)(2,1)S(1)}, u32[]{:S(2)}, u32[]{:S(2)}) collective-permute-start(bf16[16,2,32,128]{3,2,1,0:T(8,128)(2,1)S(1)} %get-tuple-element.37), channel_id=1, source_target_pairs={{0,97},{1,96},{32,1},{33,0},{64,33},{65,32},{96,65},{97,64},{2,99}... | collective-permute-start | bytes 786440 | tf_op jit(solution)/shard_map/ppermute | solution.py:382
  73.1 37.1 %collective-permute-start.13 = (bf16[16,2,32,128]{3,2,1,0:T(8,128)(2,1)S(1)}, bf16[16,2,32,128]{3,2,1,0:T(8,128)(2,1)S(1)}, u32[]{:S(2)}, u32[]{:S(2)}) collective-permute-start(bf16[16,2,32,128]{3,2,1,0:T(8,128)(2,1)S(1)} %get-tuple-element.38), channel_id=1, source_target_pairs={{0,65},{1,64},{32,97},{33,96},{64,1},{65,0},{96,33},{97,32},{2,67}... | collective-permute-start | bytes 786440 | tf_op jit(solution)/shard_map/ppermute | solution.py:382
  77.1 33.1 %collective-permute-start.7 = (bf16[16,2,32,128]{3,2,1,0:T(8,128)(2,1)}, bf16[16,2,32,128]{3,2,1,0:T(8,128)(2,1)S(1)}, u32[]{:S(2)}, u32[]{:S(2)}) collective-permute-start(bf16[16,2,32,128]{3,2,1,0:T(8,128)(2,1)} %get-tuple-element.32), channel_id=1, source_target_pairs={{0,1},{1,0},{32,33},{33,32},{64,65},{65,64},{96,97},{97,96},{2,3},... | collective-permute-start | bytes 786440 | tf_op jit(solution)/shard_map/ppermute | solution.py:382
  77.8 32.4 %collective-permute-start.8 = (bf16[16,2,32,128]{3,2,1,0:T(8,128)(2,1)}, bf16[16,2,32,128]{3,2,1,0:T(8,128)(2,1)S(1)}, u32[]{:S(2)}, u32[]{:S(2)}) collective-permute-start(bf16[16,2,32,128]{3,2,1,0:T(8,128)(2,1)} %get-tuple-element.33), channel_id=1, source_target_pairs={{0,32},{1,33},{32,64},{33,65},{64,96},{65,97},{96,0},{97,1},{2,34}... | collective-permute-start | bytes 786440 | tf_op jit(solution)/shard_map/ppermute | solution.py:382
  85.6 24.6 %collective-permute-start.9 = (bf16[16,2,32,128]{3,2,1,0:T(8,128)(2,1)}, bf16[16,2,32,128]{3,2,1,0:T(8,128)(2,1)S(1)}, u32[]{:S(2)}, u32[]{:S(2)}) collective-permute-start(bf16[16,2,32,128]{3,2,1,0:T(8,128)(2,1)} %get-tuple-element.34), channel_id=1, source_target_pairs={{0,96},{1,97},{32,0},{33,1},{64,32},{65,33},{96,64},{97,65},{2,98}... | collective-permute-start | bytes 786440 | tf_op jit(solution)/shard_map/ppermute | solution.py:382
  145.9 5.9 %collective-permute-start.15 = (bf16[16,2048]{1,0:T(8,128)(2,1)S(1)}, bf16[16,2048]{1,0:T(8,128)(2,1)S(1)}, u32[]{:S(2)}, u32[]{:S(2)}) collective-permute-start(bf16[16,2048]{1,0:T(8,128)(2,1)S(1)} %shard_map.95.a), channel_id=1, source_target_pairs={{0,96},{32,0},{64,32},{96,64},{1,97},{33,1},{65,33},{97,65},{2,98}... | collective-permute-start | bytes 196616 | tf_op jit(solution)/shard_map/ppermute | solution.py:284
  146.0 6.5 %collective-permute-start.16 = (bf16[16,2048]{1,0:T(8,128)(2,1)S(1)}, bf16[16,2048]{1,0:T(8,128)(2,1)S(1)}, u32[]{:S(2)}, u32[]{:S(2)}) collective-permute-start(bf16[16,2048]{1,0:T(8,128)(2,1)S(1)} %shard_map.95.a), channel_id=1, source_target_pairs={{0,32},{32,64},{64,96},{96,0},{1,33},{33,65},{65,97},{97,1},{2,34}... | collective-permute-start | bytes 196616 | tf_op jit(solution)/shard_map/ppermute | solution.py:284
  147.5 6.6 %collective-permute-start.17 = (bf16[16,2048]{1,0:T(8,128)(2,1)S(1)}, bf16[16,2048]{1,0:T(8,128)(2,1)S(1)}, u32[]{:S(2)}, u32[]{:S(2)}) collective-permute-start(bf16[16,2048]{1,0:T(8,128)(2,1)S(1)} %shard_map.95.a), channel_id=1, source_target_pairs={{0,64},{32,96},{64,0},{96,32},{1,65},{33,97},{65,1},{97,33},{2,66}... | collective-permute-start | bytes 196616 | tf_op jit(solution)/shard_map/ppermute | solution.py:284
  148.7 7.4 %collective-permute-start.14 = (bf16[16,2048]{1,0:T(8,128)(2,1)S(1)}, bf16[16,2048]{1,0:T(8,128)(2,1)S(1)}, u32[]{:S(2)}, u32[]{:S(2)}) collective-permute-start(bf16[16,2048]{1,0:T(8,128)(2,1)S(1)} %shard_map.95.a), channel_id=1, source_target_pairs={{0,1},{1,0},{2,3},{3,2},{4,5},{5,4},{6,7},{7,6},{8,9},{9,8},{10,11... | collective-permute-start | bytes 196616 | tf_op jit(solution)/shard_map/ppermute | solution.py:288
  151.8 7.2 %collective-permute-start.18 = (bf16[16,2048]{1,0:T(8,128)(2,1)S(1)}, bf16[16,2048]{1,0:T(8,128)(2,1)S(1)}, u32[]{:S(2)}, u32[]{:S(2)}) collective-permute-start(bf16[16,2048]{1,0:T(8,128)(2,1)S(1)} %collective-permute-done.15.refs_1_), channel_id=1, source_target_pairs={{0,1},{1,0},{2,3},{3,2},{4,5},{5,4},{6,7},{7,6},{8,9},{9,8},{10,11... | collective-permute-start | bytes 196616 | tf_op jit(solution)/shard_map/ppermute | solution.py:288
  152.6 6.4 %collective-permute-start.19 = (bf16[16,2048]{1,0:T(8,128)(2,1)S(1)}, bf16[16,2048]{1,0:T(8,128)(2,1)S(1)}, u32[]{:S(2)}, u32[]{:S(2)}) collective-permute-start(bf16[16,2048]{1,0:T(8,128)(2,1)S(1)} %collective-permute-done.16.refs_2_), channel_id=1, source_target_pairs={{0,1},{1,0},{2,3},{3,2},{4,5},{5,4},{6,7},{7,6},{8,9},{9,8},{10,11... | collective-permute-start | bytes 196616 | tf_op jit(solution)/shard_map/ppermute | solution.py:288
  154.1 4.9 %collective-permute-start.20 = (bf16[16,2048]{1,0:T(8,128)(2,1)S(1)}, bf16[16,2048]{1,0:T(8,128)(2,1)S(1)}, u32[]{:S(2)}, u32[]{:S(2)}) collective-permute-start(bf16[16,2048]{1,0:T(8,128)(2,1)S(1)} %collective-permute-done.17.refs_3_), channel_id=1, source_target_pairs={{0,1},{1,0},{2,3},{3,2},{4,5},{5,4},{6,7},{7,6},{8,9},{9,8},{10,11... | collective-permute-start | bytes 196616 | tf_op jit(solution)/shard_map/ppermute | solution.py:288

commit v9 on v8

--- a/solution.py
+++ b/solution.py
@@ -19,10 +19,11 @@
 TENSOR = ("x", "z", "c")
 FIRST = ((0, 1), (1, 1), (2, 1), (3, 1))
 REST = ((0, 0), (1, 0), (2, 0), (3, 0))
-NEAR = ((0, 0), (0, 1))
+NEAR = ((0, 0),)
+LAST = ((0, 1),)
 FAR = ((1, 0), (3, 0), (2, 0), (1, 1), (3, 1), (2, 1))
-MOVES = ((0, 0), (0, 1), (1, 0), (3, 0), (2, 0), (1, 1), (3, 1), (2, 1))
-EARLY = 4
+MOVES = ((1, 0), (3, 0), (2, 0), (1, 1), (3, 1), (2, 1), (0, 1), (0, 0))
+EARLY = 2
 
 EPS = 1e-05
 ROPE_BASE = 500000.0
@@ -41,16 +42,16 @@
     return jax.ShapeDtypeStruct(shape, dtype)
 
 
-def call(kernel, out, specs, *args, scratch=(), params=LIMIT):
-    is_out = lambda v: not isinstance(v, (list, tuple))
-    outs = jax.tree.map(lambda v: VMEM if isinstance(v, jax.ShapeDtypeStruct) else HBM, out, is_leaf=is_out)
+def call(kernel, out, specs, *args, scratch=()):
+    one = lambda v: HBM if getattr(v, "memory_space", None) == pltpu.HBM else VMEM
+    outs = [one(v) for v in out] if isinstance(out, list) else one(out)
     return pl.pallas_call(
         kernel,
         in_specs=specs,
         out_specs=outs,
         out_shape=out,
         scratch_shapes=scratch,
-        compiler_params=params,
+        compiler_params=LIMIT,
     )(*args)
 
 
@@ -77,15 +78,15 @@
     out[...] = jnp.broadcast_to((a[...] + b[...]) + (c[...] + d[...]), out.shape)
 
 
-def head_of(place, j, d):
-    core = 1 - place[2] if d else place[2]
-    return lax.rem(place[0] + j, NX) * NC + core
-
-
-def in_copies(place, moves, wq, wkv, out, sems):
+def head_of(j, d):
+    my_x, my_c = lax.axis_index("x"), lax.axis_index("c")
+    return lax.rem(my_x + j, NX) * NC + (1 - my_c if d else my_c)
+
+
+def in_copies(moves, wq, wkv, out, sems):
     copies = []
     for k, (j, d) in enumerate(moves):
-        head = head_of(place, j, d)
+        head = head_of(j, d)
         for part, (source, start, width, at) in enumerate(
             (
                 (wq, head * QW, QW, 0),
@@ -103,10 +104,10 @@
     return copies
 
 
-def out_copies(place, moves, wo, out, sems):
+def out_copies(moves, wo, out, sems):
     return [
         pltpu.make_async_copy(
-            wo.at[pl.ds(pl.multiple_of(head_of(place, j, d) * QW, HD), QW)],
+            wo.at[pl.ds(pl.multiple_of(head_of(j, d) * QW, HD), QW)],
             out.at[k],
             sems.at[k],
         )
@@ -121,16 +122,16 @@
         copy.wait()
 
 
-def fetch_in_kernel(place, wq, wkv, out, sems):
-    run_all(in_copies(place, FIRST, wq, wkv, out, sems))
-
-
-def fetch_cache_kernel(moves, staged, place, cache, *refs):
+def fetch_in_kernel(wq, wkv, out, sems):
+    run_all(in_copies(FIRST, wq, wkv, out, sems))
+
+
+def fetch_cache_kernel(moves, staged, cache, *refs):
     outs, held, sems, out_sems = refs[:-3], *refs[-3:]
     first, second = [], []
     for k, (j, d) in enumerate(moves):
         to = held.at[k] if k in staged else outs[k]
-        first.append(pltpu.make_async_copy(cache.at[head_of(place, j, d)], to, sems.at[k]))
+        first.append(pltpu.make_async_copy(cache.at[head_of(j, d)], to, sems.at[k]))
         first[k].start()
     for k in range(len(moves)):
         first[k].wait()
@@ -150,8 +151,8 @@
         out[k] = jnp.dot(normed, w[k], preferred_element_type=F32)
 
 
-def project_kernel(place, normed, wq, wkv, out, w, sems):
-    copies = in_copies(place, REST, wq, wkv, w, sems)
+def project_kernel(normed, wq, wkv, out, w, sems):
+    copies = in_copies(REST, wq, wkv, w, sems)
     for copy in copies:
         copy.start()
     for k in range(NX):
@@ -173,14 +174,13 @@
         out[pl.ds(k, n, stride=ROWS), :] = total
 
 
-def queries_kernel(place, parts, cosine, sine, q_out, new_score, new_value):
+def queries_kernel(parts, cosine, sine, q_out, new_score, new_value):
     n = parts.shape[0] // ROWS
     total = parts[:ROWS]
     for k in range(1, n):
         total = total + parts[k * ROWS : (k + 1) * ROWS]
     lead = total[: GROUP + 1]
-    mine = pl.ds(place[1], 1)
-    turned = lead * cosine[mine] + pltpu.roll(lead, HD // 2, 1) * sine[mine]
+    turned = lead * cosine[...] + pltpu.roll(lead, HD // 2, 1) * sine[...]
     turned = turned.astype(BF16)
     q = turned[:GROUP]
     q_out[...] = jnp.broadcast_to(q[None], q_out.shape)
@@ -190,22 +190,22 @@
     new_value[...] = total[GROUP + 1 :].astype(BF16).astype(F32)
 
 
-def visible_kernel(local, place, lengths, q, out):
-    del q
-    index = lax.broadcasted_iota(jnp.int32, (1, out.shape[1]), 1)
+def hold_kernel(q, out):
+    out[...] = q[...]
+
+
+def attend_kernel(lengths, slabs, q, *refs):
+    caches, out, scores, weights = refs[: len(MOVES)], *refs[len(MOVES) :]
+    n = q.shape[0]
+    local = caches[0].shape[2]
+    my_x, my_z, my_c = (lax.axis_index(a) for a in TENSOR)
+    head = my_x * NC + my_c
+    index = lax.broadcasted_iota(jnp.int32, (1, len(MOVES) * local), 1)
     position = index % local
     for k, (j, d) in enumerate(MOVES):
-        core = 1 - place[2] if d else place[2]
-        block = (lax.rem(place[0] + (NX - j), NX) * NZ + place[1]) * NC + core
+        core = 1 - my_c if d else my_c
+        block = (lax.rem(my_x + (NX - j), NX) * NZ + my_z) * NC + core
         position = jnp.where(index // local == k, position + block * local, position)
-    for b in range(out.shape[0]):
-        out[b : b + 1] = (position < lengths[b]).astype(F32)
-
-
-def attend_kernel(place, slabs, seen, q, *refs):
-    caches, out, scores, weights = refs[: len(MOVES)], *refs[len(MOVES) :]
-    n = q.shape[0]
-    head = place[0] * NC + place[2]
     mask = diagonal(GROUP)
     for b in range(n):
         slab = slabs[head, b]
@@ -215,7 +215,7 @@
         )
     for b in range(n):
         rows = slice(b * GROUP, (b + 1) * GROUP)
-        visible = seen[b : b + 1] > 0
+        visible = position < lengths[b]
         score = jnp.where(visible, scores[rows], NEG)
         top = jnp.max(score, axis=1, keepdims=True)
         weight = jnp.where(visible, jnp.exp(score - top), 0.0)
@@ -257,26 +257,27 @@
         out[:, k * HD : (k + 1) * HD] = wide[:, k, :].astype(BF16)
 
 
-def output_near_kernel(place, a, b, wo, x, out, w_far, w, sems, far_sems):
-    near = out_copies(place, NEAR, wo, w, sems)
-    far = out_copies(place, FAR, wo, w_far, far_sems)
+def output_near_kernel(rows, wo, x, out, w_far, w, sem, far_sems):
+    near = out_copies(NEAR, wo, w, sem)
+    far = out_copies(FAR, wo, w_far, far_sems)
     for copy in near + far:
         copy.start()
     for copy in near:
         copy.wait()
-    total = x[...].astype(F32)
-    for k, rows in enumerate((a, b)):
-        total = total + jnp.dot(rows[...], w[k], preferred_element_type=F32)
-    out[...] = total
+    out[...] = x[...].astype(F32) + jnp.dot(rows[...], w[0], preferred_element_type=F32)
     for copy in far:
         copy.wait()
 
 
-def output_far_kernel(*refs):
-    near, *rows, w, out = refs
+def output_far_kernel(near, *refs):
+    rows, (last, w_far, wo, out, w, sem) = refs[: len(FAR)], refs[len(FAR) :]
+    copies = out_copies(LAST, wo, w, sem)
+    copies[0].start()
     total = near[...]
     for k, block in enumerate(rows):
-        total = total + jnp.dot(block[...], w[k], preferred_element_type=F32)
+        total = total + jnp.dot(block[...], w_far[k], preferred_element_type=F32)
+    copies[0].wait()
+    total = total + jnp.dot(last[...], w[0], preferred_element_type=F32)
     out[...] = total.astype(BF16)
 
 
@@ -297,16 +298,17 @@
     w_q, w_kv, w_o, kv_cache = (
         pltpu.with_memory_space_constraint(v, pltpu.HBM) for v in (w_q, w_kv, w_o, kv_cache)
     )
-    place = jnp.stack([lax.axis_index(a) for a in TENSOR]).astype(jnp.int32)
 
     lane = jnp.arange(HD, dtype=jnp.int32)[None]
     frequency = ROPE_BASE ** (-2.0 * (lane % (HD // 2)).astype(F32) / HD)
     angles = lengths.astype(F32)[:, None] * frequency
-    cosine = jnp.cos(angles)
-    sine = jnp.sin(angles) * jnp.where(lane < HD // 2, -1.0, 1.0)
+    mine = jnp.arange(n, dtype=jnp.int32)[:, None] == lax.axis_index("z")
+    chosen = lambda table: jnp.sum(jnp.where(mine, table, 0.0), axis=0, keepdims=True)
+    cosine = chosen(jnp.cos(angles))
+    sine = chosen(jnp.sin(angles) * jnp.where(lane < HD // 2, -1.0, 1.0))
 
     line = struct((1, HD), F32)
-    own = call(squares_kernel, line, [VMEM], hidden_in, params=None)
+    own = call(squares_kernel, line, [VMEM], hidden_in)
     lines = [own]
     for k in (1, 3, 2):
         lines.append(shift_x(own, k))
@@ -319,15 +321,14 @@
     held = call(
         fetch_in_kernel,
         struct((len(FIRST), depth, PW), BF16),
-        [SMEM, HBM, HBM],
-        place,
+        [HBM, HBM],
         w_q,
         w_kv,
         scratch=[dmas(FIRST)],
     )
 
     cache = []
-    for moves, staged in ((MOVES[:EARLY], range(1, EARLY)), (MOVES[EARLY:], ())):
+    for moves, staged in ((MOVES[:EARLY], range(EARLY)), (MOVES[EARLY:], ())):
         block = kv_cache.shape[1:]
         cache += call(
             functools.partial(fetch_cache_kernel, moves, staged),
@@ -335,8 +336,7 @@
                 pltpu.HBM(block, BF16) if k in staged else struct(block, BF16)
                 for k in range(len(moves))
             ],
-            [SMEM, HBM],
-            place,
+            [HBM],
             kv_cache,
             scratch=[
                 pltpu.VMEM((len(moves),) + block, BF16),
@@ -350,7 +350,7 @@
     product = struct((NX, n, PW), F32)
     normed, sent = call(
         project_first_kernel,
-        [struct((n, depth), BF16), product],
+        [struct((n, depth), BF16), pltpu.VMEM((NX, n, PW), F32)],
         [VMEM] * 4,
         sums,
         hidden_in,
@@ -361,8 +361,7 @@
     kept = call(
         project_kernel,
         product,
-        [SMEM, VMEM, HBM, HBM],
-        place,
+        [VMEM, HBM, HBM],
         normed,
         w_q,
         w_kv,
@@ -373,7 +372,7 @@
     for k in (1, 3, 2):
         parts.append(shift_x(blocks[k], k))
     rows = call(x_sum_kernel, struct((n * ROWS, HD), F32), [VMEM] * NX, *parts)
-    for k, (j, d) in enumerate(MOVES[1:], 1):
+    for k, (j, d) in enumerate(MOVES[:-1]):
         pairs = [
             (x * NC + c, (x + j) % NX * NC + (c + d) % NC)
             for x in range(NX)
@@ -384,29 +383,20 @@
     q, new_score, new_value = call(
         queries_kernel,
         [struct((n, GROUP, HD), BF16), struct((1, HD), F32), struct((1, HD), F32)],
-        [SMEM] + [VMEM] * 3,
-        place,
+        [VMEM] * 3,
         rows,
         cosine,
         sine,
     )
     q = across_z(q)
 
-    visible = call(
-        functools.partial(visible_kernel, local),
-        struct((n, seen), F32),
-        [SMEM, SMEM, VMEM],
-        place,
-        lengths,
-        q,
-    )
+    q = call(hold_kernel, struct(q.shape, BF16), [VMEM], q)
     partial = call(
         attend_kernel,
         struct((n * ROWS, HD), F32),
-        [SMEM, SMEM] + [VMEM] * (2 + len(MOVES)),
-        place,
+        [SMEM, SMEM] + [VMEM] * (1 + len(MOVES)),
+        lengths,
         slab_index,
-        visible,
         q,
         *cache,
         scratch=[pltpu.VMEM((n * GROUP, seen), F32), pltpu.VMEM((n * GROUP, seen), BF16)],
@@ -428,27 +418,27 @@
         rows[k, 0] = shift_x(done, -k)
     for k in (0, 1, 3, 2):
         rows[k, 1] = swap_c(rows[k, 0])
+    block = (QW, w_o.shape[1])
+    read = [pltpu.VMEM((1,) + block, BF16), pltpu.SemaphoreType.DMA((1,))]
     total, w_far = call(
         output_near_kernel,
-        [struct((n, depth), F32), struct((len(FAR), QW, w_o.shape[1]), BF16)],
-        [SMEM, VMEM, VMEM, HBM, VMEM],
-        place,
-        *(rows[move] for move in NEAR),
+        [struct((n, depth), F32), struct((len(FAR),) + block, BF16)],
+        [VMEM, HBM, VMEM],
+        rows[0, 0],
         w_o,
         hidden_in,
-        scratch=[
-            pltpu.VMEM((len(NEAR), QW, w_o.shape[1]), BF16),
-            pltpu.SemaphoreType.DMA((len(NEAR),)),
-            pltpu.SemaphoreType.DMA((len(FAR),)),
-        ],
+        scratch=read + [pltpu.SemaphoreType.DMA((len(FAR),))],
     )
     return call(
         output_far_kernel,
         struct((n, depth), BF16),
-        [VMEM] * (2 + len(FAR)),
+        [VMEM] * (3 + len(FAR)) + [HBM],
         total,
         *(rows[move] for move in FAR),
+        rows[0, 1],
         w_far,
+        w_o,
+        scratch=read,
     )
 
 

time: 161 us -> 165 us (1.025)
  waiting for transfers between devices: 25.6 us -> 30.2 us
  Pallas kernels: 19.1 us -> 14.9 us
  starting transfers between devices: 57.4 us -> 61.1 us
    pallas_call x16, Pallas kernels: 19.1 us -> 14.9 us  [call(): pl.pallas_call(kernel, in_specs=specs, out_specs=outs, out_shape=out, scr...]
    ppermute x7, waiting for transfers between devices: 7.37 us -> 11.5 us  [step(): cache[k] = lax.ppermute(cache[k], ('x', 'c'), pairs)]
    ppermute x7, starting transfers between devices: 7.51 us -> 11 us  [step(): cache[k] = lax.ppermute(cache[k], ('x', 'c'), pairs)]
  transfers between devices with their start and end apart: 23 -> 23, of which waited for: 6 -> 7; matrix products, arithmetic and copies ran while one was open for 0% -> 0% of each run, Pallas kernels for 8% -> 6%
where the time goes in v9:
time: 165 us; the launch traced here: 164 us
  starting transfers between devices  61.1 us (37%)
  blocking collectives  56.8 us (34%)
  waiting for transfers between devices  30.2 us (18%)
  Pallas kernels  14.9 us (9%)
    all_to_all x3, blocking collectives, across_z(): return lax.all_to_all(value, 'z', 0, 0, tiled=True)  56.8 us
    all_to_all x1, starting transfers between devices, step(): lax.all_to_all(sums.reshape(NZ * NC, 1, HD), ('z', 'c'), 0, 0, tiled=True)  26.1 us
    pallas_call x16, Pallas kernels, call(): pl.pallas_call(kernel, in_specs=specs, out_specs=outs, out_shape=out, scr...  14.9 us
    ppermute x7, waiting for transfers between devices, step(): cache[k] = lax.ppermute(cache[k], ('x', 'c'), pairs)  11.5 us
    ppermute x7, starting transfers between devices, step(): cache[k] = lax.ppermute(cache[k], ('x', 'c'), pairs)  11 us
    ppermute x9, starting transfers between devices, shift_x(): return lax.ppermute(value, 'x', [(i, (i + by) % NX) for i in range(NX)])  10.3 us
    all_to_all x1, waiting for transfers between devices, step(): lax.all_to_all(sums.reshape(NZ * NC, 1, HD), ('z', 'c'), 0, 0, tiled=True)  9.83 us
    ppermute x5, starting transfers between devices, swap_c(): return lax.ppermute(value, 'c', [(0, 1), (1, 0)])  9.7 us
  transfers between devices with their start and end apart: 23, of which 7 were waited for; matrix products, arithmetic and copies ran while one was open for 0% of the time, Pallas kernels for 6%

profile of v9, /device:TPU:33, one launch (start us, length us, event | category | flops | bytes accessed | tf_op | source)
XLA Modules:
  0.0 164.2 jit_solution(13454743196594286455)
XLA Ops:
  0.0 0.7 copy-done
  0.7 0.1 shard_map.82.a
  0.8 2.2 %collective-permute-start = (f32[1,128]{1,0:T(1,128)S(1)}, f32[1,128]{1,0:T(1,128)S(1)}, u32[]{:S(2)}, u32[]{:S(2)}) collective-permute-start(f32[1,128]{1,0:T(1,128)S(1)} %shard_map.82.a), channel_id=1, source_target_pairs={{0,32},{32,64},{64,96},{96,0},{1,33},{33,65},{65,97},{97,1},{2,34}... | collective-permute-start | bytes 1544 | tf_op jit(solution)/shard_map/ppermute | solution.py:285
  3.0 1.7 %collective-permute-start.1 = (f32[1,128]{1,0:T(1,128)S(1)}, f32[1,128]{1,0:T(1,128)S(1)}, u32[]{:S(2)}, u32[]{:S(2)}) collective-permute-start(f32[1,128]{1,0:T(1,128)S(1)} %shard_map.82.a), channel_id=1, source_target_pairs={{0,96},{32,0},{64,32},{96,64},{1,97},{33,1},{65,33},{97,65},{2,98}... | collective-permute-start | bytes 1544 | tf_op jit(solution)/shard_map/ppermute | solution.py:285
  4.7 1.5 collective-permute-start.2
  6.1 2.5 %collective-permute-done.2.d = f32[1,128]{1,0:T(1,128)S(1)} collective-permute-done((f32[1,128]{1,0:T(1,128)S(1)}, f32[1,128]{1,0:T(1,128)S(1)}, u32[]{:S(2)}, u32[]{:S(2)}) %collective-permute-start.2) | collective-permute-done | bytes 544 | tf_op jit(solution)/shard_map/ppermute | solution.py:285
  8.6 0.6 shard_map.83
  9.2 26.1 %all-to-all-start = ((f32[32,1,128]{2,1,0:T(1,128)}), f32[32,1,128]{2,1,0:T(1,128)S(1)}, u32[]{:S(2)}, u32[]{:S(2)}) async-start(f32[32,1,128]{2,1,0:T(1,128)} %bitcast.1), calls=%async_computation | async-start | bytes 32768 | tf_op jit(solution)/shard_map/all_to_all | solution.py:316
  35.3 1.7 %shard_map.84.w = bf16[4,128,2304]{2,1,0:T(8,128)(2,1)S(1)} custom-call(bf16[128,16384]{1,0:T(8,128)(2,1)} %wq.3, bf16[128,2048]{1,0:T(8,128)(2,1)} %wkv.3), custom_call_target="tpu_custom_call" | custom-call | tf_op jit(solution)/shard_map/pallas_call | solution.py:48
  37.0 9.8 %all-to-all-done = f32[32,1,128]{2,1,0:T(1,128)S(1)} async-done(((f32[32,1,128]{2,1,0:T(1,128)}), f32[32,1,128]{2,1,0:T(1,128)S(1)}, u32[]{:S(2)}, u32[]{:S(2)}) %all-to-all-start) | async-done | bytes 16416 | tf_op jit(solution)/shard_map/all_to_all | solution.py:316
  46.9 0.5 shard_map.85
  47.4 1.0 collective-permute-start.3
  48.4 2.0 %shard_map.86.a = f32[4,16,2304]{2,1,0:T(8,128)S(1)} custom-call(bf16[16,128]{1,0:T(8,128)(2,1)S(1)} %get-tuple-element.24.normed, bf16[128,16384]{1,0:T(8,128)(2,1)} %wq.3, bf16[128,2048]{1,0:T(8,128)(2,1)} %wkv.3), custom_call_target="tpu_custom_call" | custom-call | tf_op jit(solution)/shard_map/pallas_call | solution.py:48
  50.4 0.1 shard_map.87
  50.4 0.2 collective-permute-start.4
  50.6 2.6 %collective-permute-start.5 = (f32[16,2304]{1,0:T(8,128)S(1)}, f32[16,2304]{1,0:T(8,128)S(1)}, u32[]{:S(2)}, u32[]{:S(2)}) collective-permute-start(f32[16,2304]{1,0:T(8,128)S(1)} %get-tuple-element.28), channel_id=1, source_target_pairs={{0,96},{32,0},{64,32},{96,64},{1,97},{33,1},{65,33},{97,65},{2,98}... | collective-permute-start | bytes 442376 | tf_op jit(solution)/shard_map/ppermute | solution.py:285
  53.2 0.5 collective-permute-start.6
  53.8 3.4 %collective-permute-done.4.b = f32[16,2304]{1,0:T(8,128)S(1)} collective-permute-done((f32[16,2304]{1,0:T(8,128)S(1)}, f32[16,2304]{1,0:T(8,128)S(1)}, u32[]{:S(2)}, u32[]{:S(2)}) %collective-permute-start.4) | collective-permute-done | bytes 147488 | tf_op jit(solution)/shard_map/ppermute | solution.py:285
  57.1 2.0 %collective-permute-done.5.c = f32[16,2304]{1,0:T(8,128)S(1)} collective-permute-done((f32[16,2304]{1,0:T(8,128)S(1)}, f32[16,2304]{1,0:T(8,128)S(1)}, u32[]{:S(2)}, u32[]{:S(2)}) %collective-permute-start.5) | collective-permute-done | bytes 147488 | tf_op jit(solution)/shard_map/ppermute | solution.py:285
  59.1 1.0 collective-permute-done.6.d
  60.1 0.7 shard_map.88
  60.8 4.0 %all-to-all-start.1 = ((f32[16,1,2304]{2,1,0:T(1,128)}), f32[16,1,2304]{2,1,0:T(1,128)S(1)}, u32[]{:S(2)}, u32[]{:S(2)}) async-start(f32[16,1,2304]{2,1,0:T(1,128)} %bitcast.4), calls=%async_computation.1 | async-start | bytes 294912 | tf_op jit(solution)/shard_map/all_to_all | solution.py:293
  64.8 1.5 shard_map.92
  66.3 2.0 %collective-permute-start.10 = (bf16[16,2,32,128]{3,2,1,0:T(8,128)(2,1)S(1)}, bf16[16,2,32,128]{3,2,1,0:T(8,128)(2,1)S(1)}, u32[]{:S(2)}, u32[]{:S(2)}) collective-permute-start(bf16[16,2,32,128]{3,2,1,0:T(8,128)(2,1)S(1)} %get-tuple-element.34), channel_id=1, source_target_pairs={{0,33},{1,32},{32,65},{33,64},{64,97},{65,96},{96,1},{97,0},{2,35}... | collective-permute-start | bytes 786440 | tf_op jit(solution)/shard_map/ppermute | solution.py:381
  68.3 1.8 %collective-permute-start.11 = (bf16[16,2,32,128]{3,2,1,0:T(8,128)(2,1)S(1)}, bf16[16,2,32,128]{3,2,1,0:T(8,128)(2,1)S(1)}, u32[]{:S(2)}, u32[]{:S(2)}) collective-permute-start(bf16[16,2,32,128]{3,2,1,0:T(8,128)(2,1)S(1)} %get-tuple-element.35), channel_id=1, source_target_pairs={{0,97},{1,96},{32,1},{33,0},{64,33},{65,32},{96,65},{97,64},{2,99}... | collective-permute-start | bytes 786440 | tf_op jit(solution)/shard_map/ppermute | solution.py:381
  70.1 0.3 collective-permute-start.12
  70.4 1.2 collective-permute-start.13
  71.6 1.9 %collective-permute-start.9 = (bf16[16,2,32,128]{3,2,1,0:T(8,128)(2,1)S(1)}, bf16[16,2,32,128]{3,2,1,0:T(8,128)(2,1)S(1)}, u32[]{:S(2)}, u32[]{:S(2)}) collective-permute-start(bf16[16,2,32,128]{3,2,1,0:T(8,128)(2,1)S(1)} %get-tuple-element.33), channel_id=1, source_target_pairs={{0,64},{1,65},{32,96},{33,97},{64,0},{65,1},{96,32},{97,33},{2,66}... | collective-permute-start | bytes 786440 | tf_op jit(solution)/shard_map/ppermute | solution.py:381
  73.5 1.8 %shard_map.91 = (bf16[16,2,32,128]{3,2,1,0:T(8,128)(2,1)}, bf16[16,2,32,128]{3,2,1,0:T(8,128)(2,1)}) custom-call(bf16[8,16,2,32,128]{4,3,2,1,0:T(8,128)(2,1)} %cache.3), custom_call_target="tpu_custom_call" | custom-call | tf_op jit(solution)/shard_map/pallas_call | solution.py:48
  75.3 1.6 collective-permute-done.10.refs_3_
  77.0 9.8 %collective-permute-done.11.refs_4_ = bf16[16,2,32,128]{3,2,1,0:T(8,128)(2,1)S(1)} collective-permute-done((bf16[16,2,32,128]{3,2,1,0:T(8,128)(2,1)S(1)}, bf16[16,2,32,128]{3,2,1,0:T(8,128)(2,1)S(1)}, u32[]{:S(2)}, u32[]{:S(2)}) %collective-permute-start.11) | collective-permute-done | bytes 262176 | tf_op jit(solution)/shard_map/ppermute | solution.py:381
  86.8 3.8 %collective-permute-start.8 = (bf16[16,2,32,128]{3,2,1,0:T(8,128)(2,1)}, bf16[16,2,32,128]{3,2,1,0:T(8,128)(2,1)S(1)}, u32[]{:S(2)}, u32[]{:S(2)}) collective-permute-start(bf16[16,2,32,128]{3,2,1,0:T(8,128)(2,1)} %get-tuple-element.32), channel_id=1, source_target_pairs={{0,96},{1,97},{32,0},{33,1},{64,32},{65,33},{96,64},{97,65},{2,98}... | collective-permute-start | bytes 786440 | tf_op jit(solution)/shard_map/ppermute | solution.py:381
  90.6 0.1 fusion.4
  90.7 0.2 shard_map.89
  90.9 22.7 %all_to_all.25.q = bf16[16,16,128]{2,1,0:T(8,128)(2,1)S(1)} all-to-all(bf16[16,16,128]{2,1,0:T(8,128)(2,1)S(1)} %get-tuple-element.30), channel_id=1, replica_groups=mesh['groups'=2,'x'=4,'z'=16,'c'=2] {'z'}, dimensions={0} | all-to-all | bytes 131072 | tf_op jit(solution)/shard_map/all_to_all | solution.py:293
  113.7 1.2 shard_map.93
  114.9 15.8 %all_to_all.26 = f32[16,1,2304]{2,1,0:T(1,128)S(1)} all-to-all(f32[16,1,2304]{2,1,0:T(1,128)S(1)} %bitcast.11), channel_id=1, replica_groups=mesh['groups'=2,'x'=4,'z'=16,'c'=2] {'z'}, dimensions={0} | all-to-all | bytes 294912 | tf_op jit(solution)/shard_map/all_to_all | solution.py:293
  130.7 0.1 shard_map.94
  130.9 18.3 %all_to_all.27.heads = bf16[16,16,128]{2,1,0:T(8,128)(2,1)S(1)} all-to-all(bf16[16,16,128]{2,1,0:T(8,128)(2,1)S(1)} %shard_map.94), channel_id=1, replica_groups=mesh['groups'=2,'x'=4,'z'=16,'c'=2] {'z'}, dimensions={0} | all-to-all | bytes 131072 | tf_op jit(solution)/shard_map/all_to_all | solution.py:293
  149.1 0.1 shard_map.95.rows
  149.3 0.3 collective-permute-start.14
  149.6 1.3 collective-permute-start.15
  150.9 3.0 %collective-permute-start.20 = (bf16[16,2048]{1,0:T(8,128)(2,1)S(1)}, bf16[16,2048]{1,0:T(8,128)(2,1)S(1)}, u32[]{:S(2)}, u32[]{:S(2)}) collective-permute-start(bf16[16,2048]{1,0:T(8,128)(2,1)S(1)} %shard_map.95.rows), channel_id=1, source_target_pairs={{0,1},{1,0},{2,3},{3,2},{4,5},{5,4},{6,7},{7,6},{8,9},{9,8},{10,11... | collective-permute-start | bytes 196616 | tf_op jit(solution)/shard_map/ppermute | solution.py:289
  153.9 2.2 %collective-permute-start.17 = (bf16[16,2048]{1,0:T(8,128)(2,1)S(1)}, bf16[16,2048]{1,0:T(8,128)(2,1)S(1)}, u32[]{:S(2)}, u32[]{:S(2)}) collective-permute-start(bf16[16,2048]{1,0:T(8,128)(2,1)S(1)} %collective-permute-done.14.refs_0_), channel_id=1, source_target_pairs={{0,1},{1,0},{2,3},{3,2},{4,5},{5,4},{6,7},{7,6},{8,9},{9,8},{10,11... | collective-permute-start | bytes 196616 | tf_op jit(solution)/shard_map/ppermute | solution.py:289
  156.1 1.5 collective-permute-start.18
  157.6 2.0 %collective-permute-start.19 = (bf16[16,2048]{1,0:T(8,128)(2,1)S(1)}, bf16[16,2048]{1,0:T(8,128)(2,1)S(1)}, u32[]{:S(2)}, u32[]{:S(2)}) collective-permute-start(bf16[16,2048]{1,0:T(8,128)(2,1)S(1)} %collective-permute-done.16.refs_2_), channel_id=1, source_target_pairs={{0,1},{1,0},{2,3},{3,2},{4,5},{5,4},{6,7},{7,6},{8,9},{9,8},{10,11... | collective-permute-start | bytes 196616 | tf_op jit(solution)/shard_map/ppermute | solution.py:289
  159.6 2.1 %shard_map.96 = (f32[16,128]{1,0:T(8,128)S(1)}, bf16[6,2048,128]{2,1,0:T(8,128)(2,1)S(1)}) custom-call(bf16[16,2048]{1,0:T(8,128)(2,1)S(1)} %shard_map.95.rows, bf16[16384,128]{1,0:T(8,128)(2,1)} %refs_8_.1, bf16[16,128]{1,0:T(8,128)(2,1)S(1)} %copy-done.1), custom_call_target="tpu_custom_call" | custom-call | tf_op jit(solution)/shard_map/pallas_call | solution.py:48
  161.8 2.3 %shard_map.97 = bf16[16,128]{1,0:T(8,128)(2,1)} custom-call(f32[16,128]{1,0:T(8,128)S(1)} %get-tuple-element.41.near, bf16[16,2048]{1,0:T(8,128)(2,1)S(1)} %collective-permute-done.14.refs_0_, bf16[16,2048]{1,0:T(8,128)(2,1)S(1)} %collective-permute-done.15.refs_1_, bf16[16,2048]{1,0:T(8,128)(2,1)S(1)} %collective-permute-done.16.refs_2_, ...), custom_call_target="tpu_custom_call" | custom-call | tf_op jit(solution)/shard_map/pallas_call | solution.py:48
  (31 shorter events, 0.1 us)
Async XLA Ops:
  0.0 0.7 copy-start
  0.8 5.3 %collective-permute-start = (f32[1,128]{1,0:T(1,128)S(1)}, f32[1,128]{1,0:T(1,128)S(1)}, u32[]{:S(2)}, u32[]{:S(2)}) collective-permute-start(f32[1,128]{1,0:T(1,128)S(1)} %shard_map.82.a), channel_id=1, source_target_pairs={{0,32},{32,64},{64,96},{96,0},{1,33},{33,65},{65,97},{97,1},{2,34}... | collective-permute-start | bytes 1544 | tf_op jit(solution)/shard_map/ppermute | solution.py:285
  3.0 3.1 %collective-permute-start.1 = (f32[1,128]{1,0:T(1,128)S(1)}, f32[1,128]{1,0:T(1,128)S(1)}, u32[]{:S(2)}, u32[]{:S(2)}) collective-permute-start(f32[1,128]{1,0:T(1,128)S(1)} %shard_map.82.a), channel_id=1, source_target_pairs={{0,96},{32,0},{64,32},{96,64},{1,97},{33,1},{65,33},{97,65},{2,98}... | collective-permute-start | bytes 1544 | tf_op jit(solution)/shard_map/ppermute | solution.py:285
  4.7 3.9 %collective-permute-start.2 = (f32[1,128]{1,0:T(1,128)S(1)}, f32[1,128]{1,0:T(1,128)S(1)}, u32[]{:S(2)}, u32[]{:S(2)}) collective-permute-start(f32[1,128]{1,0:T(1,128)S(1)} %shard_map.82.a), channel_id=1, source_target_pairs={{0,64},{32,96},{64,0},{96,32},{1,65},{33,97},{65,1},{97,33},{2,66}... | collective-permute-start | bytes 1544 | tf_op jit(solution)/shard_map/ppermute | solution.py:285
  9.2 37.7 %all-to-all-start = ((f32[32,1,128]{2,1,0:T(1,128)}), f32[32,1,128]{2,1,0:T(1,128)S(1)}, u32[]{:S(2)}, u32[]{:S(2)}) async-start(f32[32,1,128]{2,1,0:T(1,128)} %bitcast.1), calls=%async_computation | async-start | bytes 32768 | tf_op jit(solution)/shard_map/all_to_all | solution.py:316
  35.3 11.6 %copy-start.1 = (bf16[16,128]{1,0:T(8,128)(2,1)S(1)}, bf16[16,128]{1,0:T(8,128)(2,1)}, u32[]{:S(2)}) copy-start(bf16[16,128]{1,0:T(8,128)(2,1)} %x.5) | copy-start | bytes 12292
  35.3 11.6 %copy-start.4 = (bf16[128]{0:T(256)(128)(2,1)S(1)}, bf16[128]{0:T(256)(128)(2,1)}, u32[]{:S(2)}) copy-start(bf16[128]{0:T(256)(128)(2,1)} %param.9) | copy-start | bytes 772
  47.4 3.0 %collective-permute-start.3 = (f32[4,16,2304]{2,1,0:T(8,128)S(1)}, f32[4,16,2304]{2,1,0:T(8,128)S(1)}, u32[]{:S(2)}, u32[]{:S(2)}) collective-permute-start(f32[4,16,2304]{2,1,0:T(8,128)S(1)} %get-tuple-element.25), channel_id=1, source_target_pairs={{0,1},{1,0},{2,3},{3,2},{4,5},{5,4},{6,7},{7,6},{8,9},{9,8},{10,11... | collective-permute-start | bytes 1769480 | tf_op jit(solution)/shard_map/ppermute | solution.py:289
  50.3 25.0 %copy-start.3 = (s32[16]{0:T(128)S(1)}, s32[16]{0:T(128)}, u32[]{:S(2)}) copy-start(s32[16]{0:T(128)} %lengths.1) | copy-start | bytes 196
  50.3 63.3 %copy-start.2 = (s32[8,16]{1,0:T(8,128)S(1)}, s32[8,16]{1,0:T(8,128)}, u32[]{:S(2)}) copy-start(s32[8,16]{1,0:T(8,128)} %slabs.1) | copy-start | bytes 1540
  50.4 6.7 %collective-permute-start.4 = (f32[16,2304]{1,0:T(8,128)S(1)}, f32[16,2304]{1,0:T(8,128)S(1)}, u32[]{:S(2)}, u32[]{:S(2)}) collective-permute-start(f32[16,2304]{1,0:T(8,128)S(1)} %get-tuple-element.27), channel_id=1, source_target_pairs={{0,32},{32,64},{64,96},{96,0},{1,33},{33,65},{65,97},{97,1},{2,34}... | collective-permute-start | bytes 442376 | tf_op jit(solution)/shard_map/ppermute | solution.py:285
  50.6 8.5 %collective-permute-start.5 = (f32[16,2304]{1,0:T(8,128)S(1)}, f32[16,2304]{1,0:T(8,128)S(1)}, u32[]{:S(2)}, u32[]{:S(2)}) collective-permute-start(f32[16,2304]{1,0:T(8,128)S(1)} %get-tuple-element.28), channel_id=1, source_target_pairs={{0,96},{32,0},{64,32},{96,64},{1,97},{33,1},{65,33},{97,65},{2,98}... | collective-permute-start | bytes 442376 | tf_op jit(solution)/shard_map/ppermute | solution.py:285
  53.2 6.9 %collective-permute-start.6 = (f32[16,2304]{1,0:T(8,128)S(1)}, f32[16,2304]{1,0:T(8,128)S(1)}, u32[]{:S(2)}, u32[]{:S(2)}) collective-permute-start(f32[16,2304]{1,0:T(8,128)S(1)} %get-tuple-element.29), channel_id=1, source_target_pairs={{0,64},{32,96},{64,0},{96,32},{1,65},{33,97},{65,1},{97,33},{2,66}... | collective-permute-start | bytes 442376 | tf_op jit(solution)/shard_map/ppermute | solution.py:285
  60.8 29.9 %all-to-all-start.1 = ((f32[16,1,2304]{2,1,0:T(1,128)}), f32[16,1,2304]{2,1,0:T(1,128)S(1)}, u32[]{:S(2)}, u32[]{:S(2)}) async-start(f32[16,1,2304]{2,1,0:T(1,128)} %bitcast.4), calls=%async_computation.1 | async-start | bytes 294912 | tf_op jit(solution)/shard_map/all_to_all | solution.py:293
  66.3 10.7 %collective-permute-start.10 = (bf16[16,2,32,128]{3,2,1,0:T(8,128)(2,1)S(1)}, bf16[16,2,32,128]{3,2,1,0:T(8,128)(2,1)S(1)}, u32[]{:S(2)}, u32[]{:S(2)}) collective-permute-start(bf16[16,2,32,128]{3,2,1,0:T(8,128)(2,1)S(1)} %get-tuple-element.34), channel_id=1, source_target_pairs={{0,33},{1,32},{32,65},{33,64},{64,97},{65,96},{96,1},{97,0},{2,35}... | collective-permute-start | bytes 786440 | tf_op jit(solution)/shard_map/ppermute | solution.py:381
  68.3 18.5 %collective-permute-start.11 = (bf16[16,2,32,128]{3,2,1,0:T(8,128)(2,1)S(1)}, bf16[16,2,32,128]{3,2,1,0:T(8,128)(2,1)S(1)}, u32[]{:S(2)}, u32[]{:S(2)}) collective-permute-start(bf16[16,2,32,128]{3,2,1,0:T(8,128)(2,1)S(1)} %get-tuple-element.35), channel_id=1, source_target_pairs={{0,97},{1,96},{32,1},{33,0},{64,33},{65,32},{96,65},{97,64},{2,99}... | collective-permute-start | bytes 786440 | tf_op jit(solution)/shard_map/ppermute | solution.py:381
  70.1 43.5 %collective-permute-start.12 = (bf16[16,2,32,128]{3,2,1,0:T(8,128)(2,1)S(1)}, bf16[16,2,32,128]{3,2,1,0:T(8,128)(2,1)S(1)}, u32[]{:S(2)}, u32[]{:S(2)}) collective-permute-start(bf16[16,2,32,128]{3,2,1,0:T(8,128)(2,1)S(1)} %get-tuple-element.36), channel_id=1, source_target_pairs={{0,65},{1,64},{32,97},{33,96},{64,1},{65,0},{96,33},{97,32},{2,67}... | collective-permute-start | bytes 786440 | tf_op jit(solution)/shard_map/ppermute | solution.py:381
  70.4 43.3 %collective-permute-start.13 = (bf16[16,2,32,128]{3,2,1,0:T(8,128)(2,1)S(1)}, bf16[16,2,32,128]{3,2,1,0:T(8,128)(2,1)S(1)}, u32[]{:S(2)}, u32[]{:S(2)}) collective-permute-start(bf16[16,2,32,128]{3,2,1,0:T(8,128)(2,1)S(1)} %get-tuple-element.37), channel_id=1, source_target_pairs={{0,1},{1,0},{32,33},{33,32},{64,65},{65,64},{96,97},{97,96},{2,3},... | collective-permute-start | bytes 786440 | tf_op jit(solution)/shard_map/ppermute | solution.py:381
  71.6 42.1 %collective-permute-start.9 = (bf16[16,2,32,128]{3,2,1,0:T(8,128)(2,1)S(1)}, bf16[16,2,32,128]{3,2,1,0:T(8,128)(2,1)S(1)}, u32[]{:S(2)}, u32[]{:S(2)}) collective-permute-start(bf16[16,2,32,128]{3,2,1,0:T(8,128)(2,1)S(1)} %get-tuple-element.33), channel_id=1, source_target_pairs={{0,64},{1,65},{32,96},{33,97},{64,0},{65,1},{96,32},{97,33},{2,66}... | collective-permute-start | bytes 786440 | tf_op jit(solution)/shard_map/ppermute | solution.py:381
  77.0 36.7 %collective-permute-start.7 = (bf16[16,2,32,128]{3,2,1,0:T(8,128)(2,1)}, bf16[16,2,32,128]{3,2,1,0:T(8,128)(2,1)S(1)}, u32[]{:S(2)}, u32[]{:S(2)}) collective-permute-start(bf16[16,2,32,128]{3,2,1,0:T(8,128)(2,1)} %get-tuple-element.31), channel_id=1, source_target_pairs={{0,32},{1,33},{32,64},{33,65},{64,96},{65,97},{96,0},{97,1},{2,34}... | collective-permute-start | bytes 786440 | tf_op jit(solution)/shard_map/ppermute | solution.py:381
  86.8 26.9 %collective-permute-start.8 = (bf16[16,2,32,128]{3,2,1,0:T(8,128)(2,1)}, bf16[16,2,32,128]{3,2,1,0:T(8,128)(2,1)S(1)}, u32[]{:S(2)}, u32[]{:S(2)}) collective-permute-start(bf16[16,2,32,128]{3,2,1,0:T(8,128)(2,1)} %get-tuple-element.32), channel_id=1, source_target_pairs={{0,96},{1,97},{32,0},{33,1},{64,32},{65,33},{96,64},{97,65},{2,98}... | collective-permute-start | bytes 786440 | tf_op jit(solution)/shard_map/ppermute | solution.py:381
  149.3 4.6 %collective-permute-start.14 = (bf16[16,2048]{1,0:T(8,128)(2,1)S(1)}, bf16[16,2048]{1,0:T(8,128)(2,1)S(1)}, u32[]{:S(2)}, u32[]{:S(2)}) collective-permute-start(bf16[16,2048]{1,0:T(8,128)(2,1)S(1)} %shard_map.95.rows), channel_id=1, source_target_pairs={{0,96},{32,0},{64,32},{96,64},{1,97},{33,1},{65,33},{97,65},{2,98}... | collective-permute-start | bytes 196616 | tf_op jit(solution)/shard_map/ppermute | solution.py:285
  149.6 6.5 %collective-permute-start.15 = (bf16[16,2048]{1,0:T(8,128)(2,1)S(1)}, bf16[16,2048]{1,0:T(8,128)(2,1)S(1)}, u32[]{:S(2)}, u32[]{:S(2)}) collective-permute-start(bf16[16,2048]{1,0:T(8,128)(2,1)S(1)} %shard_map.95.rows), channel_id=1, source_target_pairs={{0,32},{32,64},{64,96},{96,0},{1,33},{33,65},{65,97},{97,1},{2,34}... | collective-permute-start | bytes 196616 | tf_op jit(solution)/shard_map/ppermute | solution.py:285
  150.8 6.8 %collective-permute-start.16 = (bf16[16,2048]{1,0:T(8,128)(2,1)S(1)}, bf16[16,2048]{1,0:T(8,128)(2,1)S(1)}, u32[]{:S(2)}, u32[]{:S(2)}) collective-permute-start(bf16[16,2048]{1,0:T(8,128)(2,1)S(1)} %shard_map.95.rows), channel_id=1, source_target_pairs={{0,64},{32,96},{64,0},{96,32},{1,65},{33,97},{65,1},{97,33},{2,66}... | collective-permute-start | bytes 196616 | tf_op jit(solution)/shard_map/ppermute | solution.py:285
  150.9 10.8 %collective-permute-start.20 = (bf16[16,2048]{1,0:T(8,128)(2,1)S(1)}, bf16[16,2048]{1,0:T(8,128)(2,1)S(1)}, u32[]{:S(2)}, u32[]{:S(2)}) collective-permute-start(bf16[16,2048]{1,0:T(8,128)(2,1)S(1)} %shard_map.95.rows), channel_id=1, source_target_pairs={{0,1},{1,0},{2,3},{3,2},{4,5},{5,4},{6,7},{7,6},{8,9},{9,8},{10,11... | collective-permute-start | bytes 196616 | tf_op jit(solution)/shard_map/ppermute | solution.py:289
  153.9 7.9 %collective-permute-start.17 = (bf16[16,2048]{1,0:T(8,128)(2,1)S(1)}, bf16[16,2048]{1,0:T(8,128)(2,1)S(1)}, u32[]{:S(2)}, u32[]{:S(2)}) collective-permute-start(bf16[16,2048]{1,0:T(8,128)(2,1)S(1)} %collective-permute-done.14.refs_0_), channel_id=1, source_target_pairs={{0,1},{1,0},{2,3},{3,2},{4,5},{5,4},{6,7},{7,6},{8,9},{9,8},{10,11... | collective-permute-start | bytes 196616 | tf_op jit(solution)/shard_map/ppermute | solution.py:289
  156.1 5.6 %collective-permute-start.18 = (bf16[16,2048]{1,0:T(8,128)(2,1)S(1)}, bf16[16,2048]{1,0:T(8,128)(2,1)S(1)}, u32[]{:S(2)}, u32[]{:S(2)}) collective-permute-start(bf16[16,2048]{1,0:T(8,128)(2,1)S(1)} %collective-permute-done.15.refs_1_), channel_id=1, source_target_pairs={{0,1},{1,0},{2,3},{3,2},{4,5},{5,4},{6,7},{7,6},{8,9},{9,8},{10,11... | collective-permute-start | bytes 196616 | tf_op jit(solution)/shard_map/ppermute | solution.py:289
  157.6 4.1 %collective-permute-start.19 = (bf16[16,2048]{1,0:T(8,128)(2,1)S(1)}, bf16[16,2048]{1,0:T(8,128)(2,1)S(1)}, u32[]{:S(2)}, u32[]{:S(2)}) collective-permute-start(bf16[16,2048]{1,0:T(8,128)(2,1)S(1)} %collective-permute-done.16.refs_2_), channel_id=1, source_target_pairs={{0,1},{1,0},{2,3},{3,2},{4,5},{5,4},{6,7},{7,6},{8,9},{9,8},{10,11... | collective-permute-start | bytes 196616 | tf_op jit(solution)/shard_map/ppermute | solution.py:289

commit v10 on v9

--- a/solution.py
+++ b/solution.py
@@ -19,11 +19,10 @@
 TENSOR = ("x", "z", "c")
 FIRST = ((0, 1), (1, 1), (2, 1), (3, 1))
 REST = ((0, 0), (1, 0), (2, 0), (3, 0))
-NEAR = ((0, 0),)
-LAST = ((0, 1),)
+NEAR = ((0, 0), (0, 1))
 FAR = ((1, 0), (3, 0), (2, 0), (1, 1), (3, 1), (2, 1))
-MOVES = ((1, 0), (3, 0), (2, 0), (1, 1), (3, 1), (2, 1), (0, 1), (0, 0))
-EARLY = 2
+MOVES = ((0, 1), (1, 0), (3, 0), (2, 0), (1, 1), (3, 1), (2, 1), (0, 0))
+EARLY = 3
 
 EPS = 1e-05
 ROPE_BASE = 500000.0
@@ -257,27 +256,26 @@
         out[:, k * HD : (k + 1) * HD] = wide[:, k, :].astype(BF16)
 
 
-def output_near_kernel(rows, wo, x, out, w_far, w, sem, far_sems):
-    near = out_copies(NEAR, wo, w, sem)
+def output_near_kernel(a, b, wo, x, out, w_far, w, sems, far_sems):
+    near = out_copies(NEAR, wo, w, sems)
     far = out_copies(FAR, wo, w_far, far_sems)
     for copy in near + far:
         copy.start()
     for copy in near:
         copy.wait()
-    out[...] = x[...].astype(F32) + jnp.dot(rows[...], w[0], preferred_element_type=F32)
+    total = x[...].astype(F32)
+    for k, rows in enumerate((a, b)):
+        total = total + jnp.dot(rows[...], w[k], preferred_element_type=F32)
+    out[...] = total
     for copy in far:
         copy.wait()
 
 
-def output_far_kernel(near, *refs):
-    rows, (last, w_far, wo, out, w, sem) = refs[: len(FAR)], refs[len(FAR) :]
-    copies = out_copies(LAST, wo, w, sem)
-    copies[0].start()
+def output_far_kernel(*refs):
+    near, *rows, w, out = refs
     total = near[...]
     for k, block in enumerate(rows):
-        total = total + jnp.dot(block[...], w_far[k], preferred_element_type=F32)
-    copies[0].wait()
-    total = total + jnp.dot(last[...], w[0], preferred_element_type=F32)
+        total = total + jnp.dot(block[...], w[k], preferred_element_type=F32)
     out[...] = total.astype(BF16)
 
 
@@ -350,7 +348,7 @@
     product = struct((NX, n, PW), F32)
     normed, sent = call(
         project_first_kernel,
-        [struct((n, depth), BF16), pltpu.VMEM((NX, n, PW), F32)],
+        [struct((n, depth), BF16), product],
         [VMEM] * 4,
         sums,
         hidden_in,
@@ -418,27 +416,26 @@
         rows[k, 0] = shift_x(done, -k)
     for k in (0, 1, 3, 2):
         rows[k, 1] = swap_c(rows[k, 0])
-    block = (QW, w_o.shape[1])
-    read = [pltpu.VMEM((1,) + block, BF16), pltpu.SemaphoreType.DMA((1,))]
     total, w_far = call(
         output_near_kernel,
-        [struct((n, depth), F32), struct((len(FAR),) + block, BF16)],
-        [VMEM, HBM, VMEM],
-        rows[0, 0],
+        [struct((n, depth), F32), struct((len(FAR), QW, w_o.shape[1]), BF16)],
+        [VMEM, VMEM, HBM, VMEM],
+        *(rows[move] for move in NEAR),
         w_o,
         hidden_in,
-        scratch=read + [pltpu.SemaphoreType.DMA((len(FAR),))],
+        scratch=[
+            pltpu.VMEM((len(NEAR), QW, w_o.shape[1]), BF16),
+            pltpu.SemaphoreType.DMA((len(NEAR),)),
+            pltpu.SemaphoreType.DMA((len(FAR),)),
+        ],
     )
     return call(
         output_far_kernel,
         struct((n, depth), BF16),
-        [VMEM] * (3 + len(FAR)) + [HBM],
+        [VMEM] * (2 + len(FAR)),
         total,
         *(rows[move] for move in FAR),
-        rows[0, 1],
         w_far,
-        w_o,
-        scratch=read,
     )
 
 

time: 165 us -> 157 us (0.952)
  starting transfers between devices: 61.1 us -> 57.5 us
  waiting for transfers between devices: 30.2 us -> 26.7 us
    ppermute x7, waiting for transfers between devices: 11.5 us -> 7.98 us  [step(): cache[k] = lax.ppermute(cache[k], ('x', 'c'), pairs)]
    ppermute x7, starting transfers between devices: 11 us -> 7.61 us  [step(): cache[k] = lax.ppermute(cache[k], ('x', 'c'), pairs)]
  transfers between devices with their start and end apart: 23 -> 23, of which waited for: 7 -> 6; matrix products, arithmetic and copies ran while one was open for 0% -> 0% of each run, Pallas kernels for 6% -> 6%
where the time goes in v10:
time: 157 us; the launch traced here: 156 us
  starting transfers between devices  57.5 us (37%)
  blocking collectives  57 us (36%)
  waiting for transfers between devices  26.7 us (17%)
  Pallas kernels  14.1 us (9%)
    all_to_all x3, blocking collectives, across_z(): return lax.all_to_all(value, 'z', 0, 0, tiled=True)  57 us
    all_to_all x1, starting transfers between devices, step(): lax.all_to_all(sums.reshape(NZ * NC, 1, HD), ('z', 'c'), 0, 0, tiled=True)  26.1 us
    pallas_call x16, Pallas kernels, call(): pl.pallas_call(kernel, in_specs=specs, out_specs=outs, out_shape=out, scr...  14.1 us
    ppermute x9, starting transfers between devices, shift_x(): return lax.ppermute(value, 'x', [(i, (i + by) % NX) for i in range(NX)])  11.4 us
    all_to_all x1, waiting for transfers between devices, step(): lax.all_to_all(sums.reshape(NZ * NC, 1, HD), ('z', 'c'), 0, 0, tiled=True)  9.83 us
    ppermute x9, waiting for transfers between devices, shift_x(): return lax.ppermute(value, 'x', [(i, (i + by) % NX) for i in range(NX)])  8.86 us
    ppermute x5, starting transfers between devices, swap_c(): return lax.ppermute(value, 'c', [(0, 1), (1, 0)])  8.39 us
    ppermute x7, waiting for transfers between devices, step(): cache[k] = lax.ppermute(cache[k], ('x', 'c'), pairs)  7.98 us
  transfers between devices with their start and end apart: 23, of which 6 were waited for; matrix products, arithmetic and copies ran while one was open for 0% of the time, Pallas kernels for 6%

profile of v10, /device:TPU:33, one launch (start us, length us, event | category | flops | bytes accessed | tf_op | source)
XLA Modules:
  0.0 156.3 jit_solution(426247838162381728)
XLA Ops:
  0.0 0.7 copy-done
  0.7 0.1 shard_map.82.a
  0.8 2.2 %collective-permute-start = (f32[1,128]{1,0:T(1,128)S(1)}, f32[1,128]{1,0:T(1,128)S(1)}, u32[]{:S(2)}, u32[]{:S(2)}) collective-permute-start(f32[1,128]{1,0:T(1,128)S(1)} %shard_map.82.a), channel_id=1, source_target_pairs={{0,32},{32,64},{64,96},{96,0},{1,33},{33,65},{65,97},{97,1},{2,34}... | collective-permute-start | bytes 1544 | tf_op jit(solution)/shard_map/ppermute | solution.py:283
  3.0 1.7 %collective-permute-start.1 = (f32[1,128]{1,0:T(1,128)S(1)}, f32[1,128]{1,0:T(1,128)S(1)}, u32[]{:S(2)}, u32[]{:S(2)}) collective-permute-start(f32[1,128]{1,0:T(1,128)S(1)} %shard_map.82.a), channel_id=1, source_target_pairs={{0,96},{32,0},{64,32},{96,64},{1,97},{33,1},{65,33},{97,65},{2,98}... | collective-permute-start | bytes 1544 | tf_op jit(solution)/shard_map/ppermute | solution.py:283
  4.7 1.5 collective-permute-start.2
  6.1 2.5 %collective-permute-done.2.d = f32[1,128]{1,0:T(1,128)S(1)} collective-permute-done((f32[1,128]{1,0:T(1,128)S(1)}, f32[1,128]{1,0:T(1,128)S(1)}, u32[]{:S(2)}, u32[]{:S(2)}) %collective-permute-start.2) | collective-permute-done | bytes 544 | tf_op jit(solution)/shard_map/ppermute | solution.py:283
  8.6 0.6 shard_map.83
  9.2 26.1 %all-to-all-start = ((f32[32,1,128]{2,1,0:T(1,128)}), f32[32,1,128]{2,1,0:T(1,128)S(1)}, u32[]{:S(2)}, u32[]{:S(2)}) async-start(f32[32,1,128]{2,1,0:T(1,128)} %bitcast.1), calls=%async_computation | async-start | bytes 32768 | tf_op jit(solution)/shard_map/all_to_all | solution.py:314
  35.3 1.7 %shard_map.84.w = bf16[4,128,2304]{2,1,0:T(8,128)(2,1)S(1)} custom-call(bf16[128,16384]{1,0:T(8,128)(2,1)} %wq.3, bf16[128,2048]{1,0:T(8,128)(2,1)} %wkv.3), custom_call_target="tpu_custom_call" | custom-call | tf_op jit(solution)/shard_map/pallas_call | solution.py:47
  37.0 9.8 %all-to-all-done = f32[32,1,128]{2,1,0:T(1,128)S(1)} async-done(((f32[32,1,128]{2,1,0:T(1,128)}), f32[32,1,128]{2,1,0:T(1,128)S(1)}, u32[]{:S(2)}, u32[]{:S(2)}) %all-to-all-start) | async-done | bytes 16416 | tf_op jit(solution)/shard_map/all_to_all | solution.py:314
  46.9 0.5 shard_map.85
  47.4 1.0 collective-permute-start.3
  48.4 2.0 %shard_map.86.a = f32[4,16,2304]{2,1,0:T(8,128)S(1)} custom-call(bf16[16,128]{1,0:T(8,128)(2,1)S(1)} %get-tuple-element.24.normed, bf16[128,16384]{1,0:T(8,128)(2,1)} %wq.3, bf16[128,2048]{1,0:T(8,128)(2,1)} %wkv.3), custom_call_target="tpu_custom_call" | custom-call | tf_op jit(solution)/shard_map/pallas_call | solution.py:47
  50.4 0.2 collective-permute-start.4
  50.6 2.6 %collective-permute-start.5 = (f32[16,2304]{1,0:T(8,128)S(1)}, f32[16,2304]{1,0:T(8,128)S(1)}, u32[]{:S(2)}, u32[]{:S(2)}) collective-permute-start(f32[16,2304]{1,0:T(8,128)S(1)} %get-tuple-element.28), channel_id=1, source_target_pairs={{0,96},{32,0},{64,32},{96,64},{1,97},{33,1},{65,33},{97,65},{2,98}... | collective-permute-start | bytes 442376 | tf_op jit(solution)/shard_map/ppermute | solution.py:283
  53.2 0.5 collective-permute-start.6
  53.8 3.4 %collective-permute-done.4.b = f32[16,2304]{1,0:T(8,128)S(1)} collective-permute-done((f32[16,2304]{1,0:T(8,128)S(1)}, f32[16,2304]{1,0:T(8,128)S(1)}, u32[]{:S(2)}, u32[]{:S(2)}) %collective-permute-start.4) | collective-permute-done | bytes 147488 | tf_op jit(solution)/shard_map/ppermute | solution.py:283
  57.1 2.0 %collective-permute-done.5.c = f32[16,2304]{1,0:T(8,128)S(1)} collective-permute-done((f32[16,2304]{1,0:T(8,128)S(1)}, f32[16,2304]{1,0:T(8,128)S(1)}, u32[]{:S(2)}, u32[]{:S(2)}) %collective-permute-start.5) | collective-permute-done | bytes 147488 | tf_op jit(solution)/shard_map/ppermute | solution.py:283
  59.1 1.0 collective-permute-done.6.d
  60.1 0.7 shard_map.88
  60.8 4.0 %all-to-all-start.1 = ((f32[16,1,2304]{2,1,0:T(1,128)}), f32[16,1,2304]{2,1,0:T(1,128)S(1)}, u32[]{:S(2)}, u32[]{:S(2)}) async-start(f32[16,1,2304]{2,1,0:T(1,128)} %bitcast.4), calls=%async_computation.1 | async-start | bytes 294912 | tf_op jit(solution)/shard_map/all_to_all | solution.py:291
  64.8 1.4 shard_map.92
  66.2 0.2 collective-permute-start.10
  66.4 4.4 %collective-permute-start.11 = (bf16[16,2,32,128]{3,2,1,0:T(8,128)(2,1)S(1)}, bf16[16,2,32,128]{3,2,1,0:T(8,128)(2,1)S(1)}, u32[]{:S(2)}, u32[]{:S(2)}) collective-permute-start(bf16[16,2,32,128]{3,2,1,0:T(8,128)(2,1)S(1)} %get-tuple-element.35), channel_id=1, source_target_pairs={{0,33},{1,32},{32,65},{33,64},{64,97},{65,96},{96,1},{97,0},{2,35}... | collective-permute-start | bytes 786440 | tf_op jit(solution)/shard_map/ppermute | solution.py:379
  70.8 0.1 collective-permute-start.12
  70.9 1.5 collective-permute-start.13
  72.3 1.9 %shard_map.91 = (bf16[16,2,32,128]{3,2,1,0:T(8,128)(2,1)}, bf16[16,2,32,128]{3,2,1,0:T(8,128)(2,1)}, bf16[16,2,32,128]{3,2,1,0:T(8,128)(2,1)}) custom-call(bf16[8,16,2,32,128]{4,3,2,1,0:T(8,128)(2,1)} %cache.3), custom_call_target="tpu_custom_call" | custom-call | tf_op jit(solution)/shard_map/pallas_call | solution.py:47
  74.2 0.7 collective-permute-start.7
  75.0 0.4 collective-permute-start.8
  75.4 8.0 %collective-permute-done.11.refs_4_ = bf16[16,2,32,128]{3,2,1,0:T(8,128)(2,1)S(1)} collective-permute-done((bf16[16,2,32,128]{3,2,1,0:T(8,128)(2,1)S(1)}, bf16[16,2,32,128]{3,2,1,0:T(8,128)(2,1)S(1)}, u32[]{:S(2)}, u32[]{:S(2)}) %collective-permute-start.11) | collective-permute-done | bytes 262176 | tf_op jit(solution)/shard_map/ppermute | solution.py:379
  83.4 0.3 collective-permute-start.9
  83.7 0.1 fusion.4
  83.8 0.2 shard_map.89
  84.0 22.8 %all_to_all.25.q = bf16[16,16,128]{2,1,0:T(8,128)(2,1)S(1)} all-to-all(bf16[16,16,128]{2,1,0:T(8,128)(2,1)S(1)} %get-tuple-element.30), channel_id=1, replica_groups=mesh['groups'=2,'x'=4,'z'=16,'c'=2] {'z'}, dimensions={0} | all-to-all | bytes 131072 | tf_op jit(solution)/shard_map/all_to_all | solution.py:291
  106.9 1.2 shard_map.93
  108.1 15.8 %all_to_all.26 = f32[16,1,2304]{2,1,0:T(1,128)S(1)} all-to-all(f32[16,1,2304]{2,1,0:T(1,128)S(1)} %bitcast.11), channel_id=1, replica_groups=mesh['groups'=2,'x'=4,'z'=16,'c'=2] {'z'}, dimensions={0} | all-to-all | bytes 294912 | tf_op jit(solution)/shard_map/all_to_all | solution.py:291
  123.8 0.1 shard_map.94
  124.0 18.4 %all_to_all.27.heads = bf16[16,16,128]{2,1,0:T(8,128)(2,1)S(1)} all-to-all(bf16[16,16,128]{2,1,0:T(8,128)(2,1)S(1)} %shard_map.94), channel_id=1, replica_groups=mesh['groups'=2,'x'=4,'z'=16,'c'=2] {'z'}, dimensions={0} | all-to-all | bytes 131072 | tf_op jit(solution)/shard_map/all_to_all | solution.py:291
  142.4 0.1 shard_map.95.a
  142.5 0.1 collective-permute-start.15
  142.7 1.4 collective-permute-start.16
  144.1 1.2 collective-permute-start.17
  145.3 3.1 %collective-permute-start.14 = (bf16[16,2048]{1,0:T(8,128)(2,1)S(1)}, bf16[16,2048]{1,0:T(8,128)(2,1)S(1)}, u32[]{:S(2)}, u32[]{:S(2)}) collective-permute-start(bf16[16,2048]{1,0:T(8,128)(2,1)S(1)} %shard_map.95.a), channel_id=1, source_target_pairs={{0,1},{1,0},{2,3},{3,2},{4,5},{5,4},{6,7},{7,6},{8,9},{9,8},{10,11... | collective-permute-start | bytes 196616 | tf_op jit(solution)/shard_map/ppermute | solution.py:287
  148.5 0.7 collective-permute-start.18
  149.2 1.5 collective-permute-start.19
  150.7 2.0 %collective-permute-start.20 = (bf16[16,2048]{1,0:T(8,128)(2,1)S(1)}, bf16[16,2048]{1,0:T(8,128)(2,1)S(1)}, u32[]{:S(2)}, u32[]{:S(2)}) collective-permute-start(bf16[16,2048]{1,0:T(8,128)(2,1)S(1)} %collective-permute-done.17.refs_3_), channel_id=1, source_target_pairs={{0,1},{1,0},{2,3},{3,2},{4,5},{5,4},{6,7},{7,6},{8,9},{9,8},{10,11... | collective-permute-start | bytes 196616 | tf_op jit(solution)/shard_map/ppermute | solution.py:287
  152.8 2.3 %shard_map.96 = (f32[16,128]{1,0:T(8,128)S(1)}, bf16[6,2048,128]{2,1,0:T(8,128)(2,1)S(1)}) custom-call(bf16[16,2048]{1,0:T(8,128)(2,1)S(1)} %shard_map.95.a, bf16[16,2048]{1,0:T(8,128)(2,1)S(1)} %collective-permute-done.14.b, bf16[16384,128]{1,0:T(8,128)(2,1)} %wo.1, bf16[16,128]{1,0:T(8,128)(2,1)S(1)} %copy-done.1), custom_call_target="tpu_custom_call" | custom-call | tf_op jit(solution)/shard_map/pallas_call | solution.py:47
  155.1 1.1 shard_map.97
  (31 shorter events, 0.2 us)
Async XLA Ops:
  0.0 0.7 copy-start
  0.8 5.3 %collective-permute-start = (f32[1,128]{1,0:T(1,128)S(1)}, f32[1,128]{1,0:T(1,128)S(1)}, u32[]{:S(2)}, u32[]{:S(2)}) collective-permute-start(f32[1,128]{1,0:T(1,128)S(1)} %shard_map.82.a), channel_id=1, source_target_pairs={{0,32},{32,64},{64,96},{96,0},{1,33},{33,65},{65,97},{97,1},{2,34}... | collective-permute-start | bytes 1544 | tf_op jit(solution)/shard_map/ppermute | solution.py:283
  3.0 3.1 %collective-permute-start.1 = (f32[1,128]{1,0:T(1,128)S(1)}, f32[1,128]{1,0:T(1,128)S(1)}, u32[]{:S(2)}, u32[]{:S(2)}) collective-permute-start(f32[1,128]{1,0:T(1,128)S(1)} %shard_map.82.a), channel_id=1, source_target_pairs={{0,96},{32,0},{64,32},{96,64},{1,97},{33,1},{65,33},{97,65},{2,98}... | collective-permute-start | bytes 1544 | tf_op jit(solution)/shard_map/ppermute | solution.py:283
  4.7 3.9 %collective-permute-start.2 = (f32[1,128]{1,0:T(1,128)S(1)}, f32[1,128]{1,0:T(1,128)S(1)}, u32[]{:S(2)}, u32[]{:S(2)}) collective-permute-start(f32[1,128]{1,0:T(1,128)S(1)} %shard_map.82.a), channel_id=1, source_target_pairs={{0,64},{32,96},{64,0},{96,32},{1,65},{33,97},{65,1},{97,33},{2,66}... | collective-permute-start | bytes 1544 | tf_op jit(solution)/shard_map/ppermute | solution.py:283
  9.2 37.7 %all-to-all-start = ((f32[32,1,128]{2,1,0:T(1,128)}), f32[32,1,128]{2,1,0:T(1,128)S(1)}, u32[]{:S(2)}, u32[]{:S(2)}) async-start(f32[32,1,128]{2,1,0:T(1,128)} %bitcast.1), calls=%async_computation | async-start | bytes 32768 | tf_op jit(solution)/shard_map/all_to_all | solution.py:314
  35.3 11.6 %copy-start.1 = (bf16[16,128]{1,0:T(8,128)(2,1)S(1)}, bf16[16,128]{1,0:T(8,128)(2,1)}, u32[]{:S(2)}) copy-start(bf16[16,128]{1,0:T(8,128)(2,1)} %x.5) | copy-start | bytes 12292
  35.3 11.6 %copy-start.4 = (bf16[128]{0:T(256)(128)(2,1)S(1)}, bf16[128]{0:T(256)(128)(2,1)}, u32[]{:S(2)}) copy-start(bf16[128]{0:T(256)(128)(2,1)} %param.9) | copy-start | bytes 772
  47.4 3.0 %collective-permute-start.3 = (f32[4,16,2304]{2,1,0:T(8,128)S(1)}, f32[4,16,2304]{2,1,0:T(8,128)S(1)}, u32[]{:S(2)}, u32[]{:S(2)}) collective-permute-start(f32[4,16,2304]{2,1,0:T(8,128)S(1)} %get-tuple-element.25), channel_id=1, source_target_pairs={{0,1},{1,0},{2,3},{3,2},{4,5},{5,4},{6,7},{7,6},{8,9},{9,8},{10,11... | collective-permute-start | bytes 1769480 | tf_op jit(solution)/shard_map/ppermute | solution.py:287
  50.3 24.7 %copy-start.3 = (s32[16]{0:T(128)S(1)}, s32[16]{0:T(128)}, u32[]{:S(2)}) copy-start(s32[16]{0:T(128)} %lengths.1) | copy-start | bytes 196
  50.3 56.5 %copy-start.2 = (s32[8,16]{1,0:T(8,128)S(1)}, s32[8,16]{1,0:T(8,128)}, u32[]{:S(2)}) copy-start(s32[8,16]{1,0:T(8,128)} %slabs.1) | copy-start | bytes 1540
  50.4 6.7 %collective-permute-start.4 = (f32[16,2304]{1,0:T(8,128)S(1)}, f32[16,2304]{1,0:T(8,128)S(1)}, u32[]{:S(2)}, u32[]{:S(2)}) collective-permute-start(f32[16,2304]{1,0:T(8,128)S(1)} %get-tuple-element.27), channel_id=1, source_target_pairs={{0,32},{32,64},{64,96},{96,0},{1,33},{33,65},{65,97},{97,1},{2,34}... | collective-permute-start | bytes 442376 | tf_op jit(solution)/shard_map/ppermute | solution.py:283
  50.6 8.5 %collective-permute-start.5 = (f32[16,2304]{1,0:T(8,128)S(1)}, f32[16,2304]{1,0:T(8,128)S(1)}, u32[]{:S(2)}, u32[]{:S(2)}) collective-permute-start(f32[16,2304]{1,0:T(8,128)S(1)} %get-tuple-element.28), channel_id=1, source_target_pairs={{0,96},{32,0},{64,32},{96,64},{1,97},{33,1},{65,33},{97,65},{2,98}... | collective-permute-start | bytes 442376 | tf_op jit(solution)/shard_map/ppermute | solution.py:283
  53.2 6.9 %collective-permute-start.6 = (f32[16,2304]{1,0:T(8,128)S(1)}, f32[16,2304]{1,0:T(8,128)S(1)}, u32[]{:S(2)}, u32[]{:S(2)}) collective-permute-start(f32[16,2304]{1,0:T(8,128)S(1)} %get-tuple-element.29), channel_id=1, source_target_pairs={{0,64},{32,96},{64,0},{96,32},{1,65},{33,97},{65,1},{97,33},{2,66}... | collective-permute-start | bytes 442376 | tf_op jit(solution)/shard_map/ppermute | solution.py:283
  60.8 23.0 %all-to-all-start.1 = ((f32[16,1,2304]{2,1,0:T(1,128)}), f32[16,1,2304]{2,1,0:T(1,128)S(1)}, u32[]{:S(2)}, u32[]{:S(2)}) async-start(f32[16,1,2304]{2,1,0:T(1,128)} %bitcast.4), calls=%async_computation.1 | async-start | bytes 294912 | tf_op jit(solution)/shard_map/all_to_all | solution.py:291
  66.2 8.8 %collective-permute-start.10 = (bf16[16,2,32,128]{3,2,1,0:T(8,128)(2,1)S(1)}, bf16[16,2,32,128]{3,2,1,0:T(8,128)(2,1)S(1)}, u32[]{:S(2)}, u32[]{:S(2)}) collective-permute-start(bf16[16,2,32,128]{3,2,1,0:T(8,128)(2,1)S(1)} %get-tuple-element.34), channel_id=1, source_target_pairs={{0,64},{1,65},{32,96},{33,97},{64,0},{65,1},{96,32},{97,33},{2,66}... | collective-permute-start | bytes 786440 | tf_op jit(solution)/shard_map/ppermute | solution.py:379
  66.4 17.0 %collective-permute-start.11 = (bf16[16,2,32,128]{3,2,1,0:T(8,128)(2,1)S(1)}, bf16[16,2,32,128]{3,2,1,0:T(8,128)(2,1)S(1)}, u32[]{:S(2)}, u32[]{:S(2)}) collective-permute-start(bf16[16,2,32,128]{3,2,1,0:T(8,128)(2,1)S(1)} %get-tuple-element.35), channel_id=1, source_target_pairs={{0,33},{1,32},{32,65},{33,64},{64,97},{65,96},{96,1},{97,0},{2,35}... | collective-permute-start | bytes 786440 | tf_op jit(solution)/shard_map/ppermute | solution.py:379
  70.8 36.0 %collective-permute-start.12 = (bf16[16,2,32,128]{3,2,1,0:T(8,128)(2,1)S(1)}, bf16[16,2,32,128]{3,2,1,0:T(8,128)(2,1)S(1)}, u32[]{:S(2)}, u32[]{:S(2)}) collective-permute-start(bf16[16,2,32,128]{3,2,1,0:T(8,128)(2,1)S(1)} %get-tuple-element.36), channel_id=1, source_target_pairs={{0,97},{1,96},{32,1},{33,0},{64,33},{65,32},{96,65},{97,64},{2,99}... | collective-permute-start | bytes 786440 | tf_op jit(solution)/shard_map/ppermute | solution.py:379
  70.9 35.9 %collective-permute-start.13 = (bf16[16,2,32,128]{3,2,1,0:T(8,128)(2,1)S(1)}, bf16[16,2,32,128]{3,2,1,0:T(8,128)(2,1)S(1)}, u32[]{:S(2)}, u32[]{:S(2)}) collective-permute-start(bf16[16,2,32,128]{3,2,1,0:T(8,128)(2,1)S(1)} %get-tuple-element.37), channel_id=1, source_target_pairs={{0,65},{1,64},{32,97},{33,96},{64,1},{65,0},{96,33},{97,32},{2,67}... | collective-permute-start | bytes 786440 | tf_op jit(solution)/shard_map/ppermute | solution.py:379
  74.2 32.6 %collective-permute-start.7 = (bf16[16,2,32,128]{3,2,1,0:T(8,128)(2,1)}, bf16[16,2,32,128]{3,2,1,0:T(8,128)(2,1)S(1)}, u32[]{:S(2)}, u32[]{:S(2)}) collective-permute-start(bf16[16,2,32,128]{3,2,1,0:T(8,128)(2,1)} %get-tuple-element.31), channel_id=1, source_target_pairs={{0,1},{1,0},{32,33},{33,32},{64,65},{65,64},{96,97},{97,96},{2,3},... | collective-permute-start | bytes 786440 | tf_op jit(solution)/shard_map/ppermute | solution.py:379
  75.0 31.8 %collective-permute-start.8 = (bf16[16,2,32,128]{3,2,1,0:T(8,128)(2,1)}, bf16[16,2,32,128]{3,2,1,0:T(8,128)(2,1)S(1)}, u32[]{:S(2)}, u32[]{:S(2)}) collective-permute-start(bf16[16,2,32,128]{3,2,1,0:T(8,128)(2,1)} %get-tuple-element.32), channel_id=1, source_target_pairs={{0,32},{1,33},{32,64},{33,65},{64,96},{65,97},{96,0},{97,1},{2,34}... | collective-permute-start | bytes 786440 | tf_op jit(solution)/shard_map/ppermute | solution.py:379
  83.4 23.4 %collective-permute-start.9 = (bf16[16,2,32,128]{3,2,1,0:T(8,128)(2,1)}, bf16[16,2,32,128]{3,2,1,0:T(8,128)(2,1)S(1)}, u32[]{:S(2)}, u32[]{:S(2)}) collective-permute-start(bf16[16,2,32,128]{3,2,1,0:T(8,128)(2,1)} %get-tuple-element.33), channel_id=1, source_target_pairs={{0,96},{1,97},{32,0},{33,1},{64,32},{65,33},{96,64},{97,65},{2,98}... | collective-permute-start | bytes 786440 | tf_op jit(solution)/shard_map/ppermute | solution.py:379
  142.5 5.9 %collective-permute-start.15 = (bf16[16,2048]{1,0:T(8,128)(2,1)S(1)}, bf16[16,2048]{1,0:T(8,128)(2,1)S(1)}, u32[]{:S(2)}, u32[]{:S(2)}) collective-permute-start(bf16[16,2048]{1,0:T(8,128)(2,1)S(1)} %shard_map.95.a), channel_id=1, source_target_pairs={{0,96},{32,0},{64,32},{96,64},{1,97},{33,1},{65,33},{97,65},{2,98}... | collective-permute-start | bytes 196616 | tf_op jit(solution)/shard_map/ppermute | solution.py:283
  142.7 6.5 %collective-permute-start.16 = (bf16[16,2048]{1,0:T(8,128)(2,1)S(1)}, bf16[16,2048]{1,0:T(8,128)(2,1)S(1)}, u32[]{:S(2)}, u32[]{:S(2)}) collective-permute-start(bf16[16,2048]{1,0:T(8,128)(2,1)S(1)} %shard_map.95.a), channel_id=1, source_target_pairs={{0,32},{32,64},{64,96},{96,0},{1,33},{33,65},{65,97},{97,1},{2,34}... | collective-permute-start | bytes 196616 | tf_op jit(solution)/shard_map/ppermute | solution.py:283
  144.1 6.6 %collective-permute-start.17 = (bf16[16,2048]{1,0:T(8,128)(2,1)S(1)}, bf16[16,2048]{1,0:T(8,128)(2,1)S(1)}, u32[]{:S(2)}, u32[]{:S(2)}) collective-permute-start(bf16[16,2048]{1,0:T(8,128)(2,1)S(1)} %shard_map.95.a), channel_id=1, source_target_pairs={{0,64},{32,96},{64,0},{96,32},{1,65},{33,97},{65,1},{97,33},{2,66}... | collective-permute-start | bytes 196616 | tf_op jit(solution)/shard_map/ppermute | solution.py:283
  145.3 7.4 %collective-permute-start.14 = (bf16[16,2048]{1,0:T(8,128)(2,1)S(1)}, bf16[16,2048]{1,0:T(8,128)(2,1)S(1)}, u32[]{:S(2)}, u32[]{:S(2)}) collective-permute-start(bf16[16,2048]{1,0:T(8,128)(2,1)S(1)} %shard_map.95.a), channel_id=1, source_target_pairs={{0,1},{1,0},{2,3},{3,2},{4,5},{5,4},{6,7},{7,6},{8,9},{9,8},{10,11... | collective-permute-start | bytes 196616 | tf_op jit(solution)/shard_map/ppermute | solution.py:287
  148.5 6.6 %collective-permute-start.18 = (bf16[16,2048]{1,0:T(8,128)(2,1)S(1)}, bf16[16,2048]{1,0:T(8,128)(2,1)S(1)}, u32[]{:S(2)}, u32[]{:S(2)}) collective-permute-start(bf16[16,2048]{1,0:T(8,128)(2,1)S(1)} %collective-permute-done.15.refs_1_), channel_id=1, source_target_pairs={{0,1},{1,0},{2,3},{3,2},{4,5},{5,4},{6,7},{7,6},{8,9},{9,8},{10,11... | collective-permute-start | bytes 196616 | tf_op jit(solution)/shard_map/ppermute | solution.py:287
  149.2 5.9 %collective-permute-start.19 = (bf16[16,2048]{1,0:T(8,128)(2,1)S(1)}, bf16[16,2048]{1,0:T(8,128)(2,1)S(1)}, u32[]{:S(2)}, u32[]{:S(2)}) collective-permute-start(bf16[16,2048]{1,0:T(8,128)(2,1)S(1)} %collective-permute-done.16.refs_2_), channel_id=1, source_target_pairs={{0,1},{1,0},{2,3},{3,2},{4,5},{5,4},{6,7},{7,6},{8,9},{9,8},{10,11... | collective-permute-start | bytes 196616 | tf_op jit(solution)/shard_map/ppermute | solution.py:287
  150.7 4.4 %collective-permute-start.20 = (bf16[16,2048]{1,0:T(8,128)(2,1)S(1)}, bf16[16,2048]{1,0:T(8,128)(2,1)S(1)}, u32[]{:S(2)}, u32[]{:S(2)}) collective-permute-start(bf16[16,2048]{1,0:T(8,128)(2,1)S(1)} %collective-permute-done.17.refs_3_), channel_id=1, source_target_pairs={{0,1},{1,0},{2,3},{3,2},{4,5},{5,4},{6,7},{7,6},{8,9},{9,8},{10,11... | collective-permute-start | bytes 196616 | tf_op jit(solution)/shard_map/ppermute | solution.py:287

commit v11 on v10

--- a/solution.py
+++ b/solution.py
@@ -21,8 +21,8 @@
 REST = ((0, 0), (1, 0), (2, 0), (3, 0))
 NEAR = ((0, 0), (0, 1))
 FAR = ((1, 0), (3, 0), (2, 0), (1, 1), (3, 1), (2, 1))
-MOVES = ((0, 1), (1, 0), (3, 0), (2, 0), (1, 1), (3, 1), (2, 1), (0, 0))
-EARLY = 3
+MOVES = ((1, 0), (3, 0), (2, 0), (2, 1), (1, 1), (3, 1), (0, 1), (0, 0))
+EARLY = 2
 
 EPS = 1e-05
 ROPE_BASE = 500000.0
@@ -348,7 +348,7 @@
     product = struct((NX, n, PW), F32)
     normed, sent = call(
         project_first_kernel,
-        [struct((n, depth), BF16), product],
+        [struct((n, depth), BF16), pltpu.VMEM((NX, n, PW), F32)],
         [VMEM] * 4,
         sums,
         hidden_in,

time: 157 us -> 156 us (level)
  blocking collectives: 57 us -> 54.4 us
  starting transfers between devices: 57.5 us -> 59.7 us
    all_to_all x3, blocking collectives: 57 us -> 54.4 us  [across_z(): return lax.all_to_all(value, 'z', 0, 0, tiled=True)]
    ppermute x9, starting transfers between devices: 11.4 us -> 13.7 us  [shift_x(): return lax.ppermute(value, 'x', [(i, (i + by) % NX) for i in range(NX)])]
  transfers between devices with their start and end apart: 23 -> 23, of which waited for: 6 -> 7; matrix products, arithmetic and copies ran while one was open for 0% -> 0% of each run, Pallas kernels for 6% -> 6%
where the time goes in v11:
time: 156 us; the launch traced here: 155 us
  starting transfers between devices  59.7 us (38%)
  blocking collectives  54.4 us (35%)
  waiting for transfers between devices  25.9 us (17%)
  Pallas kernels  14 us (9%)
    all_to_all x3, blocking collectives, across_z(): return lax.all_to_all(value, 'z', 0, 0, tiled=True)  54.4 us
    all_to_all x1, starting transfers between devices, step(): lax.all_to_all(sums.reshape(NZ * NC, 1, HD), ('z', 'c'), 0, 0, tiled=True)  26.1 us
    pallas_call x16, Pallas kernels, call(): pl.pallas_call(kernel, in_specs=specs, out_specs=outs, out_shape=out, scr...  14 us
    ppermute x9, starting transfers between devices, shift_x(): return lax.ppermute(value, 'x', [(i, (i + by) % NX) for i in range(NX)])  13.7 us
    all_to_all x1, waiting for transfers between devices, step(): lax.all_to_all(sums.reshape(NZ * NC, 1, HD), ('z', 'c'), 0, 0, tiled=True)  9.83 us
    ppermute x9, waiting for transfers between devices, shift_x(): return lax.ppermute(value, 'x', [(i, (i + by) % NX) for i in range(NX)])  8.86 us
    ppermute x5, starting transfers between devices, swap_c(): return lax.ppermute(value, 'c', [(0, 1), (1, 0)])  8.43 us
    ppermute x7, starting transfers between devices, step(): cache[k] = lax.ppermute(cache[k], ('x', 'c'), pairs)  7.55 us
  transfers between devices with their start and end apart: 23, of which 7 were waited for; matrix products, arithmetic and copies ran while one was open for 0% of the time, Pallas kernels for 6%

profile of v11, /device:TPU:33, one launch (start us, length us, event | category | flops | bytes accessed | tf_op | source)
XLA Modules:
  0.0 155.3 jit_solution(17425010465740611381)
XLA Ops:
  0.0 0.7 copy-done
  0.7 0.1 shard_map.82.a
  0.8 2.2 %collective-permute-start = (f32[1,128]{1,0:T(1,128)S(1)}, f32[1,128]{1,0:T(1,128)S(1)}, u32[]{:S(2)}, u32[]{:S(2)}) collective-permute-start(f32[1,128]{1,0:T(1,128)S(1)} %shard_map.82.a), channel_id=1, source_target_pairs={{0,32},{32,64},{64,96},{96,0},{1,33},{33,65},{65,97},{97,1},{2,34}... | collective-permute-start | bytes 1544 | tf_op jit(solution)/shard_map/ppermute | solution.py:283
  3.0 1.7 %collective-permute-start.1 = (f32[1,128]{1,0:T(1,128)S(1)}, f32[1,128]{1,0:T(1,128)S(1)}, u32[]{:S(2)}, u32[]{:S(2)}) collective-permute-start(f32[1,128]{1,0:T(1,128)S(1)} %shard_map.82.a), channel_id=1, source_target_pairs={{0,96},{32,0},{64,32},{96,64},{1,97},{33,1},{65,33},{97,65},{2,98}... | collective-permute-start | bytes 1544 | tf_op jit(solution)/shard_map/ppermute | solution.py:283
  4.7 1.5 collective-permute-start.2
  6.1 2.5 %collective-permute-done.2.d = f32[1,128]{1,0:T(1,128)S(1)} collective-permute-done((f32[1,128]{1,0:T(1,128)S(1)}, f32[1,128]{1,0:T(1,128)S(1)}, u32[]{:S(2)}, u32[]{:S(2)}) %collective-permute-start.2) | collective-permute-done | bytes 544 | tf_op jit(solution)/shard_map/ppermute | solution.py:283
  8.6 0.6 shard_map.83
  9.2 26.1 %all-to-all-start = ((f32[32,1,128]{2,1,0:T(1,128)}), f32[32,1,128]{2,1,0:T(1,128)S(1)}, u32[]{:S(2)}, u32[]{:S(2)}) async-start(f32[32,1,128]{2,1,0:T(1,128)} %bitcast.1), calls=%async_computation | async-start | bytes 32768 | tf_op jit(solution)/shard_map/all_to_all | solution.py:314
  35.3 1.7 %shard_map.84.w = bf16[4,128,2304]{2,1,0:T(8,128)(2,1)S(1)} custom-call(bf16[128,16384]{1,0:T(8,128)(2,1)} %wq.3, bf16[128,2048]{1,0:T(8,128)(2,1)} %wkv.3), custom_call_target="tpu_custom_call" | custom-call | tf_op jit(solution)/shard_map/pallas_call | solution.py:47
  37.0 9.8 %all-to-all-done = f32[32,1,128]{2,1,0:T(1,128)S(1)} async-done(((f32[32,1,128]{2,1,0:T(1,128)}), f32[32,1,128]{2,1,0:T(1,128)S(1)}, u32[]{:S(2)}, u32[]{:S(2)}) %all-to-all-start) | async-done | bytes 16416 | tf_op jit(solution)/shard_map/all_to_all | solution.py:314
  46.9 0.5 shard_map.85
  47.4 1.0 collective-permute-start.3
  48.4 2.0 %shard_map.86.a = f32[4,16,2304]{2,1,0:T(8,128)S(1)} custom-call(bf16[16,128]{1,0:T(8,128)(2,1)S(1)} %get-tuple-element.24.normed, bf16[128,16384]{1,0:T(8,128)(2,1)} %wq.3, bf16[128,2048]{1,0:T(8,128)(2,1)} %wkv.3), custom_call_target="tpu_custom_call" | custom-call | tf_op jit(solution)/shard_map/pallas_call | solution.py:47
  50.4 0.2 collective-permute-start.4
  50.6 2.6 %collective-permute-start.5 = (f32[16,2304]{1,0:T(8,128)S(1)}, f32[16,2304]{1,0:T(8,128)S(1)}, u32[]{:S(2)}, u32[]{:S(2)}) collective-permute-start(f32[16,2304]{1,0:T(8,128)S(1)} %get-tuple-element.28), channel_id=1, source_target_pairs={{0,96},{32,0},{64,32},{96,64},{1,97},{33,1},{65,33},{97,65},{2,98}... | collective-permute-start | bytes 442376 | tf_op jit(solution)/shard_map/ppermute | solution.py:283
  53.2 0.5 collective-permute-start.6
  53.8 3.4 %collective-permute-done.4.b = f32[16,2304]{1,0:T(8,128)S(1)} collective-permute-done((f32[16,2304]{1,0:T(8,128)S(1)}, f32[16,2304]{1,0:T(8,128)S(1)}, u32[]{:S(2)}, u32[]{:S(2)}) %collective-permute-start.4) | collective-permute-done | bytes 147488 | tf_op jit(solution)/shard_map/ppermute | solution.py:283
  57.1 2.0 %collective-permute-done.5.c = f32[16,2304]{1,0:T(8,128)S(1)} collective-permute-done((f32[16,2304]{1,0:T(8,128)S(1)}, f32[16,2304]{1,0:T(8,128)S(1)}, u32[]{:S(2)}, u32[]{:S(2)}) %collective-permute-start.5) | collective-permute-done | bytes 147488 | tf_op jit(solution)/shard_map/ppermute | solution.py:283
  59.1 1.0 collective-permute-done.6.d
  60.1 0.7 shard_map.88
  60.8 4.0 %all-to-all-start.1 = ((f32[16,1,2304]{2,1,0:T(1,128)}), f32[16,1,2304]{2,1,0:T(1,128)S(1)}, u32[]{:S(2)}, u32[]{:S(2)}) async-start(f32[16,1,2304]{2,1,0:T(1,128)} %bitcast.4), calls=%async_computation.1 | async-start | bytes 294912 | tf_op jit(solution)/shard_map/all_to_all | solution.py:291
  64.8 1.5 shard_map.92
  66.3 1.6 %collective-permute-start.10 = (bf16[16,2,32,128]{3,2,1,0:T(8,128)(2,1)S(1)}, bf16[16,2,32,128]{3,2,1,0:T(8,128)(2,1)S(1)}, u32[]{:S(2)}, u32[]{:S(2)}) collective-permute-start(bf16[16,2,32,128]{3,2,1,0:T(8,128)(2,1)S(1)} %get-tuple-element.34), channel_id=1, source_target_pairs={{0,65},{1,64},{32,97},{33,96},{64,1},{65,0},{96,33},{97,32},{2,67}... | collective-permute-start | bytes 786440 | tf_op jit(solution)/shard_map/ppermute | solution.py:379
  67.9 1.9 %collective-permute-start.11 = (bf16[16,2,32,128]{3,2,1,0:T(8,128)(2,1)S(1)}, bf16[16,2,32,128]{3,2,1,0:T(8,128)(2,1)S(1)}, u32[]{:S(2)}, u32[]{:S(2)}) collective-permute-start(bf16[16,2,32,128]{3,2,1,0:T(8,128)(2,1)S(1)} %get-tuple-element.35), channel_id=1, source_target_pairs={{0,33},{1,32},{32,65},{33,64},{64,97},{65,96},{96,1},{97,0},{2,35}... | collective-permute-start | bytes 786440 | tf_op jit(solution)/shard_map/ppermute | solution.py:379
  69.8 1.0 collective-permute-start.12
  70.8 0.3 collective-permute-start.13
  71.1 1.7 %collective-permute-start.9 = (bf16[16,2,32,128]{3,2,1,0:T(8,128)(2,1)S(1)}, bf16[16,2,32,128]{3,2,1,0:T(8,128)(2,1)S(1)}, u32[]{:S(2)}, u32[]{:S(2)}) collective-permute-start(bf16[16,2,32,128]{3,2,1,0:T(8,128)(2,1)S(1)} %get-tuple-element.33), channel_id=1, source_target_pairs={{0,64},{1,65},{32,96},{33,97},{64,0},{65,1},{96,32},{97,33},{2,66}... | collective-permute-start | bytes 786440 | tf_op jit(solution)/shard_map/ppermute | solution.py:379
  72.8 1.8 %shard_map.91 = (bf16[16,2,32,128]{3,2,1,0:T(8,128)(2,1)}, bf16[16,2,32,128]{3,2,1,0:T(8,128)(2,1)}) custom-call(bf16[8,16,2,32,128]{4,3,2,1,0:T(8,128)(2,1)} %cache.3), custom_call_target="tpu_custom_call" | custom-call | tf_op jit(solution)/shard_map/pallas_call | solution.py:47
  74.6 1.8 %collective-permute-done.10.refs_3_ = bf16[16,2,32,128]{3,2,1,0:T(8,128)(2,1)S(1)} collective-permute-done((bf16[16,2,32,128]{3,2,1,0:T(8,128)(2,1)S(1)}, bf16[16,2,32,128]{3,2,1,0:T(8,128)(2,1)S(1)}, u32[]{:S(2)}, u32[]{:S(2)}) %collective-permute-start.10) | collective-permute-done | bytes 262176 | tf_op jit(solution)/shard_map/ppermute | solution.py:379
  76.4 1.1 collective-permute-start.7
  77.4 5.5 %collective-permute-done.11.refs_4_ = bf16[16,2,32,128]{3,2,1,0:T(8,128)(2,1)S(1)} collective-permute-done((bf16[16,2,32,128]{3,2,1,0:T(8,128)(2,1)S(1)}, bf16[16,2,32,128]{3,2,1,0:T(8,128)(2,1)S(1)}, u32[]{:S(2)}, u32[]{:S(2)}) %collective-permute-start.11) | collective-permute-done | bytes 262176 | tf_op jit(solution)/shard_map/ppermute | solution.py:379
  82.9 0.1 fusion.4
  83.0 0.2 shard_map.89
  83.2 22.7 %all_to_all.25.q = bf16[16,16,128]{2,1,0:T(8,128)(2,1)S(1)} all-to-all(bf16[16,16,128]{2,1,0:T(8,128)(2,1)S(1)} %get-tuple-element.30), channel_id=1, replica_groups=mesh['groups'=2,'x'=4,'z'=16,'c'=2] {'z'}, dimensions={0} | all-to-all | bytes 131072 | tf_op jit(solution)/shard_map/all_to_all | solution.py:291
  106.0 1.2 shard_map.93
  107.2 14.9 %all_to_all.26 = f32[16,1,2304]{2,1,0:T(1,128)S(1)} all-to-all(f32[16,1,2304]{2,1,0:T(1,128)S(1)} %bitcast.11), channel_id=1, replica_groups=mesh['groups'=2,'x'=4,'z'=16,'c'=2] {'z'}, dimensions={0} | all-to-all | bytes 294912 | tf_op jit(solution)/shard_map/all_to_all | solution.py:291
  122.1 0.1 shard_map.94
  122.2 16.9 %all_to_all.27.heads = bf16[16,16,128]{2,1,0:T(8,128)(2,1)S(1)} all-to-all(bf16[16,16,128]{2,1,0:T(8,128)(2,1)S(1)} %shard_map.94), channel_id=1, replica_groups=mesh['groups'=2,'x'=4,'z'=16,'c'=2] {'z'}, dimensions={0} | all-to-all | bytes 131072 | tf_op jit(solution)/shard_map/all_to_all | solution.py:291
  139.1 0.1 shard_map.95.a
  139.2 1.4 collective-permute-start.15
  140.6 2.0 %collective-permute-start.16 = (bf16[16,2048]{1,0:T(8,128)(2,1)S(1)}, bf16[16,2048]{1,0:T(8,128)(2,1)S(1)}, u32[]{:S(2)}, u32[]{:S(2)}) collective-permute-start(bf16[16,2048]{1,0:T(8,128)(2,1)S(1)} %shard_map.95.a), channel_id=1, source_target_pairs={{0,32},{32,64},{64,96},{96,0},{1,33},{33,65},{65,97},{97,1},{2,34}... | collective-permute-start | bytes 196616 | tf_op jit(solution)/shard_map/ppermute | solution.py:283
  142.6 1.7 %collective-permute-start.17 = (bf16[16,2048]{1,0:T(8,128)(2,1)S(1)}, bf16[16,2048]{1,0:T(8,128)(2,1)S(1)}, u32[]{:S(2)}, u32[]{:S(2)}) collective-permute-start(bf16[16,2048]{1,0:T(8,128)(2,1)S(1)} %shard_map.95.a), channel_id=1, source_target_pairs={{0,64},{32,96},{64,0},{96,32},{1,65},{33,97},{65,1},{97,33},{2,66}... | collective-permute-start | bytes 196616 | tf_op jit(solution)/shard_map/ppermute | solution.py:283
  144.3 3.6 %collective-permute-start.14 = (bf16[16,2048]{1,0:T(8,128)(2,1)S(1)}, bf16[16,2048]{1,0:T(8,128)(2,1)S(1)}, u32[]{:S(2)}, u32[]{:S(2)}) collective-permute-start(bf16[16,2048]{1,0:T(8,128)(2,1)S(1)} %shard_map.95.a), channel_id=1, source_target_pairs={{0,1},{1,0},{2,3},{3,2},{4,5},{5,4},{6,7},{7,6},{8,9},{9,8},{10,11... | collective-permute-start | bytes 196616 | tf_op jit(solution)/shard_map/ppermute | solution.py:287
  147.9 0.2 collective-permute-start.18
  148.1 1.7 %collective-permute-start.19 = (bf16[16,2048]{1,0:T(8,128)(2,1)S(1)}, bf16[16,2048]{1,0:T(8,128)(2,1)S(1)}, u32[]{:S(2)}, u32[]{:S(2)}) collective-permute-start(bf16[16,2048]{1,0:T(8,128)(2,1)S(1)} %collective-permute-done.16.refs_2_), channel_id=1, source_target_pairs={{0,1},{1,0},{2,3},{3,2},{4,5},{5,4},{6,7},{7,6},{8,9},{9,8},{10,11... | collective-permute-start | bytes 196616 | tf_op jit(solution)/shard_map/ppermute | solution.py:287
  149.9 1.9 %collective-permute-start.20 = (bf16[16,2048]{1,0:T(8,128)(2,1)S(1)}, bf16[16,2048]{1,0:T(8,128)(2,1)S(1)}, u32[]{:S(2)}, u32[]{:S(2)}) collective-permute-start(bf16[16,2048]{1,0:T(8,128)(2,1)S(1)} %collective-permute-done.17.refs_3_), channel_id=1, source_target_pairs={{0,1},{1,0},{2,3},{3,2},{4,5},{5,4},{6,7},{7,6},{8,9},{9,8},{10,11... | collective-permute-start | bytes 196616 | tf_op jit(solution)/shard_map/ppermute | solution.py:287
  151.8 2.3 %shard_map.96 = (f32[16,128]{1,0:T(8,128)S(1)}, bf16[6,2048,128]{2,1,0:T(8,128)(2,1)S(1)}) custom-call(bf16[16,2048]{1,0:T(8,128)(2,1)S(1)} %shard_map.95.a, bf16[16,2048]{1,0:T(8,128)(2,1)S(1)} %collective-permute-done.14.b, bf16[16384,128]{1,0:T(8,128)(2,1)} %wo.1, bf16[16,128]{1,0:T(8,128)(2,1)S(1)} %copy-done.1), custom_call_target="tpu_custom_call" | custom-call | tf_op jit(solution)/shard_map/pallas_call | solution.py:47
  154.1 1.1 shard_map.97
  (31 shorter events, 0.2 us)
Async XLA Ops:
  0.0 0.7 copy-start
  0.8 5.3 %collective-permute-start = (f32[1,128]{1,0:T(1,128)S(1)}, f32[1,128]{1,0:T(1,128)S(1)}, u32[]{:S(2)}, u32[]{:S(2)}) collective-permute-start(f32[1,128]{1,0:T(1,128)S(1)} %shard_map.82.a), channel_id=1, source_target_pairs={{0,32},{32,64},{64,96},{96,0},{1,33},{33,65},{65,97},{97,1},{2,34}... | collective-permute-start | bytes 1544 | tf_op jit(solution)/shard_map/ppermute | solution.py:283
  3.0 3.1 %collective-permute-start.1 = (f32[1,128]{1,0:T(1,128)S(1)}, f32[1,128]{1,0:T(1,128)S(1)}, u32[]{:S(2)}, u32[]{:S(2)}) collective-permute-start(f32[1,128]{1,0:T(1,128)S(1)} %shard_map.82.a), channel_id=1, source_target_pairs={{0,96},{32,0},{64,32},{96,64},{1,97},{33,1},{65,33},{97,65},{2,98}... | collective-permute-start | bytes 1544 | tf_op jit(solution)/shard_map/ppermute | solution.py:283
  4.7 3.9 %collective-permute-start.2 = (f32[1,128]{1,0:T(1,128)S(1)}, f32[1,128]{1,0:T(1,128)S(1)}, u32[]{:S(2)}, u32[]{:S(2)}) collective-permute-start(f32[1,128]{1,0:T(1,128)S(1)} %shard_map.82.a), channel_id=1, source_target_pairs={{0,64},{32,96},{64,0},{96,32},{1,65},{33,97},{65,1},{97,33},{2,66}... | collective-permute-start | bytes 1544 | tf_op jit(solution)/shard_map/ppermute | solution.py:283
  9.2 37.7 %all-to-all-start = ((f32[32,1,128]{2,1,0:T(1,128)}), f32[32,1,128]{2,1,0:T(1,128)S(1)}, u32[]{:S(2)}, u32[]{:S(2)}) async-start(f32[32,1,128]{2,1,0:T(1,128)} %bitcast.1), calls=%async_computation | async-start | bytes 32768 | tf_op jit(solution)/shard_map/all_to_all | solution.py:314
  35.3 11.6 %copy-start.1 = (bf16[16,128]{1,0:T(8,128)(2,1)S(1)}, bf16[16,128]{1,0:T(8,128)(2,1)}, u32[]{:S(2)}) copy-start(bf16[16,128]{1,0:T(8,128)(2,1)} %x.5) | copy-start | bytes 12292
  35.3 11.6 %copy-start.4 = (bf16[128]{0:T(256)(128)(2,1)S(1)}, bf16[128]{0:T(256)(128)(2,1)}, u32[]{:S(2)}) copy-start(bf16[128]{0:T(256)(128)(2,1)} %param.9) | copy-start | bytes 772
  47.4 3.0 %collective-permute-start.3 = (f32[4,16,2304]{2,1,0:T(8,128)S(1)}, f32[4,16,2304]{2,1,0:T(8,128)S(1)}, u32[]{:S(2)}, u32[]{:S(2)}) collective-permute-start(f32[4,16,2304]{2,1,0:T(8,128)S(1)} %get-tuple-element.25), channel_id=1, source_target_pairs={{0,1},{1,0},{2,3},{3,2},{4,5},{5,4},{6,7},{7,6},{8,9},{9,8},{10,11... | collective-permute-start | bytes 1769480 | tf_op jit(solution)/shard_map/ppermute | solution.py:287
  50.3 24.2 %copy-start.3 = (s32[16]{0:T(128)S(1)}, s32[16]{0:T(128)}, u32[]{:S(2)}) copy-start(s32[16]{0:T(128)} %lengths.1) | copy-start | bytes 196
  50.3 55.6 %copy-start.2 = (s32[8,16]{1,0:T(8,128)S(1)}, s32[8,16]{1,0:T(8,128)}, u32[]{:S(2)}) copy-start(s32[8,16]{1,0:T(8,128)} %slabs.1) | copy-start | bytes 1540
  50.4 6.7 %collective-permute-start.4 = (f32[16,2304]{1,0:T(8,128)S(1)}, f32[16,2304]{1,0:T(8,128)S(1)}, u32[]{:S(2)}, u32[]{:S(2)}) collective-permute-start(f32[16,2304]{1,0:T(8,128)S(1)} %get-tuple-element.27), channel_id=1, source_target_pairs={{0,32},{32,64},{64,96},{96,0},{1,33},{33,65},{65,97},{97,1},{2,34}... | collective-permute-start | bytes 442376 | tf_op jit(solution)/shard_map/ppermute | solution.py:283
  50.6 8.5 %collective-permute-start.5 = (f32[16,2304]{1,0:T(8,128)S(1)}, f32[16,2304]{1,0:T(8,128)S(1)}, u32[]{:S(2)}, u32[]{:S(2)}) collective-permute-start(f32[16,2304]{1,0:T(8,128)S(1)} %get-tuple-element.28), channel_id=1, source_target_pairs={{0,96},{32,0},{64,32},{96,64},{1,97},{33,1},{65,33},{97,65},{2,98}... | collective-permute-start | bytes 442376 | tf_op jit(solution)/shard_map/ppermute | solution.py:283
  53.2 6.9 %collective-permute-start.6 = (f32[16,2304]{1,0:T(8,128)S(1)}, f32[16,2304]{1,0:T(8,128)S(1)}, u32[]{:S(2)}, u32[]{:S(2)}) collective-permute-start(f32[16,2304]{1,0:T(8,128)S(1)} %get-tuple-element.29), channel_id=1, source_target_pairs={{0,64},{32,96},{64,0},{96,32},{1,65},{33,97},{65,1},{97,33},{2,66}... | collective-permute-start | bytes 442376 | tf_op jit(solution)/shard_map/ppermute | solution.py:283
  60.8 22.2 %all-to-all-start.1 = ((f32[16,1,2304]{2,1,0:T(1,128)}), f32[16,1,2304]{2,1,0:T(1,128)S(1)}, u32[]{:S(2)}, u32[]{:S(2)}) async-start(f32[16,1,2304]{2,1,0:T(1,128)} %bitcast.4), calls=%async_computation.1 | async-start | bytes 294912 | tf_op jit(solution)/shard_map/all_to_all | solution.py:291
  66.3 10.1 %collective-permute-start.10 = (bf16[16,2,32,128]{3,2,1,0:T(8,128)(2,1)S(1)}, bf16[16,2,32,128]{3,2,1,0:T(8,128)(2,1)S(1)}, u32[]{:S(2)}, u32[]{:S(2)}) collective-permute-start(bf16[16,2,32,128]{3,2,1,0:T(8,128)(2,1)S(1)} %get-tuple-element.34), channel_id=1, source_target_pairs={{0,65},{1,64},{32,97},{33,96},{64,1},{65,0},{96,33},{97,32},{2,67}... | collective-permute-start | bytes 786440 | tf_op jit(solution)/shard_map/ppermute | solution.py:379
  67.9 15.0 %collective-permute-start.11 = (bf16[16,2,32,128]{3,2,1,0:T(8,128)(2,1)S(1)}, bf16[16,2,32,128]{3,2,1,0:T(8,128)(2,1)S(1)}, u32[]{:S(2)}, u32[]{:S(2)}) collective-permute-start(bf16[16,2,32,128]{3,2,1,0:T(8,128)(2,1)S(1)} %get-tuple-element.35), channel_id=1, source_target_pairs={{0,33},{1,32},{32,65},{33,64},{64,97},{65,96},{96,1},{97,0},{2,35}... | collective-permute-start | bytes 786440 | tf_op jit(solution)/shard_map/ppermute | solution.py:379
  69.8 36.1 %collective-permute-start.12 = (bf16[16,2,32,128]{3,2,1,0:T(8,128)(2,1)S(1)}, bf16[16,2,32,128]{3,2,1,0:T(8,128)(2,1)S(1)}, u32[]{:S(2)}, u32[]{:S(2)}) collective-permute-start(bf16[16,2,32,128]{3,2,1,0:T(8,128)(2,1)S(1)} %get-tuple-element.36), channel_id=1, source_target_pairs={{0,97},{1,96},{32,1},{33,0},{64,33},{65,32},{96,65},{97,64},{2,99}... | collective-permute-start | bytes 786440 | tf_op jit(solution)/shard_map/ppermute | solution.py:379
  70.8 35.1 %collective-permute-start.13 = (bf16[16,2,32,128]{3,2,1,0:T(8,128)(2,1)S(1)}, bf16[16,2,32,128]{3,2,1,0:T(8,128)(2,1)S(1)}, u32[]{:S(2)}, u32[]{:S(2)}) collective-permute-start(bf16[16,2,32,128]{3,2,1,0:T(8,128)(2,1)S(1)} %get-tuple-element.37), channel_id=1, source_target_pairs={{0,1},{1,0},{32,33},{33,32},{64,65},{65,64},{96,97},{97,96},{2,3},... | collective-permute-start | bytes 786440 | tf_op jit(solution)/shard_map/ppermute | solution.py:379
  71.1 34.9 %collective-permute-start.9 = (bf16[16,2,32,128]{3,2,1,0:T(8,128)(2,1)S(1)}, bf16[16,2,32,128]{3,2,1,0:T(8,128)(2,1)S(1)}, u32[]{:S(2)}, u32[]{:S(2)}) collective-permute-start(bf16[16,2,32,128]{3,2,1,0:T(8,128)(2,1)S(1)} %get-tuple-element.33), channel_id=1, source_target_pairs={{0,64},{1,65},{32,96},{33,97},{64,0},{65,1},{96,32},{97,33},{2,66}... | collective-permute-start | bytes 786440 | tf_op jit(solution)/shard_map/ppermute | solution.py:379
  76.4 29.6 %collective-permute-start.7 = (bf16[16,2,32,128]{3,2,1,0:T(8,128)(2,1)}, bf16[16,2,32,128]{3,2,1,0:T(8,128)(2,1)S(1)}, u32[]{:S(2)}, u32[]{:S(2)}) collective-permute-start(bf16[16,2,32,128]{3,2,1,0:T(8,128)(2,1)} %get-tuple-element.31), channel_id=1, source_target_pairs={{0,32},{1,33},{32,64},{33,65},{64,96},{65,97},{96,0},{97,1},{2,34}... | collective-permute-start | bytes 786440 | tf_op jit(solution)/shard_map/ppermute | solution.py:379
  82.9 23.1 %collective-permute-start.8 = (bf16[16,2,32,128]{3,2,1,0:T(8,128)(2,1)}, bf16[16,2,32,128]{3,2,1,0:T(8,128)(2,1)S(1)}, u32[]{:S(2)}, u32[]{:S(2)}) collective-permute-start(bf16[16,2,32,128]{3,2,1,0:T(8,128)(2,1)} %get-tuple-element.32), channel_id=1, source_target_pairs={{0,96},{1,97},{32,0},{33,1},{64,32},{65,33},{96,64},{97,65},{2,98}... | collective-permute-start | bytes 786440 | tf_op jit(solution)/shard_map/ppermute | solution.py:379
  139.2 8.7 %collective-permute-start.15 = (bf16[16,2048]{1,0:T(8,128)(2,1)S(1)}, bf16[16,2048]{1,0:T(8,128)(2,1)S(1)}, u32[]{:S(2)}, u32[]{:S(2)}) collective-permute-start(bf16[16,2048]{1,0:T(8,128)(2,1)S(1)} %shard_map.95.a), channel_id=1, source_target_pairs={{0,96},{32,0},{64,32},{96,64},{1,97},{33,1},{65,33},{97,65},{2,98}... | collective-permute-start | bytes 196616 | tf_op jit(solution)/shard_map/ppermute | solution.py:283
  140.6 7.5 %collective-permute-start.16 = (bf16[16,2048]{1,0:T(8,128)(2,1)S(1)}, bf16[16,2048]{1,0:T(8,128)(2,1)S(1)}, u32[]{:S(2)}, u32[]{:S(2)}) collective-permute-start(bf16[16,2048]{1,0:T(8,128)(2,1)S(1)} %shard_map.95.a), channel_id=1, source_target_pairs={{0,32},{32,64},{64,96},{96,0},{1,33},{33,65},{65,97},{97,1},{2,34}... | collective-permute-start | bytes 196616 | tf_op jit(solution)/shard_map/ppermute | solution.py:283
  142.6 7.2 %collective-permute-start.17 = (bf16[16,2048]{1,0:T(8,128)(2,1)S(1)}, bf16[16,2048]{1,0:T(8,128)(2,1)S(1)}, u32[]{:S(2)}, u32[]{:S(2)}) collective-permute-start(bf16[16,2048]{1,0:T(8,128)(2,1)S(1)} %shard_map.95.a), channel_id=1, source_target_pairs={{0,64},{32,96},{64,0},{96,32},{1,65},{33,97},{65,1},{97,33},{2,66}... | collective-permute-start | bytes 196616 | tf_op jit(solution)/shard_map/ppermute | solution.py:283
  144.3 7.5 %collective-permute-start.14 = (bf16[16,2048]{1,0:T(8,128)(2,1)S(1)}, bf16[16,2048]{1,0:T(8,128)(2,1)S(1)}, u32[]{:S(2)}, u32[]{:S(2)}) collective-permute-start(bf16[16,2048]{1,0:T(8,128)(2,1)S(1)} %shard_map.95.a), channel_id=1, source_target_pairs={{0,1},{1,0},{2,3},{3,2},{4,5},{5,4},{6,7},{7,6},{8,9},{9,8},{10,11... | collective-permute-start | bytes 196616 | tf_op jit(solution)/shard_map/ppermute | solution.py:287
  147.9 6.2 %collective-permute-start.18 = (bf16[16,2048]{1,0:T(8,128)(2,1)S(1)}, bf16[16,2048]{1,0:T(8,128)(2,1)S(1)}, u32[]{:S(2)}, u32[]{:S(2)}) collective-permute-start(bf16[16,2048]{1,0:T(8,128)(2,1)S(1)} %collective-permute-done.15.refs_1_), channel_id=1, source_target_pairs={{0,1},{1,0},{2,3},{3,2},{4,5},{5,4},{6,7},{7,6},{8,9},{9,8},{10,11... | collective-permute-start | bytes 196616 | tf_op jit(solution)/shard_map/ppermute | solution.py:287
  148.1 6.0 %collective-permute-start.19 = (bf16[16,2048]{1,0:T(8,128)(2,1)S(1)}, bf16[16,2048]{1,0:T(8,128)(2,1)S(1)}, u32[]{:S(2)}, u32[]{:S(2)}) collective-permute-start(bf16[16,2048]{1,0:T(8,128)(2,1)S(1)} %collective-permute-done.16.refs_2_), channel_id=1, source_target_pairs={{0,1},{1,0},{2,3},{3,2},{4,5},{5,4},{6,7},{7,6},{8,9},{9,8},{10,11... | collective-permute-start | bytes 196616 | tf_op jit(solution)/shard_map/ppermute | solution.py:287
  149.9 4.3 %collective-permute-start.20 = (bf16[16,2048]{1,0:T(8,128)(2,1)S(1)}, bf16[16,2048]{1,0:T(8,128)(2,1)S(1)}, u32[]{:S(2)}, u32[]{:S(2)}) collective-permute-start(bf16[16,2048]{1,0:T(8,128)(2,1)S(1)} %collective-permute-done.17.refs_3_), channel_id=1, source_target_pairs={{0,1},{1,0},{2,3},{3,2},{4,5},{5,4},{6,7},{7,6},{8,9},{9,8},{10,11... | collective-permute-start | bytes 196616 | tf_op jit(solution)/shard_map/ppermute | solution.py:287
